TPU v7x, 128 devices: a whole 4x4x4 slice. The times are simulated.
128 devices in a mesh: blk: 16 (over z_lo, y, core), seq: 8 (over x, z_hi).
Axes of the slice: x: 4, y: 4, z: 4 (z_hi: 2, z_lo: 2; z = z_hi * 2 + z_lo), core: 2. Of those that a mesh axis runs over, the one named last changes fastest.
Arguments:
- layer_input: bfloat16 [16, 1024, 8192], P('blk', 'seq'), may hold values from -6 to 6
- queries: bfloat16 [16, 1024, 4096], P('blk', 'seq'), may hold values from -48 to 48, as said below
- grad_out: bfloat16 [16, 1024, 4096], P('blk', 'seq'), may hold values from -6 to 6
- segment_ids: int32 [16, 1024], P('blk', 'seq'), may hold values from 0 to 3, never falling along the last dimension, each value on 1 to 512 neighbouring positions
- kv_weight: bfloat16 [8192, 1024], P(('blk', 'seq')), may hold values from -0.0625 to 0.0625
- norm_gain: float32 [8192], replicated, may hold values from 0.5 to 1.5
Outputs:
- attended: bfloat16 [16, 1024, 4096], P('blk', 'seq')
- grad_queries: bfloat16 [16, 1024, 4096], P('blk', 'seq')
- grad_input: bfloat16 [16, 1024, 8192], P('blk', 'seq')
- grad_weight: float32 [8192, 1024], P(('blk', 'seq'))
- grad_gain: float32 [8192], replicated
Inputs may be any that keep to these rules, and one draw needn't show every extreme that they name: Projected queries; some rows may be larger than others.
All inputs are finite; a program needn't handle non-finite values.
Results may differ from a plain program's by a relative error of at most 0.02.
The roundings to bfloat16 on the way count: a program that leaves them out, or rounds other values in their place, can miss the bound.
Values may be sent and summed in bfloat16 or wider, within the bound.
No kernel may reach another device: no remote copies, remote signals or barrier semaphores. Data moves between devices by JAX's collectives and lax.ppermute only.
A program may use at most 128 MiB of HBM per device.

v0:
```python
import jax
import jax.numpy as jnp
from jax import lax
from jax.sharding import PartitionSpec as P

HEAD = 128


epsilon = 1e-05


def cut_along(shard, dim, length):
    lengths = shard.shape
    pieces = shard.reshape(*lengths[:dim], length, lengths[dim] // length, *lengths[dim + 1 :])
    return jnp.moveaxis(pieces, dim, 0)


def sum_at_owner(shard, axis, dim):
    length = lax.axis_size(axis)
    pieces = lax.all_to_all(cut_along(shard, dim, length), axis, 0, 0, tiled=True)
    return jnp.sum(pieces, axis=0)


def shards(layer_input, queries, grad_out, segment_ids, kv_weight, norm_gain):
    f32 = jnp.float32
    tok_rows = layer_input.shape[1]
    model_width = layer_input.shape[2]
    seq_devices = lax.axis_size("seq")
    blk_devices = lax.axis_size("blk")
    length = tok_rows * seq_devices
    seq_index = lax.axis_index("seq")
    kv_total = kv_weight.shape[1]
    kv_width = kv_total // 2
    kv_heads = kv_width // HEAD
    query_count = queries.shape[2] // HEAD
    group_size = query_count // kv_heads
    score_scale = HEAD ** (-0.5)
    piece_cols = kv_weight.shape[0]
    source = layer_input[0].astype(f32)
    inv_rms = lax.rsqrt(jnp.mean(source * source, axis=1, keepdims=True) + epsilon)
    scaled = source * inv_rms
    normed = (scaled * norm_gain).astype(jnp.bfloat16)
    split_cols = normed.reshape(tok_rows, blk_devices, seq_devices, piece_cols)
    columns = lax.all_to_all(split_cols, "seq", split_axis=2, concat_axis=0, tiled=True).reshape(
        length, blk_devices * piece_cols
    )
    weight_slab = lax.all_gather(kv_weight, "blk", axis=0, tiled=True)
    query_heads = queries[0].reshape(tok_rows, kv_heads, group_size, HEAD)
    query_pos = seq_index * tok_rows + jnp.arange(tok_rows, dtype=jnp.int32)
    query_doc = segment_ids[0]
    grad_heads = grad_out[0].reshape(tok_rows, kv_heads, group_size, HEAD).transpose(1, 2, 0, 3)

    def scores_of(kv_piece, doc_piece):
        rows_here = kv_piece.shape[0]
        key_heads = kv_piece[:, :kv_width].reshape(rows_here, kv_heads, HEAD)
        raw_scores = (
            jnp.einsum("qgjd,kgd->gjqk", query_heads, key_heads, preferred_element_type=f32)
            * score_scale
        )
        key_pos = jnp.arange(rows_here, dtype=jnp.int32)
        allowed = (key_pos[None, :] <= query_pos[:, None]) & (
            doc_piece[None, :] == query_doc[:, None]
        )
        return (jnp.where(allowed, raw_scores, -1e30), allowed, key_heads)

    stat_shape = (kv_heads, group_size, tok_rows, 1)
    kv_own = sum_at_owner(
        jnp.dot(columns, weight_slab, preferred_element_type=f32), "seq", 0
    ).astype(jnp.bfloat16)
    row_max = jnp.full(stat_shape, -1e30, f32)
    kv_piece = lax.all_gather(kv_own, "seq", axis=0, tiled=True)
    doc_piece = lax.all_gather(query_doc, "seq", axis=0, tiled=True)
    rows_here = kv_piece.shape[0]
    masked, allowed, key_heads = scores_of(kv_piece, doc_piece)
    new_max = jnp.maximum(row_max, jnp.max(masked, axis=-1, keepdims=True))
    expo_terms = jnp.where(allowed, jnp.exp(masked - new_max), 0.0)
    value_heads = kv_piece[:, kv_width:].reshape(rows_here, kv_heads, HEAD)
    weights = expo_terms.astype(jnp.bfloat16)
    weighted = jnp.einsum("gjqk,kgd->gjqd", weights, value_heads, preferred_element_type=f32)
    row_sum = jnp.sum(expo_terms, axis=-1, keepdims=True)
    row_max, row_sum, weighted = (new_max, row_sum, weighted)
    summed = weighted / row_sum
    attended = (
        summed.transpose(2, 0, 1, 3).reshape(tok_rows, query_count * HEAD).astype(jnp.bfloat16)
    )
    log_total = row_max + jnp.log(row_sum)
    attended_heads = attended.reshape(tok_rows, kv_heads, group_size, HEAD).transpose(1, 2, 0, 3)
    row_delta = jnp.sum(grad_heads.astype(f32) * attended_heads.astype(f32), axis=-1, keepdims=True)
    kv_piece = lax.all_gather(kv_own, "seq", axis=0, tiled=True)
    doc_piece = lax.all_gather(query_doc, "seq", axis=0, tiled=True)
    rows_here = kv_piece.shape[0]
    masked, allowed, key_heads = scores_of(kv_piece, doc_piece)
    softmax_probs = jnp.where(allowed, jnp.exp(masked - log_total), 0.0)
    value_heads = kv_piece[:, kv_width:].reshape(rows_here, kv_heads, HEAD)
    grad_probs = jnp.einsum("gjqd,kgd->gjqk", grad_heads, value_heads, preferred_element_type=f32)
    grad_scores = (softmax_probs * (grad_probs - row_delta)).astype(jnp.bfloat16)
    probs_half = softmax_probs.astype(jnp.bfloat16)
    grad_values = jnp.einsum("gjqk,gjqd->kgd", probs_half, grad_heads, preferred_element_type=f32)
    grad_keys = (
        jnp.einsum("gjqk,qgjd->kgd", grad_scores, query_heads, preferred_element_type=f32)
        * score_scale
    )
    grad_query = (
        jnp.einsum("gjqk,kgd->qgjd", grad_scores, key_heads, preferred_element_type=f32)
        * score_scale
    )
    new_rows = jnp.concatenate(
        [grad_keys.reshape(rows_here, kv_width), grad_values.reshape(rows_here, kv_width)], axis=1
    )
    grad_rows = new_rows
    grad_query, grad_rows = (grad_query, grad_rows)
    grad_own = sum_at_owner(grad_rows, "seq", 0).astype(jnp.bfloat16)
    grad_kv = lax.all_gather(grad_own, "seq", axis=0, tiled=True)
    grad_queries = grad_query.reshape(tok_rows, query_count * HEAD).astype(jnp.bfloat16)
    slab_back = lax.all_gather(kv_weight, "blk", axis=0, tiled=True)
    grad_weight = lax.psum_scatter(
        lax.dot_general(columns, grad_kv, (((0,), (0,)), ((), ())), preferred_element_type=f32),
        "blk",
        scatter_dimension=0,
        tiled=True,
    )
    grad_cols = lax.dot_general(
        grad_kv, slab_back, (((1,), (1,)), ((), ())), preferred_element_type=f32
    ).astype(jnp.bfloat16)
    grad_cols = grad_cols.reshape(length, blk_devices, 1, piece_cols)
    grad_normed = lax.all_to_all(grad_cols, "seq", split_axis=0, concat_axis=2, tiled=True).reshape(
        tok_rows, model_width
    )
    grad_norm = grad_normed.astype(f32)
    grad_gain = lax.psum(jnp.sum(grad_norm * scaled, axis=0), ("blk", "seq"))
    grad_hat = grad_norm * norm_gain
    grad_input = inv_rms * (grad_hat - scaled * jnp.mean(grad_hat * scaled, axis=1, keepdims=True))
    return (
        attended[None],
        grad_queries[None],
        grad_input.astype(jnp.bfloat16)[None],
        grad_weight,
        grad_gain,
    )


def solution(mesh):
    in_specs = (
        P("blk", "seq", None),
        P("blk", "seq", None),
        P("blk", "seq", None),
        P("blk", "seq"),
        P(("blk", "seq"), None),
        P(),
    )
    out_specs = (
        P("blk", "seq", None),
        P("blk", "seq", None),
        P("blk", "seq", None),
        P(("blk", "seq"), None),
        P(),
    )
    return jax.shard_map(shards, mesh=mesh, in_specs=in_specs, out_specs=out_specs, check_vma=False)
```

profile of v0, /device:TPU:1, one launch (start us, length us, event | category | flops | bytes accessed | tf_op | source)
XLA Modules:
  0.0 534.0 jit_solution(473694179402004484)
XLA Ops:
  7.2 0.0 all-gather.5.cloned.1.call-start
  7.2 0.7 all-gather.5.cloned.1.call-update
  7.9 0.0 all-gather.7.cloned.1.call-start
  8.0 3.2 copy.148
  11.2 2.2 convert_element_type.140
  13.4 0.1 mul.121
  13.5 1.1 multiply_reduce_fusion.2
  14.6 2.9 multiply_convert_fusion
  17.5 0.2 copy.149
  17.7 38.3 %all_to_all.34 = bf16[128,16,8,64]{0,3,1,2:T(8,128)(2,1)} all-to-all(bf16[128,16,8,64]{0,3,1,2:T(8,128)(2,1)S(1)} %copy.149), channel_id=1, replica_groups=mesh['blk'=16,'seq'=8] {'seq'}, dimensions={2} | all-to-all | bytes 4194304 | tf_op jit(solution)/shard_map/all_to_all | solution.py:44
  56.0 8.3 %all-gather.5.cloned.1.call-done = bf16[1024,1024]{1,0:T(8,128)(2,1)} async-done(((bf16[64,1024]{1,0:T(8,128)(2,1)}), bf16[1024,1024]{1,0:T(8,128)(2,1)}) %all-gather.5.cloned.1.call-update) | async-done | bytes 2097168 | tf_op jit(solution)/shard_map/all_gather | solution.py:47
  64.3 4.6 fusion.22
  68.9 55.1 %all_to_all.35 = f32[8,128,1024]{2,1,0:T(8,128)} all-to-all(f32[8,128,1024]{2,1,0:T(8,128)S(1)} %fusion.22), channel_id=1, replica_groups=mesh['blk'=16,'seq'=8] {'seq'}, dimensions={0} | all-to-all | bytes 8388608 | tf_op jit(solution)/shard_map/all_to_all | solution.py:20
  124.1 3.4 reduce_sum.66
  127.5 0.0 all-gather.9.cloned.1.call-start
  127.6 1.2 copy.192
  128.8 2.3 copy.156
  131.0 17.4 %all-gather = s32[1,1024]{1,0:T(1,128)S(1)} all-gather(s32[1,128]{1,0:T(1,128)S(1)} %copy-done.8), channel_id=2, replica_groups=mesh['blk'=16,'seq'=8] {'seq'}, dimensions={1}, use_global_device_ids=true | all-gather | bytes 4608 | tf_op jit(solution)/shard_map/all_gather | solution.py:72
  148.4 0.2 fusion.29
  148.6 29.9 %all-gather.7.cloned.1.call-done = bf16[1024,1024]{1,0:T(8,128)(2,1)} async-done(((bf16[128,1024]{1,0:T(8,128)(2,1)}), bf16[1024,1024]{1,0:T(8,128)(2,1)}) %all-gather.7.cloned.1.call-update) | async-done | bytes 2097168 | tf_op jit(solution)/shard_map/all_gather | solution.py:71
  178.5 3.0 fusion.32
  181.5 1.5 copy.151
  183.0 9.1 %fusion.33 = (f32[4,8,128]{2,1,0:T(8,128)S(1)}, f32[4,8,128,1024]{2,3,1,0:T(8,128)}) fusion(bf16[1024,4,128,1]{0,2,3,1:T(8,128)(2,1)S(1)} %bitcast.122, bf16[128,4,8,128]{3,2,1,0:T(8,128)(2,1)} %bitcast.124, pred[128,1024]{0,1:T(8,128)(4,1)S(1)} %fusion.29), kind=kOutput, calls=%fused_computation.52 | convolution fusion | flops 1086320640 | bytes 19021824 | tf_op jit(solution)/shard_map/qgjd,kgd->gjqk/dot_general | solution.py:57
  192.1 2.3 copy.154
  194.4 8.7 %fusion.1 = f32[4,8,128]{2,1,0:T(8,128)S(1)} fusion(f32[4,8,128,1024]{2,3,1,0:T(8,128)} %get-tuple-element.45, f32[4,8,128]{2,1,0:T(8,128)S(1)} %broadcast_maximum_fusion, pred[128,1024]{0,1:T(8,128)(4,1)S(1)} %fusion.29), kind=kLoop, calls=%fused_computation.5 | loop fusion | flops 12578816 | bytes 16941056 | tf_op jit(solution)/shard_map/reduce_sum | solution.py:80
  203.1 9.9 %fusion.21 = (bf16[128,4,8,128]{0,3,2,1:T(8,128)(2,1)}, f32[4,8,128,128]{2,3,1,0:T(8,128)S(1)}) fusion(f32[128,4,8]{0,2,1:T(8,128)S(1)} %bitcast.140, bf16[1024,4,128,1]{0,2,3,1:T(8,128)(2,1)S(1)} %bitcast.138, f32[4,8,128,1024]{2,3,1,0:T(8,128)} %get-tuple-element.45, f32[4,8,128]{2,1,0:T(8,128)S(1)} %broadcast_maximum_fusion, ...), kind=kOutput, calls=%fused_computation.32 | convolution fusion | flops 1087373312 | bytes 21135360 | tf_op jit(solution)/shard_map/gjqk,kgd->gjqd/dot_general | solution.py:79
  212.9 0.5 multiply_reduce_fusion.3
  213.4 9.5 %fusion.24 = f32[1024,4,128]{2,0,1:T(8,128)} fusion(bf16[4,8,128,128]{2,3,1,0:T(8,128)(2,1)S(1)} %bitcast.131, f32[4,8,128,1024]{2,3,1,0:T(8,128)} %get-tuple-element.45, f32[4,8,128]{2,1,0:T(8,128)S(1)} %log_add_fusion, pred[128,1024]{0,1:T(8,128)(4,1)S(1)} %fusion.29), kind=kOutput, calls=%fused_computation.39 | convolution fusion | flops 1086324736 | bytes 20070400 | tf_op jit(solution)/shard_map/gjqk,gjqd->kgd/dot_general | solution.py:98
  222.9 10.5 %fusion = bf16[4,8,128,1024]{2,3,1,0:T(8,128)(2,1)} fusion(f32[4,8,128,1024]{2,3,1,0:T(8,128)} %get-tuple-element.45, bf16[1024,4,128,1]{0,2,3,1:T(8,128)(2,1)S(1)} %bitcast.139, bf16[4,8,128,128]{2,3,1,0:T(8,128)(2,1)S(1)} %bitcast.132, f32[4,8,128]{2,1,0:T(8,128)S(1)} %multiply_reduce_fusion.3, f32[4,8,128]{2,1,0:T(8,128)S(1)} %log_add_fusion, ...), kind=kOutput, calls=%fused_computation.1 | convolution fusion | flops 1094713344 | bytes 27426816 | tf_op jit(solution)/shard_map/gjqd,kgd->gjqk/dot_general | solution.py:95
  233.4 2.9 copy.163
  236.4 3.5 copy.194
  239.8 7.1 %fusion.20 = f32[1024,4,128]{2,0,1:T(8,128)} fusion(bf16[4,8,128,1024]{2,3,1,0:T(8,128)(2,1)} %fusion, bf16[128,4,8,128]{3,2,1,0:T(8,128)(2,1)S(1)} %bitcast.125), kind=kOutput, calls=%fused_computation.30 | convolution fusion | flops 1074266112 | bytes 11534336 | tf_op jit(solution)/shard_map/gjqk,qgjd->kgd/dot_general | solution.py:100
  246.9 2.9 copy.161
  249.8 2.2 copy.193
  252.0 0.3 pad_maximum_fusion
  252.3 0.8 copy.164
  253.1 50.9 %all_to_all.36 = f32[8,128,1024]{1,2,0:T(8,128)} all-to-all(f32[8,128,1024]{1,2,0:T(8,128)S(1)} %copy.164), channel_id=1, replica_groups=mesh['blk'=16,'seq'=8] {'seq'}, dimensions={0} | all-to-all | bytes 8388608 | tf_op jit(solution)/shard_map/all_to_all | solution.py:20
  304.1 3.2 reduce_sum.69
  307.3 0.3 reduce-scatter.2.cloned.1.call-start
  307.5 4.7 copy.171
  312.2 51.3 %all-gather.9.cloned.1.call-done = bf16[1024,1024]{0,1:T(8,128)(2,1)} async-done(((bf16[128,1024]{0,1:T(8,128)(2,1)}), bf16[1024,1024]{0,1:T(8,128)(2,1)}) %all-gather.9.cloned.1.call-update) | async-done | bytes 2097168 | tf_op jit(solution)/shard_map/all_gather | solution.py:113
  363.5 6.5 %fusion.17 = f32[1024,1024]{1,0:T(8,128)} fusion(bf16[1024,1024]{0,1:T(8,128)(2,1)} %all-gather.9.cloned.1.call-done, bf16[128,8,8,128]{3,2,1,0:T(8,128)(2,1)} %bitcast.135), kind=kOutput, calls=%fused_computation.26 | convolution fusion | flops 2147483648 | bytes 8388608 | tf_op jit(solution)/shard_map/dot_general | solution.py:117
  370.0 5.9 %convolution_convert_fusion = bf16[1024,1024]{0,1:T(8,128)(2,1)} fusion(bf16[1024,1024]{1,0:T(8,128)(2,1)} %all-gather.5.cloned.1.call-done, bf16[1024,1024]{0,1:T(8,128)(2,1)} %all-gather.9.cloned.1.call-done), kind=kOutput, calls=%fused_computation.38 | convolution fusion | flops 2148532224 | bytes 6291456 | tf_op jit(solution)/shard_map/dot_general | solution.py:122
  375.9 6.2 %copy.166 = bf16[1024,16,1,64]{3,1,2,0:T(8,128)(2,1)} copy(bf16[1024,16,1,64]{0,3,1,2:T(8,128)(2,1)} %bitcast.134) | data formatting | bytes 4194304 | tf_op jit(solution)/shard_map/reshape | solution.py:125
  382.1 7.6 %reshape.223 = bf16[8,2,65536]{2,1,0:T(2,128)(2,1)} reshape(bf16[1024,1,16,64]{3,2,1,0:T(8,128)(2,1)} %bitcast.119) | data formatting | bytes 4194304
  389.7 4.6 all-to-all-start.3
  394.3 1.0 copy.169
  395.4 2.3 copy.173
  397.6 5.6 %multiply_convert_fusion.1 = bf16[4,128,8,128]{3,1,2,0:T(8,128)(2,1)} fusion(bf16[1024,4,128,1]{0,2,3,1:T(8,128)(2,1)S(1)} %bitcast.123, bf16[4,8,128,1024]{2,3,1,0:T(8,128)(2,1)} %fusion), kind=kOutput, calls=%fused_computation.35 | convolution fusion | flops 1074790400 | bytes 10485760 | tf_op jit(solution)/shard_map/gjqk,kgd->qgjd/dot_general | solution.py:104
  403.3 2.3 copy.174
  405.5 22.6 %all-to-all-done.3 = bf16[8,2,65536]{2,1,0:T(2,128)(2,1)} async-done(((bf16[8,2,65536]{2,1,0:T(2,128)(2,1)}), bf16[8,2,65536]{2,1,0:T(2,128)(2,1)}, u32[]{:S(2)}, u32[]{:S(2)}) %all-to-all-start.3) | async-done | bytes 2097184 | tf_op jit(solution)/shard_map/all_to_all | solution.py:126
  428.2 7.4 %reshape.224 = bf16[1024,1,16,64]{3,2,1,0:T(8,128)(2,1)} reshape(bf16[8,2,65536]{2,1,0:T(2,128)(2,1)} %all-to-all-done.3) | data formatting | bytes 4194304
  435.6 5.5 %copy.167 = bf16[1024,16,1,64]{0,3,2,1:T(8,128)(2,1)} copy(bf16[1024,16,1,64]{3,1,2,0:T(8,128)(2,1)} %bitcast.120) | data formatting | bytes 4194304 | tf_op jit(solution)/shard_map/all_to_all | solution.py:126
  441.0 2.1 convert_element_type.146
  443.1 1.0 copy.195
  444.2 0.7 copy.168
  444.9 1.4 copy-done
  446.3 0.1 copy-done.4
  446.4 4.8 multiply_reduce_fusion
  451.3 4.4 fusion.16
  455.7 4.1 copy.175
  459.7 0.2 copy.172
  459.9 0.1 reduce_sum.72
  460.0 67.2 %psum.7 = f32[8192]{0:T(1024)} all-reduce(f32[8192]{0:T(1024)S(1)} %reduce_sum.72), channel_id=1, replica_groups=mesh['blk'=16,'seq'=8] {'blk','seq'}, use_global_device_ids=true, to_apply=%region_9.10 | all-reduce | flops 8192 | bytes 65536 | tf_op jit(solution)/shard_map/psum | solution.py:130
  (25 shorter events, 0.1 us)
Async XLA Ops:
  7.2 57.1 %all-gather.5.cloned.1.call-start = ((), (), s32[]{:S(2)}) async-start(), calls=%async_computation.5 | async-start | bytes 2228224 | tf_op jit(solution)/shard_map/all_gather | solution.py:47
  7.9 5.5 %copy-start.7 = (f32[8192]{0:T(1024)S(1)}, f32[8192]{0:T(1024)}, u32[]{:S(2)}) copy-start(f32[8192]{0:T(1024)} %param.11) | copy-start | bytes 98308
  7.9 170.6 %all-gather.7.cloned.1.call-start = ((), (), s32[]{:S(2)}) async-start(), calls=%async_computation.6 | async-start | bytes 2359296 | tf_op jit(solution)/shard_map/all_gather | solution.py:71
  124.0 3.5 copy-start.5
  124.0 7.0 %copy-start.8 = (s32[1,128]{1,0:T(1,128)S(1)}, s32[1,128]{1,0:T(1,128)}, u32[]{:S(2)}) copy-start(s32[1,128]{1,0:T(1,128)} %param.9) | copy-start | bytes 1540
  127.5 236.0 %all-gather.9.cloned.1.call-start = ((), (), s32[]{:S(2)}) async-start(), calls=%async_computation.7 | async-start | bytes 2359296 | tf_op jit(solution)/shard_map/all_gather | solution.py:113
  194.4 8.7 %copy-start.6 = (bf16[1024,512]{0,1:T(8,128)(2,1)S(1)}, bf16[1024,512]{0,1:T(8,128)(2,1)}, u32[]{:S(2)}) copy-start(bf16[1024,512]{0,1:T(8,128)(2,1)} %copy.154) | copy-start | bytes 3145732
  203.1 9.9 %copy-start.3 = (bf16[1,128,4096]{1,2,0:T(8,128)(2,1)S(1)}, bf16[1,128,4096]{1,2,0:T(8,128)(2,1)}, u32[]{:S(2)}) copy-start(bf16[1,128,4096]{1,2,0:T(8,128)(2,1)} %copy.156) | copy-start | bytes 3145732
  236.4 3.5 copy-start.1
  249.8 2.2 copy-start.2
  307.3 220.0 %reduce-scatter.2.cloned.1.call-start = ((), (), s32[]{:S(2)}) async-start(), calls=%async_computation.8 | async-start | bytes 4456448 | tf_op jit(solution)/shard_map/reduce_scatter | solution.py:116
  389.7 38.5 %all-to-all-start.3 = ((bf16[8,2,65536]{2,1,0:T(2,128)(2,1)}), bf16[8,2,65536]{2,1,0:T(2,128)(2,1)}, u32[]{:S(2)}, u32[]{:S(2)}) async-start(bf16[8,2,65536]{2,1,0:T(2,128)(2,1)} %reshape.223), calls=%async_computation.3 | async-start | bytes 4194304 | tf_op jit(solution)/shard_map/all_to_all | solution.py:126
  444.1 2.2 copy-start
  444.2 2.3 copy-start.4
Sparse Core Ops, SparseCore 0:
  9.7 54.5 all-gather.4
  127.6 50.8 all-gather.6
  307.4 56.0 all-gather.8
  370.2 72.2 reduce-scatter.1
where the time goes:
time: 540 us; the launch traced here: 534 us
  blocking collectives  229 us (42%)
  waiting for transfers between devices  113 us (21%)
  local copies, waits for them, and re-layouts  70.6 us (13%)
  matrix products  68.7 us (13%)
  other arithmetic  33.7 us (6%)
  between operations  14.2 us (3%)
    all_to_all x2, blocking collectives, sum_at_owner(): lax.all_to_all(cut_along(shard, dim, length), axis, 0, 0, tiled=True)  106 us
    psum x1, blocking collectives, shards(): grad_gain = lax.psum(jnp.sum(grad_norm * scaled, axis=0), ('blk', 'seq'))  67.2 us
    all_gather x1, waiting for transfers between devices, shards(): grad_kv = lax.all_gather(grad_own, 'seq', axis=0, tiled=True)  51.3 us
    unnamed x29, local copies, waits for them, and re-layouts  38.6 us
    all_to_all x1, blocking collectives, shards(): lax.all_to_all(split_cols, 'seq', split_axis=2, concat_axis=0, tiled=True)  38.3 us
    all_gather x1, waiting for transfers between devices, shards(): kv_piece = lax.all_gather(kv_own, 'seq', axis=0, tiled=True)  29.9 us
    all_to_all x1, waiting for transfers between devices, shards(): lax.all_to_all(grad_cols, 'seq', split_axis=0, concat_axis=2, tiled=True)  22.6 us
    all_gather x1, blocking collectives, shards(): doc_piece = lax.all_gather(query_doc, 'seq', axis=0, tiled=True)  17.4 us
  transfers between devices with their start and end apart: 5, of which 4 were waited for; matrix products, arithmetic and copies ran while one was open for 15% of the time, Pallas kernels for 0%

commit v1 on v0

v1 whole, which is shorter than its diff:
```python
import jax
import jax.numpy as jnp
from jax import lax
from jax.experimental import pallas as pl
from jax.experimental.pallas import tpu as pltpu
from jax.sharding import Mesh, PartitionSpec as P

HEAD = 128
UNIT = 128
BACK = 4
EPSILON = 1e-05
BF16 = jnp.bfloat16
F32 = jnp.float32
VMEM_LIMIT = 56 * 1024 * 1024

SIZES = {"zlo": 2, "y": 4, "core": 2, "x": 4, "zhi": 2}
BLK = ("zlo", "y", "core")
SEQ = ("x", "zhi")
REL4 = (0, -1, 1, 2)


def shift(value, axis, by):
    n = SIZES[axis]
    return lax.ppermute(value, axis, [(i, (i + by) % n) for i in range(n)])


def shift_seq(value, by):
    n = SIZES["x"] * SIZES["zhi"]
    pairs = [(i, i + by) for i in range(n) if 0 <= i + by < n]
    return lax.ppermute(value, SEQ, pairs)


def rows(pieces):
    return jnp.concatenate(pieces, axis=0)


def ring4(value, axis):
    half = value.shape[0] // 2
    before = shift(value, axis, 1)
    after = shift(value, axis, -1)
    return [value, before, after, shift(before[:half], axis, 1), shift(after[half:], axis, -1)]


def gather_weight(weight):
    other = shift(weight, "zhi", 1)
    unit = jnp.where(
        lax.axis_index("zhi") == 0, rows([weight, other]), rows([other, weight])
    )
    half = unit.shape[1] // 2
    pair = rows([unit, shift(unit, "zlo", 1)])
    left = rows(ring4(pair[:, :half], "y"))
    right = rows(ring4(pair[:, half:], "x"))
    return ring4(left, "x"), ring4(right, "y")


def unit_table():
    zlo, y, x = lax.axis_index("zlo"), lax.axis_index("y"), lax.axis_index("x")
    rel = jnp.array(REL4, jnp.int32)
    zs = (zlo + jnp.arange(2, dtype=jnp.int32)) % 2
    ys, xs = (y + rel) % 4, (x + rel) % 4
    left = (zs[None, None, :] * 4 + ys[None, :, None]) * 4 + xs[:, None, None]
    right = (zs[None, None, :] * 4 + ys[:, None, None]) * 4 + xs[None, :, None]
    return jnp.stack([left, right]).reshape(64).astype(jnp.int32)


PIECES = tuple(
    (side, side * 32 + first, count)
    for side in (0, 1)
    for first, count in ((0, 8), (8, 8), (16, 8), (24, 4), (28, 4))
)


def norm_kernel(core_ref, x_ref, gain_ref, own_ref, send_ref, inv_ref):
    source = x_ref[...].astype(F32)
    inv = lax.rsqrt(jnp.mean(source * source, axis=1, keepdims=True) + EPSILON)
    inv_ref[...] = jnp.broadcast_to(inv, inv_ref.shape)
    first = core_ref[0] == 0
    for u in range(32):
        lo = ((u // 4) * 8 + u % 4) * UNIT
        hi = lo + 4 * UNIT
        parts = []
        for at in (lo, hi):
            part = x_ref[:, at : at + UNIT].astype(F32) * inv * gain_ref[:, at : at + UNIT]
            parts.append(part.astype(BF16))
        own_ref[u] = jnp.where(first, parts[0], parts[1])
        send_ref[u] = jnp.where(first, parts[1], parts[0])


def normalize(core, source, gain):
    tokens, width = source.shape
    step = 32
    return pl.pallas_call(
        norm_kernel,
        grid=(tokens // step,),
        in_specs=[
            pl.BlockSpec(memory_space=pltpu.SMEM),
            pl.BlockSpec((step, width), lambda i: (i, 0)),
            pl.BlockSpec((1, width), lambda i: (0, 0)),
        ],
        out_specs=[
            pl.BlockSpec((32, step, UNIT), lambda i: (0, i, 0)),
            pl.BlockSpec((32, step, UNIT), lambda i: (0, i, 0)),
            pl.BlockSpec((step, UNIT), lambda i: (i, 0)),
        ],
        out_shape=[
            jax.ShapeDtypeStruct((32, tokens, UNIT), BF16),
            jax.ShapeDtypeStruct((32, tokens, UNIT), BF16),
            jax.ShapeDtypeStruct((tokens, UNIT), F32),
        ],
        name="norm",
    )(core, source, gain)


def project_kernel(table_ref, own_ref, other_ref, *refs):
    pieces, (mine_ref, theirs_ref) = refs[:-2], refs[-2:]
    tokens = own_ref.shape[1]
    for side in (0, 1):
        total = None
        for (at_side, first, count), piece in zip(PIECES, pieces):
            if at_side != side:
                continue
            top, low = [], []
            for j in range(count):
                u = table_ref[first + j]
                top.append(own_ref[u])
                low.append(other_ref[u])
            lhs = jnp.concatenate(
                [jnp.concatenate(top, axis=1), jnp.concatenate(low, axis=1)], axis=0
            )
            term = jnp.dot(lhs, piece[...], preferred_element_type=F32)
            total = term if total is None else total + term
        cols = slice(side * total.shape[1], (side + 1) * total.shape[1])
        mine_ref[:, cols] = total[:tokens]
        theirs_ref[:, cols] = total[tokens:]


def project(table, own, other, pieces):
    tokens = own.shape[1]
    width = 2 * pieces[0].shape[1]
    whole = pl.BlockSpec(memory_space=pltpu.VMEM)
    return pl.pallas_call(
        project_kernel,
        in_specs=[pl.BlockSpec(memory_space=pltpu.SMEM)] + [whole] * (2 + len(pieces)),
        out_specs=[whole, whole],
        out_shape=[jax.ShapeDtypeStruct((tokens, width), F32)] * 2,
        compiler_params=pltpu.CompilerParams(vmem_limit_bytes=VMEM_LIMIT),
        name="project",
    )(table, own, other, *pieces)


def attention_kernel(bias_ref, q_ref, go_ref, *refs):
    keys, values = refs[: BACK + 1], refs[BACK + 1 : 2 * BACK + 2]
    att_ref, dq_ref, own_ref = refs[2 * BACK + 2 : 2 * BACK + 5]
    back_refs = refs[2 * BACK + 5 : 3 * BACK + 5]
    probs_ref, grads_ref, q_rows, go_rows = refs[3 * BACK + 5 :]
    head = pl.program_id(0)
    scale = HEAD ** (-0.5)
    group = q_ref.shape[1] // HEAD
    tokens = q_ref.shape[0]
    key = jnp.concatenate([r[...] for r in keys], axis=0)
    value = jnp.concatenate([r[...] for r in values], axis=0)
    key_t = key.astype(F32).T.astype(BF16)
    value_t = value.astype(F32).T.astype(BF16)
    bias = bias_ref[...]
    nt = (((1,), (1,)), ((), ()))
    for j in range(group):
        cols = slice(j * HEAD, (j + 1) * HEAD)
        q = q_ref[:, cols]
        go = go_ref[:, cols]
        q_rows[j * tokens : (j + 1) * tokens, :] = q
        go_rows[j * tokens : (j + 1) * tokens, :] = go
        score = lax.dot_general(key, q, nt, preferred_element_type=F32) * scale + bias
        top = jnp.max(score, axis=0, keepdims=True)
        expo = jnp.exp(score - top)
        total = jnp.sum(expo, axis=0, keepdims=True)
        summed = jnp.dot(value_t, expo.astype(BF16), preferred_element_type=F32) / total
        att = summed.astype(BF16).astype(F32)
        go_t = go.astype(F32).T
        delta = jnp.sum(att * go_t, axis=0, keepdims=True)
        att_ref[:, cols] = att.T.astype(BF16)
        probs = expo * (1.0 / total)
        grad_probs = lax.dot_general(value, go, nt, preferred_element_type=F32)
        grad_scores = (probs * (grad_probs - delta)).astype(BF16)
        probs_ref[:, cols] = probs.astype(BF16)
        grads_ref[:, cols] = grad_scores
        dq = jnp.dot(key_t, grad_scores, preferred_element_type=F32) * scale
        dq_ref[:, cols] = dq.T.astype(BF16)
    grad_key = jnp.dot(grads_ref[...], q_rows[...], preferred_element_type=F32) * scale
    grad_value = jnp.dot(probs_ref[...], go_rows[...], preferred_element_type=F32)
    kv_width = own_ref.shape[1] // 2
    key_at = pl.multiple_of(head * HEAD, HEAD)
    value_at = pl.multiple_of(kv_width + head * HEAD, HEAD)
    own_ref[:, pl.ds(key_at, HEAD)] = grad_key[:tokens]
    own_ref[:, pl.ds(value_at, HEAD)] = grad_value[:tokens]
    for k, ref in enumerate(back_refs):
        at = slice((k + 1) * tokens, (k + 2) * tokens)
        ref[:, pl.ds(key_at, HEAD)] = grad_key[at].astype(BF16)
        ref[:, pl.ds(value_at, HEAD)] = grad_value[at].astype(BF16)


def attention(bias, queries, grad_out, kv_blocks):
    tokens, q_width = queries.shape
    kv_total = kv_blocks[0].shape[1]
    kv_heads = kv_total // 2 // HEAD
    group_cols = q_width // kv_heads
    span = (BACK + 1) * tokens
    q_spec = pl.BlockSpec((tokens, group_cols), lambda h: (0, h))
    key_spec = pl.BlockSpec((tokens, HEAD), lambda h: (0, h))
    value_spec = pl.BlockSpec((tokens, HEAD), lambda h: (0, kv_heads + h))
    grad_spec = pl.BlockSpec((tokens, kv_total), lambda h: (0, 0))
    return pl.pallas_call(
        attention_kernel,
        grid=(kv_heads,),
        in_specs=[pl.BlockSpec((span, tokens), lambda h: (0, 0)), q_spec, q_spec]
        + [key_spec] * (BACK + 1)
        + [value_spec] * (BACK + 1),
        out_specs=[q_spec, q_spec] + [grad_spec] * (BACK + 1),
        out_shape=[
            jax.ShapeDtypeStruct((tokens, q_width), BF16),
            jax.ShapeDtypeStruct((tokens, q_width), BF16),
            jax.ShapeDtypeStruct((tokens, kv_total), F32),
        ]
        + [jax.ShapeDtypeStruct((tokens, kv_total), BF16)] * BACK,
        scratch_shapes=[
            pltpu.VMEM((span, group_cols), BF16),
            pltpu.VMEM((span, group_cols), BF16),
            pltpu.VMEM((tokens * group_cols // HEAD, HEAD), BF16),
            pltpu.VMEM((tokens * group_cols // HEAD, HEAD), BF16),
        ],
        compiler_params=pltpu.CompilerParams(vmem_limit_bytes=VMEM_LIMIT),
        name="attention",
    )(bias, queries, grad_out, *kv_blocks, *kv_blocks)


def grad_normed_kernel(table_ref, mine_ref, theirs_ref, *refs):
    pieces, (own_ref, send_ref, acc_ref) = refs[:-3], refs[-3:]
    tokens = mine_ref.shape[0]
    nt = (((1,), (1,)), ((), ()))
    for (side, first, count), piece in zip(PIECES, pieces):
        width = piece.shape[1]
        cols = slice(side * width, (side + 1) * width)
        lhs = jnp.concatenate([mine_ref[:, cols], theirs_ref[:, cols]], axis=0)
        term = lax.dot_general(lhs, piece[...], nt, preferred_element_type=F32)
        for j in range(count):
            u = table_ref[first + j]
            part = term[:, j * UNIT : (j + 1) * UNIT]
            if side == 0:
                acc_ref[u] = part
            else:
                part = (part + acc_ref[u]).astype(BF16)
                own_ref[u] = part[:tokens]
                send_ref[u] = part[tokens:]


def grad_normed(table, mine, theirs, pieces):
    tokens = mine.shape[0]
    whole = pl.BlockSpec(memory_space=pltpu.VMEM)
    return pl.pallas_call(
        grad_normed_kernel,
        in_specs=[pl.BlockSpec(memory_space=pltpu.SMEM)] + [whole] * (2 + len(pieces)),
        out_specs=[whole, whole],
        out_shape=[jax.ShapeDtypeStruct((32, tokens, UNIT), BF16)] * 2,
        scratch_shapes=[pltpu.VMEM((32, 2 * tokens, UNIT), F32)],
        compiler_params=pltpu.CompilerParams(vmem_limit_bytes=VMEM_LIMIT),
        name="grad_normed",
    )(table, mine, theirs, *pieces)


def norm_back_kernel(core_ref, own_ref, recv_ref, x_ref, inv_ref, gain_ref, out_ref, sum_ref):
    first = core_ref[0] == 0
    inv = inv_ref[:, :1]
    width = x_ref.shape[1]
    step = x_ref.shape[0]

    @pl.when(pl.program_id(0) == 0)
    def _():
        sum_ref[...] = jnp.zeros_like(sum_ref)

    def unit(at):
        u = (at // 8) * 4 + at % 4
        same = first if (at % 8) < 4 else jnp.logical_not(first)
        cols = slice(at * UNIT, (at + 1) * UNIT)
        grad = jnp.where(same, own_ref[u], recv_ref[u]).astype(F32)
        scaled = x_ref[:, cols].astype(F32) * inv
        return cols, grad, scaled

    dots = jnp.zeros((step, UNIT), F32)
    for at in range(width // UNIT):
        cols, grad, scaled = unit(at)
        both = grad * scaled
        sum_ref[:, cols] += jnp.sum(both.reshape(step // 8, 8, UNIT), axis=0)
        dots += both * gain_ref[:, cols]
    mean = jnp.sum(dots, axis=1, keepdims=True) * (1.0 / width)
    for at in range(width // UNIT):
        cols, grad, scaled = unit(at)
        out_ref[:, cols] = (inv * (grad * gain_ref[:, cols] - scaled * mean)).astype(BF16)


def norm_back(core, own, recv, source, inv, gain):
    tokens, width = source.shape
    step = 32
    unit_spec = pl.BlockSpec((32, step, UNIT), lambda i: (0, i, 0))
    return pl.pallas_call(
        norm_back_kernel,
        grid=(tokens // step,),
        in_specs=[
            pl.BlockSpec(memory_space=pltpu.SMEM),
            unit_spec,
            unit_spec,
            pl.BlockSpec((step, width), lambda i: (i, 0)),
            pl.BlockSpec((step, UNIT), lambda i: (i, 0)),
            pl.BlockSpec((1, width), lambda i: (0, 0)),
        ],
        out_specs=[
            pl.BlockSpec((step, width), lambda i: (i, 0)),
            pl.BlockSpec((8, width), lambda i: (0, 0)),
        ],
        out_shape=[
            jax.ShapeDtypeStruct((tokens, width), BF16),
            jax.ShapeDtypeStruct((8, width), F32),
        ],
        name="norm_back",
    )(core, own, recv, source, inv, gain)


def grad_weight_kernel(*refs):
    columns, grads, out_ref = refs[:8], refs[8:16], refs[16]
    grad = jnp.concatenate([g[...] for g in grads], axis=0)
    for j in range(0, columns[0].shape[0], 2):
        lhs = jnp.concatenate(
            [jnp.concatenate([c[j], c[j + 1]], axis=1) for c in columns], axis=0
        )
        part = lax.dot_general(
            lhs, grad, (((0,), (0,)), ((), ())), preferred_element_type=F32
        ).astype(BF16)
        out_ref[j] = part[:UNIT]
        out_ref[j + 1] = part[UNIT:]


def grad_weight_part(columns, grads):
    units, width = columns[0].shape[0], grads[0].shape[1]
    whole = pl.BlockSpec(memory_space=pltpu.VMEM)
    return pl.pallas_call(
        grad_weight_kernel,
        in_specs=[whole] * 16,
        out_specs=whole,
        out_shape=jax.ShapeDtypeStruct((units, UNIT, width), BF16),
        compiler_params=pltpu.CompilerParams(vmem_limit_bytes=VMEM_LIMIT),
        name="grad_weight",
    )(*columns, *grads)


def sum_everywhere(value):
    for axis in ("core", "zlo", "zhi"):
        value = value + shift(value, axis, 1)
    for axis in ("y", "x"):
        value = value + shift(value, axis, 1) + shift(value, axis, 2) + shift(value, axis, 3)
    return value


def shards(layer_input, queries, grad_out, segment_ids, kv_weight, norm_gain):
    source = layer_input[0]
    tokens = source.shape[0]
    core = lax.axis_index("core").astype(jnp.int32)[None]
    place = lax.axis_index("x") * SIZES["zhi"] + lax.axis_index("zhi")
    gain = norm_gain[None]
    table = unit_table()

    doc = segment_ids[0]
    docs = [doc] + [
        jnp.where(place >= k, shift_seq(doc, k), -1) for k in range(1, BACK + 1)
    ]
    local = jnp.arange(tokens, dtype=jnp.int32)
    causal = rows([local] + [jnp.full((tokens,), -1, jnp.int32)] * BACK)
    allowed = (rows(docs)[:, None] == doc[None, :]) & (causal[:, None] <= local[None, :])
    bias = jnp.where(allowed, 0.0, -1e30).astype(F32)

    left, right = gather_weight(kv_weight)
    pieces = left + right
    own, send, inv = normalize(core, source, gain)
    other = shift(send, "core", 1)

    kv_mine, kv_theirs = project(table, own, other, pieces)
    kv_own = (kv_mine + shift(kv_theirs, "core", 1)).astype(BF16)

    def column_block(by):
        at = (lax.axis_index("x") + by) % 4
        return [
            lax.dynamic_index_in_dim(n.reshape(8, 4, tokens, UNIT), at, 1, keepdims=False)
            for n in (own, other)
        ]

    columns = []
    for by in range(4):
        columns += [shift(block, "x", by) if by else block for block in column_block(by)]

    kv_blocks = [kv_own] + [shift_seq(kv_own, k) for k in range(1, BACK + 1)]
    attended, grad_queries, grad_here, *grad_back = attention(
        bias, queries[0], grad_out[0], kv_blocks
    )
    total = grad_here
    for k, part in enumerate(grad_back):
        total = total + shift_seq(part, -(k + 1)).astype(F32)
    grad_own = total.astype(BF16)
    grad_other = shift(grad_own, "core", 1)

    grads = [grad_own, grad_other]
    for by in range(1, 4):
        far = shift(grad_own, "x", by)
        grads += [far, shift(far, "core", 1)]

    mine, theirs = grad_normed(table, grad_own, grad_other, pieces)
    grad_input, gain_rows = norm_back(
        core, mine, shift(theirs, "core", 1), source, inv, gain
    )
    grad_gain = sum_everywhere(jnp.sum(gain_rows, axis=0))

    partial = grad_weight_part(columns, grads).reshape(16, 64, kv_weight.shape[1])
    arrived = lax.all_to_all(partial, ("zlo", "y", "zhi"), 0, 0, tiled=True)
    grad_weight = jnp.sum(arrived.astype(F32), axis=0)
    return attended[None], grad_queries[None], grad_input[None], grad_weight, grad_gain


def solution(mesh):
    fine = Mesh(mesh.devices.reshape(tuple(SIZES.values())), tuple(SIZES))
    tokens = P(BLK, SEQ, None)
    weight = P(BLK + SEQ, None)
    return jax.shard_map(
        shards,
        mesh=fine,
        in_specs=(tokens, tokens, tokens, P(BLK, SEQ), weight, P()),
        out_specs=(tokens, tokens, tokens, weight, P()),
        check_vma=False,
    )
```

time: 540 us -> 271 us (0.50)
  blocking collectives: 229 us -> 0 us
  starting transfers between devices: 4.98 us -> 124 us
  matrix products: 68.7 us -> 0 us
  local copies, waits for them, and re-layouts: 70.6 us -> 16 us
  Pallas kernels: 0 us -> 52 us
  waiting for transfers between devices: 113 us -> 65 us
  other arithmetic: 33.7 us -> 7.21 us
  between operations: 14.2 us -> 1.21 us
    all_to_all x3 -> x0, blocking collectives: 144 us -> none  [the longest x2 106 us: sum_at_owner(): lax.all_to_all(cut_along(shard, dim, length), axis, 0, 0, tiled=True)]
    ppermute x0 -> x55, starting transfers between devices: none -> 120 us  [the longest x43 95.6 us: shift(): return lax.ppermute(value, axis, [(i, (i + by) % n) for i in range(n)])]
    all_gather x3 -> x0, waiting for transfers between devices: 89.5 us -> none  [the longest x1 51.3 us: shards(): grad_kv = lax.all_gather(grad_own, 'seq', axis=0, tiled=True)]
    dot_general x9 -> x0, matrix products: 68.7 us -> none  [the longest x1 10.5 us: shards(): jnp.einsum('gjqd,kgd->gjqk', grad_heads, value_heads, preferred_element_t...]
    psum x1 -> x0, blocking collectives: 67.2 us -> none  [shards(): grad_gain = lax.psum(jnp.sum(grad_norm * scaled, axis=0), ('blk', 'seq'))]
    ppermute x0 -> x55, waiting for transfers between devices: none -> 65 us  [the longest x43 51.2 us: shift(): return lax.ppermute(value, axis, [(i, (i + by) % n) for i in range(n)])]
    pallas_call x0 -> x6, Pallas kernels: none -> 52 us  [the longest x1 21.6 us: attention(): pl.pallas_call(attention_kernel, grid=(kv_heads,), in_specs=[pl.BlockSpec...]
    unnamed x29 -> x63, local copies, waits for them, and re-layouts: 38.6 us -> 6.58 us
  transfers between devices with their start and end apart: 5 -> 56, of which waited for: 4 -> 23; matrix products, arithmetic and copies ran while one was open for 15% -> 7% of each run, Pallas kernels for 0% -> 9%
where the time goes in v1:
time: 271 us; the launch traced here: 266 us
  starting transfers between devices  124 us (46%)
  waiting for transfers between devices  65 us (24%)
  Pallas kernels  52 us (19%)
  local copies, waits for them, and re-layouts  16 us (6%)
  other arithmetic  7.21 us (3%)
    ppermute x43, starting transfers between devices, shift(): return lax.ppermute(value, axis, [(i, (i + by) % n) for i in range(n)])  95.6 us
    ppermute x43, waiting for transfers between devices, shift(): return lax.ppermute(value, axis, [(i, (i + by) % n) for i in range(n)])  51.2 us
    ppermute x12, starting transfers between devices, shift_seq(): return lax.ppermute(value, SEQ, pairs)  24.7 us
    pallas_call x1, Pallas kernels, attention(): pl.pallas_call(attention_kernel, grid=(kv_heads,), in_specs=[pl.BlockSpec...  21.6 us
    ppermute x12, waiting for transfers between devices, shift_seq(): return lax.ppermute(value, SEQ, pairs)  13.8 us
    pallas_call x1, Pallas kernels, grad_normed(): pl.pallas_call(grad_normed_kernel, in_specs=[pl.BlockSpec(memory_space=pl...  7.38 us
    pallas_call x1, Pallas kernels, project(): pl.pallas_call(project_kernel, in_specs=[pl.BlockSpec(memory_space=pltpu....  7.23 us
    unnamed x63, local copies, waits for them, and re-layouts  6.58 us
  transfers between devices with their start and end apart: 56, of which 23 were waited for; matrix products, arithmetic and copies ran while one was open for 7% of the time, Pallas kernels for 9%

profile of v1, /device:TPU:1, one launch (start us, length us, event | category | flops | bytes accessed | tf_op | source)
XLA Modules:
  0.0 265.6 jit_solution(11774226826448476448)
XLA Ops:
  0.6 4.5 %collective-permute-start.5 = (bf16[64,1024]{1,0:T(8,128)(2,1)}, bf16[64,1024]{1,0:T(8,128)(2,1)S(1)}, u32[]{:S(2)}, u32[]{:S(2)}) collective-permute-start(bf16[64,1024]{1,0:T(8,128)(2,1)} %param.11), channel_id=1, source_target_pairs={{0,1},{1,0},{2,3},{3,2},{4,5},{5,4},{6,7},{7,6},{8,9},{9,8},{10,11... | collective-permute-start | bytes 393224 | tf_op jit(solution)/shard_map/ppermute | solution.py:24
  5.1 3.4 %collective-permute-done.5 = bf16[64,1024]{1,0:T(8,128)(2,1)S(1)} collective-permute-done((bf16[64,1024]{1,0:T(8,128)(2,1)}, bf16[64,1024]{1,0:T(8,128)(2,1)S(1)}, u32[]{:S(2)}, u32[]{:S(2)}) %collective-permute-start.5) | collective-permute-done | bytes 131104 | tf_op jit(solution)/shard_map/ppermute | solution.py:24
  10.4 5.9 %collective-permute-done.6 = bf16[128,1024]{1,0:T(8,128)(2,1)S(1)} collective-permute-done((bf16[128,1024]{1,0:T(8,128)(2,1)S(1)}, bf16[128,1024]{1,0:T(8,128)(2,1)S(1)}, u32[]{:S(2)}, u32[]{:S(2)}) %collective-permute-start.6) | collective-permute-done | bytes 262176 | tf_op jit(solution)/shard_map/ppermute | solution.py:24
  18.4 1.5 collective-permute-start.16
  19.9 1.3 collective-permute-start.7
  21.2 1.4 collective-permute-start.8
  22.6 1.6 collective-permute-done.15
  24.3 2.7 %collective-permute-start.18 = (bf16[128,512]{1,0:T(8,128)(2,1)S(1)}, bf16[128,512]{1,0:T(8,128)(2,1)S(1)}, u32[]{:S(2)}, u32[]{:S(2)}) collective-permute-start(bf16[128,512]{1,0:T(8,128)(2,1)S(1)} %slice.47), channel_id=1, source_target_pairs={{0,6},{2,0},{4,2},{6,4},{1,7},{3,1},{5,3},{7,5},{8,14},{10,8},{12,... | collective-permute-start | bytes 393224 | tf_op jit(solution)/shard_map/ppermute | solution.py:24
  27.0 1.4 collective-permute-start.9
  28.4 1.5 collective-permute-start.10
  34.2 2.7 %collective-permute-start.20 = (bf16[1024,512]{1,0:T(8,128)(2,1)}, bf16[1024,512]{1,0:T(8,128)(2,1)S(1)}, u32[]{:S(2)}, u32[]{:S(2)}) collective-permute-start(bf16[1024,512]{1,0:T(8,128)(2,1)} %constant_dynamic-update-slice_fusion.6.refs_5_), channel_id=1, source_target_pairs={{0,48},{16,0},{32,16},{48,32},{1,49},{17,1},{33,17},{49,33},{2,50}... | collective-permute-start | bytes 3145736 | tf_op jit(solution)/shard_map/ppermute | solution.py:24
  38.2 2.7 %collective-permute-start.12 = (bf16[1024,512]{1,0:T(8,128)(2,1)}, bf16[1024,512]{1,0:T(8,128)(2,1)}, u32[]{:S(2)}, u32[]{:S(2)}) collective-permute-start(bf16[1024,512]{1,0:T(8,128)(2,1)} %constant_dynamic-update-slice_fusion.1.refs_0_), channel_id=1, source_target_pairs={{0,6},{2,0},{4,2},{6,4},{1,7},{3,1},{5,3},{7,5},{8,14},{10,8},{12,... | collective-permute-start | bytes 3145736 | tf_op jit(solution)/shard_map/ppermute | solution.py:24
  40.9 4.4 %norm.1 = (bf16[32,128,128]{2,1,0:T(8,128)(2,1)}, bf16[32,128,128]{2,1,0:T(8,128)(2,1)}, f32[128,128]{1,0:T(8,128)}) custom-call(s32[1]{0:T(128)} %bitcast.3.core_ref, bf16[128,8192]{1,0:T(8,128)(2,1)} %bitcast.46, f32[1,8192]{1,0:T(1,128)} %bitcast.51), custom_call_target="tpu_custom_call" | custom-call | tf_op jit(solution)/shard_map/norm/pallas_call | solution.py:92
  45.2 5.1 %collective-permute-start.4 = (bf16[32,128,128]{2,1,0:T(8,128)(2,1)}, bf16[32,128,128]{2,1,0:T(8,128)(2,1)}, u32[]{:S(2)}, u32[]{:S(2)}) collective-permute-start(bf16[32,128,128]{2,1,0:T(8,128)(2,1)} %get-tuple-element.22), channel_id=1, source_target_pairs={{0,8},{8,0},{1,9},{9,1},{2,10},{10,2},{3,11},{11,3},{4,12},{12,4},... | collective-permute-start | bytes 3145736 | tf_op jit(solution)/shard_map/ppermute | solution.py:24
  50.5 5.8 %collective-permute-done.19.refs_6_ = bf16[1024,512]{1,0:T(8,128)(2,1)S(1)} collective-permute-done((bf16[1024,512]{1,0:T(8,128)(2,1)}, bf16[1024,512]{1,0:T(8,128)(2,1)S(1)}, u32[]{:S(2)}, u32[]{:S(2)}) %collective-permute-start.19) | collective-permute-done | bytes 1048608 | tf_op jit(solution)/shard_map/ppermute | solution.py:24
  58.1 2.7 %collective-permute-start.22 = (bf16[512,512]{1,0:T(8,128)(2,1)}, bf16[512,512]{1,0:T(8,128)(2,1)}, u32[]{:S(2)}, u32[]{:S(2)}) collective-permute-start(bf16[512,512]{1,0:T(8,128)(2,1)} %slice.49), channel_id=1, source_target_pairs={{0,48},{16,0},{32,16},{48,32},{1,49},{17,1},{33,17},{49,33},{2,50}... | collective-permute-start | bytes 1572872 | tf_op jit(solution)/shard_map/ppermute | solution.py:24
  61.7 1.9 slice.45
  63.6 2.7 %collective-permute-start.14 = (bf16[512,512]{1,0:T(8,128)(2,1)}, bf16[512,512]{1,0:T(8,128)(2,1)}, u32[]{:S(2)}, u32[]{:S(2)}) collective-permute-start(bf16[512,512]{1,0:T(8,128)(2,1)} %slice.45), channel_id=1, source_target_pairs={{0,6},{2,0},{4,2},{6,4},{1,7},{3,1},{5,3},{7,5},{8,14},{10,8},{12,... | collective-permute-start | bytes 1572872 | tf_op jit(solution)/shard_map/ppermute | solution.py:24
  67.0 3.4 %collective-permute-start = (s32[128]{0:T(128)S(1)}, s32[128]{0:T(128)S(1)}, u32[]{:S(2)}, u32[]{:S(2)}) collective-permute-start(s32[128]{0:T(128)S(1)} %bitcast.53), channel_id=1, source_target_pairs={{0,1},{1,2},{2,3},{3,4},{4,5},{5,6},{6,7},{8,9},{9,10},{10,11},{11... | collective-permute-start | bytes 1544 | tf_op jit(solution)/shard_map/ppermute | solution.py:30
  71.7 4.3 %collective-permute-start.2 = (s32[128]{0:T(128)S(1)}, s32[128]{0:T(128)S(1)}, u32[]{:S(2)}, u32[]{:S(2)}) collective-permute-start(s32[128]{0:T(128)S(1)} %bitcast.55), channel_id=1, source_target_pairs={{0,3},{1,4},{2,5},{3,6},{4,7},{8,11},{9,12},{10,13},{11,14},{12,15... | collective-permute-start | bytes 1544 | tf_op jit(solution)/shard_map/ppermute | solution.py:30
  76.0 1.7 collective-permute-start.3
  77.7 7.2 %project.1 = (f32[128,1024]{1,0:T(8,128)}, f32[128,1024]{1,0:T(8,128)}) custom-call(s32[64]{0:T(128)} %reshape.119.table_ref, bf16[32,128,128]{2,1,0:T(8,128)(2,1)} %get-tuple-element.21.own_ref, bf16[32,128,128]{2,1,0:T(8,128)(2,1)} %collective-permute-done.4.other_ref, bf16[1024,512]{1,0:T(8,128)(2,1)} %constant_dynamic-update-slice_fusion.1.refs_0_, ...), custom_call_target="tpu_custom_call" | custom-call | tf_op jit(solution)/shard_map/project/pallas_call | solution.py:141
  85.0 7.0 %collective-permute-start.23 = (f32[128,1024]{1,0:T(8,128)}, f32[128,1024]{1,0:T(8,128)S(1)}, u32[]{:S(2)}, u32[]{:S(2)}) collective-permute-start(f32[128,1024]{1,0:T(8,128)} %get-tuple-element.24), channel_id=1, source_target_pairs={{0,8},{8,0},{1,9},{9,1},{2,10},{10,2},{3,11},{11,3},{4,12},{12,4},... | collective-permute-start | bytes 1572872 | tf_op jit(solution)/shard_map/ppermute | solution.py:24
  92.0 1.7 collective-permute-done.23
  94.9 4.0 %collective-permute-start.24 = (bf16[128,1024]{1,0:T(8,128)(2,1)S(1)}, bf16[128,1024]{1,0:T(8,128)(2,1)S(1)}, u32[]{:S(2)}, u32[]{:S(2)}) collective-permute-start(bf16[128,1024]{1,0:T(8,128)(2,1)S(1)} %add_convert_fusion.1.refs_0_.refs_5_), channel_id=1, source_target_pairs={{0,1},{1,2},{2,3},{3,4},{4,5},{5,6},{6,7},{8,9},{9,10},{10,11},{11... | collective-permute-start | bytes 786440 | tf_op jit(solution)/shard_map/ppermute | solution.py:30
  98.8 1.3 collective-permute-start.25
  100.2 1.7 collective-permute-start.26
  101.8 2.0 collective-permute-start.27
  105.4 5.6 %collective-permute-done.26.refs_3_.refs_8_ = bf16[128,1024]{1,0:T(8,128)(2,1)S(1)} collective-permute-done((bf16[128,1024]{1,0:T(8,128)(2,1)S(1)}, bf16[128,1024]{1,0:T(8,128)(2,1)S(1)}, u32[]{:S(2)}, u32[]{:S(2)}) %collective-permute-start.26) | collective-permute-done | bytes 262176 | tf_op jit(solution)/shard_map/ppermute | solution.py:30
  111.0 5.6 %collective-permute-done.27.refs_4_.refs_9_ = bf16[128,1024]{1,0:T(8,128)(2,1)S(1)} collective-permute-done((bf16[128,1024]{1,0:T(8,128)(2,1)S(1)}, bf16[128,1024]{1,0:T(8,128)(2,1)S(1)}, u32[]{:S(2)}, u32[]{:S(2)}) %collective-permute-start.27) | collective-permute-done | bytes 262176 | tf_op jit(solution)/shard_map/ppermute | solution.py:30
  117.4 21.6 %attention.1 = (bf16[128,4096]{1,0:T(8,128)(2,1)}, bf16[128,4096]{1,0:T(8,128)(2,1)}, f32[128,1024]{1,0:T(8,128)}, bf16[128,1024]{1,0:T(8,128)(2,1)}, bf16[128,1...) custom-call(f32[640,128]{1,0:T(8,128)} %fusion.1.bias_ref, bf16[128,4096]{1,0:T(8,128)(2,1)} %bitcast.49, ...), custom_call_target="tpu_custom_call" | custom-call | tf_op jit(solution)/shard_map/attention/pallas_call | solution.py:211
  145.0 7.0 %collective-permute-start.34 = (bf16[8,128,128]{2,1,0:T(8,128)(2,1)S(1)}, bf16[8,128,128]{2,1,0:T(8,128)(2,1)S(1)}, u32[]{:S(2)}, u32[]{:S(2)}) collective-permute-start(bf16[8,128,128]{2,1,0:T(8,128)(2,1)S(1)} %get-tuple-element.47), channel_id=1, source_target_pairs={{0,2},{2,4},{4,6},{6,0},{1,3},{3,5},{5,7},{7,1},{8,10},{10,12},{12... | collective-permute-start | bytes 786440 | tf_op jit(solution)/shard_map/ppermute | solution.py:24
  152.0 2.0 dynamic-slice_bitcast_fusion
  154.0 4.2 %collective-permute-start.36 = (bf16[8,128,128]{2,1,0:T(8,128)(2,1)S(1)}, bf16[8,128,128]{2,1,0:T(8,128)(2,1)S(1)}, u32[]{:S(2)}, u32[]{:S(2)}) collective-permute-start(bf16[8,128,128]{2,1,0:T(8,128)(2,1)S(1)} %get-tuple-element.46), channel_id=1, source_target_pairs={{0,4},{2,6},{4,0},{6,2},{1,5},{3,7},{5,1},{7,3},{8,12},{10,14},{12... | collective-permute-start | bytes 786440 | tf_op jit(solution)/shard_map/ppermute | solution.py:24
  158.3 1.5 collective-permute-start.38
  159.9 2.2 collective-permute-start.35
  162.0 1.8 collective-permute-done.31
  163.9 2.8 %collective-permute-start.37 = (bf16[8,128,128]{2,1,0:T(8,128)(2,1)S(1)}, bf16[8,128,128]{2,1,0:T(8,128)(2,1)S(1)}, u32[]{:S(2)}, u32[]{:S(2)}) collective-permute-start(bf16[8,128,128]{2,1,0:T(8,128)(2,1)S(1)} %get-tuple-element.42), channel_id=1, source_target_pairs={{0,4},{2,6},{4,0},{6,2},{1,5},{3,7},{5,1},{7,3},{8,12},{10,14},{12... | collective-permute-start | bytes 786440 | tf_op jit(solution)/shard_map/ppermute | solution.py:24
  166.8 4.0 %collective-permute-done.34.refs_2_ = bf16[8,128,128]{2,1,0:T(8,128)(2,1)S(1)} collective-permute-done((bf16[8,128,128]{2,1,0:T(8,128)(2,1)S(1)}, bf16[8,128,128]{2,1,0:T(8,128)(2,1)S(1)}, u32[]{:S(2)}, u32[]{:S(2)}) %collective-permute-start.34) | collective-permute-done | bytes 262176 | tf_op jit(solution)/shard_map/ppermute | solution.py:24
  170.8 1.7 collective-permute-start.40
  172.6 2.6 collective-permute-done.36.refs_4_
  176.1 6.0 %collective-permute-start.44 = (bf16[128,1024]{1,0:T(8,128)(2,1)S(1)}, bf16[128,1024]{1,0:T(8,128)(2,1)S(1)}, u32[]{:S(2)}, u32[]{:S(2)}) collective-permute-start(bf16[128,1024]{1,0:T(8,128)(2,1)S(1)} %add_convert_fusion.mine_ref.refs_8_), channel_id=1, source_target_pairs={{0,6},{2,0},{4,2},{6,4},{1,7},{3,1},{5,3},{7,5},{8,14},{10,8},{12,... | collective-permute-start | bytes 786440 | tf_op jit(solution)/shard_map/ppermute | solution.py:24
  182.2 2.2 collective-permute-start.39
  184.4 2.0 collective-permute-done.37.refs_5_
  186.4 3.8 %collective-permute-start.32 = (bf16[128,1024]{1,0:T(8,128)(2,1)S(1)}, bf16[128,1024]{1,0:T(8,128)(2,1)S(1)}, u32[]{:S(2)}, u32[]{:S(2)}) collective-permute-start(bf16[128,1024]{1,0:T(8,128)(2,1)S(1)} %add_convert_fusion.mine_ref.refs_8_), channel_id=1, source_target_pairs={{0,8},{8,0},{1,9},{9,1},{2,10},{10,2},{3,11},{11,3},{4,12},{12,4},... | collective-permute-start | bytes 786440 | tf_op jit(solution)/shard_map/ppermute | solution.py:24
  190.2 3.0 %collective-permute-done.40.refs_10_ = bf16[128,1024]{1,0:T(8,128)(2,1)S(1)} collective-permute-done((bf16[128,1024]{1,0:T(8,128)(2,1)S(1)}, bf16[128,1024]{1,0:T(8,128)(2,1)S(1)}, u32[]{:S(2)}, u32[]{:S(2)}) %collective-permute-start.40) | collective-permute-done | bytes 262176 | tf_op jit(solution)/shard_map/ppermute | solution.py:24
  193.2 1.5 collective-permute-start.41
  194.7 3.0 %collective-permute-done.42.refs_12_ = bf16[128,1024]{1,0:T(8,128)(2,1)S(1)} collective-permute-done((bf16[128,1024]{1,0:T(8,128)(2,1)S(1)}, bf16[128,1024]{1,0:T(8,128)(2,1)S(1)}, u32[]{:S(2)}, u32[]{:S(2)}) %collective-permute-start.42) | collective-permute-done | bytes 262176 | tf_op jit(solution)/shard_map/ppermute | solution.py:24
  197.7 2.1 collective-permute-start.43
  202.0 5.8 %grad_weight.1 = bf16[8,128,1024]{2,1,0:T(8,128)(2,1)} custom-call(bf16[8,128,128]{2,1,0:T(8,128)(2,1)} %get-tuple-element.48.refs_0_, bf16[8,128,128]{2,1,0:T(8,128)(2,1)} %get-tuple-element.44.refs_1_, bf16[8,128,128]{2,1,0:T(8,128)(2,1)} %copy-done.13, bf16[8,128,128]{2,1,0:T(8,128)(2,1)} %copy-done.16, bf16[8,128,128]{2,1,0:T(8,128)(2,1)} %copy-done.14, ...), custom_call_target="tpu_custom_call" | custom-call | tf_op jit(solution)/shard_map/grad_weight/pallas_call | solution.py:343
  207.8 3.9 %all-to-all-start = ((bf16[16,64,1024]{2,1,0:T(8,128)(2,1)}), bf16[16,64,1024]{2,1,0:T(8,128)(2,1)S(1)}, u32[]{:S(2)}, u32[]{:S(2)}) async-start(bf16[16,64,1024]{2,1,0:T(8,128)(2,1)} %bitcast.45), calls=%async_computation | async-start | bytes 4194304 | tf_op jit(solution)/shard_map/all_to_all | solution.py:419
  211.7 7.4 %grad_normed.1 = (bf16[32,128,128]{2,1,0:T(8,128)(2,1)}, bf16[32,128,128]{2,1,0:T(8,128)(2,1)}) custom-call(s32[64]{0:T(128)} %reshape.119.table_ref, bf16[128,1024]{1,0:T(8,128)(2,1)} %copy-done.4, bf16[128,1024]{1,0:T(8,128)(2,1)} %copy-done.7, bf16[1024,512]{1,0:T(8,128)(2,1)} %constant_dynamic-update-slice_fusion.1.refs_0_, bf16[1024,512]{1,0:T(8,128)(2,1)} %copy-done.2, ...), custom_call_target="tpu_custom_call" | custom-call | tf_op jit(solution)/shard_map/grad_normed/pallas_call | solution.py:258
  219.5 2.5 collective-permute-done.33.recv_ref
  223.0 5.6 %norm_back.1 = (bf16[128,8192]{1,0:T(8,128)(2,1)}, f32[8,8192]{1,0:T(8,128)}) custom-call(s32[1]{0:T(128)} %bitcast.3.core_ref, bf16[32,128,128]{2,1,0:T(8,128)(2,1)} %get-tuple-element.32.own_ref, bf16[32,128,128]{2,1,0:T(8,128)(2,1)} %copy-done.6, bf16[128,8192]{1,0:T(8,128)(2,1)} %bitcast.47, f32[128,128]{1,0:T(8,128)} %get-tuple-element.34.inv_ref, ...), custom_call_target="tpu_custom_call" | custom-call | tf_op jit(solution)/shard_map/norm_back/pallas_call | solution.py:303
  230.9 1.3 collective-permute-start.47
  232.2 5.1 %collective-permute-done.47 = f32[8192]{0:T(1024)S(1)} collective-permute-done((f32[8192]{0:T(1024)S(1)}, f32[8192]{0:T(1024)S(1)}, u32[]{:S(2)}, u32[]{:S(2)}) %collective-permute-start.47) | collective-permute-done | bytes 32800 | tf_op jit(solution)/shard_map/ppermute | solution.py:24
  237.4 2.4 collective-permute-start.48
  239.7 4.7 %collective-permute-done.48 = f32[8192]{0:T(1024)S(1)} collective-permute-done((f32[8192]{0:T(1024)S(1)}, f32[8192]{0:T(1024)S(1)}, u32[]{:S(2)}, u32[]{:S(2)}) %collective-permute-start.48) | collective-permute-done | bytes 32800 | tf_op jit(solution)/shard_map/ppermute | solution.py:24
  244.4 5.4 %collective-permute-start.49 = (f32[8192]{0:T(1024)S(1)}, f32[8192]{0:T(1024)S(1)}, u32[]{:S(2)}, u32[]{:S(2)}) collective-permute-start(f32[8192]{0:T(1024)S(1)} %add.233), channel_id=1, source_target_pairs={{0,16},{16,32},{32,48},{48,0},{1,17},{17,33},{33,49},{49,1},{2,18}... | collective-permute-start | bytes 98312 | tf_op jit(solution)/shard_map/ppermute | solution.py:24
  250.5 1.9 collective-permute-start.51
  252.3 1.8 collective-permute-done.50
  254.2 5.4 %collective-permute-start.52 = (f32[8192]{0:T(1024)S(1)}, f32[8192]{0:T(1024)S(1)}, u32[]{:S(2)}, u32[]{:S(2)}) collective-permute-start(f32[8192]{0:T(1024)S(1)} %add_add_fusion.1), channel_id=1, source_target_pairs={{0,2},{2,4},{4,6},{6,0},{1,3},{3,5},{5,7},{7,1},{8,10},{10,12},{12... | collective-permute-start | bytes 98312 | tf_op jit(solution)/shard_map/ppermute | solution.py:24
  259.6 2.5 collective-permute-start.54
  262.1 1.8 collective-permute-done.53
  (152 shorter events, 33.4 us)
Async XLA Ops:
  0.6 7.9 %collective-permute-start.5 = (bf16[64,1024]{1,0:T(8,128)(2,1)}, bf16[64,1024]{1,0:T(8,128)(2,1)S(1)}, u32[]{:S(2)}, u32[]{:S(2)}) collective-permute-start(bf16[64,1024]{1,0:T(8,128)(2,1)} %param.11), channel_id=1, source_target_pairs={{0,1},{1,0},{2,3},{3,2},{4,5},{5,4},{6,7},{7,6},{8,9},{9,8},{10,11... | collective-permute-start | bytes 393224 | tf_op jit(solution)/shard_map/ppermute | solution.py:24
  9.6 6.7 %collective-permute-start.6 = (bf16[128,1024]{1,0:T(8,128)(2,1)S(1)}, bf16[128,1024]{1,0:T(8,128)(2,1)S(1)}, u32[]{:S(2)}, u32[]{:S(2)}) collective-permute-start(bf16[128,1024]{1,0:T(8,128)(2,1)S(1)} %maximum_select_fusion), channel_id=1, source_target_pairs={{0,64},{64,0},{1,65},{65,1},{2,66},{66,2},{3,67},{67,3},{4,68},{68... | collective-permute-start | bytes 786440 | tf_op jit(solution)/shard_map/ppermute | solution.py:24
  17.2 7.0 %collective-permute-start.15 = (bf16[256,512]{1,0:T(8,128)(2,1)S(1)}, bf16[256,512]{1,0:T(8,128)(2,1)S(1)}, u32[]{:S(2)}, u32[]{:S(2)}) collective-permute-start(bf16[256,512]{1,0:T(8,128)(2,1)S(1)} %get-tuple-element.38), channel_id=1, source_target_pairs={{0,2},{2,4},{4,6},{6,0},{1,3},{3,5},{5,7},{7,1},{8,10},{10,12},{12... | collective-permute-start | bytes 786440 | tf_op jit(solution)/shard_map/ppermute | solution.py:24
  18.4 5.9 %collective-permute-start.16 = (bf16[256,512]{1,0:T(8,128)(2,1)S(1)}, bf16[256,512]{1,0:T(8,128)(2,1)S(1)}, u32[]{:S(2)}, u32[]{:S(2)}) collective-permute-start(bf16[256,512]{1,0:T(8,128)(2,1)S(1)} %get-tuple-element.38), channel_id=1, source_target_pairs={{0,6},{2,0},{4,2},{6,4},{1,7},{3,1},{5,3},{7,5},{8,14},{10,8},{12,... | collective-permute-start | bytes 786440 | tf_op jit(solution)/shard_map/ppermute | solution.py:24
  19.9 7.1 %collective-permute-start.7 = (bf16[256,512]{1,0:T(8,128)(2,1)S(1)}, bf16[256,512]{1,0:T(8,128)(2,1)S(1)}, u32[]{:S(2)}, u32[]{:S(2)}) collective-permute-start(bf16[256,512]{1,0:T(8,128)(2,1)S(1)} %get-tuple-element.50), channel_id=1, source_target_pairs={{0,16},{16,32},{32,48},{48,0},{1,17},{17,33},{33,49},{49,1},{2,18}... | collective-permute-start | bytes 786440 | tf_op jit(solution)/shard_map/ppermute | solution.py:24
  21.2 7.2 %collective-permute-start.8 = (bf16[256,512]{1,0:T(8,128)(2,1)S(1)}, bf16[256,512]{1,0:T(8,128)(2,1)S(1)}, u32[]{:S(2)}, u32[]{:S(2)}) collective-permute-start(bf16[256,512]{1,0:T(8,128)(2,1)S(1)} %get-tuple-element.50), channel_id=1, source_target_pairs={{0,48},{16,0},{32,16},{48,32},{1,49},{17,1},{33,17},{49,33},{2,50}... | collective-permute-start | bytes 786440 | tf_op jit(solution)/shard_map/ppermute | solution.py:24
  24.2 8.7 %collective-permute-start.17 = (bf16[128,512]{1,0:T(8,128)(2,1)S(1)}, bf16[128,512]{1,0:T(8,128)(2,1)S(1)}, u32[]{:S(2)}, u32[]{:S(2)}) collective-permute-start(bf16[128,512]{1,0:T(8,128)(2,1)S(1)} %slice.46), channel_id=1, source_target_pairs={{0,2},{2,4},{4,6},{6,0},{1,3},{3,5},{5,7},{7,1},{8,10},{10,12},{12... | collective-permute-start | bytes 393224 | tf_op jit(solution)/shard_map/ppermute | solution.py:24
  24.3 9.2 %collective-permute-start.18 = (bf16[128,512]{1,0:T(8,128)(2,1)S(1)}, bf16[128,512]{1,0:T(8,128)(2,1)S(1)}, u32[]{:S(2)}, u32[]{:S(2)}) collective-permute-start(bf16[128,512]{1,0:T(8,128)(2,1)S(1)} %slice.47), channel_id=1, source_target_pairs={{0,6},{2,0},{4,2},{6,4},{1,7},{3,1},{5,3},{7,5},{8,14},{10,8},{12,... | collective-permute-start | bytes 393224 | tf_op jit(solution)/shard_map/ppermute | solution.py:24
  27.0 9.8 %collective-permute-start.9 = (bf16[128,512]{1,0:T(8,128)(2,1)S(1)}, bf16[128,512]{1,0:T(8,128)(2,1)S(1)}, u32[]{:S(2)}, u32[]{:S(2)}) collective-permute-start(bf16[128,512]{1,0:T(8,128)(2,1)S(1)} %slice.42), channel_id=1, source_target_pairs={{0,16},{16,32},{32,48},{48,0},{1,17},{17,33},{33,49},{49,1},{2,18}... | collective-permute-start | bytes 393224 | tf_op jit(solution)/shard_map/ppermute | solution.py:24
  28.4 9.1 %collective-permute-start.10 = (bf16[128,512]{1,0:T(8,128)(2,1)S(1)}, bf16[128,512]{1,0:T(8,128)(2,1)S(1)}, u32[]{:S(2)}, u32[]{:S(2)}) collective-permute-start(bf16[128,512]{1,0:T(8,128)(2,1)S(1)} %slice.43), channel_id=1, source_target_pairs={{0,48},{16,0},{32,16},{48,32},{1,49},{17,1},{33,17},{49,33},{2,50}... | collective-permute-start | bytes 393224 | tf_op jit(solution)/shard_map/ppermute | solution.py:24
  34.2 22.1 %collective-permute-start.19 = (bf16[1024,512]{1,0:T(8,128)(2,1)}, bf16[1024,512]{1,0:T(8,128)(2,1)S(1)}, u32[]{:S(2)}, u32[]{:S(2)}) collective-permute-start(bf16[1024,512]{1,0:T(8,128)(2,1)} %constant_dynamic-update-slice_fusion.6.refs_5_), channel_id=1, source_target_pairs={{0,16},{16,32},{32,48},{48,0},{1,17},{17,33},{33,49},{49,1},{2,18}... | collective-permute-start | bytes 3145736 | tf_op jit(solution)/shard_map/ppermute | solution.py:24
  34.2 23.0 %collective-permute-start.20 = (bf16[1024,512]{1,0:T(8,128)(2,1)}, bf16[1024,512]{1,0:T(8,128)(2,1)S(1)}, u32[]{:S(2)}, u32[]{:S(2)}) collective-permute-start(bf16[1024,512]{1,0:T(8,128)(2,1)} %constant_dynamic-update-slice_fusion.6.refs_5_), channel_id=1, source_target_pairs={{0,48},{16,0},{32,16},{48,32},{1,49},{17,1},{33,17},{49,33},{2,50}... | collective-permute-start | bytes 3145736 | tf_op jit(solution)/shard_map/ppermute | solution.py:24
  38.2 22.6 %collective-permute-start.11 = (bf16[1024,512]{1,0:T(8,128)(2,1)}, bf16[1024,512]{1,0:T(8,128)(2,1)S(1)}, u32[]{:S(2)}, u32[]{:S(2)}) collective-permute-start(bf16[1024,512]{1,0:T(8,128)(2,1)} %constant_dynamic-update-slice_fusion.1.refs_0_), channel_id=1, source_target_pairs={{0,2},{2,4},{4,6},{6,0},{1,3},{3,5},{5,7},{7,1},{8,10},{10,12},{12... | collective-permute-start | bytes 3145736 | tf_op jit(solution)/shard_map/ppermute | solution.py:24
  38.2 23.5 %collective-permute-start.12 = (bf16[1024,512]{1,0:T(8,128)(2,1)}, bf16[1024,512]{1,0:T(8,128)(2,1)}, u32[]{:S(2)}, u32[]{:S(2)}) collective-permute-start(bf16[1024,512]{1,0:T(8,128)(2,1)} %constant_dynamic-update-slice_fusion.1.refs_0_), channel_id=1, source_target_pairs={{0,6},{2,0},{4,2},{6,4},{1,7},{3,1},{5,3},{7,5},{8,14},{10,8},{12,... | collective-permute-start | bytes 3145736 | tf_op jit(solution)/shard_map/ppermute | solution.py:24
  45.2 21.7 %collective-permute-start.4 = (bf16[32,128,128]{2,1,0:T(8,128)(2,1)}, bf16[32,128,128]{2,1,0:T(8,128)(2,1)}, u32[]{:S(2)}, u32[]{:S(2)}) collective-permute-start(bf16[32,128,128]{2,1,0:T(8,128)(2,1)} %get-tuple-element.22), channel_id=1, source_target_pairs={{0,8},{8,0},{1,9},{9,1},{2,10},{10,2},{3,11},{11,3},{4,12},{12,4},... | collective-permute-start | bytes 3145736 | tf_op jit(solution)/shard_map/ppermute | solution.py:24
  57.2 13.2 %collective-permute-start.21 = (bf16[512,512]{1,0:T(8,128)(2,1)}, bf16[512,512]{1,0:T(8,128)(2,1)}, u32[]{:S(2)}, u32[]{:S(2)}) collective-permute-start(bf16[512,512]{1,0:T(8,128)(2,1)} %slice.48), channel_id=1, source_target_pairs={{0,16},{16,32},{32,48},{48,0},{1,17},{17,33},{33,49},{49,1},{2,18}... | collective-permute-start | bytes 1572872 | tf_op jit(solution)/shard_map/ppermute | solution.py:24
  58.1 13.6 %collective-permute-start.22 = (bf16[512,512]{1,0:T(8,128)(2,1)}, bf16[512,512]{1,0:T(8,128)(2,1)}, u32[]{:S(2)}, u32[]{:S(2)}) collective-permute-start(bf16[512,512]{1,0:T(8,128)(2,1)} %slice.49), channel_id=1, source_target_pairs={{0,48},{16,0},{32,16},{48,32},{1,49},{17,1},{33,17},{49,33},{2,50}... | collective-permute-start | bytes 1572872 | tf_op jit(solution)/shard_map/ppermute | solution.py:24
  61.7 14.3 %collective-permute-start.13 = (bf16[512,512]{1,0:T(8,128)(2,1)}, bf16[512,512]{1,0:T(8,128)(2,1)}, u32[]{:S(2)}, u32[]{:S(2)}) collective-permute-start(bf16[512,512]{1,0:T(8,128)(2,1)} %slice.44), channel_id=1, source_target_pairs={{0,2},{2,4},{4,6},{6,0},{1,3},{3,5},{5,7},{7,1},{8,10},{10,12},{12... | collective-permute-start | bytes 1572872 | tf_op jit(solution)/shard_map/ppermute | solution.py:24
  63.6 14.1 %collective-permute-start.14 = (bf16[512,512]{1,0:T(8,128)(2,1)}, bf16[512,512]{1,0:T(8,128)(2,1)}, u32[]{:S(2)}, u32[]{:S(2)}) collective-permute-start(bf16[512,512]{1,0:T(8,128)(2,1)} %slice.45), channel_id=1, source_target_pairs={{0,6},{2,0},{4,2},{6,4},{1,7},{3,1},{5,3},{7,5},{8,14},{10,8},{12,... | collective-permute-start | bytes 1572872 | tf_op jit(solution)/shard_map/ppermute | solution.py:24
  67.0 25.0 %collective-permute-start = (s32[128]{0:T(128)S(1)}, s32[128]{0:T(128)S(1)}, u32[]{:S(2)}, u32[]{:S(2)}) collective-permute-start(s32[128]{0:T(128)S(1)} %bitcast.53), channel_id=1, source_target_pairs={{0,1},{1,2},{2,3},{3,4},{4,5},{5,6},{6,7},{8,9},{9,10},{10,11},{11... | collective-permute-start | bytes 1544 | tf_op jit(solution)/shard_map/ppermute | solution.py:30
  70.4 21.6 %collective-permute-start.1 = (s32[128]{0:T(128)S(1)}, s32[128]{0:T(128)S(1)}, u32[]{:S(2)}, u32[]{:S(2)}) collective-permute-start(s32[128]{0:T(128)S(1)} %bitcast.54), channel_id=1, source_target_pairs={{0,2},{1,3},{2,4},{3,5},{4,6},{5,7},{8,10},{9,11},{10,12},{11,13},... | collective-permute-start | bytes 1544 | tf_op jit(solution)/shard_map/ppermute | solution.py:30
  71.7 20.3 %collective-permute-start.2 = (s32[128]{0:T(128)S(1)}, s32[128]{0:T(128)S(1)}, u32[]{:S(2)}, u32[]{:S(2)}) collective-permute-start(s32[128]{0:T(128)S(1)} %bitcast.55), channel_id=1, source_target_pairs={{0,3},{1,4},{2,5},{3,6},{4,7},{8,11},{9,12},{10,13},{11,14},{12,15... | collective-permute-start | bytes 1544 | tf_op jit(solution)/shard_map/ppermute | solution.py:30
  76.0 27.8 %collective-permute-start.3 = (s32[128]{0:T(128)S(1)}, s32[128]{0:T(128)S(1)}, u32[]{:S(2)}, u32[]{:S(2)}) collective-permute-start(s32[128]{0:T(128)S(1)} %bitcast.56), channel_id=1, source_target_pairs={{0,4},{1,5},{2,6},{3,7},{8,12},{9,13},{10,14},{11,15},{16,20},{17,... | collective-permute-start | bytes 1544 | tf_op jit(solution)/shard_map/ppermute | solution.py:30
  77.7 26.1 %copy-start.25 = (s32[640]{0:T(1024)S(1)}, s32[640]{0:T(1024)}, u32[]{:S(2)}) copy-start(s32[640]{0:T(1024)} %constant.100.clone.1) | copy-start | bytes 7684
  85.0 8.8 %collective-permute-start.23 = (f32[128,1024]{1,0:T(8,128)}, f32[128,1024]{1,0:T(8,128)S(1)}, u32[]{:S(2)}, u32[]{:S(2)}) collective-permute-start(f32[128,1024]{1,0:T(8,128)} %get-tuple-element.24), channel_id=1, source_target_pairs={{0,8},{8,0},{1,9},{9,1},{2,10},{10,2},{3,11},{11,3},{4,12},{12,4},... | collective-permute-start | bytes 1572872 | tf_op jit(solution)/shard_map/ppermute | solution.py:24
  94.8 21.8 %copy-start.5 = (bf16[128,1024]{1,0:T(8,128)(2,1)}, bf16[128,1024]{1,0:T(8,128)(2,1)S(1)}, u32[]{:S(2)}) copy-start(bf16[128,1024]{1,0:T(8,128)(2,1)S(1)} %add_convert_fusion.1.refs_0_.refs_5_) | copy-start | bytes 786436
  94.9 10.0 %collective-permute-start.24 = (bf16[128,1024]{1,0:T(8,128)(2,1)S(1)}, bf16[128,1024]{1,0:T(8,128)(2,1)S(1)}, u32[]{:S(2)}, u32[]{:S(2)}) collective-permute-start(bf16[128,1024]{1,0:T(8,128)(2,1)S(1)} %add_convert_fusion.1.refs_0_.refs_5_), channel_id=1, source_target_pairs={{0,1},{1,2},{2,3},{3,4},{4,5},{5,6},{6,7},{8,9},{9,10},{10,11},{11... | collective-permute-start | bytes 786440 | tf_op jit(solution)/shard_map/ppermute | solution.py:30
  98.8 6.6 %collective-permute-start.25 = (bf16[128,1024]{1,0:T(8,128)(2,1)S(1)}, bf16[128,1024]{1,0:T(8,128)(2,1)S(1)}, u32[]{:S(2)}, u32[]{:S(2)}) collective-permute-start(bf16[128,1024]{1,0:T(8,128)(2,1)S(1)} %add_convert_fusion.1.refs_0_.refs_5_), channel_id=1, source_target_pairs={{0,2},{1,3},{2,4},{3,5},{4,6},{5,7},{8,10},{9,11},{10,12},{11,13},... | collective-permute-start | bytes 786440 | tf_op jit(solution)/shard_map/ppermute | solution.py:30
  100.2 10.9 %collective-permute-start.26 = (bf16[128,1024]{1,0:T(8,128)(2,1)S(1)}, bf16[128,1024]{1,0:T(8,128)(2,1)S(1)}, u32[]{:S(2)}, u32[]{:S(2)}) collective-permute-start(bf16[128,1024]{1,0:T(8,128)(2,1)S(1)} %add_convert_fusion.1.refs_0_.refs_5_), channel_id=1, source_target_pairs={{0,3},{1,4},{2,5},{3,6},{4,7},{8,11},{9,12},{10,13},{11,14},{12,15... | collective-permute-start | bytes 786440 | tf_op jit(solution)/shard_map/ppermute | solution.py:30
  101.8 14.8 %collective-permute-start.27 = (bf16[128,1024]{1,0:T(8,128)(2,1)S(1)}, bf16[128,1024]{1,0:T(8,128)(2,1)S(1)}, u32[]{:S(2)}, u32[]{:S(2)}) collective-permute-start(bf16[128,1024]{1,0:T(8,128)(2,1)S(1)} %add_convert_fusion.1.refs_0_.refs_5_), channel_id=1, source_target_pairs={{0,4},{1,5},{2,6},{3,7},{8,12},{9,13},{10,14},{11,15},{16,20},{17,... | collective-permute-start | bytes 786440 | tf_op jit(solution)/shard_map/ppermute | solution.py:30
  117.4 26.8 %copy-start.3 = (bf16[32,128,128]{2,1,0:T(8,128)(2,1)S(1)}, bf16[32,128,128]{2,1,0:T(8,128)(2,1)}, u32[]{:S(2)}) copy-start(bf16[32,128,128]{2,1,0:T(8,128)(2,1)} %get-tuple-element.21.own_ref) | copy-start | bytes 3145732
  139.0 15.1 %collective-permute-start.28 = (bf16[128,1024]{1,0:T(8,128)(2,1)}, bf16[128,1024]{1,0:T(8,128)(2,1)S(1)}, u32[]{:S(2)}, u32[]{:S(2)}) collective-permute-start(bf16[128,1024]{1,0:T(8,128)(2,1)} %get-tuple-element.28), channel_id=1, source_target_pairs={{1,0},{2,1},{3,2},{4,3},{5,4},{6,5},{7,6},{9,8},{10,9},{11,10},{12... | collective-permute-start | bytes 786440 | tf_op jit(solution)/shard_map/ppermute | solution.py:30
  140.3 18.0 %collective-permute-start.29 = (bf16[128,1024]{1,0:T(8,128)(2,1)}, bf16[128,1024]{1,0:T(8,128)(2,1)S(1)}, u32[]{:S(2)}, u32[]{:S(2)}) collective-permute-start(bf16[128,1024]{1,0:T(8,128)(2,1)} %get-tuple-element.29), channel_id=1, source_target_pairs={{2,0},{3,1},{4,2},{5,3},{6,4},{7,5},{10,8},{11,9},{12,10},{13,11},... | collective-permute-start | bytes 786440 | tf_op jit(solution)/shard_map/ppermute | solution.py:30
  141.6 18.3 %collective-permute-start.30 = (bf16[128,1024]{1,0:T(8,128)(2,1)}, bf16[128,1024]{1,0:T(8,128)(2,1)S(1)}, u32[]{:S(2)}, u32[]{:S(2)}) collective-permute-start(bf16[128,1024]{1,0:T(8,128)(2,1)} %get-tuple-element.30), channel_id=1, source_target_pairs={{3,0},{4,1},{5,2},{6,3},{7,4},{11,8},{12,9},{13,10},{14,11},{15,12... | collective-permute-start | bytes 786440 | tf_op jit(solution)/shard_map/ppermute | solution.py:30
  142.9 21.0 %collective-permute-start.31 = (bf16[128,1024]{1,0:T(8,128)(2,1)}, bf16[128,1024]{1,0:T(8,128)(2,1)S(1)}, u32[]{:S(2)}, u32[]{:S(2)}) collective-permute-start(bf16[128,1024]{1,0:T(8,128)(2,1)} %get-tuple-element.31), channel_id=1, source_target_pairs={{4,0},{5,1},{6,2},{7,3},{12,8},{13,9},{14,10},{15,11},{20,16},{21,... | collective-permute-start | bytes 786440 | tf_op jit(solution)/shard_map/ppermute | solution.py:30
  144.2 22.4 %copy-start.12 = (f32[128,1024]{1,0:T(8,128)S(1)}, f32[128,1024]{1,0:T(8,128)}, u32[]{:S(2)}) copy-start(f32[128,1024]{1,0:T(8,128)} %get-tuple-element.27) | copy-start | bytes 1572868
  145.0 25.8 %collective-permute-start.34 = (bf16[8,128,128]{2,1,0:T(8,128)(2,1)S(1)}, bf16[8,128,128]{2,1,0:T(8,128)(2,1)S(1)}, u32[]{:S(2)}, u32[]{:S(2)}) collective-permute-start(bf16[8,128,128]{2,1,0:T(8,128)(2,1)S(1)} %get-tuple-element.47), channel_id=1, source_target_pairs={{0,2},{2,4},{4,6},{6,0},{1,3},{3,5},{5,7},{7,1},{8,10},{10,12},{12... | collective-permute-start | bytes 786440 | tf_op jit(solution)/shard_map/ppermute | solution.py:24
  154.0 21.1 %collective-permute-start.36 = (bf16[8,128,128]{2,1,0:T(8,128)(2,1)S(1)}, bf16[8,128,128]{2,1,0:T(8,128)(2,1)S(1)}, u32[]{:S(2)}, u32[]{:S(2)}) collective-permute-start(bf16[8,128,128]{2,1,0:T(8,128)(2,1)S(1)} %get-tuple-element.46), channel_id=1, source_target_pairs={{0,4},{2,6},{4,0},{6,2},{1,5},{3,7},{5,1},{7,3},{8,12},{10,14},{12... | collective-permute-start | bytes 786440 | tf_op jit(solution)/shard_map/ppermute | solution.py:24
  158.3 17.9 %collective-permute-start.38 = (bf16[8,128,128]{2,1,0:T(8,128)(2,1)S(1)}, bf16[8,128,128]{2,1,0:T(8,128)(2,1)S(1)}, u32[]{:S(2)}, u32[]{:S(2)}) collective-permute-start(bf16[8,128,128]{2,1,0:T(8,128)(2,1)S(1)} %get-tuple-element.45), channel_id=1, source_target_pairs={{0,6},{2,0},{4,2},{6,4},{1,7},{3,1},{5,3},{7,5},{8,14},{10,8},{12,... | collective-permute-start | bytes 786440 | tf_op jit(solution)/shard_map/ppermute | solution.py:24
  159.9 22.3 %collective-permute-start.35 = (bf16[8,128,128]{2,1,0:T(8,128)(2,1)S(1)}, bf16[8,128,128]{2,1,0:T(8,128)(2,1)S(1)}, u32[]{:S(2)}, u32[]{:S(2)}) collective-permute-start(bf16[8,128,128]{2,1,0:T(8,128)(2,1)S(1)} %get-tuple-element.43), channel_id=1, source_target_pairs={{0,2},{2,4},{4,6},{6,0},{1,3},{3,5},{5,7},{7,1},{8,10},{10,12},{12... | collective-permute-start | bytes 786440 | tf_op jit(solution)/shard_map/ppermute | solution.py:24
  163.9 22.6 %collective-permute-start.37 = (bf16[8,128,128]{2,1,0:T(8,128)(2,1)S(1)}, bf16[8,128,128]{2,1,0:T(8,128)(2,1)S(1)}, u32[]{:S(2)}, u32[]{:S(2)}) collective-permute-start(bf16[8,128,128]{2,1,0:T(8,128)(2,1)S(1)} %get-tuple-element.42), channel_id=1, source_target_pairs={{0,4},{2,6},{4,0},{6,2},{1,5},{3,7},{5,1},{7,3},{8,12},{10,14},{12... | collective-permute-start | bytes 786440 | tf_op jit(solution)/shard_map/ppermute | solution.py:24
  166.8 34.5 %copy-start.4 = (bf16[128,1024]{1,0:T(8,128)(2,1)}, bf16[128,1024]{1,0:T(8,128)(2,1)S(1)}, u32[]{:S(2)}) copy-start(bf16[128,1024]{1,0:T(8,128)(2,1)S(1)} %add_convert_fusion.mine_ref.refs_8_) | copy-start | bytes 786436
  170.8 30.5 %copy-start.13 = (bf16[8,128,128]{2,1,0:T(8,128)(2,1)}, bf16[8,128,128]{2,1,0:T(8,128)(2,1)S(1)}, u32[]{:S(2)}) copy-start(bf16[8,128,128]{2,1,0:T(8,128)(2,1)S(1)} %collective-permute-done.34.refs_2_) | copy-start | bytes 786436
  170.8 22.4 %collective-permute-start.40 = (bf16[128,1024]{1,0:T(8,128)(2,1)S(1)}, bf16[128,1024]{1,0:T(8,128)(2,1)S(1)}, u32[]{:S(2)}, u32[]{:S(2)}) collective-permute-start(bf16[128,1024]{1,0:T(8,128)(2,1)S(1)} %add_convert_fusion.mine_ref.refs_8_), channel_id=1, source_target_pairs={{0,2},{2,4},{4,6},{6,0},{1,3},{3,5},{5,7},{7,1},{8,10},{10,12},{12... | collective-permute-start | bytes 786440 | tf_op jit(solution)/shard_map/ppermute | solution.py:24
  175.1 26.1 %copy-start.14 = (bf16[8,128,128]{2,1,0:T(8,128)(2,1)}, bf16[8,128,128]{2,1,0:T(8,128)(2,1)S(1)}, u32[]{:S(2)}) copy-start(bf16[8,128,128]{2,1,0:T(8,128)(2,1)S(1)} %collective-permute-done.36.refs_4_) | copy-start | bytes 786436
  175.1 22.5 %collective-permute-start.42 = (bf16[128,1024]{1,0:T(8,128)(2,1)S(1)}, bf16[128,1024]{1,0:T(8,128)(2,1)S(1)}, u32[]{:S(2)}, u32[]{:S(2)}) collective-permute-start(bf16[128,1024]{1,0:T(8,128)(2,1)S(1)} %add_convert_fusion.mine_ref.refs_8_), channel_id=1, source_target_pairs={{0,4},{2,6},{4,0},{6,2},{1,5},{3,7},{5,1},{7,3},{8,12},{10,14},{12... | collective-permute-start | bytes 786440 | tf_op jit(solution)/shard_map/ppermute | solution.py:24
  176.1 25.2 %copy-start.15 = (bf16[8,128,128]{2,1,0:T(8,128)(2,1)}, bf16[8,128,128]{2,1,0:T(8,128)(2,1)S(1)}, u32[]{:S(2)}) copy-start(bf16[8,128,128]{2,1,0:T(8,128)(2,1)S(1)} %collective-permute-done.38.refs_6_) | copy-start | bytes 786436
  176.1 23.6 %collective-permute-start.44 = (bf16[128,1024]{1,0:T(8,128)(2,1)S(1)}, bf16[128,1024]{1,0:T(8,128)(2,1)S(1)}, u32[]{:S(2)}, u32[]{:S(2)}) collective-permute-start(bf16[128,1024]{1,0:T(8,128)(2,1)S(1)} %add_convert_fusion.mine_ref.refs_8_), channel_id=1, source_target_pairs={{0,6},{2,0},{4,2},{6,4},{1,7},{3,1},{5,3},{7,5},{8,14},{10,8},{12,... | collective-permute-start | bytes 786440 | tf_op jit(solution)/shard_map/ppermute | solution.py:24
  182.2 17.6 %collective-permute-start.39 = (bf16[8,128,128]{2,1,0:T(8,128)(2,1)S(1)}, bf16[8,128,128]{2,1,0:T(8,128)(2,1)S(1)}, u32[]{:S(2)}, u32[]{:S(2)}) collective-permute-start(bf16[8,128,128]{2,1,0:T(8,128)(2,1)S(1)} %get-tuple-element.41), channel_id=1, source_target_pairs={{0,6},{2,0},{4,2},{6,4},{1,7},{3,1},{5,3},{7,5},{8,14},{10,8},{12,... | collective-permute-start | bytes 786440 | tf_op jit(solution)/shard_map/ppermute | solution.py:24
  186.4 13.4 %collective-permute-start.32 = (bf16[128,1024]{1,0:T(8,128)(2,1)S(1)}, bf16[128,1024]{1,0:T(8,128)(2,1)S(1)}, u32[]{:S(2)}, u32[]{:S(2)}) collective-permute-start(bf16[128,1024]{1,0:T(8,128)(2,1)S(1)} %add_convert_fusion.mine_ref.refs_8_), channel_id=1, source_target_pairs={{0,8},{8,0},{1,9},{9,1},{2,10},{10,2},{3,11},{11,3},{4,12},{12,4},... | collective-permute-start | bytes 786440 | tf_op jit(solution)/shard_map/ppermute | solution.py:24
  193.2 6.7 %collective-permute-start.41 = (bf16[128,1024]{1,0:T(8,128)(2,1)S(1)}, bf16[128,1024]{1,0:T(8,128)(2,1)S(1)}, u32[]{:S(2)}, u32[]{:S(2)}) collective-permute-start(bf16[128,1024]{1,0:T(8,128)(2,1)S(1)} %collective-permute-done.40.refs_10_), channel_id=1, source_target_pairs={{0,8},{8,0},{1,9},{9,1},{2,10},{10,2},{3,11},{11,3},{4,12},{12,4},... | collective-permute-start | bytes 786440 | tf_op jit(solution)/shard_map/ppermute | solution.py:24
  197.7 3.2 %collective-permute-start.43 = (bf16[128,1024]{1,0:T(8,128)(2,1)S(1)}, bf16[128,1024]{1,0:T(8,128)(2,1)S(1)}, u32[]{:S(2)}, u32[]{:S(2)}) collective-permute-start(bf16[128,1024]{1,0:T(8,128)(2,1)S(1)} %collective-permute-done.42.refs_12_), channel_id=1, source_target_pairs={{0,8},{8,0},{1,9},{9,1},{2,10},{10,2},{3,11},{11,3},{4,12},{12,4},... | collective-permute-start | bytes 786440 | tf_op jit(solution)/shard_map/ppermute | solution.py:24
  199.7 1.5 collective-permute-start.45
  207.8 56.7 %all-to-all-start = ((bf16[16,64,1024]{2,1,0:T(8,128)(2,1)}), bf16[16,64,1024]{2,1,0:T(8,128)(2,1)S(1)}, u32[]{:S(2)}, u32[]{:S(2)}) async-start(bf16[16,64,1024]{2,1,0:T(8,128)(2,1)} %bitcast.45), calls=%async_computation | async-start | bytes 4194304 | tf_op jit(solution)/shard_map/all_to_all | solution.py:419
  219.1 2.9 %collective-permute-start.33 = (bf16[32,128,128]{2,1,0:T(8,128)(2,1)}, bf16[32,128,128]{2,1,0:T(8,128)(2,1)S(1)}, u32[]{:S(2)}, u32[]{:S(2)}) collective-permute-start(bf16[32,128,128]{2,1,0:T(8,128)(2,1)} %get-tuple-element.33), channel_id=1, source_target_pairs={{0,8},{8,0},{1,9},{9,1},{2,10},{10,2},{3,11},{11,3},{4,12},{12,4},... | collective-permute-start | bytes 3145736 | tf_op jit(solution)/shard_map/ppermute | solution.py:24
  229.6 1.3 collective-permute-start.46
  230.9 6.5 %collective-permute-start.47 = (f32[8192]{0:T(1024)S(1)}, f32[8192]{0:T(1024)S(1)}, u32[]{:S(2)}, u32[]{:S(2)}) collective-permute-start(f32[8192]{0:T(1024)S(1)} %add.231), channel_id=1, source_target_pairs={{0,64},{64,0},{1,65},{65,1},{2,66},{66,2},{3,67},{67,3},{4,68},{68... | collective-permute-start | bytes 98312 | tf_op jit(solution)/shard_map/ppermute | solution.py:24
  237.4 7.1 %collective-permute-start.48 = (f32[8192]{0:T(1024)S(1)}, f32[8192]{0:T(1024)S(1)}, u32[]{:S(2)}, u32[]{:S(2)}) collective-permute-start(f32[8192]{0:T(1024)S(1)} %add.232), channel_id=1, source_target_pairs={{0,1},{1,0},{2,3},{3,2},{4,5},{5,4},{6,7},{7,6},{8,9},{9,8},{10,11... | collective-permute-start | bytes 98312 | tf_op jit(solution)/shard_map/ppermute | solution.py:24
  244.4 7.9 %collective-permute-start.49 = (f32[8192]{0:T(1024)S(1)}, f32[8192]{0:T(1024)S(1)}, u32[]{:S(2)}, u32[]{:S(2)}) collective-permute-start(f32[8192]{0:T(1024)S(1)} %add.233), channel_id=1, source_target_pairs={{0,16},{16,32},{32,48},{48,0},{1,17},{17,33},{33,49},{49,1},{2,18}... | collective-permute-start | bytes 98312 | tf_op jit(solution)/shard_map/ppermute | solution.py:24
  249.8 4.3 %collective-permute-start.50 = (f32[8192]{0:T(1024)S(1)}, f32[8192]{0:T(1024)S(1)}, u32[]{:S(2)}, u32[]{:S(2)}) collective-permute-start(f32[8192]{0:T(1024)S(1)} %add.233), channel_id=1, source_target_pairs={{0,32},{16,48},{32,0},{48,16},{1,33},{17,49},{33,1},{49,17},{2,34}... | collective-permute-start | bytes 98312 | tf_op jit(solution)/shard_map/ppermute | solution.py:24
  250.5 3.7 %collective-permute-start.51 = (f32[8192]{0:T(1024)S(1)}, f32[8192]{0:T(1024)S(1)}, u32[]{:S(2)}, u32[]{:S(2)}) collective-permute-start(f32[8192]{0:T(1024)S(1)} %add.233), channel_id=1, source_target_pairs={{0,48},{16,0},{32,16},{48,32},{1,49},{17,1},{33,17},{49,33},{2,50}... | collective-permute-start | bytes 98312 | tf_op jit(solution)/shard_map/ppermute | solution.py:24
  254.2 7.9 %collective-permute-start.52 = (f32[8192]{0:T(1024)S(1)}, f32[8192]{0:T(1024)S(1)}, u32[]{:S(2)}, u32[]{:S(2)}) collective-permute-start(f32[8192]{0:T(1024)S(1)} %add_add_fusion.1), channel_id=1, source_target_pairs={{0,2},{2,4},{4,6},{6,0},{1,3},{3,5},{5,7},{7,1},{8,10},{10,12},{12... | collective-permute-start | bytes 98312 | tf_op jit(solution)/shard_map/ppermute | solution.py:24
  259.6 4.3 %collective-permute-start.53 = (f32[8192]{0:T(1024)S(1)}, f32[8192]{0:T(1024)S(1)}, u32[]{:S(2)}, u32[]{:S(2)}) collective-permute-start(f32[8192]{0:T(1024)S(1)} %add_add_fusion.1), channel_id=1, source_target_pairs={{0,4},{2,6},{4,0},{6,2},{1,5},{3,7},{5,1},{7,3},{8,12},{10,14},{12... | collective-permute-start | bytes 98312 | tf_op jit(solution)/shard_map/ppermute | solution.py:24
  259.6 4.3 %collective-permute-start.54 = (f32[8192]{0:T(1024)S(1)}, f32[8192]{0:T(1024)S(1)}, u32[]{:S(2)}, u32[]{:S(2)}) collective-permute-start(f32[8192]{0:T(1024)S(1)} %add_add_fusion.1), channel_id=1, source_target_pairs={{0,6},{2,0},{4,2},{6,4},{1,7},{3,1},{5,3},{7,5},{8,14},{10,8},{12,... | collective-permute-start | bytes 98312 | tf_op jit(solution)/shard_map/ppermute | solution.py:24
  (20 other events, 163.9 us)

commit v2 on v1

--- a/solution.py
+++ b/solution.py
@@ -4,6 +4,7 @@
 from jax.experimental import pallas as pl
 from jax.experimental.pallas import tpu as pltpu
 from jax.sharding import Mesh, PartitionSpec as P
+
 
 HEAD = 128
 UNIT = 128
@@ -41,16 +42,60 @@
     return [value, before, after, shift(before[:half], axis, 1), shift(after[half:], axis, -1)]
 
 
+def ring4_halves(first, second, axis):
+    before_first = shift(first, axis, 1)
+    after_second = shift(second, axis, -1)
+    before_second = shift(second, axis, 1)
+    after_first = shift(first, axis, -1)
+    far_first = shift(before_first, axis, 1)
+    far_second = shift(after_second, axis, -1)
+    near = [first, second, before_first, before_second, after_first, after_second]
+    return near, [far_first, far_second]
+
+
+def join_kernel(*refs):
+    pieces, (first_ref, second_ref, sems) = refs[:5], refs[5:]
+    size = pieces[0].shape[0]
+    copies = []
+    for i, piece in enumerate(pieces):
+        n = piece.shape[0]
+        out = first_ref if i < 2 else second_ref
+        at = (0, size, 0, size, size + n)[i]
+        copies.append(pltpu.make_async_copy(piece, out.at[pl.ds(at, n)], sems.at[i]))
+    for copy in copies:
+        copy.start()
+    for copy in copies:
+        copy.wait()
+
+
+def join(pieces):
+    size, width = pieces[0].shape
+    anywhere = pl.BlockSpec(memory_space=pl.ANY)
+    return pl.pallas_call(
+        join_kernel,
+        in_specs=[anywhere] * 5,
+        out_specs=[anywhere] * 2,
+        out_shape=[jax.ShapeDtypeStruct((2 * size, width), BF16)] * 2,
+        scratch_shapes=[pltpu.SemaphoreType.DMA((5,))],
+        name="join",
+    )(*pieces)
+
+
 def gather_weight(weight):
     other = shift(weight, "zhi", 1)
-    unit = jnp.where(
-        lax.axis_index("zhi") == 0, rows([weight, other]), rows([other, weight])
+    across = shift(weight, "zlo", 1)
+    both = lax.ppermute(weight, ("zlo", "zhi"), [(i, 3 - i) for i in range(4)])
+    pair = jnp.where(
+        lax.axis_index("zhi") == 0,
+        rows([weight, other, across, both]),
+        rows([other, weight, both, across]),
     )
-    half = unit.shape[1] // 2
-    pair = rows([unit, shift(unit, "zlo", 1)])
-    left = rows(ring4(pair[:, :half], "y"))
-    right = rows(ring4(pair[:, half:], "x"))
-    return ring4(left, "x"), ring4(right, "y")
+    half = pair.shape[1] // 2
+    left = ring4(pair[:, :half], "y")
+    right = ring4(pair[:, half:], "x")
+    left_near, left_far = ring4_halves(*join(left), "x")
+    right_near, right_far = ring4_halves(*join(right), "y")
+    return left_near + right_near, left_far + right_far
 
 
 def unit_table():
@@ -58,16 +103,14 @@
     rel = jnp.array(REL4, jnp.int32)
     zs = (zlo + jnp.arange(2, dtype=jnp.int32)) % 2
     ys, xs = (y + rel) % 4, (x + rel) % 4
-    left = (zs[None, None, :] * 4 + ys[None, :, None]) * 4 + xs[:, None, None]
-    right = (zs[None, None, :] * 4 + ys[:, None, None]) * 4 + xs[None, :, None]
+    left = xs[:, None, None] * 8 + zs[None, None, :] * 4 + ys[None, :, None]
+    right = xs[None, :, None] * 8 + zs[None, None, :] * 4 + ys[:, None, None]
     return jnp.stack([left, right]).reshape(64).astype(jnp.int32)
 
 
-PIECES = tuple(
-    (side, side * 32 + first, count)
-    for side in (0, 1)
-    for first, count in ((0, 8), (8, 8), (16, 8), (24, 4), (28, 4))
-)
+NEAR = tuple((side, side * 32 + first) for side in (0, 1) for first in (0, 4, 8, 12, 16, 20))
+FAR = tuple((side, side * 32 + first) for side in (0, 1) for first in (24, 28))
+COUNT = 4
 
 
 def norm_kernel(core_ref, x_ref, gain_ref, own_ref, send_ref, inv_ref):
@@ -76,7 +119,7 @@
     inv_ref[...] = jnp.broadcast_to(inv, inv_ref.shape)
     first = core_ref[0] == 0
     for u in range(32):
-        lo = ((u // 4) * 8 + u % 4) * UNIT
+        lo = ((u % 8) * 8 + u // 8) * UNIT
         hi = lo + 4 * UNIT
         parts = []
         for at in (lo, hi):
@@ -111,41 +154,94 @@
     )(core, source, gain)
 
 
-def project_kernel(table_ref, own_ref, other_ref, *refs):
+def spread_kernel(x_ref, own_ref, other_ref, *refs):
+    outs, sems = refs[:4], refs[4]
+    copies = []
+    for by, out in enumerate(outs):
+        at = lax.rem(x_ref[0] + by, 4) * 8
+        for i, source in enumerate((own_ref, other_ref)):
+            copies.append(
+                pltpu.make_async_copy(source.at[pl.ds(at, 8)], out.at[i], sems.at[2 * by + i])
+            )
+    for copy in copies:
+        copy.start()
+    for copy in copies:
+        copy.wait()
+
+
+def spread(x, own, other):
+    tokens = own.shape[1]
+    anywhere = pl.BlockSpec(memory_space=pl.ANY)
+    return pl.pallas_call(
+        spread_kernel,
+        in_specs=[pl.BlockSpec(memory_space=pltpu.SMEM), anywhere, anywhere],
+        out_specs=[anywhere] * 4,
+        out_shape=[jax.ShapeDtypeStruct((2, 8, tokens, UNIT), BF16)] * 4,
+        scratch_shapes=[pltpu.SemaphoreType.DMA((8,))],
+        name="spread",
+    )(x, own, other)
+
+
+def project_sum(table_ref, own_ref, other_ref, pieces, refs, side):
+    total = None
+    for (at_side, first), piece in zip(pieces, refs):
+        if at_side != side:
+            continue
+        top = [own_ref[table_ref[first + j]] for j in range(COUNT)]
+        low = [other_ref[table_ref[first + j]] for j in range(COUNT)]
+        lhs = jnp.concatenate(
+            [jnp.concatenate(top, axis=1), jnp.concatenate(low, axis=1)], axis=0
+        )
+        term = jnp.dot(lhs, piece[...], preferred_element_type=F32)
+        total = term if total is None else total + term
+    return total
+
+
+def project_near_kernel(table_ref, own_ref, other_ref, *refs):
+    out_ref = refs[-1]
+    for side in (0, 1):
+        total = project_sum(table_ref, own_ref, other_ref, NEAR, refs[:-1], side)
+        width = total.shape[1]
+        out_ref[:, side * width : (side + 1) * width] = total
+
+
+def project_near(table, own, other, pieces):
+    tokens = own.shape[1]
+    width = 2 * pieces[0].shape[1]
+    whole = pl.BlockSpec(memory_space=pltpu.VMEM)
+    return pl.pallas_call(
+        project_near_kernel,
+        in_specs=[pl.BlockSpec(memory_space=pltpu.SMEM)] + [whole] * (2 + len(pieces)),
+        out_specs=whole,
+        out_shape=jax.ShapeDtypeStruct((2 * tokens, width), F32),
+        compiler_params=pltpu.CompilerParams(vmem_limit_bytes=VMEM_LIMIT),
+        name="project_near",
+    )(table, own, other, *pieces)
+
+
+def project_far_kernel(table_ref, own_ref, other_ref, near_ref, *refs):
     pieces, (mine_ref, theirs_ref) = refs[:-2], refs[-2:]
     tokens = own_ref.shape[1]
     for side in (0, 1):
-        total = None
-        for (at_side, first, count), piece in zip(PIECES, pieces):
-            if at_side != side:
-                continue
-            top, low = [], []
-            for j in range(count):
-                u = table_ref[first + j]
-                top.append(own_ref[u])
-                low.append(other_ref[u])
-            lhs = jnp.concatenate(
-                [jnp.concatenate(top, axis=1), jnp.concatenate(low, axis=1)], axis=0
-            )
-            term = jnp.dot(lhs, piece[...], preferred_element_type=F32)
-            total = term if total is None else total + term
-        cols = slice(side * total.shape[1], (side + 1) * total.shape[1])
+        total = project_sum(table_ref, own_ref, other_ref, FAR, pieces, side)
+        width = total.shape[1]
+        cols = slice(side * width, (side + 1) * width)
+        total = total + near_ref[:, cols]
         mine_ref[:, cols] = total[:tokens]
         theirs_ref[:, cols] = total[tokens:]
 
 
-def project(table, own, other, pieces):
+def project_far(table, own, other, near, pieces):
     tokens = own.shape[1]
-    width = 2 * pieces[0].shape[1]
     whole = pl.BlockSpec(memory_space=pltpu.VMEM)
     return pl.pallas_call(
-        project_kernel,
-        in_specs=[pl.BlockSpec(memory_space=pltpu.SMEM)] + [whole] * (2 + len(pieces)),
+        project_far_kernel,
+        in_specs=[pl.BlockSpec(memory_space=pltpu.SMEM)] + [whole] * (3 + len(pieces)),
         out_specs=[whole, whole],
-        out_shape=[jax.ShapeDtypeStruct((tokens, width), F32)] * 2,
+        out_shape=[jax.ShapeDtypeStruct((tokens, near.shape[1]), F32)] * 2,
         compiler_params=pltpu.CompilerParams(vmem_limit_bytes=VMEM_LIMIT),
-        name="project",
-    )(table, own, other, *pieces)
+        name="project_far",
+    )(table, own, other, near, *pieces)
 
 
 def attention_kernel(bias_ref, q_ref, go_ref, *refs):
@@ -236,12 +332,13 @@
     pieces, (own_ref, send_ref, acc_ref) = refs[:-3], refs[-3:]
     tokens = mine_ref.shape[0]
     nt = (((1,), (1,)), ((), ()))
-    for (side, first, count), piece in zip(PIECES, pieces):
+    order = sorted(zip(NEAR + FAR, pieces), key=lambda entry: entry[0])
+    for (side, first), piece in order:
         width = piece.shape[1]
         cols = slice(side * width, (side + 1) * width)
         lhs = jnp.concatenate([mine_ref[:, cols], theirs_ref[:, cols]], axis=0)
         term = lax.dot_general(lhs, piece[...], nt, preferred_element_type=F32)
-        for j in range(count):
+        for j in range(COUNT):
             u = table_ref[first + j]
             part = term[:, j * UNIT : (j + 1) * UNIT]
             if side == 0:
@@ -277,7 +374,7 @@
         sum_ref[...] = jnp.zeros_like(sum_ref)
 
     def unit(at):
-        u = (at // 8) * 4 + at % 4
+        u = (at % 4) * 8 + at // 8
         same = first if (at % 8) < 4 else jnp.logical_not(first)
         cols = slice(at * UNIT, (at + 1) * UNIT)
         grad = jnp.where(same, own_ref[u], recv_ref[u]).astype(F32)
@@ -324,11 +421,16 @@
 
 
 def grad_weight_kernel(*refs):
-    columns, grads, out_ref = refs[:8], refs[8:16], refs[16]
+    columns, grads, out_ref = refs[:4], refs[4:12], refs[12]
     grad = jnp.concatenate([g[...] for g in grads], axis=0)
-    for j in range(0, columns[0].shape[0], 2):
+    for j in range(0, columns[0].shape[1], 2):
         lhs = jnp.concatenate(
-            [jnp.concatenate([c[j], c[j + 1]], axis=1) for c in columns], axis=0
+            [
+                jnp.concatenate([c[i, j], c[i, j + 1]], axis=1)
+                for c in columns
+                for i in (0, 1)
+            ],
+            axis=0,
         )
         part = lax.dot_general(
             lhs, grad, (((0,), (0,)), ((), ())), preferred_element_type=F32
@@ -338,11 +440,11 @@
 
 
 def grad_weight_part(columns, grads):
-    units, width = columns[0].shape[0], grads[0].shape[1]
+    units, width = columns[0].shape[1], grads[0].shape[1]
     whole = pl.BlockSpec(memory_space=pltpu.VMEM)
     return pl.pallas_call(
         grad_weight_kernel,
-        in_specs=[whole] * 16,
+        in_specs=[whole] * 12,
         out_specs=whole,
         out_shape=jax.ShapeDtypeStruct((units, UNIT, width), BF16),
         compiler_params=pltpu.CompilerParams(vmem_limit_bytes=VMEM_LIMIT),
@@ -358,43 +460,34 @@
     return value
 
 
-def shards(layer_input, queries, grad_out, segment_ids, kv_weight, norm_gain):
+def step(layer_input, queries, grad_out, segment_ids, kv_weight, norm_gain):
     source = layer_input[0]
     tokens = source.shape[0]
     core = lax.axis_index("core").astype(jnp.int32)[None]
+    x = lax.axis_index("x").astype(jnp.int32)[None]
     place = lax.axis_index("x") * SIZES["zhi"] + lax.axis_index("zhi")
     gain = norm_gain[None]
     table = unit_table()
 
     doc = segment_ids[0]
-    docs = [doc] + [
-        jnp.where(place >= k, shift_seq(doc, k), -1) for k in range(1, BACK + 1)
-    ]
+    moved = [shift_seq(doc, k) for k in range(1, BACK + 1)]
+    docs = [doc] + [jnp.where(place > k, d, -1) for k, d in enumerate(moved)]
     local = jnp.arange(tokens, dtype=jnp.int32)
     causal = rows([local] + [jnp.full((tokens,), -1, jnp.int32)] * BACK)
     allowed = (rows(docs)[:, None] == doc[None, :]) & (causal[:, None] <= local[None, :])
     bias = jnp.where(allowed, 0.0, -1e30).astype(F32)
 
-    left, right = gather_weight(kv_weight)
-    pieces = left + right
+    near, far = gather_weight(kv_weight)
     own, send, inv = normalize(core, source, gain)
     other = shift(send, "core", 1)
-
-    kv_mine, kv_theirs = project(table, own, other, pieces)
+    blocks = spread(x, own, other)
+
+    kv_near = project_near(table, own, other, near)
+    kv_mine, kv_theirs = project_far(table, own, other, kv_near, far)
     kv_own = (kv_mine + shift(kv_theirs, "core", 1)).astype(BF16)
 
-    def column_block(by):
-        at = (lax.axis_index("x") + by) % 4
-        return [
-            lax.dynamic_index_in_dim(n.reshape(8, 4, tokens, UNIT), at, 1, keepdims=False)
-            for n in (own, other)
-        ]
-
-    columns = []
-    for by in range(4):
-        columns += [shift(block, "x", by) if by else block for block in column_block(by)]
-
     kv_blocks = [kv_own] + [shift_seq(kv_own, k) for k in range(1, BACK + 1)]
+    columns = [shift(block, "x", by) if by else block for by, block in enumerate(blocks)]
     attended, grad_queries, grad_here, *grad_back = attention(
         bias, queries[0], grad_out[0], kv_blocks
     )
@@ -403,21 +496,18 @@
         total = total + shift_seq(part, -(k + 1)).astype(F32)
     grad_own = total.astype(BF16)
     grad_other = shift(grad_own, "core", 1)
-
     grads = [grad_own, grad_other]
-    for by in range(1, 4):
-        far = shift(grad_own, "x", by)
-        grads += [far, shift(far, "core", 1)]
-
-    mine, theirs = grad_normed(table, grad_own, grad_other, pieces)
-    grad_input, gain_rows = norm_back(
-        core, mine, shift(theirs, "core", 1), source, inv, gain
-    )
-    grad_gain = sum_everywhere(jnp.sum(gain_rows, axis=0))
-
+    fars = [shift(grad_own, "x", by) for by in range(1, 4)]
+    for block in fars:
+        grads += [block, shift(block, "core", 1)]
+
+    mine, theirs = grad_normed(table, grad_own, grad_other, near + far)
+    theirs = shift(theirs, "core", 1)
+    grad_input, gain_rows = norm_back(core, mine, theirs, source, inv, gain)
     partial = grad_weight_part(columns, grads).reshape(16, 64, kv_weight.shape[1])
     arrived = lax.all_to_all(partial, ("zlo", "y", "zhi"), 0, 0, tiled=True)
     grad_weight = jnp.sum(arrived.astype(F32), axis=0)
+    grad_gain = sum_everywhere(jnp.sum(gain_rows, axis=0))
     return attended[None], grad_queries[None], grad_input[None], grad_weight, grad_gain
 
 
@@ -426,7 +516,7 @@
     tokens = P(BLK, SEQ, None)
     weight = P(BLK + SEQ, None)
     return jax.shard_map(
-        shards,
+        step,
         mesh=fine,
         in_specs=(tokens, tokens, tokens, P(BLK, SEQ), weight, P()),
         out_specs=(tokens, tokens, tokens, weight, P()),

time: 271 us -> 386 us (1.42)
  Pallas kernels: 52 us -> 185 us
  starting transfers between devices: 124 us -> 111 us
  local copies, waits for them, and re-layouts: 16 us -> 5.69 us
  waiting for transfers between devices: 65 us -> 70.7 us
    pallas_call x2 -> x6, Pallas kernels: 13 us -> 147 us  [the longest x2 65.8 us: join(): pl.pallas_call(join_kernel, in_specs=[anywhere] * 5, out_specs=[anywhere]...]
    ppermute x43 -> x44, starting transfers between devices: 95.6 us -> 81.1 us  [shift(): return lax.ppermute(value, axis, [(i, (i + by) % n) for i in range(n)])]
    ppermute x43 -> x44, waiting for transfers between devices: 51.2 us -> 58.1 us  [shift(): return lax.ppermute(value, axis, [(i, (i + by) % n) for i in range(n)])]
  transfers between devices with their start and end apart: 56 -> 58, of which waited for: 23 -> 23; matrix products, arithmetic and copies ran while one was open for 7% -> 1% of each run, Pallas kernels for 9% -> 42%
where the time goes in v2:
time: 386 us; the launch traced here: 380 us
  Pallas kernels  185 us (48%)
  starting transfers between devices  111 us (29%)
  waiting for transfers between devices  70.7 us (18%)
  other arithmetic  6.35 us (2%)
  local copies, waits for them, and re-layouts  5.69 us (1%)
    ppermute x44, starting transfers between devices, shift(): return lax.ppermute(value, axis, [(i, (i + by) % n) for i in range(n)])  81.1 us
    pallas_call x2, Pallas kernels, join(): pl.pallas_call(join_kernel, in_specs=[anywhere] * 5, out_specs=[anywhere]...  65.8 us
    pallas_call x1, Pallas kernels, spread(): pl.pallas_call(spread_kernel, in_specs=[pl.BlockSpec(memory_space=pltpu.S...  64.7 us
    ppermute x44, waiting for transfers between devices, shift(): return lax.ppermute(value, axis, [(i, (i + by) % n) for i in range(n)])  58.1 us
    ppermute x12, starting transfers between devices, shift_seq(): return lax.ppermute(value, SEQ, pairs)  25.7 us
    pallas_call x1, Pallas kernels, attention(): pl.pallas_call(attention_kernel, grid=(kv_heads,), in_specs=[pl.BlockSpec...  21.5 us
    ppermute x12, waiting for transfers between devices, shift_seq(): return lax.ppermute(value, SEQ, pairs)  12.5 us
  transfers between devices with their start and end apart: 58, of which 23 were waited for; matrix products, arithmetic and copies ran while one was open for 1% of the time, Pallas kernels for 42%

profile of v2, /device:TPU:1, one launch (start us, length us, event | category | flops | bytes accessed | tf_op | source)
XLA Modules:
  0.0 380.3 jit_solution(5371300790502810214)
XLA Ops:
  0.6 4.5 %collective-permute-start.5 = (bf16[64,1024]{1,0:T(8,128)(2,1)}, bf16[64,1024]{1,0:T(8,128)(2,1)S(1)}, u32[]{:S(2)}, u32[]{:S(2)}) collective-permute-start(bf16[64,1024]{1,0:T(8,128)(2,1)} %param.11), channel_id=1, source_target_pairs={{0,1},{1,0},{2,3},{3,2},{4,5},{5,4},{6,7},{7,6},{8,9},{9,8},{10,11... | collective-permute-start | bytes 393224 | tf_op jit(solution)/shard_map/ppermute | solution.py:25
  5.9 2.7 collective-permute-done.5
  8.5 3.3 collective-permute-done.6
  13.1 1.3 collective-permute-start.16
  14.4 1.5 collective-permute-start.17
  15.9 1.3 collective-permute-start.8
  17.1 1.4 collective-permute-start.9
  18.6 2.1 collective-permute-done.16.refs_1_
  20.8 2.7 collective-permute-start.19
  23.6 1.4 collective-permute-start.10
  25.0 1.5 collective-permute-start.11
  27.8 32.9 %join.3 = (bf16[512,512]{1,0:T(8,128)(2,1)}, bf16[512,512]{1,0:T(8,128)(2,1)}) custom-call(bf16[256,512]{1,0:T(8,128)(2,1)} %copy-done.16, bf16[256,512]{1,0:T(8,128)(2,1)} %copy-done.19, bf16[256,512]{1,0:T(8,128)(2,1)} %copy-done.20, bf16[128,512]{1,0:T(8,128)(2,1)} %copy-done.33, bf16[128,512]{1,0:T(8,128)(2,1)} %copy-done.34), custom_call_target="tpu_custom_call" | custom-call | tf_op jit(solution)/shard_map/join/pallas_call | solution.py:74
  61.4 2.1 collective-permute-start.23
  64.8 32.9 %join.2 = (bf16[512,512]{1,0:T(8,128)(2,1)}, bf16[512,512]{1,0:T(8,128)(2,1)}) custom-call(bf16[256,512]{1,0:T(8,128)(2,1)} %copy-done.15, bf16[256,512]{1,0:T(8,128)(2,1)} %copy-done.17, bf16[256,512]{1,0:T(8,128)(2,1)} %copy-done.18, bf16[128,512]{1,0:T(8,128)(2,1)} %copy-done.31, bf16[128,512]{1,0:T(8,128)(2,1)} %copy-done.32), custom_call_target="tpu_custom_call" | custom-call | tf_op jit(solution)/shard_map/join/pallas_call | solution.py:74
  97.8 2.7 collective-permute-start.15
  100.5 4.4 %norm.1 = (bf16[32,128,128]{2,1,0:T(8,128)(2,1)}, bf16[32,128,128]{2,1,0:T(8,128)(2,1)}, f32[128,128]{1,0:T(8,128)}) custom-call(s32[1]{0:T(128)} %bitcast.3.core_ref, bf16[128,8192]{1,0:T(8,128)(2,1)} %bitcast.13, f32[1,8192]{1,0:T(1,128)} %bitcast.17), custom_call_target="tpu_custom_call" | custom-call | tf_op jit(solution)/shard_map/norm/pallas_call | solution.py:135
  104.8 4.6 %collective-permute-start.4 = (bf16[32,128,128]{2,1,0:T(8,128)(2,1)}, bf16[32,128,128]{2,1,0:T(8,128)(2,1)S(1)}, u32[]{:S(2)}, u32[]{:S(2)}) collective-permute-start(bf16[32,128,128]{2,1,0:T(8,128)(2,1)} %get-tuple-element.30), channel_id=1, source_target_pairs={{0,8},{8,0},{1,9},{9,1},{2,10},{10,2},{3,11},{11,3},{4,12},{12,4},... | collective-permute-start | bytes 3145736 | tf_op jit(solution)/shard_map/ppermute | solution.py:25
  109.5 2.7 collective-permute-start.22
  112.2 2.7 collective-permute-start.14
  115.0 9.2 %collective-permute-done.21.refs_9_ = bf16[512,512]{1,0:T(8,128)(2,1)} collective-permute-done((bf16[512,512]{1,0:T(8,128)(2,1)S(1)}, bf16[512,512]{1,0:T(8,128)(2,1)}, u32[]{:S(2)}, u32[]{:S(2)}) %collective-permute-start.21) | collective-permute-done | bytes 524320 | tf_op jit(solution)/shard_map/ppermute | solution.py:25
  124.3 2.7 collective-permute-start.27
  126.9 2.7 collective-permute-start.25
  130.3 5.1 %collective-permute-start = (s32[128]{0:T(128)S(1)}, s32[128]{0:T(128)S(1)}, u32[]{:S(2)}, u32[]{:S(2)}) collective-permute-start(s32[128]{0:T(128)S(1)} %bitcast.19), channel_id=1, source_target_pairs={{0,1},{1,2},{2,3},{3,4},{4,5},{5,6},{6,7},{8,9},{9,10},{10,11},{11... | collective-permute-start | bytes 1544 | tf_op jit(solution)/shard_map/ppermute | solution.py:31
  135.4 6.1 %project_near.1.near_ref = f32[256,1024]{1,0:T(8,128)} custom-call(s32[64]{0:T(128)} %reshape.105.table_ref, bf16[32,128,128]{2,1,0:T(8,128)(2,1)} %get-tuple-element.29.own_ref, bf16[32,128,128]{2,1,0:T(8,128)(2,1)} %copy-done, bf16[512,512]{1,0:T(8,128)(2,1)} %get-tuple-element.31.refs_0_, bf16[512,512]{1,0:T(8,128)(2,1)} %get-tuple-element.32.refs_1_, ...), custom_call_target="tpu_custom_call" | custom-call | tf_op jit(solution)/shard_map/project_near/pallas_call | solution.py:212
  141.6 1.3 collective-permute-start.1
  142.9 2.6 collective-permute-start.2
  145.6 3.0 collective-permute-start.3
  148.6 4.1 %project_far.1 = (f32[128,1024]{1,0:T(8,128)}, f32[128,1024]{1,0:T(8,128)}) custom-call(s32[64]{0:T(128)} %reshape.105.table_ref, bf16[32,128,128]{2,1,0:T(8,128)(2,1)} %get-tuple-element.29.own_ref, bf16[32,128,128]{2,1,0:T(8,128)(2,1)} %copy-done, f32[256,1024]{1,0:T(8,128)} %project_near.1.near_ref, ...), custom_call_target="tpu_custom_call" | custom-call | tf_op jit(solution)/shard_map/project_far/pallas_call | solution.py:237
  152.7 2.6 collective-permute-start.28
  155.4 1.7 collective-permute-done.28
  158.2 4.0 %collective-permute-start.29 = (bf16[128,1024]{1,0:T(8,128)(2,1)S(1)}, bf16[128,1024]{1,0:T(8,128)(2,1)S(1)}, u32[]{:S(2)}, u32[]{:S(2)}) collective-permute-start(bf16[128,1024]{1,0:T(8,128)(2,1)S(1)} %add_convert_fusion.1.refs_0_.refs_5_), channel_id=1, source_target_pairs={{0,1},{1,2},{2,3},{3,4},{4,5},{5,6},{6,7},{8,9},{9,10},{10,11},{11... | collective-permute-start | bytes 786440 | tf_op jit(solution)/shard_map/ppermute | solution.py:31
  162.2 1.5 collective-permute-start.30
  163.7 1.7 collective-permute-start.31
  165.3 1.3 collective-permute-start.32
  168.9 5.6 %collective-permute-done.31.refs_3_.refs_8_ = bf16[128,1024]{1,0:T(8,128)(2,1)S(1)} collective-permute-done((bf16[128,1024]{1,0:T(8,128)(2,1)S(1)}, bf16[128,1024]{1,0:T(8,128)(2,1)S(1)}, u32[]{:S(2)}, u32[]{:S(2)}) %collective-permute-start.31) | collective-permute-done | bytes 262176 | tf_op jit(solution)/shard_map/ppermute | solution.py:31
  174.5 5.6 %collective-permute-done.32.refs_4_.refs_9_ = bf16[128,1024]{1,0:T(8,128)(2,1)S(1)} collective-permute-done((bf16[128,1024]{1,0:T(8,128)(2,1)S(1)}, bf16[128,1024]{1,0:T(8,128)(2,1)S(1)}, u32[]{:S(2)}, u32[]{:S(2)}) %collective-permute-start.32) | collective-permute-done | bytes 262176 | tf_op jit(solution)/shard_map/ppermute | solution.py:31
  180.8 21.5 %attention.1 = (bf16[128,4096]{1,0:T(8,128)(2,1)}, bf16[128,4096]{1,0:T(8,128)(2,1)}, f32[128,1024]{1,0:T(8,128)}, bf16[128,1024]{1,0:T(8,128)(2,1)}, bf16[128,1...) custom-call(f32[640,128]{1,0:T(8,128)} %fusion.1.bias_ref, bf16[128,4096]{1,0:T(8,128)(2,1)} %bitcast.15, ...), custom_call_target="tpu_custom_call" | custom-call | tf_op jit(solution)/shard_map/attention/pallas_call | solution.py:307
  202.4 1.4 collective-permute-start.33
  203.8 1.3 collective-permute-start.34
  205.1 1.3 collective-permute-start.35
  206.4 1.3 collective-permute-start.36
  207.7 64.7 %spread.1 = (bf16[2,8,128,128]{3,2,1,0:T(8,128)(2,1)}, bf16[2,8,128,128]{3,2,1,0:T(8,128)(2,1)}, bf16[2,8,128,128]{3,2,1,0:T(8,128)(2,1)}, bf16[2,8,128,128]{3,2,1,0:T(8,128)(2,1)}) custom-call(s32[1]{0:T(128)} %bitcast.9.x_ref, bf16[32,128,128]{2,1,0:T(8,128)(2,1)} %get-tuple-element.29.own_ref, bf16[32,128,128]{2,1,0:T(8,128)(2,1)} %copy-done), custom_call_target="tpu_custom_call" | custom-call | tf_op jit(solution)/shard_map/spread/pallas_call | solution.py:175
  272.4 6.9 %collective-permute-start.39 = (bf16[2,8,128,128]{3,2,1,0:T(8,128)(2,1)}, bf16[2,8,128,128]{3,2,1,0:T(8,128)(2,1)S(1)}, u32[]{:S(2)}, u32[]{:S(2)}) collective-permute-start(bf16[2,8,128,128]{3,2,1,0:T(8,128)(2,1)} %get-tuple-element.49), channel_id=1, source_target_pairs={{0,2},{2,4},{4,6},{6,0},{1,3},{3,5},{5,7},{7,1},{8,10},{10,12},{12... | collective-permute-start | bytes 1572872 | tf_op jit(solution)/shard_map/ppermute | solution.py:25
  279.3 4.2 %collective-permute-start.40 = (bf16[2,8,128,128]{3,2,1,0:T(8,128)(2,1)}, bf16[2,8,128,128]{3,2,1,0:T(8,128)(2,1)S(1)}, u32[]{:S(2)}, u32[]{:S(2)}) collective-permute-start(bf16[2,8,128,128]{3,2,1,0:T(8,128)(2,1)} %get-tuple-element.50), channel_id=1, source_target_pairs={{0,4},{2,6},{4,0},{6,2},{1,5},{3,7},{5,1},{7,3},{8,12},{10,14},{12... | collective-permute-start | bytes 1572872 | tf_op jit(solution)/shard_map/ppermute | solution.py:25
  283.9 2.7 collective-permute-start.41
  286.5 6.8 %collective-permute-done.39.refs_1_ = bf16[2,8,128,128]{3,2,1,0:T(8,128)(2,1)S(1)} collective-permute-done((bf16[2,8,128,128]{3,2,1,0:T(8,128)(2,1)}, bf16[2,8,128,128]{3,2,1,0:T(8,128)(2,1)S(1)}, u32[]{:S(2)}, u32[]{:S(2)}) %collective-permute-start.39) | collective-permute-done | bytes 524320 | tf_op jit(solution)/shard_map/ppermute | solution.py:25
  294.5 11.0 %collective-permute-done.40.refs_2_ = bf16[2,8,128,128]{3,2,1,0:T(8,128)(2,1)S(1)} collective-permute-done((bf16[2,8,128,128]{3,2,1,0:T(8,128)(2,1)}, bf16[2,8,128,128]{3,2,1,0:T(8,128)(2,1)S(1)}, u32[]{:S(2)}, u32[]{:S(2)}) %collective-permute-start.40) | collective-permute-done | bytes 524320 | tf_op jit(solution)/shard_map/ppermute | solution.py:25
  305.5 4.4 %collective-permute-start.37 = (bf16[128,1024]{1,0:T(8,128)(2,1)S(1)}, bf16[128,1024]{1,0:T(8,128)(2,1)S(1)}, u32[]{:S(2)}, u32[]{:S(2)}) collective-permute-start(bf16[128,1024]{1,0:T(8,128)(2,1)S(1)} %add_convert_fusion.mine_ref.refs_4_), channel_id=1, source_target_pairs={{0,8},{8,0},{1,9},{9,1},{2,10},{10,2},{3,11},{11,3},{4,12},{12,4},... | collective-permute-start | bytes 786440 | tf_op jit(solution)/shard_map/ppermute | solution.py:25
  310.2 2.9 collective-permute-start.43
  313.1 3.6 collective-permute-done.44.refs_8_
  316.7 2.4 collective-permute-start.45
  321.4 5.8 %grad_weight.1 = bf16[8,128,1024]{2,1,0:T(8,128)(2,1)} custom-call(bf16[2,8,128,128]{3,2,1,0:T(8,128)(2,1)} %get-tuple-element.48.refs_0_, bf16[2,8,128,128]{3,2,1,0:T(8,128)(2,1)} %copy-done.21, bf16[2,8,128,128]{3,2,1,0:T(8,128)(2,1)} %copy-done.22, bf16[2,8,128,128]{3,2,1,0:T(8,128)(2,1)} %copy-done.23, bf16[128,1024]{1,0:T(8,128)(2,1)} %copy-done.1, ...), custom_call_target="tpu_custom_call" | custom-call | tf_op jit(solution)/shard_map/grad_weight/pallas_call | solution.py:445
  327.2 4.0 %all-to-all-start = ((bf16[16,64,1024]{2,1,0:T(8,128)(2,1)}), bf16[16,64,1024]{2,1,0:T(8,128)(2,1)S(1)}, u32[]{:S(2)}, u32[]{:S(2)}) async-start(bf16[16,64,1024]{2,1,0:T(8,128)(2,1)} %bitcast.12), calls=%async_computation | async-start | bytes 4194304 | tf_op jit(solution)/shard_map/all_to_all | solution.py:508
  331.2 7.4 %grad_normed.1 = (bf16[32,128,128]{2,1,0:T(8,128)(2,1)}, bf16[32,128,128]{2,1,0:T(8,128)(2,1)}) custom-call(s32[64]{0:T(128)} %reshape.105.table_ref, bf16[128,1024]{1,0:T(8,128)(2,1)} %copy-done.1, bf16[128,1024]{1,0:T(8,128)(2,1)} %copy-done.10, bf16[512,512]{1,0:T(8,128)(2,1)} %get-tuple-element.31.refs_0_, bf16[512,512]{1,0:T(8,128)(2,1)} %get-tuple-element.32.refs_1_, ...), custom_call_target="tpu_custom_call" | custom-call | tf_op jit(solution)/shard_map/grad_normed/pallas_call | solution.py:355
  339.1 2.5 collective-permute-done.38.recv_ref
  342.6 5.6 %norm_back.1 = (bf16[128,8192]{1,0:T(8,128)(2,1)}, f32[8,8192]{1,0:T(8,128)}) custom-call(s32[1]{0:T(128)} %bitcast.3.core_ref, bf16[32,128,128]{2,1,0:T(8,128)(2,1)} %get-tuple-element.44.own_ref, bf16[32,128,128]{2,1,0:T(8,128)(2,1)} %copy-done.9, bf16[128,8192]{1,0:T(8,128)(2,1)} %bitcast.14, f32[128,128]{1,0:T(8,128)} %get-tuple-element.46.inv_ref, ...), custom_call_target="tpu_custom_call" | custom-call | tf_op jit(solution)/shard_map/norm_back/pallas_call | solution.py:400
  350.6 1.6 collective-permute-start.49
  352.2 8.0 %collective-permute-done.49 = f32[8192]{0:T(1024)S(1)} collective-permute-done((f32[8192]{0:T(1024)S(1)}, f32[8192]{0:T(1024)S(1)}, u32[]{:S(2)}, u32[]{:S(2)}) %collective-permute-start.49) | collective-permute-done | bytes 32800 | tf_op jit(solution)/shard_map/ppermute | solution.py:25
  360.2 4.9 %collective-permute-start.50 = (f32[8192]{0:T(1024)S(1)}, f32[8192]{0:T(1024)S(1)}, u32[]{:S(2)}, u32[]{:S(2)}) collective-permute-start(f32[8192]{0:T(1024)S(1)} %add.182), channel_id=1, source_target_pairs={{0,1},{1,0},{2,3},{3,2},{4,5},{5,4},{6,7},{7,6},{8,9},{9,8},{10,11... | collective-permute-start | bytes 98312 | tf_op jit(solution)/shard_map/ppermute | solution.py:25
  365.2 1.3 collective-permute-done.50
  366.5 2.3 collective-permute-start.51
  369.7 2.0 collective-permute-start.53
  371.7 1.4 collective-permute-done.52
  373.9 2.0 collective-permute-start.55
  (166 shorter events, 24.5 us)
Async XLA Ops:
  0.6 7.9 %collective-permute-start.5 = (bf16[64,1024]{1,0:T(8,128)(2,1)}, bf16[64,1024]{1,0:T(8,128)(2,1)S(1)}, u32[]{:S(2)}, u32[]{:S(2)}) collective-permute-start(bf16[64,1024]{1,0:T(8,128)(2,1)} %param.11), channel_id=1, source_target_pairs={{0,1},{1,0},{2,3},{3,2},{4,5},{5,4},{6,7},{7,6},{8,9},{9,8},{10,11... | collective-permute-start | bytes 393224 | tf_op jit(solution)/shard_map/ppermute | solution.py:25
  5.1 6.7 %collective-permute-start.6 = (bf16[64,1024]{1,0:T(8,128)(2,1)}, bf16[64,1024]{1,0:T(8,128)(2,1)S(1)}, u32[]{:S(2)}, u32[]{:S(2)}) collective-permute-start(bf16[64,1024]{1,0:T(8,128)(2,1)} %param.11), channel_id=1, source_target_pairs={{0,64},{64,0},{1,65},{65,1},{2,66},{66,2},{3,67},{67,3},{4,68},{68... | collective-permute-start | bytes 393224 | tf_op jit(solution)/shard_map/ppermute | solution.py:25
  5.9 6.1 %collective-permute-start.7 = (bf16[64,1024]{1,0:T(8,128)(2,1)}, bf16[64,1024]{1,0:T(8,128)(2,1)S(1)}, u32[]{:S(2)}, u32[]{:S(2)}) collective-permute-start(bf16[64,1024]{1,0:T(8,128)(2,1)} %param.11), channel_id=1, source_target_pairs={{0,65},{1,64},{64,1},{65,0},{2,67},{3,66},{66,3},{67,2},{4,69},{5,... | collective-permute-start | bytes 393224 | tf_op jit(solution)/shard_map/ppermute | solution.py:87
  13.1 50.4 %copy-start.15 = (bf16[256,512]{1,0:T(8,128)(2,1)}, bf16[256,512]{1,0:T(8,128)(2,1)S(1)}, u32[]{:S(2)}) copy-start(bf16[256,512]{1,0:T(8,128)(2,1)S(1)} %get-tuple-element.54.refs_0_) | copy-start | bytes 786436
  13.1 7.6 %collective-permute-start.16 = (bf16[256,512]{1,0:T(8,128)(2,1)S(1)}, bf16[256,512]{1,0:T(8,128)(2,1)S(1)}, u32[]{:S(2)}, u32[]{:S(2)}) collective-permute-start(bf16[256,512]{1,0:T(8,128)(2,1)S(1)} %get-tuple-element.53.refs_0_), channel_id=1, source_target_pairs={{0,2},{2,4},{4,6},{6,0},{1,3},{3,5},{5,7},{7,1},{8,10},{10,12},{12... | collective-permute-start | bytes 786440 | tf_op jit(solution)/shard_map/ppermute | solution.py:25
  14.4 6.4 %collective-permute-start.17 = (bf16[256,512]{1,0:T(8,128)(2,1)S(1)}, bf16[256,512]{1,0:T(8,128)(2,1)S(1)}, u32[]{:S(2)}, u32[]{:S(2)}) collective-permute-start(bf16[256,512]{1,0:T(8,128)(2,1)S(1)} %get-tuple-element.53.refs_0_), channel_id=1, source_target_pairs={{0,6},{2,0},{4,2},{6,4},{1,7},{3,1},{5,3},{7,5},{8,14},{10,8},{12,... | collective-permute-start | bytes 786440 | tf_op jit(solution)/shard_map/ppermute | solution.py:25
  15.9 7.7 %collective-permute-start.8 = (bf16[256,512]{1,0:T(8,128)(2,1)S(1)}, bf16[256,512]{1,0:T(8,128)(2,1)S(1)}, u32[]{:S(2)}, u32[]{:S(2)}) collective-permute-start(bf16[256,512]{1,0:T(8,128)(2,1)S(1)} %get-tuple-element.54.refs_0_), channel_id=1, source_target_pairs={{0,16},{16,32},{32,48},{48,0},{1,17},{17,33},{33,49},{49,1},{2,18}... | collective-permute-start | bytes 786440 | tf_op jit(solution)/shard_map/ppermute | solution.py:25
  17.1 7.8 %collective-permute-start.9 = (bf16[256,512]{1,0:T(8,128)(2,1)S(1)}, bf16[256,512]{1,0:T(8,128)(2,1)S(1)}, u32[]{:S(2)}, u32[]{:S(2)}) collective-permute-start(bf16[256,512]{1,0:T(8,128)(2,1)S(1)} %get-tuple-element.54.refs_0_), channel_id=1, source_target_pairs={{0,48},{16,0},{32,16},{48,32},{1,49},{17,1},{33,17},{49,33},{2,50}... | collective-permute-start | bytes 786440 | tf_op jit(solution)/shard_map/ppermute | solution.py:25
  20.7 5.8 %collective-permute-start.18 = (bf16[128,512]{1,0:T(8,128)(2,1)S(1)}, bf16[128,512]{1,0:T(8,128)(2,1)S(1)}, u32[]{:S(2)}, u32[]{:S(2)}) collective-permute-start(bf16[128,512]{1,0:T(8,128)(2,1)S(1)} %slice.28), channel_id=1, source_target_pairs={{0,2},{2,4},{4,6},{6,0},{1,3},{3,5},{5,7},{7,1},{8,10},{10,12},{12... | collective-permute-start | bytes 393224 | tf_op jit(solution)/shard_map/ppermute | solution.py:25
  20.8 5.7 %collective-permute-start.19 = (bf16[128,512]{1,0:T(8,128)(2,1)S(1)}, bf16[128,512]{1,0:T(8,128)(2,1)S(1)}, u32[]{:S(2)}, u32[]{:S(2)}) collective-permute-start(bf16[128,512]{1,0:T(8,128)(2,1)S(1)} %slice.29), channel_id=1, source_target_pairs={{0,6},{2,0},{4,2},{6,4},{1,7},{3,1},{5,3},{7,5},{8,14},{10,8},{12,... | collective-permute-start | bytes 393224 | tf_op jit(solution)/shard_map/ppermute | solution.py:25
  23.6 39.9 %collective-permute-start.10 = (bf16[128,512]{1,0:T(8,128)(2,1)S(1)}, bf16[128,512]{1,0:T(8,128)(2,1)S(1)}, u32[]{:S(2)}, u32[]{:S(2)}) collective-permute-start(bf16[128,512]{1,0:T(8,128)(2,1)S(1)} %slice.25), channel_id=1, source_target_pairs={{0,16},{16,32},{32,48},{48,0},{1,17},{17,33},{33,49},{49,1},{2,18}... | collective-permute-start | bytes 393224 | tf_op jit(solution)/shard_map/ppermute | solution.py:25
  24.9 90.0 %copy-start.37 = (s32[4]{0:T(128)S(1)}, s32[4]{0:T(128)}, u32[]{:S(2)}) copy-start(s32[4]{0:T(128)} %constant.71.clone) | copy-start | bytes 52
  24.9 105.4 %copy-start.36 = (s32[1,128]{1,0:T(1,128)S(1)}, s32[1,128]{1,0:T(1,128)}, u32[]{:S(2)}) copy-start(s32[1,128]{1,0:T(1,128)} %param.10) | copy-start | bytes 1540
  25.0 38.5 %collective-permute-start.11 = (bf16[128,512]{1,0:T(8,128)(2,1)S(1)}, bf16[128,512]{1,0:T(8,128)(2,1)S(1)}, u32[]{:S(2)}, u32[]{:S(2)}) collective-permute-start(bf16[128,512]{1,0:T(8,128)(2,1)S(1)} %slice.26), channel_id=1, source_target_pairs={{0,48},{16,0},{32,16},{48,32},{1,49},{17,1},{33,17},{49,33},{2,50}... | collective-permute-start | bytes 393224 | tf_op jit(solution)/shard_map/ppermute | solution.py:25
  60.7 48.7 %copy-start.4 = (bf16[512,512]{1,0:T(8,128)(2,1)S(1)}, bf16[512,512]{1,0:T(8,128)(2,1)}, u32[]{:S(2)}) copy-start(bf16[512,512]{1,0:T(8,128)(2,1)} %get-tuple-element.34.refs_7_) | copy-start | bytes 1572868
  60.7 48.8 %copy-start.3 = (bf16[512,512]{1,0:T(8,128)(2,1)S(1)}, bf16[512,512]{1,0:T(8,128)(2,1)}, u32[]{:S(2)}) copy-start(bf16[512,512]{1,0:T(8,128)(2,1)} %get-tuple-element.33.refs_6_) | copy-start | bytes 1572868
  60.7 48.7 %collective-permute-start.20 = (bf16[512,512]{1,0:T(8,128)(2,1)}, bf16[512,512]{1,0:T(8,128)(2,1)S(1)}, u32[]{:S(2)}, u32[]{:S(2)}) collective-permute-start(bf16[512,512]{1,0:T(8,128)(2,1)} %get-tuple-element.33.refs_6_), channel_id=1, source_target_pairs={{0,16},{16,32},{32,48},{48,0},{1,17},{17,33},{33,49},{49,1},{2,18}... | collective-permute-start | bytes 1572872 | tf_op jit(solution)/shard_map/ppermute | solution.py:25
  61.4 48.1 %collective-permute-start.23 = (bf16[512,512]{1,0:T(8,128)(2,1)}, bf16[512,512]{1,0:T(8,128)(2,1)S(1)}, u32[]{:S(2)}, u32[]{:S(2)}) collective-permute-start(bf16[512,512]{1,0:T(8,128)(2,1)} %get-tuple-element.34.refs_7_), channel_id=1, source_target_pairs={{0,48},{16,0},{32,16},{48,32},{1,49},{17,1},{33,17},{49,33},{2,50}... | collective-permute-start | bytes 1572872 | tf_op jit(solution)/shard_map/ppermute | solution.py:25
  97.7 14.5 %collective-permute-start.12 = (bf16[512,512]{1,0:T(8,128)(2,1)}, bf16[512,512]{1,0:T(8,128)(2,1)}, u32[]{:S(2)}, u32[]{:S(2)}) collective-permute-start(bf16[512,512]{1,0:T(8,128)(2,1)} %get-tuple-element.31.refs_0_), channel_id=1, source_target_pairs={{0,2},{2,4},{4,6},{6,0},{1,3},{3,5},{5,7},{7,1},{8,10},{10,12},{12... | collective-permute-start | bytes 1572872 | tf_op jit(solution)/shard_map/ppermute | solution.py:25
  97.8 14.4 %collective-permute-start.15 = (bf16[512,512]{1,0:T(8,128)(2,1)}, bf16[512,512]{1,0:T(8,128)(2,1)}, u32[]{:S(2)}, u32[]{:S(2)}) collective-permute-start(bf16[512,512]{1,0:T(8,128)(2,1)} %get-tuple-element.32.refs_1_), channel_id=1, source_target_pairs={{0,6},{2,0},{4,2},{6,4},{1,7},{3,1},{5,3},{7,5},{8,14},{10,8},{12,... | collective-permute-start | bytes 1572872 | tf_op jit(solution)/shard_map/ppermute | solution.py:25
  104.8 25.5 %collective-permute-start.4 = (bf16[32,128,128]{2,1,0:T(8,128)(2,1)}, bf16[32,128,128]{2,1,0:T(8,128)(2,1)S(1)}, u32[]{:S(2)}, u32[]{:S(2)}) collective-permute-start(bf16[32,128,128]{2,1,0:T(8,128)(2,1)} %get-tuple-element.30), channel_id=1, source_target_pairs={{0,8},{8,0},{1,9},{9,1},{2,10},{10,2},{3,11},{11,3},{4,12},{12,4},... | collective-permute-start | bytes 3145736 | tf_op jit(solution)/shard_map/ppermute | solution.py:25
  109.4 14.8 %collective-permute-start.21 = (bf16[512,512]{1,0:T(8,128)(2,1)S(1)}, bf16[512,512]{1,0:T(8,128)(2,1)}, u32[]{:S(2)}, u32[]{:S(2)}) collective-permute-start(bf16[512,512]{1,0:T(8,128)(2,1)S(1)} %copy-done.4), channel_id=1, source_target_pairs={{0,16},{16,32},{32,48},{48,0},{1,17},{17,33},{33,49},{49,1},{2,18}... | collective-permute-start | bytes 1572872 | tf_op jit(solution)/shard_map/ppermute | solution.py:25
  109.5 14.7 %collective-permute-start.22 = (bf16[512,512]{1,0:T(8,128)(2,1)S(1)}, bf16[512,512]{1,0:T(8,128)(2,1)}, u32[]{:S(2)}, u32[]{:S(2)}) collective-permute-start(bf16[512,512]{1,0:T(8,128)(2,1)S(1)} %copy-done.3), channel_id=1, source_target_pairs={{0,48},{16,0},{32,16},{48,32},{1,49},{17,1},{33,17},{49,33},{2,50}... | collective-permute-start | bytes 1572872 | tf_op jit(solution)/shard_map/ppermute | solution.py:25
  112.2 14.7 %collective-permute-start.13 = (bf16[512,512]{1,0:T(8,128)(2,1)}, bf16[512,512]{1,0:T(8,128)(2,1)}, u32[]{:S(2)}, u32[]{:S(2)}) collective-permute-start(bf16[512,512]{1,0:T(8,128)(2,1)} %get-tuple-element.32.refs_1_), channel_id=1, source_target_pairs={{0,2},{2,4},{4,6},{6,0},{1,3},{3,5},{5,7},{7,1},{8,10},{10,12},{12... | collective-permute-start | bytes 1572872 | tf_op jit(solution)/shard_map/ppermute | solution.py:25
  112.2 14.7 %collective-permute-start.14 = (bf16[512,512]{1,0:T(8,128)(2,1)}, bf16[512,512]{1,0:T(8,128)(2,1)}, u32[]{:S(2)}, u32[]{:S(2)}) collective-permute-start(bf16[512,512]{1,0:T(8,128)(2,1)} %get-tuple-element.31.refs_0_), channel_id=1, source_target_pairs={{0,6},{2,0},{4,2},{6,4},{1,7},{3,1},{5,3},{7,5},{8,14},{10,8},{12,... | collective-permute-start | bytes 1572872 | tf_op jit(solution)/shard_map/ppermute | solution.py:25
  124.3 17.3 %collective-permute-start.26 = (bf16[512,512]{1,0:T(8,128)(2,1)S(1)}, bf16[512,512]{1,0:T(8,128)(2,1)S(1)}, u32[]{:S(2)}, u32[]{:S(2)}) collective-permute-start(bf16[512,512]{1,0:T(8,128)(2,1)S(1)} %collective-permute-done.20.refs_8_), channel_id=1, source_target_pairs={{0,16},{16,32},{32,48},{48,0},{1,17},{17,33},{33,49},{49,1},{2,18}... | collective-permute-start | bytes 1572872 | tf_op jit(solution)/shard_map/ppermute | solution.py:25
  124.3 18.6 %collective-permute-start.27 = (bf16[512,512]{1,0:T(8,128)(2,1)S(1)}, bf16[512,512]{1,0:T(8,128)(2,1)S(1)}, u32[]{:S(2)}, u32[]{:S(2)}) collective-permute-start(bf16[512,512]{1,0:T(8,128)(2,1)S(1)} %collective-permute-done.23.refs_11_), channel_id=1, source_target_pairs={{0,48},{16,0},{32,16},{48,32},{1,49},{17,1},{33,17},{49,33},{2,50}... | collective-permute-start | bytes 1572872 | tf_op jit(solution)/shard_map/ppermute | solution.py:25
  126.9 18.6 %collective-permute-start.24 = (bf16[512,512]{1,0:T(8,128)(2,1)}, bf16[512,512]{1,0:T(8,128)(2,1)}, u32[]{:S(2)}, u32[]{:S(2)}) collective-permute-start(bf16[512,512]{1,0:T(8,128)(2,1)} %collective-permute-done.12.refs_2_), channel_id=1, source_target_pairs={{0,2},{2,4},{4,6},{6,0},{1,3},{3,5},{5,7},{7,1},{8,10},{10,12},{12... | collective-permute-start | bytes 1572872 | tf_op jit(solution)/shard_map/ppermute | solution.py:25
  126.9 21.6 %collective-permute-start.25 = (bf16[512,512]{1,0:T(8,128)(2,1)}, bf16[512,512]{1,0:T(8,128)(2,1)}, u32[]{:S(2)}, u32[]{:S(2)}) collective-permute-start(bf16[512,512]{1,0:T(8,128)(2,1)} %collective-permute-done.15.refs_5_), channel_id=1, source_target_pairs={{0,6},{2,0},{4,2},{6,4},{1,7},{3,1},{5,3},{7,5},{8,14},{10,8},{12,... | collective-permute-start | bytes 1572872 | tf_op jit(solution)/shard_map/ppermute | solution.py:25
  130.3 25.0 %collective-permute-start = (s32[128]{0:T(128)S(1)}, s32[128]{0:T(128)S(1)}, u32[]{:S(2)}, u32[]{:S(2)}) collective-permute-start(s32[128]{0:T(128)S(1)} %bitcast.19), channel_id=1, source_target_pairs={{0,1},{1,2},{2,3},{3,4},{4,5},{5,6},{6,7},{8,9},{9,10},{10,11},{11... | collective-permute-start | bytes 1544 | tf_op jit(solution)/shard_map/ppermute | solution.py:31
  141.6 13.7 %collective-permute-start.1 = (s32[128]{0:T(128)S(1)}, s32[128]{0:T(128)S(1)}, u32[]{:S(2)}, u32[]{:S(2)}) collective-permute-start(s32[128]{0:T(128)S(1)} %bitcast.20), channel_id=1, source_target_pairs={{0,2},{1,3},{2,4},{3,5},{4,6},{5,7},{8,10},{9,11},{10,12},{11,13},... | collective-permute-start | bytes 1544 | tf_op jit(solution)/shard_map/ppermute | solution.py:31
  142.9 12.4 %collective-permute-start.2 = (s32[128]{0:T(128)S(1)}, s32[128]{0:T(128)S(1)}, u32[]{:S(2)}, u32[]{:S(2)}) collective-permute-start(s32[128]{0:T(128)S(1)} %bitcast.21), channel_id=1, source_target_pairs={{0,3},{1,4},{2,5},{3,6},{4,7},{8,11},{9,12},{10,13},{11,14},{12,15... | collective-permute-start | bytes 1544 | tf_op jit(solution)/shard_map/ppermute | solution.py:31
  145.6 21.1 %collective-permute-start.3 = (s32[128]{0:T(128)S(1)}, s32[128]{0:T(128)S(1)}, u32[]{:S(2)}, u32[]{:S(2)}) collective-permute-start(s32[128]{0:T(128)S(1)} %bitcast.22), channel_id=1, source_target_pairs={{0,4},{1,5},{2,6},{3,7},{8,12},{9,13},{10,14},{11,15},{16,20},{17,... | collective-permute-start | bytes 1544 | tf_op jit(solution)/shard_map/ppermute | solution.py:31
  152.7 4.3 %collective-permute-start.28 = (f32[128,1024]{1,0:T(8,128)}, f32[128,1024]{1,0:T(8,128)S(1)}, u32[]{:S(2)}, u32[]{:S(2)}) collective-permute-start(f32[128,1024]{1,0:T(8,128)} %get-tuple-element.36), channel_id=1, source_target_pairs={{0,8},{8,0},{1,9},{9,1},{2,10},{10,2},{3,11},{11,3},{4,12},{12,4},... | collective-permute-start | bytes 1572872 | tf_op jit(solution)/shard_map/ppermute | solution.py:25
  158.2 9.5 %collective-permute-start.29 = (bf16[128,1024]{1,0:T(8,128)(2,1)S(1)}, bf16[128,1024]{1,0:T(8,128)(2,1)S(1)}, u32[]{:S(2)}, u32[]{:S(2)}) collective-permute-start(bf16[128,1024]{1,0:T(8,128)(2,1)S(1)} %add_convert_fusion.1.refs_0_.refs_5_), channel_id=1, source_target_pairs={{0,1},{1,2},{2,3},{3,4},{4,5},{5,6},{6,7},{8,9},{9,10},{10,11},{11... | collective-permute-start | bytes 786440 | tf_op jit(solution)/shard_map/ppermute | solution.py:31
  162.2 6.8 %collective-permute-start.30 = (bf16[128,1024]{1,0:T(8,128)(2,1)S(1)}, bf16[128,1024]{1,0:T(8,128)(2,1)S(1)}, u32[]{:S(2)}, u32[]{:S(2)}) collective-permute-start(bf16[128,1024]{1,0:T(8,128)(2,1)S(1)} %add_convert_fusion.1.refs_0_.refs_5_), channel_id=1, source_target_pairs={{0,2},{1,3},{2,4},{3,5},{4,6},{5,7},{8,10},{9,11},{10,12},{11,13},... | collective-permute-start | bytes 786440 | tf_op jit(solution)/shard_map/ppermute | solution.py:31
  163.7 10.9 %collective-permute-start.31 = (bf16[128,1024]{1,0:T(8,128)(2,1)S(1)}, bf16[128,1024]{1,0:T(8,128)(2,1)S(1)}, u32[]{:S(2)}, u32[]{:S(2)}) collective-permute-start(bf16[128,1024]{1,0:T(8,128)(2,1)S(1)} %add_convert_fusion.1.refs_0_.refs_5_), channel_id=1, source_target_pairs={{0,3},{1,4},{2,5},{3,6},{4,7},{8,11},{9,12},{10,13},{11,14},{12,15... | collective-permute-start | bytes 786440 | tf_op jit(solution)/shard_map/ppermute | solution.py:31
  165.3 14.8 %collective-permute-start.32 = (bf16[128,1024]{1,0:T(8,128)(2,1)S(1)}, bf16[128,1024]{1,0:T(8,128)(2,1)S(1)}, u32[]{:S(2)}, u32[]{:S(2)}) collective-permute-start(bf16[128,1024]{1,0:T(8,128)(2,1)S(1)} %add_convert_fusion.1.refs_0_.refs_5_), channel_id=1, source_target_pairs={{0,4},{1,5},{2,6},{3,7},{8,12},{9,13},{10,14},{11,15},{16,20},{17,... | collective-permute-start | bytes 786440 | tf_op jit(solution)/shard_map/ppermute | solution.py:31
  202.4 81.2 %copy-start.24 = (f32[128,1024]{1,0:T(8,128)S(1)}, f32[128,1024]{1,0:T(8,128)}, u32[]{:S(2)}) copy-start(f32[128,1024]{1,0:T(8,128)} %get-tuple-element.39) | copy-start | bytes 1572868
  202.4 77.0 %collective-permute-start.33 = (bf16[128,1024]{1,0:T(8,128)(2,1)}, bf16[128,1024]{1,0:T(8,128)(2,1)S(1)}, u32[]{:S(2)}, u32[]{:S(2)}) collective-permute-start(bf16[128,1024]{1,0:T(8,128)(2,1)} %get-tuple-element.40), channel_id=1, source_target_pairs={{1,0},{2,1},{3,2},{4,3},{5,4},{6,5},{7,6},{9,8},{10,9},{11,10},{12... | collective-permute-start | bytes 786440 | tf_op jit(solution)/shard_map/ppermute | solution.py:31
  203.8 79.7 %collective-permute-start.34 = (bf16[128,1024]{1,0:T(8,128)(2,1)}, bf16[128,1024]{1,0:T(8,128)(2,1)S(1)}, u32[]{:S(2)}, u32[]{:S(2)}) collective-permute-start(bf16[128,1024]{1,0:T(8,128)(2,1)} %get-tuple-element.41), channel_id=1, source_target_pairs={{2,0},{3,1},{4,2},{5,3},{6,4},{7,5},{10,8},{11,9},{12,10},{13,11},... | collective-permute-start | bytes 786440 | tf_op jit(solution)/shard_map/ppermute | solution.py:31
  205.1 78.5 %collective-permute-start.35 = (bf16[128,1024]{1,0:T(8,128)(2,1)}, bf16[128,1024]{1,0:T(8,128)(2,1)S(1)}, u32[]{:S(2)}, u32[]{:S(2)}) collective-permute-start(bf16[128,1024]{1,0:T(8,128)(2,1)} %get-tuple-element.42), channel_id=1, source_target_pairs={{3,0},{4,1},{5,2},{6,3},{7,4},{11,8},{12,9},{13,10},{14,11},{15,12... | collective-permute-start | bytes 786440 | tf_op jit(solution)/shard_map/ppermute | solution.py:31
  206.4 77.2 %collective-permute-start.36 = (bf16[128,1024]{1,0:T(8,128)(2,1)}, bf16[128,1024]{1,0:T(8,128)(2,1)S(1)}, u32[]{:S(2)}, u32[]{:S(2)}) collective-permute-start(bf16[128,1024]{1,0:T(8,128)(2,1)} %get-tuple-element.43), channel_id=1, source_target_pairs={{4,0},{5,1},{6,2},{7,3},{12,8},{13,9},{14,10},{15,11},{20,16},{21,... | collective-permute-start | bytes 786440 | tf_op jit(solution)/shard_map/ppermute | solution.py:31
  272.4 20.9 %collective-permute-start.39 = (bf16[2,8,128,128]{3,2,1,0:T(8,128)(2,1)}, bf16[2,8,128,128]{3,2,1,0:T(8,128)(2,1)S(1)}, u32[]{:S(2)}, u32[]{:S(2)}) collective-permute-start(bf16[2,8,128,128]{3,2,1,0:T(8,128)(2,1)} %get-tuple-element.49), channel_id=1, source_target_pairs={{0,2},{2,4},{4,6},{6,0},{1,3},{3,5},{5,7},{7,1},{8,10},{10,12},{12... | collective-permute-start | bytes 1572872 | tf_op jit(solution)/shard_map/ppermute | solution.py:25
  279.3 26.2 %collective-permute-start.40 = (bf16[2,8,128,128]{3,2,1,0:T(8,128)(2,1)}, bf16[2,8,128,128]{3,2,1,0:T(8,128)(2,1)S(1)}, u32[]{:S(2)}, u32[]{:S(2)}) collective-permute-start(bf16[2,8,128,128]{3,2,1,0:T(8,128)(2,1)} %get-tuple-element.50), channel_id=1, source_target_pairs={{0,4},{2,6},{4,0},{6,2},{1,5},{3,7},{5,1},{7,3},{8,12},{10,14},{12... | collective-permute-start | bytes 1572872 | tf_op jit(solution)/shard_map/ppermute | solution.py:25
  283.8 26.4 %collective-permute-start.42 = (bf16[128,1024]{1,0:T(8,128)(2,1)S(1)}, bf16[128,1024]{1,0:T(8,128)(2,1)S(1)}, u32[]{:S(2)}, u32[]{:S(2)}) collective-permute-start(bf16[128,1024]{1,0:T(8,128)(2,1)S(1)} %add_convert_fusion.mine_ref.refs_4_), channel_id=1, source_target_pairs={{0,2},{2,4},{4,6},{6,0},{1,3},{3,5},{5,7},{7,1},{8,10},{10,12},{12... | collective-permute-start | bytes 786440 | tf_op jit(solution)/shard_map/ppermute | solution.py:25
  283.9 35.4 %collective-permute-start.41 = (bf16[2,8,128,128]{3,2,1,0:T(8,128)(2,1)}, bf16[2,8,128,128]{3,2,1,0:T(8,128)(2,1)S(1)}, u32[]{:S(2)}, u32[]{:S(2)}) collective-permute-start(bf16[2,8,128,128]{3,2,1,0:T(8,128)(2,1)} %get-tuple-element.51), channel_id=1, source_target_pairs={{0,6},{2,0},{4,2},{6,4},{1,7},{3,1},{5,3},{7,5},{8,14},{10,8},{12,... | collective-permute-start | bytes 1572872 | tf_op jit(solution)/shard_map/ppermute | solution.py:25
  286.5 30.2 %collective-permute-start.44 = (bf16[128,1024]{1,0:T(8,128)(2,1)S(1)}, bf16[128,1024]{1,0:T(8,128)(2,1)S(1)}, u32[]{:S(2)}, u32[]{:S(2)}) collective-permute-start(bf16[128,1024]{1,0:T(8,128)(2,1)S(1)} %add_convert_fusion.mine_ref.refs_4_), channel_id=1, source_target_pairs={{0,4},{2,6},{4,0},{6,2},{1,5},{3,7},{5,1},{7,3},{8,12},{10,14},{12... | collective-permute-start | bytes 786440 | tf_op jit(solution)/shard_map/ppermute | solution.py:25
  293.3 25.8 %collective-permute-start.46 = (bf16[128,1024]{1,0:T(8,128)(2,1)S(1)}, bf16[128,1024]{1,0:T(8,128)(2,1)S(1)}, u32[]{:S(2)}, u32[]{:S(2)}) collective-permute-start(bf16[128,1024]{1,0:T(8,128)(2,1)S(1)} %add_convert_fusion.mine_ref.refs_4_), channel_id=1, source_target_pairs={{0,6},{2,0},{4,2},{6,4},{1,7},{3,1},{5,3},{7,5},{8,14},{10,8},{12,... | collective-permute-start | bytes 786440 | tf_op jit(solution)/shard_map/ppermute | solution.py:25
  305.5 13.8 %collective-permute-start.37 = (bf16[128,1024]{1,0:T(8,128)(2,1)S(1)}, bf16[128,1024]{1,0:T(8,128)(2,1)S(1)}, u32[]{:S(2)}, u32[]{:S(2)}) collective-permute-start(bf16[128,1024]{1,0:T(8,128)(2,1)S(1)} %add_convert_fusion.mine_ref.refs_4_), channel_id=1, source_target_pairs={{0,8},{8,0},{1,9},{9,1},{2,10},{10,2},{3,11},{11,3},{4,12},{12,4},... | collective-permute-start | bytes 786440 | tf_op jit(solution)/shard_map/ppermute | solution.py:25
  310.2 9.1 %collective-permute-start.43 = (bf16[128,1024]{1,0:T(8,128)(2,1)S(1)}, bf16[128,1024]{1,0:T(8,128)(2,1)S(1)}, u32[]{:S(2)}, u32[]{:S(2)}) collective-permute-start(bf16[128,1024]{1,0:T(8,128)(2,1)S(1)} %collective-permute-done.42.refs_6_), channel_id=1, source_target_pairs={{0,8},{8,0},{1,9},{9,1},{2,10},{10,2},{3,11},{11,3},{4,12},{12,4},... | collective-permute-start | bytes 786440 | tf_op jit(solution)/shard_map/ppermute | solution.py:25
  316.7 3.6 collective-permute-start.45
  319.2 1.5 collective-permute-start.47
  327.2 52.0 %all-to-all-start = ((bf16[16,64,1024]{2,1,0:T(8,128)(2,1)}), bf16[16,64,1024]{2,1,0:T(8,128)(2,1)S(1)}, u32[]{:S(2)}, u32[]{:S(2)}) async-start(bf16[16,64,1024]{2,1,0:T(8,128)(2,1)} %bitcast.12), calls=%async_computation | async-start | bytes 4194304 | tf_op jit(solution)/shard_map/all_to_all | solution.py:508
  338.5 3.1 collective-permute-start.38
  349.2 1.3 collective-permute-start.48
  350.6 9.7 %collective-permute-start.49 = (f32[8192]{0:T(1024)S(1)}, f32[8192]{0:T(1024)S(1)}, u32[]{:S(2)}, u32[]{:S(2)}) collective-permute-start(f32[8192]{0:T(1024)S(1)} %add.181), channel_id=1, source_target_pairs={{0,64},{64,0},{1,65},{65,1},{2,66},{66,2},{3,67},{67,3},{4,68},{68... | collective-permute-start | bytes 98312 | tf_op jit(solution)/shard_map/ppermute | solution.py:25
  360.2 6.3 %collective-permute-start.50 = (f32[8192]{0:T(1024)S(1)}, f32[8192]{0:T(1024)S(1)}, u32[]{:S(2)}, u32[]{:S(2)}) collective-permute-start(f32[8192]{0:T(1024)S(1)} %add.182), channel_id=1, source_target_pairs={{0,1},{1,0},{2,3},{3,2},{4,5},{5,4},{6,7},{7,6},{8,9},{9,8},{10,11... | collective-permute-start | bytes 98312 | tf_op jit(solution)/shard_map/ppermute | solution.py:25
  366.5 5.2 %collective-permute-start.51 = (f32[8192]{0:T(1024)S(1)}, f32[8192]{0:T(1024)S(1)}, u32[]{:S(2)}, u32[]{:S(2)}) collective-permute-start(f32[8192]{0:T(1024)S(1)} %add.183), channel_id=1, source_target_pairs={{0,16},{16,32},{32,48},{48,0},{1,17},{17,33},{33,49},{49,1},{2,18}... | collective-permute-start | bytes 98312 | tf_op jit(solution)/shard_map/ppermute | solution.py:25
  368.8 4.3 %collective-permute-start.52 = (f32[8192]{0:T(1024)S(1)}, f32[8192]{0:T(1024)S(1)}, u32[]{:S(2)}, u32[]{:S(2)}) collective-permute-start(f32[8192]{0:T(1024)S(1)} %add.183), channel_id=1, source_target_pairs={{0,32},{16,48},{32,0},{48,16},{1,33},{17,49},{33,1},{49,17},{2,34}... | collective-permute-start | bytes 98312 | tf_op jit(solution)/shard_map/ppermute | solution.py:25
  369.7 3.4 collective-permute-start.53
  373.1 4.0 %collective-permute-start.54 = (f32[8192]{0:T(1024)S(1)}, f32[8192]{0:T(1024)S(1)}, u32[]{:S(2)}, u32[]{:S(2)}) collective-permute-start(f32[8192]{0:T(1024)S(1)} %add_add_fusion.1), channel_id=1, source_target_pairs={{0,2},{2,4},{4,6},{6,0},{1,3},{3,5},{5,7},{7,1},{8,10},{10,12},{12... | collective-permute-start | bytes 98312 | tf_op jit(solution)/shard_map/ppermute | solution.py:25
  373.9 4.3 %collective-permute-start.55 = (f32[8192]{0:T(1024)S(1)}, f32[8192]{0:T(1024)S(1)}, u32[]{:S(2)}, u32[]{:S(2)}) collective-permute-start(f32[8192]{0:T(1024)S(1)} %add_add_fusion.1), channel_id=1, source_target_pairs={{0,4},{2,6},{4,0},{6,2},{1,5},{3,7},{5,1},{7,3},{8,12},{10,14},{12... | collective-permute-start | bytes 98312 | tf_op jit(solution)/shard_map/ppermute | solution.py:25
  375.8 2.8 collective-permute-start.56
  (32 other events, 355.5 us)

commit v3 on v2

--- a/solution.py
+++ b/solution.py
@@ -54,29 +54,24 @@
 
 
 def join_kernel(*refs):
-    pieces, (first_ref, second_ref, sems) = refs[:5], refs[5:]
+    pieces, (first_ref, second_ref) = refs[:5], refs[5:]
     size = pieces[0].shape[0]
-    copies = []
-    for i, piece in enumerate(pieces):
-        n = piece.shape[0]
-        out = first_ref if i < 2 else second_ref
-        at = (0, size, 0, size, size + n)[i]
-        copies.append(pltpu.make_async_copy(piece, out.at[pl.ds(at, n)], sems.at[i]))
-    for copy in copies:
-        copy.start()
-    for copy in copies:
-        copy.wait()
+    half = size // 2
+    first_ref[:size, :] = pieces[0][...]
+    first_ref[size:, :] = pieces[1][...]
+    second_ref[:size, :] = pieces[2][...]
+    second_ref[size : size + half, :] = pieces[3][...]
+    second_ref[size + half :, :] = pieces[4][...]
 
 
 def join(pieces):
     size, width = pieces[0].shape
-    anywhere = pl.BlockSpec(memory_space=pl.ANY)
+    whole = pl.BlockSpec(memory_space=pltpu.VMEM)
     return pl.pallas_call(
         join_kernel,
-        in_specs=[anywhere] * 5,
-        out_specs=[anywhere] * 2,
+        in_specs=[whole] * 5,
+        out_specs=[whole] * 2,
         out_shape=[jax.ShapeDtypeStruct((2 * size, width), BF16)] * 2,
-        scratch_shapes=[pltpu.SemaphoreType.DMA((5,))],
         name="join",
     )(*pieces)
 
@@ -154,30 +149,21 @@
     )(core, source, gain)
 
 
-def spread_kernel(x_ref, own_ref, other_ref, *refs):
-    outs, sems = refs[:4], refs[4]
-    copies = []
+def spread_kernel(x_ref, own_ref, other_ref, *outs):
     for by, out in enumerate(outs):
         at = lax.rem(x_ref[0] + by, 4) * 8
-        for i, source in enumerate((own_ref, other_ref)):
-            copies.append(
-                pltpu.make_async_copy(source.at[pl.ds(at, 8)], out.at[i], sems.at[2 * by + i])
-            )
-    for copy in copies:
-        copy.start()
-    for copy in copies:
-        copy.wait()
+        out[0] = own_ref[pl.ds(at, 8)]
+        out[1] = other_ref[pl.ds(at, 8)]
 
 
 def spread(x, own, other):
     tokens = own.shape[1]
-    anywhere = pl.BlockSpec(memory_space=pl.ANY)
+    whole = pl.BlockSpec(memory_space=pltpu.VMEM)
     return pl.pallas_call(
         spread_kernel,
-        in_specs=[pl.BlockSpec(memory_space=pltpu.SMEM), anywhere, anywhere],
-        out_specs=[anywhere] * 4,
+        in_specs=[pl.BlockSpec(memory_space=pltpu.SMEM), whole, whole],
+        out_specs=[whole] * 4,
         out_shape=[jax.ShapeDtypeStruct((2, 8, tokens, UNIT), BF16)] * 4,
-        scratch_shapes=[pltpu.SemaphoreType.DMA((8,))],
         name="spread",
     )(x, own, other)
 
@@ -244,15 +230,49 @@
     )(table, own, other, near, *pieces)
 
 
-def attention_kernel(bias_ref, q_ref, go_ref, *refs):
+def finish_kernel(mine_ref, other_ref, doc_ref, out_ref):
+    tokens = mine_ref.shape[0]
+    out_ref[:tokens, :] = (mine_ref[...] + other_ref[...]).astype(BF16)
+    out_ref[tokens:, :] = jnp.zeros((8, out_ref.shape[1]), BF16)
+    out_ref[tokens:, :tokens] = doc_ref[...].astype(BF16)
+
+
+def finish(mine, other, doc_rows):
+    tokens, width = mine.shape
+    whole = pl.BlockSpec(memory_space=pltpu.VMEM)
+    return pl.pallas_call(
+        finish_kernel,
+        in_specs=[whole] * 3,
+        out_specs=whole,
+        out_shape=jax.ShapeDtypeStruct((tokens + 8, width), BF16),
+        name="finish",
+    )(mine, other, doc_rows)
+
+
+def attention_kernel(doc_ref, q_ref, go_ref, *refs):
     keys, values = refs[: BACK + 1], refs[BACK + 1 : 2 * BACK + 2]
-    att_ref, dq_ref, own_ref = refs[2 * BACK + 2 : 2 * BACK + 5]
-    back_refs = refs[2 * BACK + 5 : 3 * BACK + 5]
-    probs_ref, grads_ref, q_rows, go_rows = refs[3 * BACK + 5 :]
+    docs, refs = refs[2 * BACK + 2 : 3 * BACK + 3], refs[3 * BACK + 3 :]
+    att_ref, dq_ref, own_ref = refs[:3]
+    back_refs = refs[3 : BACK + 3]
+    probs_ref, grads_ref, q_rows, go_rows, bias_ref = refs[BACK + 3 :]
     head = pl.program_id(0)
     scale = HEAD ** (-0.5)
     group = q_ref.shape[1] // HEAD
     tokens = q_ref.shape[0]
+
+    @pl.when(head == 0)
+    def _():
+        shape = (tokens, tokens)
+        later = lax.broadcasted_iota(jnp.int32, shape, 0) > lax.broadcasted_iota(
+            jnp.int32, shape, 1
+        )
+        for k, ref in enumerate(docs):
+            of_key = jnp.broadcast_to(ref[:1, :].astype(F32), shape).T
+            bias = jnp.where(of_key == doc_ref[...], 0.0, -1e30)
+            bias_ref[k * tokens : (k + 1) * tokens, :] = (
+                bias if k else jnp.where(later, -1e30, bias)
+            )
+
     key = jnp.concatenate([r[...] for r in keys], axis=0)
     value = jnp.concatenate([r[...] for r in values], axis=0)
     key_t = key.astype(F32).T.astype(BF16)
@@ -294,7 +314,7 @@
         ref[:, pl.ds(value_at, HEAD)] = grad_value[at].astype(BF16)
 
 
-def attention(bias, queries, grad_out, kv_blocks):
+def attention(doc, queries, grad_out, kv_blocks):
     tokens, q_width = queries.shape
     kv_total = kv_blocks[0].shape[1]
     kv_heads = kv_total // 2 // HEAD
@@ -303,13 +323,15 @@
     q_spec = pl.BlockSpec((tokens, group_cols), lambda h: (0, h))
     key_spec = pl.BlockSpec((tokens, HEAD), lambda h: (0, h))
     value_spec = pl.BlockSpec((tokens, HEAD), lambda h: (0, kv_heads + h))
+    doc_spec = pl.BlockSpec((8, tokens), lambda h: (tokens // 8, 0))
     grad_spec = pl.BlockSpec((tokens, kv_total), lambda h: (0, 0))
     return pl.pallas_call(
         attention_kernel,
         grid=(kv_heads,),
-        in_specs=[pl.BlockSpec((span, tokens), lambda h: (0, 0)), q_spec, q_spec]
+        in_specs=[pl.BlockSpec((1, tokens), lambda h: (0, 0)), q_spec, q_spec]
         + [key_spec] * (BACK + 1)
-        + [value_spec] * (BACK + 1),
+        + [value_spec] * (BACK + 1)
+        + [doc_spec] * (BACK + 1),
         out_specs=[q_spec, q_spec] + [grad_spec] * (BACK + 1),
         out_shape=[
             jax.ShapeDtypeStruct((tokens, q_width), BF16),
@@ -322,10 +344,11 @@
             pltpu.VMEM((span, group_cols), BF16),
             pltpu.VMEM((tokens * group_cols // HEAD, HEAD), BF16),
             pltpu.VMEM((tokens * group_cols // HEAD, HEAD), BF16),
+            pltpu.VMEM((span, tokens), F32),
         ],
         compiler_params=pltpu.CompilerParams(vmem_limit_bytes=VMEM_LIMIT),
         name="attention",
-    )(bias, queries, grad_out, *kv_blocks, *kv_blocks)
+    )(doc, queries, grad_out, *kv_blocks, *kv_blocks, *kv_blocks)
 
 
 def grad_normed_kernel(table_ref, mine_ref, theirs_ref, *refs):
@@ -363,15 +386,11 @@
     )(table, mine, theirs, *pieces)
 
 
-def norm_back_kernel(core_ref, own_ref, recv_ref, x_ref, inv_ref, gain_ref, out_ref, sum_ref):
+def norm_back_kernel(core_ref, own_ref, recv_ref, x_ref, inv_ref, gain_ref, out_ref):
     first = core_ref[0] == 0
     inv = inv_ref[:, :1]
     width = x_ref.shape[1]
     step = x_ref.shape[0]
-
-    @pl.when(pl.program_id(0) == 0)
-    def _():
-        sum_ref[...] = jnp.zeros_like(sum_ref)
 
     def unit(at):
         u = (at % 4) * 8 + at // 8
@@ -384,9 +403,7 @@
     dots = jnp.zeros((step, UNIT), F32)
     for at in range(width // UNIT):
         cols, grad, scaled = unit(at)
-        both = grad * scaled
-        sum_ref[:, cols] += jnp.sum(both.reshape(step // 8, 8, UNIT), axis=0)
-        dots += both * gain_ref[:, cols]
+        dots += grad * gain_ref[:, cols] * scaled
     mean = jnp.sum(dots, axis=1, keepdims=True) * (1.0 / width)
     for at in range(width // UNIT):
         cols, grad, scaled = unit(at)
@@ -408,56 +425,83 @@
             pl.BlockSpec((step, UNIT), lambda i: (i, 0)),
             pl.BlockSpec((1, width), lambda i: (0, 0)),
         ],
-        out_specs=[
-            pl.BlockSpec((step, width), lambda i: (i, 0)),
-            pl.BlockSpec((8, width), lambda i: (0, 0)),
-        ],
-        out_shape=[
-            jax.ShapeDtypeStruct((tokens, width), BF16),
-            jax.ShapeDtypeStruct((8, width), F32),
-        ],
+        out_specs=pl.BlockSpec((step, width), lambda i: (i, 0)),
+        out_shape=jax.ShapeDtypeStruct((tokens, width), BF16),
         name="norm_back",
     )(core, own, recv, source, inv, gain)
 
 
-def grad_weight_kernel(*refs):
-    columns, grads, out_ref = refs[:4], refs[4:12], refs[12]
+def grad_weight_kernel(place_ref, *refs):
+    columns, grads, left, right = refs[:4], refs[4:12], refs[12:14], refs[14:18]
+    out_ref, gain_ref = refs[18:]
+    rows_each = UNIT // 2
     grad = jnp.concatenate([g[...] for g in grads], axis=0)
-    for j in range(0, columns[0].shape[1], 2):
+    half = grad.shape[1] // 2
+    for i in range(4):
+        at = [place_ref[2 * i + z] for z in (0, 1)]
         lhs = jnp.concatenate(
             [
-                jnp.concatenate([c[i, j], c[i, j + 1]], axis=1)
+                jnp.concatenate([c[t, at[0]], c[t, at[1]]], axis=1)
                 for c in columns
-                for i in (0, 1)
+                for t in (0, 1)
             ],
             axis=0,
         )
-        part = lax.dot_general(
-            lhs, grad, (((0,), (0,)), ((), ())), preferred_element_type=F32
-        ).astype(BF16)
-        out_ref[j] = part[:UNIT]
-        out_ref[j + 1] = part[UNIT:]
-
-
-def grad_weight_part(columns, grads):
+        part = lax.dot_general(lhs, grad, (((0,), (0,)), ((), ())), preferred_element_type=F32)
+        weight = (
+            left[i // 2][(i % 2) * 2 * UNIT : (i % 2 + 1) * 2 * UNIT, :],
+            right[i][: 2 * UNIT, :],
+        )
+        dots = jnp.zeros((2 * UNIT, UNIT), F32)
+        for side in (0, 1):
+            both = part[:, side * half : (side + 1) * half] * weight[side].astype(F32)
+            for col in range(0, half, UNIT):
+                dots += both[:, col : col + UNIT]
+        for z in (0, 1):
+            turned = dots[z * UNIT : (z + 1) * UNIT].T
+            gain_ref[pl.ds(at[z], 1), :] = jnp.sum(turned, axis=0, keepdims=True)
+            for h in (0, 1):
+                top = z * UNIT + h * rows_each
+                out_ref[2 * at[z] + h, :rows_each, :] = part[top : top + rows_each].astype(BF16)
+    rest = jnp.concatenate([gain_ref[u : u + 1, :] for u in range(8)], axis=1)
+    terms = []
+    for _ in range(3):
+        terms.append(rest.astype(BF16).astype(F32))
+        rest = rest - terms[-1]
+    terms = jnp.concatenate(terms + [jnp.zeros((5, rest.shape[1]), F32)], axis=0).astype(BF16)
+    for block in range(out_ref.shape[0]):
+        out_ref[block, rows_each:, :] = terms
+
+
+def grad_weight_part(place, columns, grads, left, right):
     units, width = columns[0].shape[1], grads[0].shape[1]
     whole = pl.BlockSpec(memory_space=pltpu.VMEM)
     return pl.pallas_call(
         grad_weight_kernel,
-        in_specs=[whole] * 12,
+        in_specs=[pl.BlockSpec(memory_space=pltpu.SMEM)] + [whole] * 18,
         out_specs=whole,
-        out_shape=jax.ShapeDtypeStruct((units, UNIT, width), BF16),
+        out_shape=jax.ShapeDtypeStruct((2 * units, UNIT // 2 + 8, width), BF16),
+        scratch_shapes=[pltpu.VMEM((units, UNIT), F32)],
         compiler_params=pltpu.CompilerParams(vmem_limit_bytes=VMEM_LIMIT),
         name="grad_weight",
-    )(*columns, *grads)
-
-
-def sum_everywhere(value):
-    for axis in ("core", "zlo", "zhi"):
-        value = value + shift(value, axis, 1)
-    for axis in ("y", "x"):
-        value = value + shift(value, axis, 1) + shift(value, axis, 2) + shift(value, axis, 3)
-    return value
+    )(place, *columns, *grads, *left, *right)
+
+
+def gather_gain(total):
+    other = shift(total, "core", 1)
+    pair = jnp.where(
+        lax.axis_index("core") == 0, jnp.stack([total, other]), jnp.stack([other, total])
+    )
+    found = [pair] + [shift(pair, "x", by) for by in range(1, 4)]
+    x = lax.axis_index("x")
+    in_order = []
+    for at in range(4):
+        piece = found[0]
+        for by in range(1, 4):
+            piece = jnp.where((x - by) % 4 == at, found[by], piece)
+        in_order.append(piece)
+    both = jnp.stack(in_order).reshape(4, 2, 8, UNIT)
+    return both.transpose(2, 1, 0, 3).reshape(-1)
 
 
 def step(layer_input, queries, grad_out, segment_ids, kv_weight, norm_gain):
@@ -465,17 +509,15 @@
     tokens = source.shape[0]
     core = lax.axis_index("core").astype(jnp.int32)[None]
     x = lax.axis_index("x").astype(jnp.int32)[None]
-    place = lax.axis_index("x") * SIZES["zhi"] + lax.axis_index("zhi")
     gain = norm_gain[None]
     table = unit_table()
-
-    doc = segment_ids[0]
-    moved = [shift_seq(doc, k) for k in range(1, BACK + 1)]
-    docs = [doc] + [jnp.where(place > k, d, -1) for k, d in enumerate(moved)]
-    local = jnp.arange(tokens, dtype=jnp.int32)
-    causal = rows([local] + [jnp.full((tokens,), -1, jnp.int32)] * BACK)
-    allowed = (rows(docs)[:, None] == doc[None, :]) & (causal[:, None] <= local[None, :])
-    bias = jnp.where(allowed, 0.0, -1e30).astype(F32)
+    zs, ys = lax.axis_index("zlo"), lax.axis_index("y")
+    turn = jnp.arange(8, dtype=jnp.int32)
+    rel = jnp.repeat(jnp.array(REL4, jnp.int32), 2)
+    unit_place = ((zs + turn) % 2 * 4 + (ys + rel) % 4).astype(jnp.int32)
+
+    doc = (segment_ids + 1).astype(F32)
+    doc_rows = jnp.broadcast_to(doc, (8, tokens))
 
     near, far = gather_weight(kv_weight)
     own, send, inv = normalize(core, source, gain)
@@ -484,12 +526,12 @@
 
     kv_near = project_near(table, own, other, near)
     kv_mine, kv_theirs = project_far(table, own, other, kv_near, far)
-    kv_own = (kv_mine + shift(kv_theirs, "core", 1)).astype(BF16)
+    kv_own = finish(kv_mine, shift(kv_theirs, "core", 1), doc_rows)
 
     kv_blocks = [kv_own] + [shift_seq(kv_own, k) for k in range(1, BACK + 1)]
     columns = [shift(block, "x", by) if by else block for by, block in enumerate(blocks)]
     attended, grad_queries, grad_here, *grad_back = attention(
-        bias, queries[0], grad_out[0], kv_blocks
+        doc, queries[0], grad_out[0], kv_blocks
     )
     total = grad_here
     for k, part in enumerate(grad_back):
@@ -502,12 +544,15 @@
         grads += [block, shift(block, "core", 1)]
 
     mine, theirs = grad_normed(table, grad_own, grad_other, near + far)
+    left_own, right_own = near[:2], [near[6], near[8], near[10], far[2]]
+    partial = grad_weight_part(unit_place, columns, grads, left_own, right_own)
+    arrived = lax.all_to_all(partial, ("zlo", "y", "zhi"), 0, 0, tiled=True)
+    arrived = jnp.sum(arrived.astype(F32), axis=0)
+    grad_weight = arrived[: kv_weight.shape[0]]
+    sums = arrived[kv_weight.shape[0] :]
+    grad_gain = gather_gain(sums[0] + sums[1] + sums[2]) / norm_gain
     theirs = shift(theirs, "core", 1)
-    grad_input, gain_rows = norm_back(core, mine, theirs, source, inv, gain)
-    partial = grad_weight_part(columns, grads).reshape(16, 64, kv_weight.shape[1])
-    arrived = lax.all_to_all(partial, ("zlo", "y", "zhi"), 0, 0, tiled=True)
-    grad_weight = jnp.sum(arrived.astype(F32), axis=0)
-    grad_gain = sum_everywhere(jnp.sum(gain_rows, axis=0))
+    grad_input = norm_back(core, mine, theirs, source, inv, gain)
     return attended[None], grad_queries[None], grad_input[None], grad_weight, grad_gain
 
 

time: 386 us -> 288 us (0.75); the launches traced: 380 us -> 287 us
  Pallas kernels: 185 us -> 65.5 us
  waiting for transfers between devices: 70.7 us -> 111 us
  starting transfers between devices: 111 us -> 98.4 us
    pallas_call x1, Pallas kernels: 64.7 us -> 3.05 us  [spread(): pl.pallas_call(spread_kernel, in_specs=[pl.BlockSpec(memory_space=pltpu.S...]
    pallas_call x3 -> x4, Pallas kernels: 71.6 us -> 13.5 us  [the longest x1 7.07 us: grad_weight_part(): pl.pallas_call(grad_weight_kernel, in_specs=[pl.BlockSpec(memory_space=pl...]
    all_to_all x1, waiting for transfers between devices: 0.01 us -> 29.2 us  [step(): arrived = lax.all_to_all(partial, ('zlo', 'y', 'zhi'), 0, 0, tiled=True)]
    ppermute x44 -> x39, waiting for transfers between devices: 58.1 us -> 69.1 us  [shift(): return lax.ppermute(value, axis, [(i, (i + by) % n) for i in range(n)])]
    ppermute x12 -> x8, starting transfers between devices: 25.7 us -> 14.8 us  [shift_seq(): return lax.ppermute(value, SEQ, pairs)]
    ppermute x44 -> x39, starting transfers between devices: 81.1 us -> 74.7 us  [shift(): return lax.ppermute(value, axis, [(i, (i + by) % n) for i in range(n)])]
    ppermute x1, starting transfers between devices: 0.01 us -> 4.65 us  [gather_weight(): both = lax.ppermute(weight, ('zlo', 'zhi'), [(i, 3 - i) for i in range(4)])]
    ppermute x12 -> x8, waiting for transfers between devices: 12.5 us -> 13 us  [shift_seq(): return lax.ppermute(value, SEQ, pairs)]
  transfers between devices with their start and end apart: 58 -> 49, of which waited for: 23 -> 20; matrix products, arithmetic and copies ran while one was open for 1% -> 2% of each run, Pallas kernels for 42% -> 11%
where the time goes in v3:
time: 288 us; the launch traced here: 287 us
  waiting for transfers between devices  111 us (39%)
  starting transfers between devices  98.4 us (34%)
  Pallas kernels  65.5 us (23%)
  local copies, waits for them, and re-layouts  7.08 us (2%)
  other arithmetic  3.76 us (1%)
    ppermute x39, starting transfers between devices, shift(): return lax.ppermute(value, axis, [(i, (i + by) % n) for i in range(n)])  74.7 us
    ppermute x39, waiting for transfers between devices, shift(): return lax.ppermute(value, axis, [(i, (i + by) % n) for i in range(n)])  69.1 us
    all_to_all x1, waiting for transfers between devices, step(): arrived = lax.all_to_all(partial, ('zlo', 'y', 'zhi'), 0, 0, tiled=True)  29.2 us
    pallas_call x1, Pallas kernels, attention(): pl.pallas_call(attention_kernel, grid=(kv_heads,), in_specs=[pl.BlockSpec...  21.5 us
    ppermute x8, starting transfers between devices, shift_seq(): return lax.ppermute(value, SEQ, pairs)  14.8 us
    ppermute x8, waiting for transfers between devices, shift_seq(): return lax.ppermute(value, SEQ, pairs)  13 us
    pallas_call x1, Pallas kernels, grad_normed(): pl.pallas_call(grad_normed_kernel, in_specs=[pl.BlockSpec(memory_space=pl...  7.36 us
    pallas_call x1, Pallas kernels, grad_weight_part(): pl.pallas_call(grad_weight_kernel, in_specs=[pl.BlockSpec(memory_space=pl...  7.07 us
  transfers between devices with their start and end apart: 49, of which 20 were waited for; matrix products, arithmetic and copies ran while one was open for 2% of the time, Pallas kernels for 11%

profile of v3, /device:TPU:1, one launch (start us, length us, event | category | flops | bytes accessed | tf_op | source)
XLA Modules:
  0.0 287.2 jit_solution(16484111675994547238)
XLA Ops:
  0.6 4.7 %collective-permute-start.3 = (bf16[64,1024]{1,0:T(8,128)(2,1)}, bf16[64,1024]{1,0:T(8,128)(2,1)S(1)}, u32[]{:S(2)}, u32[]{:S(2)}) collective-permute-start(bf16[64,1024]{1,0:T(8,128)(2,1)} %param.12), channel_id=1, source_target_pairs={{0,65},{1,64},{64,1},{65,0},{2,67},{3,66},{66,3},{67,2},{4,69},{5,... | collective-permute-start | bytes 393224 | tf_op jit(solution)/shard_map/ppermute | solution.py:82
  5.3 1.3 collective-permute-start.1
  6.6 4.4 %norm.1 = (bf16[32,128,128]{2,1,0:T(8,128)(2,1)}, bf16[32,128,128]{2,1,0:T(8,128)(2,1)}, f32[128,128]{1,0:T(8,128)}) custom-call(s32[1]{0:T(128)} %bitcast.2.core_ref, bf16[128,8192]{1,0:T(8,128)(2,1)} %bitcast.20, f32[1,8192]{1,0:T(1,128)} %bitcast.25), custom_call_target="tpu_custom_call" | custom-call | tf_op jit(solution)/shard_map/norm/pallas_call | solution.py:130
  10.9 1.2 collective-permute-start
  13.7 1.4 collective-permute-start.4
  15.1 1.5 collective-permute-start.5
  16.6 4.9 %collective-permute-done.4.refs_1_ = bf16[256,512]{1,0:T(8,128)(2,1)S(1)} collective-permute-done((bf16[256,512]{1,0:T(8,128)(2,1)S(1)}, bf16[256,512]{1,0:T(8,128)(2,1)S(1)}, u32[]{:S(2)}, u32[]{:S(2)}) %collective-permute-start.4) | collective-permute-done | bytes 262176 | tf_op jit(solution)/shard_map/ppermute | solution.py:25
  21.6 2.7 collective-permute-start.7
  24.3 2.3 collective-permute-done.6.refs_3_
  27.9 2.2 join.2
  30.1 1.2 collective-permute-start.8
  31.3 1.2 collective-permute-start.9
  33.5 1.8 collective-permute-start.13
  35.2 23.2 %collective-permute-done.12.refs_1_ = bf16[256,512]{1,0:T(8,128)(2,1)S(1)} collective-permute-done((bf16[256,512]{1,0:T(8,128)(2,1)S(1)}, bf16[256,512]{1,0:T(8,128)(2,1)S(1)}, u32[]{:S(2)}, u32[]{:S(2)}) %collective-permute-start.12) | collective-permute-done | bytes 262176 | tf_op jit(solution)/shard_map/ppermute | solution.py:25
  58.6 2.7 collective-permute-start.15
  61.3 2.3 collective-permute-done.14.refs_3_
  63.5 1.2 collective-permute-start.10
  65.4 1.6 collective-permute-start.11
  67.0 2.2 join.3
  69.4 2.6 collective-permute-start.19
  72.1 2.5 collective-permute-done.10.refs_4_
  74.6 1.8 collective-permute-start.18
  76.3 9.6 %collective-permute-done.11.refs_5_ = bf16[512,512]{1,0:T(8,128)(2,1)} collective-permute-done((bf16[512,512]{1,0:T(8,128)(2,1)}, bf16[512,512]{1,0:T(8,128)(2,1)}, u32[]{:S(2)}, u32[]{:S(2)}) %collective-permute-start.11) | collective-permute-done | bytes 524320 | tf_op jit(solution)/shard_map/ppermute | solution.py:25
  85.9 2.7 collective-permute-start.21
  88.6 2.7 collective-permute-start.23
  92.9 6.1 %project_near.1.near_ref = f32[256,1024]{1,0:T(8,128)} custom-call(s32[64]{0:T(128)} %reshape.117.table_ref, bf16[32,128,128]{2,1,0:T(8,128)(2,1)} %get-tuple-element.27.own_ref, bf16[32,128,128]{2,1,0:T(8,128)(2,1)} %copy-done, bf16[512,512]{1,0:T(8,128)(2,1)} %get-tuple-element.29.refs_0_.refs_12_, bf16[512,512]{1,0:T(8,128)(2,1)} %get-tuple-element.30.refs_1_.refs_13_, ...), custom_call_target="tpu_custom_call" | custom-call | tf_op jit(solution)/shard_map/project_near/pallas_call | solution.py:198
  99.1 2.5 collective-permute-done.22.refs_2_.refs_14_.refs_17_
  102.4 4.1 %project_far.1 = (f32[128,1024]{1,0:T(8,128)}, f32[128,1024]{1,0:T(8,128)}) custom-call(s32[64]{0:T(128)} %reshape.117.table_ref, bf16[32,128,128]{2,1,0:T(8,128)(2,1)} %get-tuple-element.27.own_ref, bf16[32,128,128]{2,1,0:T(8,128)(2,1)} %copy-done, f32[256,1024]{1,0:T(8,128)} %project_near.1.near_ref, ...), custom_call_target="tpu_custom_call" | custom-call | tf_op jit(solution)/shard_map/project_far/pallas_call | solution.py:223
  106.5 9.1 %collective-permute-start.24 = (f32[128,1024]{1,0:T(8,128)}, f32[128,1024]{1,0:T(8,128)S(1)}, u32[]{:S(2)}, u32[]{:S(2)}) collective-permute-start(f32[128,1024]{1,0:T(8,128)} %get-tuple-element.34), channel_id=1, source_target_pairs={{0,8},{8,0},{1,9},{9,1},{2,10},{10,2},{3,11},{11,3},{4,12},{12,4},... | collective-permute-start | bytes 1572872 | tf_op jit(solution)/shard_map/ppermute | solution.py:25
  116.2 1.2 collective-permute-done.24.other_ref
  118.2 2.0 finish.1.refs_0_.refs_5_.refs_10_
  120.1 3.6 %collective-permute-start.25 = (bf16[136,1024]{1,0:T(8,128)(2,1)}, bf16[136,1024]{1,0:T(8,128)(2,1)S(1)}, u32[]{:S(2)}, u32[]{:S(2)}) collective-permute-start(bf16[136,1024]{1,0:T(8,128)(2,1)} %finish.1.refs_0_.refs_5_.refs_10_), channel_id=1, source_target_pairs={{0,1},{1,2},{2,3},{3,4},{4,5},{5,6},{6,7},{8,9},{9,10},{10,11},{11... | collective-permute-start | bytes 835592 | tf_op jit(solution)/shard_map/ppermute | solution.py:31
  123.7 1.3 collective-permute-start.26
  125.0 2.9 %collective-permute-start.27 = (bf16[136,1024]{1,0:T(8,128)(2,1)}, bf16[136,1024]{1,0:T(8,128)(2,1)S(1)}, u32[]{:S(2)}, u32[]{:S(2)}) collective-permute-start(bf16[136,1024]{1,0:T(8,128)(2,1)} %finish.1.refs_0_.refs_5_.refs_10_), channel_id=1, source_target_pairs={{0,3},{1,4},{2,5},{3,6},{4,7},{8,11},{9,12},{10,13},{11,14},{12,15... | collective-permute-start | bytes 835592 | tf_op jit(solution)/shard_map/ppermute | solution.py:31
  128.0 1.6 collective-permute-start.28
  130.7 6.0 %collective-permute-done.27.refs_3_.refs_8_.refs_13_ = bf16[136,1024]{1,0:T(8,128)(2,1)S(1)} collective-permute-done((bf16[136,1024]{1,0:T(8,128)(2,1)}, bf16[136,1024]{1,0:T(8,128)(2,1)S(1)}, u32[]{:S(2)}, u32[]{:S(2)}) %collective-permute-start.27) | collective-permute-done | bytes 278560 | tf_op jit(solution)/shard_map/ppermute | solution.py:31
  136.7 6.0 %collective-permute-done.28.refs_4_.refs_9_.refs_14_ = bf16[136,1024]{1,0:T(8,128)(2,1)S(1)} collective-permute-done((bf16[136,1024]{1,0:T(8,128)(2,1)}, bf16[136,1024]{1,0:T(8,128)(2,1)S(1)}, u32[]{:S(2)}, u32[]{:S(2)}) %collective-permute-start.28) | collective-permute-done | bytes 278560 | tf_op jit(solution)/shard_map/ppermute | solution.py:31
  143.4 21.5 %attention.1 = (bf16[128,4096]{1,0:T(8,128)(2,1)}, bf16[128,4096]{1,0:T(8,128)(2,1)}, f32[128,1024]{1,0:T(8,128)}, bf16[128,1024]{1,0:T(8,128)(2,1)}, bf16[128,1...) custom-call(f32[1,128]{1,0:T(1,128)} %get-tuple-element.61.doc_ref, ...), custom_call_target="tpu_custom_call" | custom-call | tf_op jit(solution)/shard_map/attention/pallas_call | solution.py:328
  164.8 1.4 collective-permute-start.32
  166.3 1.3 collective-permute-start.31
  167.6 1.3 collective-permute-start.30
  168.9 1.3 collective-permute-start.29
  170.2 3.1 %spread.1 = (bf16[2,8,128,128]{3,2,1,0:T(8,128)(2,1)}, bf16[2,8,128,128]{3,2,1,0:T(8,128)(2,1)}, bf16[2,8,128,128]{3,2,1,0:T(8,128)(2,1)}, bf16[2,8,128,128]{3,2,1,0:T(8,128)(2,1)}) custom-call(s32[1]{0:T(128)} %bitcast.9.x_ref, bf16[32,128,128]{2,1,0:T(8,128)(2,1)} %get-tuple-element.27.own_ref, bf16[32,128,128]{2,1,0:T(8,128)(2,1)} %copy-done), custom_call_target="tpu_custom_call" | custom-call | tf_op jit(solution)/shard_map/spread/pallas_call | solution.py:162
  173.2 7.1 %collective-permute-start.35 = (bf16[2,8,128,128]{3,2,1,0:T(8,128)(2,1)}, bf16[2,8,128,128]{3,2,1,0:T(8,128)(2,1)S(1)}, u32[]{:S(2)}, u32[]{:S(2)}) collective-permute-start(bf16[2,8,128,128]{3,2,1,0:T(8,128)(2,1)} %get-tuple-element.46), channel_id=1, source_target_pairs={{0,2},{2,4},{4,6},{6,0},{1,3},{3,5},{5,7},{7,1},{8,10},{10,12},{12... | collective-permute-start | bytes 1572872 | tf_op jit(solution)/shard_map/ppermute | solution.py:25
  180.3 4.3 %collective-permute-start.36 = (bf16[2,8,128,128]{3,2,1,0:T(8,128)(2,1)}, bf16[2,8,128,128]{3,2,1,0:T(8,128)(2,1)S(1)}, u32[]{:S(2)}, u32[]{:S(2)}) collective-permute-start(bf16[2,8,128,128]{3,2,1,0:T(8,128)(2,1)} %get-tuple-element.47), channel_id=1, source_target_pairs={{0,4},{2,6},{4,0},{6,2},{1,5},{3,7},{5,1},{7,3},{8,12},{10,14},{12... | collective-permute-start | bytes 1572872 | tf_op jit(solution)/shard_map/ppermute | solution.py:25
  184.8 3.9 %collective-permute-start.38 = (bf16[128,1024]{1,0:T(8,128)(2,1)S(1)}, bf16[128,1024]{1,0:T(8,128)(2,1)S(1)}, u32[]{:S(2)}, u32[]{:S(2)}) collective-permute-start(bf16[128,1024]{1,0:T(8,128)(2,1)S(1)} %add_convert_fusion.mine_ref.refs_4_), channel_id=1, source_target_pairs={{0,2},{2,4},{4,6},{6,0},{1,3},{3,5},{5,7},{7,1},{8,10},{10,12},{12... | collective-permute-start | bytes 786440 | tf_op jit(solution)/shard_map/ppermute | solution.py:25
  188.7 1.8 collective-permute-start.40
  190.5 3.6 %collective-permute-done.35.refs_1_ = bf16[2,8,128,128]{3,2,1,0:T(8,128)(2,1)S(1)} collective-permute-done((bf16[2,8,128,128]{3,2,1,0:T(8,128)(2,1)}, bf16[2,8,128,128]{3,2,1,0:T(8,128)(2,1)S(1)}, u32[]{:S(2)}, u32[]{:S(2)}) %collective-permute-start.35) | collective-permute-done | bytes 524320 | tf_op jit(solution)/shard_map/ppermute | solution.py:25
  194.1 1.1 collective-permute-start.42
  195.3 11.0 %collective-permute-done.36.refs_2_ = bf16[2,8,128,128]{3,2,1,0:T(8,128)(2,1)S(1)} collective-permute-done((bf16[2,8,128,128]{3,2,1,0:T(8,128)(2,1)}, bf16[2,8,128,128]{3,2,1,0:T(8,128)(2,1)S(1)}, u32[]{:S(2)}, u32[]{:S(2)}) %collective-permute-start.36) | collective-permute-done | bytes 524320 | tf_op jit(solution)/shard_map/ppermute | solution.py:25
  206.2 4.9 %collective-permute-start.33 = (bf16[128,1024]{1,0:T(8,128)(2,1)S(1)}, bf16[128,1024]{1,0:T(8,128)(2,1)S(1)}, u32[]{:S(2)}, u32[]{:S(2)}) collective-permute-start(bf16[128,1024]{1,0:T(8,128)(2,1)S(1)} %add_convert_fusion.mine_ref.refs_4_), channel_id=1, source_target_pairs={{0,8},{8,0},{1,9},{9,1},{2,10},{10,2},{3,11},{11,3},{4,12},{12,4},... | collective-permute-start | bytes 786440 | tf_op jit(solution)/shard_map/ppermute | solution.py:25
  211.1 3.2 %collective-permute-start.39 = (bf16[128,1024]{1,0:T(8,128)(2,1)S(1)}, bf16[128,1024]{1,0:T(8,128)(2,1)S(1)}, u32[]{:S(2)}, u32[]{:S(2)}) collective-permute-start(bf16[128,1024]{1,0:T(8,128)(2,1)S(1)} %collective-permute-done.38.refs_6_), channel_id=1, source_target_pairs={{0,8},{8,0},{1,9},{9,1},{2,10},{10,2},{3,11},{11,3},{4,12},{12,4},... | collective-permute-start | bytes 786440 | tf_op jit(solution)/shard_map/ppermute | solution.py:25
  214.3 3.2 %collective-permute-done.40.refs_8_ = bf16[128,1024]{1,0:T(8,128)(2,1)S(1)} collective-permute-done((bf16[128,1024]{1,0:T(8,128)(2,1)S(1)}, bf16[128,1024]{1,0:T(8,128)(2,1)S(1)}, u32[]{:S(2)}, u32[]{:S(2)}) %collective-permute-start.40) | collective-permute-done | bytes 262176 | tf_op jit(solution)/shard_map/ppermute | solution.py:25
  217.5 2.6 collective-permute-start.41
  220.1 1.2 collective-permute-done.42.refs_10_
  221.3 1.6 collective-permute-start.43
  224.7 7.1 %grad_weight.1 = bf16[16,72,1024]{2,1,0:T(8,128)(2,1)} custom-call(s32[8]{0:T(128)} %fusion.place_ref, bf16[2,8,128,128]{3,2,1,0:T(8,128)(2,1)} %get-tuple-element.45.refs_0_, bf16[2,8,128,128]{3,2,1,0:T(8,128)(2,1)} %copy-done.19, bf16[2,8,128,128]{3,2,1,0:T(8,128)(2,1)} %copy-done.20, bf16[2,8,128,128]{3,2,1,0:T(8,128)(2,1)} %copy-done.21, ...), custom_call_target="tpu_custom_call" | custom-call | tf_op jit(solution)/shard_map/grad_weight/pallas_call | solution.py:479
  231.8 4.3 %all-to-all-start = ((bf16[16,72,1024]{2,1,0:T(8,128)(2,1)}), bf16[16,72,1024]{2,1,0:T(8,128)(2,1)S(1)}, u32[]{:S(2)}, u32[]{:S(2)}) async-start(bf16[16,72,1024]{2,1,0:T(8,128)(2,1)} %grad_weight.1), calls=%async_computation | async-start | bytes 4718592 | tf_op jit(solution)/shard_map/all_to_all | solution.py:549
  236.0 7.4 %grad_normed.1 = (bf16[32,128,128]{2,1,0:T(8,128)(2,1)}, bf16[32,128,128]{2,1,0:T(8,128)(2,1)}) custom-call(s32[64]{0:T(128)} %reshape.117.table_ref, bf16[128,1024]{1,0:T(8,128)(2,1)} %copy-done.8, bf16[128,1024]{1,0:T(8,128)(2,1)} %copy-done.12, bf16[512,512]{1,0:T(8,128)(2,1)} %get-tuple-element.29.refs_0_.refs_12_, ...), custom_call_target="tpu_custom_call" | custom-call | tf_op jit(solution)/shard_map/grad_normed/pallas_call | solution.py:378
  243.7 29.2 %all-to-all-done = bf16[16,72,1024]{2,1,0:T(8,128)(2,1)S(1)} async-done(((bf16[16,72,1024]{2,1,0:T(8,128)(2,1)}), bf16[16,72,1024]{2,1,0:T(8,128)(2,1)S(1)}, u32[]{:S(2)}, u32[]{:S(2)}) %all-to-all-start) | async-done | bytes 2359328 | tf_op jit(solution)/shard_map/all_to_all | solution.py:549
  273.4 1.3 collective-permute-start.44
  275.6 2.6 collective-permute-start.45
  278.2 1.5 collective-permute-start.46
  280.3 5.5 %norm_back.1 = bf16[128,8192]{1,0:T(8,128)(2,1)} custom-call(s32[1]{0:T(128)} %bitcast.2.core_ref, bf16[32,128,128]{2,1,0:T(8,128)(2,1)} %get-tuple-element.42.own_ref, bf16[32,128,128]{2,1,0:T(8,128)(2,1)} %collective-permute-done.34.recv_ref, bf16[128,8192]{1,0:T(8,128)(2,1)} %bitcast.21, f32[128,128]{1,0:T(8,128)} %get-tuple-element.44.inv_ref, ...), custom_call_target="tpu_custom_call" | custom-call | tf_op jit(solution)/shard_map/norm_back/pallas_call | solution.py:417
  (142 shorter events, 16.1 us)
Async XLA Ops:
  0.6 11.5 %collective-permute-start.3 = (bf16[64,1024]{1,0:T(8,128)(2,1)}, bf16[64,1024]{1,0:T(8,128)(2,1)S(1)}, u32[]{:S(2)}, u32[]{:S(2)}) collective-permute-start(bf16[64,1024]{1,0:T(8,128)(2,1)} %param.12), channel_id=1, source_target_pairs={{0,65},{1,64},{64,1},{65,0},{2,67},{3,66},{66,3},{67,2},{4,69},{5,... | collective-permute-start | bytes 393224 | tf_op jit(solution)/shard_map/ppermute | solution.py:82
  5.3 6.9 %collective-permute-start.2 = (bf16[64,1024]{1,0:T(8,128)(2,1)}, bf16[64,1024]{1,0:T(8,128)(2,1)S(1)}, u32[]{:S(2)}, u32[]{:S(2)}) collective-permute-start(bf16[64,1024]{1,0:T(8,128)(2,1)} %param.12), channel_id=1, source_target_pairs={{0,64},{64,0},{1,65},{65,1},{2,66},{66,2},{3,67},{67,3},{4,68},{68... | collective-permute-start | bytes 393224 | tf_op jit(solution)/shard_map/ppermute | solution.py:25
  5.3 7.2 %collective-permute-start.1 = (bf16[64,1024]{1,0:T(8,128)(2,1)}, bf16[64,1024]{1,0:T(8,128)(2,1)S(1)}, u32[]{:S(2)}, u32[]{:S(2)}) collective-permute-start(bf16[64,1024]{1,0:T(8,128)(2,1)} %param.12), channel_id=1, source_target_pairs={{0,1},{1,0},{2,3},{3,2},{4,5},{5,4},{6,7},{7,6},{8,9},{9,8},{10,11... | collective-permute-start | bytes 393224 | tf_op jit(solution)/shard_map/ppermute | solution.py:25
  10.9 58.3 %collective-permute-start = (bf16[32,128,128]{2,1,0:T(8,128)(2,1)}, bf16[32,128,128]{2,1,0:T(8,128)(2,1)S(1)}, u32[]{:S(2)}, u32[]{:S(2)}) collective-permute-start(bf16[32,128,128]{2,1,0:T(8,128)(2,1)} %get-tuple-element.28), channel_id=1, source_target_pairs={{0,8},{8,0},{1,9},{9,1},{2,10},{10,2},{3,11},{11,3},{4,12},{12,4},... | collective-permute-start | bytes 3145736 | tf_op jit(solution)/shard_map/ppermute | solution.py:25
  13.6 58.4 %copy-start.34 = (s32[4]{0:T(128)S(1)}, s32[4]{0:T(128)}, u32[]{:S(2)}) copy-start(s32[4]{0:T(128)} %constant.117.clone) | copy-start | bytes 52
  13.7 12.9 %copy-start.14 = (bf16[256,512]{1,0:T(8,128)(2,1)}, bf16[256,512]{1,0:T(8,128)(2,1)S(1)}, u32[]{:S(2)}) copy-start(bf16[256,512]{1,0:T(8,128)(2,1)S(1)} %get-tuple-element.50.refs_0_) | copy-start | bytes 786436
  13.7 53.3 %copy-start.13 = (bf16[256,512]{1,0:T(8,128)(2,1)}, bf16[256,512]{1,0:T(8,128)(2,1)S(1)}, u32[]{:S(2)}) copy-start(bf16[256,512]{1,0:T(8,128)(2,1)S(1)} %get-tuple-element.49.refs_0_) | copy-start | bytes 786436
  13.7 7.8 %collective-permute-start.4 = (bf16[256,512]{1,0:T(8,128)(2,1)S(1)}, bf16[256,512]{1,0:T(8,128)(2,1)S(1)}, u32[]{:S(2)}, u32[]{:S(2)}) collective-permute-start(bf16[256,512]{1,0:T(8,128)(2,1)S(1)} %get-tuple-element.50.refs_0_), channel_id=1, source_target_pairs={{0,16},{16,32},{32,48},{48,0},{1,17},{17,33},{33,49},{49,1},{2,18}... | collective-permute-start | bytes 786440 | tf_op jit(solution)/shard_map/ppermute | solution.py:25
  15.1 6.5 %collective-permute-start.5 = (bf16[256,512]{1,0:T(8,128)(2,1)S(1)}, bf16[256,512]{1,0:T(8,128)(2,1)S(1)}, u32[]{:S(2)}, u32[]{:S(2)}) collective-permute-start(bf16[256,512]{1,0:T(8,128)(2,1)S(1)} %get-tuple-element.50.refs_0_), channel_id=1, source_target_pairs={{0,48},{16,0},{32,16},{48,32},{1,49},{17,1},{33,17},{49,33},{2,50}... | collective-permute-start | bytes 786440 | tf_op jit(solution)/shard_map/ppermute | solution.py:25
  21.5 5.1 %collective-permute-start.6 = (bf16[128,512]{1,0:T(8,128)(2,1)S(1)}, bf16[128,512]{1,0:T(8,128)(2,1)S(1)}, u32[]{:S(2)}, u32[]{:S(2)}) collective-permute-start(bf16[128,512]{1,0:T(8,128)(2,1)S(1)} %slice.45), channel_id=1, source_target_pairs={{0,16},{16,32},{32,48},{48,0},{1,17},{17,33},{33,49},{49,1},{2,18}... | collective-permute-start | bytes 393224 | tf_op jit(solution)/shard_map/ppermute | solution.py:25
  21.6 5.0 %collective-permute-start.7 = (bf16[128,512]{1,0:T(8,128)(2,1)S(1)}, bf16[128,512]{1,0:T(8,128)(2,1)S(1)}, u32[]{:S(2)}, u32[]{:S(2)}) collective-permute-start(bf16[128,512]{1,0:T(8,128)(2,1)S(1)} %slice.46), channel_id=1, source_target_pairs={{0,48},{16,0},{32,16},{48,32},{1,49},{17,1},{33,17},{49,33},{2,50}... | collective-permute-start | bytes 393224 | tf_op jit(solution)/shard_map/ppermute | solution.py:25
  30.1 39.1 %collective-permute-start.8 = (bf16[512,512]{1,0:T(8,128)(2,1)}, bf16[512,512]{1,0:T(8,128)(2,1)S(1)}, u32[]{:S(2)}, u32[]{:S(2)}) collective-permute-start(bf16[512,512]{1,0:T(8,128)(2,1)} %get-tuple-element.29.refs_0_.refs_12_), channel_id=1, source_target_pairs={{0,2},{2,4},{4,6},{6,0},{1,3},{3,5},{5,7},{7,1},{8,10},{10,12},{12... | collective-permute-start | bytes 1572872 | tf_op jit(solution)/shard_map/ppermute | solution.py:25
  31.3 38.1 %collective-permute-start.9 = (bf16[512,512]{1,0:T(8,128)(2,1)}, bf16[512,512]{1,0:T(8,128)(2,1)S(1)}, u32[]{:S(2)}, u32[]{:S(2)}) collective-permute-start(bf16[512,512]{1,0:T(8,128)(2,1)} %get-tuple-element.30.refs_1_.refs_13_), channel_id=1, source_target_pairs={{0,2},{2,4},{4,6},{6,0},{1,3},{3,5},{5,7},{7,1},{8,10},{10,12},{12... | collective-permute-start | bytes 1572872 | tf_op jit(solution)/shard_map/ppermute | solution.py:25
  32.5 25.9 %collective-permute-start.12 = (bf16[256,512]{1,0:T(8,128)(2,1)S(1)}, bf16[256,512]{1,0:T(8,128)(2,1)S(1)}, u32[]{:S(2)}, u32[]{:S(2)}) collective-permute-start(bf16[256,512]{1,0:T(8,128)(2,1)S(1)} %get-tuple-element.49.refs_0_), channel_id=1, source_target_pairs={{0,2},{2,4},{4,6},{6,0},{1,3},{3,5},{5,7},{7,1},{8,10},{10,12},{12... | collective-permute-start | bytes 786440 | tf_op jit(solution)/shard_map/ppermute | solution.py:25
  33.5 25.1 %collective-permute-start.13 = (bf16[256,512]{1,0:T(8,128)(2,1)S(1)}, bf16[256,512]{1,0:T(8,128)(2,1)S(1)}, u32[]{:S(2)}, u32[]{:S(2)}) collective-permute-start(bf16[256,512]{1,0:T(8,128)(2,1)S(1)} %get-tuple-element.49.refs_0_), channel_id=1, source_target_pairs={{0,6},{2,0},{4,2},{6,4},{1,7},{3,1},{5,3},{7,5},{8,14},{10,8},{12,... | collective-permute-start | bytes 786440 | tf_op jit(solution)/shard_map/ppermute | solution.py:25
  58.4 8.5 %copy-start.15 = (bf16[256,512]{1,0:T(8,128)(2,1)}, bf16[256,512]{1,0:T(8,128)(2,1)S(1)}, u32[]{:S(2)}) copy-start(bf16[256,512]{1,0:T(8,128)(2,1)S(1)} %collective-permute-done.12.refs_1_) | copy-start | bytes 786436
  58.4 5.1 %collective-permute-start.14 = (bf16[128,512]{1,0:T(8,128)(2,1)S(1)}, bf16[128,512]{1,0:T(8,128)(2,1)S(1)}, u32[]{:S(2)}, u32[]{:S(2)}) collective-permute-start(bf16[128,512]{1,0:T(8,128)(2,1)S(1)} %slice.48), channel_id=1, source_target_pairs={{0,2},{2,4},{4,6},{6,0},{1,3},{3,5},{5,7},{7,1},{8,10},{10,12},{12... | collective-permute-start | bytes 393224 | tf_op jit(solution)/shard_map/ppermute | solution.py:25
  58.6 6.2 %collective-permute-start.15 = (bf16[128,512]{1,0:T(8,128)(2,1)S(1)}, bf16[128,512]{1,0:T(8,128)(2,1)S(1)}, u32[]{:S(2)}, u32[]{:S(2)}) collective-permute-start(bf16[128,512]{1,0:T(8,128)(2,1)S(1)} %slice.49), channel_id=1, source_target_pairs={{0,6},{2,0},{4,2},{6,4},{1,7},{3,1},{5,3},{7,5},{8,14},{10,8},{12,... | collective-permute-start | bytes 393224 | tf_op jit(solution)/shard_map/ppermute | solution.py:25
  63.5 11.0 %collective-permute-start.10 = (bf16[512,512]{1,0:T(8,128)(2,1)}, bf16[512,512]{1,0:T(8,128)(2,1)S(1)}, u32[]{:S(2)}, u32[]{:S(2)}) collective-permute-start(bf16[512,512]{1,0:T(8,128)(2,1)} %get-tuple-element.29.refs_0_.refs_12_), channel_id=1, source_target_pairs={{0,6},{2,0},{4,2},{6,4},{1,7},{3,1},{5,3},{7,5},{8,14},{10,8},{12,... | collective-permute-start | bytes 1572872 | tf_op jit(solution)/shard_map/ppermute | solution.py:25
  65.4 20.5 %collective-permute-start.11 = (bf16[512,512]{1,0:T(8,128)(2,1)}, bf16[512,512]{1,0:T(8,128)(2,1)}, u32[]{:S(2)}, u32[]{:S(2)}) collective-permute-start(bf16[512,512]{1,0:T(8,128)(2,1)} %get-tuple-element.30.refs_1_.refs_13_), channel_id=1, source_target_pairs={{0,6},{2,0},{4,2},{6,4},{1,7},{3,1},{5,3},{7,5},{8,14},{10,8},{12,... | collective-permute-start | bytes 1572872 | tf_op jit(solution)/shard_map/ppermute | solution.py:25
  69.2 22.9 %copy-start = (bf16[32,128,128]{2,1,0:T(8,128)(2,1)}, bf16[32,128,128]{2,1,0:T(8,128)(2,1)S(1)}, u32[]{:S(2)}) copy-start(bf16[32,128,128]{2,1,0:T(8,128)(2,1)S(1)} %collective-permute-done.other_ref) | copy-start | bytes 3145732
  69.2 16.7 %collective-permute-start.16 = (bf16[512,512]{1,0:T(8,128)(2,1)}, bf16[512,512]{1,0:T(8,128)(2,1)S(1)}, u32[]{:S(2)}, u32[]{:S(2)}) collective-permute-start(bf16[512,512]{1,0:T(8,128)(2,1)} %get-tuple-element.31.refs_6_.refs_14_), channel_id=1, source_target_pairs={{0,16},{16,32},{32,48},{48,0},{1,17},{17,33},{33,49},{49,1},{2,18}... | collective-permute-start | bytes 1572872 | tf_op jit(solution)/shard_map/ppermute | solution.py:25
  69.3 22.9 %copy-start.9 = (bf16[512,512]{1,0:T(8,128)(2,1)}, bf16[512,512]{1,0:T(8,128)(2,1)S(1)}, u32[]{:S(2)}) copy-start(bf16[512,512]{1,0:T(8,128)(2,1)S(1)} %collective-permute-done.8.refs_2_) | copy-start | bytes 1572868
  69.3 19.3 %collective-permute-start.17 = (bf16[512,512]{1,0:T(8,128)(2,1)}, bf16[512,512]{1,0:T(8,128)(2,1)}, u32[]{:S(2)}, u32[]{:S(2)}) collective-permute-start(bf16[512,512]{1,0:T(8,128)(2,1)} %get-tuple-element.32.refs_7_), channel_id=1, source_target_pairs={{0,16},{16,32},{32,48},{48,0},{1,17},{17,33},{33,49},{49,1},{2,18}... | collective-permute-start | bytes 1572872 | tf_op jit(solution)/shard_map/ppermute | solution.py:25
  69.4 19.2 %collective-permute-start.19 = (bf16[512,512]{1,0:T(8,128)(2,1)}, bf16[512,512]{1,0:T(8,128)(2,1)}, u32[]{:S(2)}, u32[]{:S(2)}) collective-permute-start(bf16[512,512]{1,0:T(8,128)(2,1)} %get-tuple-element.32.refs_7_), channel_id=1, source_target_pairs={{0,48},{16,0},{32,16},{48,32},{1,49},{17,1},{33,17},{49,33},{2,50}... | collective-permute-start | bytes 1572872 | tf_op jit(solution)/shard_map/ppermute | solution.py:25
  74.6 14.0 %copy-start.11 = (bf16[512,512]{1,0:T(8,128)(2,1)}, bf16[512,512]{1,0:T(8,128)(2,1)S(1)}, u32[]{:S(2)}) copy-start(bf16[512,512]{1,0:T(8,128)(2,1)S(1)} %collective-permute-done.10.refs_4_) | copy-start | bytes 1572868
  74.6 17.6 %collective-permute-start.18 = (bf16[512,512]{1,0:T(8,128)(2,1)}, bf16[512,512]{1,0:T(8,128)(2,1)S(1)}, u32[]{:S(2)}, u32[]{:S(2)}) collective-permute-start(bf16[512,512]{1,0:T(8,128)(2,1)} %get-tuple-element.31.refs_6_.refs_14_), channel_id=1, source_target_pairs={{0,48},{16,0},{32,16},{48,32},{1,49},{17,1},{33,17},{49,33},{2,50}... | collective-permute-start | bytes 1572872 | tf_op jit(solution)/shard_map/ppermute | solution.py:25
  85.9 13.2 %collective-permute-start.20 = (bf16[512,512]{1,0:T(8,128)(2,1)S(1)}, bf16[512,512]{1,0:T(8,128)(2,1)}, u32[]{:S(2)}, u32[]{:S(2)}) collective-permute-start(bf16[512,512]{1,0:T(8,128)(2,1)S(1)} %collective-permute-done.8.refs_2_), channel_id=1, source_target_pairs={{0,2},{2,4},{4,6},{6,0},{1,3},{3,5},{5,7},{7,1},{8,10},{10,12},{12... | collective-permute-start | bytes 1572872 | tf_op jit(solution)/shard_map/ppermute | solution.py:25
  85.9 13.1 %collective-permute-start.21 = (bf16[512,512]{1,0:T(8,128)(2,1)}, bf16[512,512]{1,0:T(8,128)(2,1)}, u32[]{:S(2)}, u32[]{:S(2)}) collective-permute-start(bf16[512,512]{1,0:T(8,128)(2,1)} %collective-permute-done.11.refs_5_), channel_id=1, source_target_pairs={{0,6},{2,0},{4,2},{6,4},{1,7},{3,1},{5,3},{7,5},{8,14},{10,8},{12,... | collective-permute-start | bytes 1572872 | tf_op jit(solution)/shard_map/ppermute | solution.py:25
  88.6 13.0 %collective-permute-start.22 = (bf16[512,512]{1,0:T(8,128)(2,1)S(1)}, bf16[512,512]{1,0:T(8,128)(2,1)S(1)}, u32[]{:S(2)}, u32[]{:S(2)}) collective-permute-start(bf16[512,512]{1,0:T(8,128)(2,1)S(1)} %collective-permute-done.16.refs_8_.refs_15_), channel_id=1, source_target_pairs={{0,16},{16,32},{32,48},{48,0},{1,17},{17,33},{33,49},{49,1},{2,18}... | collective-permute-start | bytes 1572872 | tf_op jit(solution)/shard_map/ppermute | solution.py:25
  88.6 13.0 %collective-permute-start.23 = (bf16[512,512]{1,0:T(8,128)(2,1)}, bf16[512,512]{1,0:T(8,128)(2,1)}, u32[]{:S(2)}, u32[]{:S(2)}) collective-permute-start(bf16[512,512]{1,0:T(8,128)(2,1)} %collective-permute-done.19.refs_11_), channel_id=1, source_target_pairs={{0,48},{16,0},{32,16},{48,32},{1,49},{17,1},{33,17},{49,33},{2,50}... | collective-permute-start | bytes 1572872 | tf_op jit(solution)/shard_map/ppermute | solution.py:25
  99.1 16.6 %copy-start.35 = (s32[1,128]{1,0:T(1,128)S(1)}, s32[1,128]{1,0:T(1,128)}, u32[]{:S(2)}) copy-start(s32[1,128]{1,0:T(1,128)} %param.11) | copy-start | bytes 1540
  106.5 10.9 %collective-permute-start.24 = (f32[128,1024]{1,0:T(8,128)}, f32[128,1024]{1,0:T(8,128)S(1)}, u32[]{:S(2)}, u32[]{:S(2)}) collective-permute-start(f32[128,1024]{1,0:T(8,128)} %get-tuple-element.34), channel_id=1, source_target_pairs={{0,8},{8,0},{1,9},{9,1},{2,10},{10,2},{3,11},{11,3},{4,12},{12,4},... | collective-permute-start | bytes 1572872 | tf_op jit(solution)/shard_map/ppermute | solution.py:25
  120.1 9.5 %collective-permute-start.25 = (bf16[136,1024]{1,0:T(8,128)(2,1)}, bf16[136,1024]{1,0:T(8,128)(2,1)S(1)}, u32[]{:S(2)}, u32[]{:S(2)}) collective-permute-start(bf16[136,1024]{1,0:T(8,128)(2,1)} %finish.1.refs_0_.refs_5_.refs_10_), channel_id=1, source_target_pairs={{0,1},{1,2},{2,3},{3,4},{4,5},{5,6},{6,7},{8,9},{9,10},{10,11},{11... | collective-permute-start | bytes 835592 | tf_op jit(solution)/shard_map/ppermute | solution.py:31
  123.7 7.0 %collective-permute-start.26 = (bf16[136,1024]{1,0:T(8,128)(2,1)}, bf16[136,1024]{1,0:T(8,128)(2,1)S(1)}, u32[]{:S(2)}, u32[]{:S(2)}) collective-permute-start(bf16[136,1024]{1,0:T(8,128)(2,1)} %finish.1.refs_0_.refs_5_.refs_10_), channel_id=1, source_target_pairs={{0,2},{1,3},{2,4},{3,5},{4,6},{5,7},{8,10},{9,11},{10,12},{11,13},... | collective-permute-start | bytes 835592 | tf_op jit(solution)/shard_map/ppermute | solution.py:31
  125.0 11.6 %collective-permute-start.27 = (bf16[136,1024]{1,0:T(8,128)(2,1)}, bf16[136,1024]{1,0:T(8,128)(2,1)S(1)}, u32[]{:S(2)}, u32[]{:S(2)}) collective-permute-start(bf16[136,1024]{1,0:T(8,128)(2,1)} %finish.1.refs_0_.refs_5_.refs_10_), channel_id=1, source_target_pairs={{0,3},{1,4},{2,5},{3,6},{4,7},{8,11},{9,12},{10,13},{11,14},{12,15... | collective-permute-start | bytes 835592 | tf_op jit(solution)/shard_map/ppermute | solution.py:31
  128.0 14.7 %collective-permute-start.28 = (bf16[136,1024]{1,0:T(8,128)(2,1)}, bf16[136,1024]{1,0:T(8,128)(2,1)S(1)}, u32[]{:S(2)}, u32[]{:S(2)}) collective-permute-start(bf16[136,1024]{1,0:T(8,128)(2,1)} %finish.1.refs_0_.refs_5_.refs_10_), channel_id=1, source_target_pairs={{0,4},{1,5},{2,6},{3,7},{8,12},{9,13},{10,14},{11,15},{16,20},{17,... | collective-permute-start | bytes 835592 | tf_op jit(solution)/shard_map/ppermute | solution.py:31
  129.7 13.0 %copy-start.4 = (bf16[136,1024]{1,0:T(8,128)(2,1)}, bf16[136,1024]{1,0:T(8,128)(2,1)S(1)}, u32[]{:S(2)}) copy-start(bf16[136,1024]{1,0:T(8,128)(2,1)S(1)} %collective-permute-done.25.refs_1_.refs_6_.refs_11_) | copy-start | bytes 835588
  130.7 11.9 %copy-start.5 = (bf16[136,1024]{1,0:T(8,128)(2,1)}, bf16[136,1024]{1,0:T(8,128)(2,1)S(1)}, u32[]{:S(2)}) copy-start(bf16[136,1024]{1,0:T(8,128)(2,1)S(1)} %collective-permute-done.26.refs_2_.refs_7_.refs_12_) | copy-start | bytes 835588
  164.8 19.7 %copy-start.22 = (f32[128,1024]{1,0:T(8,128)S(1)}, f32[128,1024]{1,0:T(8,128)}, u32[]{:S(2)}) copy-start(f32[128,1024]{1,0:T(8,128)} %get-tuple-element.37) | copy-start | bytes 1572868
  164.8 15.4 %collective-permute-start.32 = (bf16[128,1024]{1,0:T(8,128)(2,1)}, bf16[128,1024]{1,0:T(8,128)(2,1)S(1)}, u32[]{:S(2)}, u32[]{:S(2)}) collective-permute-start(bf16[128,1024]{1,0:T(8,128)(2,1)} %get-tuple-element.41), channel_id=1, source_target_pairs={{4,0},{5,1},{6,2},{7,3},{12,8},{13,9},{14,10},{15,11},{20,16},{21,... | collective-permute-start | bytes 786440 | tf_op jit(solution)/shard_map/ppermute | solution.py:31
  166.3 18.3 %collective-permute-start.31 = (bf16[128,1024]{1,0:T(8,128)(2,1)}, bf16[128,1024]{1,0:T(8,128)(2,1)S(1)}, u32[]{:S(2)}, u32[]{:S(2)}) collective-permute-start(bf16[128,1024]{1,0:T(8,128)(2,1)} %get-tuple-element.40), channel_id=1, source_target_pairs={{3,0},{4,1},{5,2},{6,3},{7,4},{11,8},{12,9},{13,10},{14,11},{15,12... | collective-permute-start | bytes 786440 | tf_op jit(solution)/shard_map/ppermute | solution.py:31
  167.6 17.0 %collective-permute-start.30 = (bf16[128,1024]{1,0:T(8,128)(2,1)}, bf16[128,1024]{1,0:T(8,128)(2,1)S(1)}, u32[]{:S(2)}, u32[]{:S(2)}) collective-permute-start(bf16[128,1024]{1,0:T(8,128)(2,1)} %get-tuple-element.39), channel_id=1, source_target_pairs={{2,0},{3,1},{4,2},{5,3},{6,4},{7,5},{10,8},{11,9},{12,10},{13,11},... | collective-permute-start | bytes 786440 | tf_op jit(solution)/shard_map/ppermute | solution.py:31
  168.9 15.7 %collective-permute-start.29 = (bf16[128,1024]{1,0:T(8,128)(2,1)}, bf16[128,1024]{1,0:T(8,128)(2,1)S(1)}, u32[]{:S(2)}, u32[]{:S(2)}) collective-permute-start(bf16[128,1024]{1,0:T(8,128)(2,1)} %get-tuple-element.38), channel_id=1, source_target_pairs={{1,0},{2,1},{3,2},{4,3},{5,4},{6,5},{7,6},{9,8},{10,9},{11,10},{12... | collective-permute-start | bytes 786440 | tf_op jit(solution)/shard_map/ppermute | solution.py:31
  173.2 20.9 %collective-permute-start.35 = (bf16[2,8,128,128]{3,2,1,0:T(8,128)(2,1)}, bf16[2,8,128,128]{3,2,1,0:T(8,128)(2,1)S(1)}, u32[]{:S(2)}, u32[]{:S(2)}) collective-permute-start(bf16[2,8,128,128]{3,2,1,0:T(8,128)(2,1)} %get-tuple-element.46), channel_id=1, source_target_pairs={{0,2},{2,4},{4,6},{6,0},{1,3},{3,5},{5,7},{7,1},{8,10},{10,12},{12... | collective-permute-start | bytes 1572872 | tf_op jit(solution)/shard_map/ppermute | solution.py:25
  180.3 26.0 %collective-permute-start.36 = (bf16[2,8,128,128]{3,2,1,0:T(8,128)(2,1)}, bf16[2,8,128,128]{3,2,1,0:T(8,128)(2,1)S(1)}, u32[]{:S(2)}, u32[]{:S(2)}) collective-permute-start(bf16[2,8,128,128]{3,2,1,0:T(8,128)(2,1)} %get-tuple-element.47), channel_id=1, source_target_pairs={{0,4},{2,6},{4,0},{6,2},{1,5},{3,7},{5,1},{7,3},{8,12},{10,14},{12... | collective-permute-start | bytes 1572872 | tf_op jit(solution)/shard_map/ppermute | solution.py:25
  184.7 39.5 %copy-start.8 = (bf16[128,1024]{1,0:T(8,128)(2,1)}, bf16[128,1024]{1,0:T(8,128)(2,1)S(1)}, u32[]{:S(2)}) copy-start(bf16[128,1024]{1,0:T(8,128)(2,1)S(1)} %add_convert_fusion.mine_ref.refs_4_) | copy-start | bytes 786436
  184.8 26.4 %collective-permute-start.38 = (bf16[128,1024]{1,0:T(8,128)(2,1)S(1)}, bf16[128,1024]{1,0:T(8,128)(2,1)S(1)}, u32[]{:S(2)}, u32[]{:S(2)}) collective-permute-start(bf16[128,1024]{1,0:T(8,128)(2,1)S(1)} %add_convert_fusion.mine_ref.refs_4_), channel_id=1, source_target_pairs={{0,2},{2,4},{4,6},{6,0},{1,3},{3,5},{5,7},{7,1},{8,10},{10,12},{12... | collective-permute-start | bytes 786440 | tf_op jit(solution)/shard_map/ppermute | solution.py:25
  188.7 34.9 %collective-permute-start.37 = (bf16[2,8,128,128]{3,2,1,0:T(8,128)(2,1)}, bf16[2,8,128,128]{3,2,1,0:T(8,128)(2,1)S(1)}, u32[]{:S(2)}, u32[]{:S(2)}) collective-permute-start(bf16[2,8,128,128]{3,2,1,0:T(8,128)(2,1)} %get-tuple-element.48), channel_id=1, source_target_pairs={{0,6},{2,0},{4,2},{6,4},{1,7},{3,1},{5,3},{7,5},{8,14},{10,8},{12,... | collective-permute-start | bytes 1572872 | tf_op jit(solution)/shard_map/ppermute | solution.py:25
  188.7 28.7 %collective-permute-start.40 = (bf16[128,1024]{1,0:T(8,128)(2,1)S(1)}, bf16[128,1024]{1,0:T(8,128)(2,1)S(1)}, u32[]{:S(2)}, u32[]{:S(2)}) collective-permute-start(bf16[128,1024]{1,0:T(8,128)(2,1)S(1)} %add_convert_fusion.mine_ref.refs_4_), channel_id=1, source_target_pairs={{0,4},{2,6},{4,0},{6,2},{1,5},{3,7},{5,1},{7,3},{8,12},{10,14},{12... | collective-permute-start | bytes 786440 | tf_op jit(solution)/shard_map/ppermute | solution.py:25
  194.1 30.1 %copy-start.19 = (bf16[2,8,128,128]{3,2,1,0:T(8,128)(2,1)}, bf16[2,8,128,128]{3,2,1,0:T(8,128)(2,1)S(1)}, u32[]{:S(2)}) copy-start(bf16[2,8,128,128]{3,2,1,0:T(8,128)(2,1)S(1)} %collective-permute-done.35.refs_1_) | copy-start | bytes 1572868
  194.1 27.2 %collective-permute-start.42 = (bf16[128,1024]{1,0:T(8,128)(2,1)S(1)}, bf16[128,1024]{1,0:T(8,128)(2,1)S(1)}, u32[]{:S(2)}, u32[]{:S(2)}) collective-permute-start(bf16[128,1024]{1,0:T(8,128)(2,1)S(1)} %add_convert_fusion.mine_ref.refs_4_), channel_id=1, source_target_pairs={{0,6},{2,0},{4,2},{6,4},{1,7},{3,1},{5,3},{7,5},{8,14},{10,8},{12,... | collective-permute-start | bytes 786440 | tf_op jit(solution)/shard_map/ppermute | solution.py:25
  206.2 18.0 %copy-start.20 = (bf16[2,8,128,128]{3,2,1,0:T(8,128)(2,1)}, bf16[2,8,128,128]{3,2,1,0:T(8,128)(2,1)S(1)}, u32[]{:S(2)}) copy-start(bf16[2,8,128,128]{3,2,1,0:T(8,128)(2,1)S(1)} %collective-permute-done.36.refs_2_) | copy-start | bytes 1572868
  206.2 17.4 %collective-permute-start.33 = (bf16[128,1024]{1,0:T(8,128)(2,1)S(1)}, bf16[128,1024]{1,0:T(8,128)(2,1)S(1)}, u32[]{:S(2)}, u32[]{:S(2)}) collective-permute-start(bf16[128,1024]{1,0:T(8,128)(2,1)S(1)} %add_convert_fusion.mine_ref.refs_4_), channel_id=1, source_target_pairs={{0,8},{8,0},{1,9},{9,1},{2,10},{10,2},{3,11},{11,3},{4,12},{12,4},... | collective-permute-start | bytes 786440 | tf_op jit(solution)/shard_map/ppermute | solution.py:25
  211.1 13.1 %copy-start.25 = (bf16[128,1024]{1,0:T(8,128)(2,1)}, bf16[128,1024]{1,0:T(8,128)(2,1)S(1)}, u32[]{:S(2)}) copy-start(bf16[128,1024]{1,0:T(8,128)(2,1)S(1)} %collective-permute-done.38.refs_6_) | copy-start | bytes 786436
  211.1 12.5 %collective-permute-start.39 = (bf16[128,1024]{1,0:T(8,128)(2,1)S(1)}, bf16[128,1024]{1,0:T(8,128)(2,1)S(1)}, u32[]{:S(2)}, u32[]{:S(2)}) collective-permute-start(bf16[128,1024]{1,0:T(8,128)(2,1)S(1)} %collective-permute-done.38.refs_6_), channel_id=1, source_target_pairs={{0,8},{8,0},{1,9},{9,1},{2,10},{10,2},{3,11},{11,3},{4,12},{12,4},... | collective-permute-start | bytes 786440 | tf_op jit(solution)/shard_map/ppermute | solution.py:25
  217.5 6.2 %collective-permute-start.41 = (bf16[128,1024]{1,0:T(8,128)(2,1)S(1)}, bf16[128,1024]{1,0:T(8,128)(2,1)S(1)}, u32[]{:S(2)}, u32[]{:S(2)}) collective-permute-start(bf16[128,1024]{1,0:T(8,128)(2,1)S(1)} %collective-permute-done.40.refs_8_), channel_id=1, source_target_pairs={{0,8},{8,0},{1,9},{9,1},{2,10},{10,2},{3,11},{11,3},{4,12},{12,4},... | collective-permute-start | bytes 786440 | tf_op jit(solution)/shard_map/ppermute | solution.py:25
  221.3 2.9 %collective-permute-start.43 = (bf16[128,1024]{1,0:T(8,128)(2,1)S(1)}, bf16[128,1024]{1,0:T(8,128)(2,1)}, u32[]{:S(2)}, u32[]{:S(2)}) collective-permute-start(bf16[128,1024]{1,0:T(8,128)(2,1)S(1)} %collective-permute-done.42.refs_10_), channel_id=1, source_target_pairs={{0,8},{8,0},{1,9},{9,1},{2,10},{10,2},{3,11},{11,3},{4,12},{12,4},... | collective-permute-start | bytes 786440 | tf_op jit(solution)/shard_map/ppermute | solution.py:25
  231.8 41.2 %all-to-all-start = ((bf16[16,72,1024]{2,1,0:T(8,128)(2,1)}), bf16[16,72,1024]{2,1,0:T(8,128)(2,1)S(1)}, u32[]{:S(2)}, u32[]{:S(2)}) async-start(bf16[16,72,1024]{2,1,0:T(8,128)(2,1)} %grad_weight.1), calls=%async_computation | async-start | bytes 4718592 | tf_op jit(solution)/shard_map/all_to_all | solution.py:549
  243.4 36.9 %collective-permute-start.34 = (bf16[32,128,128]{2,1,0:T(8,128)(2,1)}, bf16[32,128,128]{2,1,0:T(8,128)(2,1)}, u32[]{:S(2)}, u32[]{:S(2)}) collective-permute-start(bf16[32,128,128]{2,1,0:T(8,128)(2,1)} %get-tuple-element.43), channel_id=1, source_target_pairs={{0,8},{8,0},{1,9},{9,1},{2,10},{10,2},{3,11},{11,3},{4,12},{12,4},... | collective-permute-start | bytes 3145736 | tf_op jit(solution)/shard_map/ppermute | solution.py:25
  273.4 2.1 collective-permute-start.44
  275.6 10.9 %collective-permute-start.45 = (f32[2,1024]{1,0:T(2,128)S(1)}, f32[2,1024]{1,0:T(2,128)S(1)}, u32[]{:S(2)}, u32[]{:S(2)}) collective-permute-start(f32[2,1024]{1,0:T(2,128)S(1)} %maximum_select_fusion.1), channel_id=1, source_target_pairs={{0,6},{2,0},{4,2},{6,4},{1,7},{3,1},{5,3},{7,5},{8,14},{10,8},{12,... | collective-permute-start | bytes 24584 | tf_op jit(solution)/shard_map/ppermute | solution.py:25
  278.2 8.3 %collective-permute-start.46 = (f32[2,1024]{1,0:T(2,128)S(1)}, f32[2,1024]{1,0:T(2,128)S(1)}, u32[]{:S(2)}, u32[]{:S(2)}) collective-permute-start(f32[2,1024]{1,0:T(2,128)S(1)} %maximum_select_fusion.1), channel_id=1, source_target_pairs={{0,4},{2,6},{4,0},{6,2},{1,5},{3,7},{5,1},{7,3},{8,12},{10,14},{12... | collective-permute-start | bytes 24584 | tf_op jit(solution)/shard_map/ppermute | solution.py:25
  279.7 6.8 %collective-permute-start.47 = (f32[2,1024]{1,0:T(2,128)S(1)}, f32[2,1024]{1,0:T(2,128)S(1)}, u32[]{:S(2)}, u32[]{:S(2)}) collective-permute-start(f32[2,1024]{1,0:T(2,128)S(1)} %maximum_select_fusion.1), channel_id=1, source_target_pairs={{0,2},{2,4},{4,6},{6,0},{1,3},{3,5},{5,7},{7,1},{8,10},{10,12},{12... | collective-permute-start | bytes 24584 | tf_op jit(solution)/shard_map/ppermute | solution.py:25
  (21 other events, 61.6 us)

commit v4 on v3

--- a/solution.py
+++ b/solution.py
@@ -1,3 +1,5 @@
+import functools
+
 import jax
 import jax.numpy as jnp
 from jax import lax
@@ -39,39 +41,36 @@
     half = value.shape[0] // 2
     before = shift(value, axis, 1)
     after = shift(value, axis, -1)
-    return [value, before, after, shift(before[:half], axis, 1), shift(after[half:], axis, -1)]
+    far = [shift(before[:half], axis, 1), shift(after[half:], axis, -1)]
+    first = join([value, before])
+    second = join([after] + far)
+    return first, second
 
 
 def ring4_halves(first, second, axis):
-    before_first = shift(first, axis, 1)
-    after_second = shift(second, axis, -1)
-    before_second = shift(second, axis, 1)
-    after_first = shift(first, axis, -1)
+    before_first, after_first = shift(first, axis, 1), shift(first, axis, -1)
+    before_second, after_second = shift(second, axis, 1), shift(second, axis, -1)
     far_first = shift(before_first, axis, 1)
     far_second = shift(after_second, axis, -1)
-    near = [first, second, before_first, before_second, after_first, after_second]
-    return near, [far_first, far_second]
+    near = [first, second, before_first, after_first]
+    return near, [before_second, after_second], [far_first, far_second]
 
 
 def join_kernel(*refs):
-    pieces, (first_ref, second_ref) = refs[:5], refs[5:]
-    size = pieces[0].shape[0]
-    half = size // 2
-    first_ref[:size, :] = pieces[0][...]
-    first_ref[size:, :] = pieces[1][...]
-    second_ref[:size, :] = pieces[2][...]
-    second_ref[size : size + half, :] = pieces[3][...]
-    second_ref[size + half :, :] = pieces[4][...]
+    out_ref, at = refs[-1], 0
+    for piece in refs[:-1]:
+        out_ref[at : at + piece.shape[0], :] = piece[...]
+        at += piece.shape[0]
 
 
 def join(pieces):
-    size, width = pieces[0].shape
     whole = pl.BlockSpec(memory_space=pltpu.VMEM)
+    size = sum(piece.shape[0] for piece in pieces)
     return pl.pallas_call(
         join_kernel,
-        in_specs=[whole] * 5,
-        out_specs=[whole] * 2,
-        out_shape=[jax.ShapeDtypeStruct((2 * size, width), BF16)] * 2,
+        in_specs=[whole] * len(pieces),
+        out_specs=whole,
+        out_shape=jax.ShapeDtypeStruct((size, pieces[0].shape[1]), BF16),
         name="join",
     )(*pieces)
 
@@ -88,9 +87,8 @@
     half = pair.shape[1] // 2
     left = ring4(pair[:, :half], "y")
     right = ring4(pair[:, half:], "x")
-    left_near, left_far = ring4_halves(*join(left), "x")
-    right_near, right_far = ring4_halves(*join(right), "y")
-    return left_near + right_near, left_far + right_far
+    lots = zip(ring4_halves(*left, "x"), ring4_halves(*right, "y"))
+    return [at_left + at_right for at_left, at_right in lots]
 
 
 def unit_table():
@@ -103,7 +101,8 @@
     return jnp.stack([left, right]).reshape(64).astype(jnp.int32)
 
 
-NEAR = tuple((side, side * 32 + first) for side in (0, 1) for first in (0, 4, 8, 12, 16, 20))
+NEAR = tuple((side, side * 32 + first) for side in (0, 1) for first in (0, 4, 8, 16))
+MORE = tuple((side, side * 32 + first) for side in (0, 1) for first in (12, 20))
 FAR = tuple((side, side * 32 + first) for side in (0, 1) for first in (24, 28))
 COUNT = 4
 
@@ -183,26 +182,30 @@
     return total
 
 
-def project_near_kernel(table_ref, own_ref, other_ref, *refs):
-    out_ref = refs[-1]
+def project_lot_kernel(table_ref, own_ref, other_ref, *refs, lot):
+    pieces, out_ref = refs[: len(lot)], refs[-1]
     for side in (0, 1):
-        total = project_sum(table_ref, own_ref, other_ref, NEAR, refs[:-1], side)
+        total = project_sum(table_ref, own_ref, other_ref, lot, pieces, side)
         width = total.shape[1]
-        out_ref[:, side * width : (side + 1) * width] = total
-
-
-def project_near(table, own, other, pieces):
+        cols = slice(side * width, (side + 1) * width)
+        if len(refs) > len(lot) + 1:
+            total = total + refs[len(lot)][:, cols]
+        out_ref[:, cols] = total
+
+
+def project_lot(table, own, other, lot, pieces, *before):
     tokens = own.shape[1]
     width = 2 * pieces[0].shape[1]
     whole = pl.BlockSpec(memory_space=pltpu.VMEM)
     return pl.pallas_call(
-        project_near_kernel,
-        in_specs=[pl.BlockSpec(memory_space=pltpu.SMEM)] + [whole] * (2 + len(pieces)),
+        functools.partial(project_lot_kernel, lot=lot),
+        in_specs=[pl.BlockSpec(memory_space=pltpu.SMEM)]
+        + [whole] * (2 + len(pieces) + len(before)),
         out_specs=whole,
         out_shape=jax.ShapeDtypeStruct((2 * tokens, width), F32),
         compiler_params=pltpu.CompilerParams(vmem_limit_bytes=VMEM_LIMIT),
-        name="project_near",
-    )(table, own, other, *pieces)
+        name="project_lot",
+    )(table, own, other, *pieces, *before)
 
 
 def project_far_kernel(table_ref, own_ref, other_ref, near_ref, *refs):
@@ -254,7 +257,8 @@
     docs, refs = refs[2 * BACK + 2 : 3 * BACK + 3], refs[3 * BACK + 3 :]
     att_ref, dq_ref, own_ref = refs[:3]
     back_refs = refs[3 : BACK + 3]
-    probs_ref, grads_ref, q_rows, go_rows, bias_ref = refs[BACK + 3 :]
+    probs_ref, grads_ref, q_rows, go_rows, bias_ref = refs[BACK + 3 : BACK + 8]
+    score_ref, expo_ref, half_ref, gp_ref = refs[BACK + 8 :]
     head = pl.program_id(0)
     scale = HEAD ** (-0.5)
     group = q_ref.shape[1] // HEAD
@@ -277,30 +281,60 @@
     value = jnp.concatenate([r[...] for r in values], axis=0)
     key_t = key.astype(F32).T.astype(BF16)
     value_t = value.astype(F32).T.astype(BF16)
-    bias = bias_ref[...]
     nt = (((1,), (1,)), ((), ()))
-    for j in range(group):
+    blocks = [slice(k * tokens, (k + 1) * tokens) for k in range(BACK + 1)]
+
+    def fold(block, op):
+        return op(block.reshape(tokens // 8, 8, tokens), axis=0)
+
+    def products(j):
         cols = slice(j * HEAD, (j + 1) * HEAD)
-        q = q_ref[:, cols]
-        go = go_ref[:, cols]
+        q, go = q_ref[:, cols], go_ref[:, cols]
         q_rows[j * tokens : (j + 1) * tokens, :] = q
         go_rows[j * tokens : (j + 1) * tokens, :] = go
-        score = lax.dot_general(key, q, nt, preferred_element_type=F32) * scale + bias
-        top = jnp.max(score, axis=0, keepdims=True)
-        expo = jnp.exp(score - top)
-        total = jnp.sum(expo, axis=0, keepdims=True)
-        summed = jnp.dot(value_t, expo.astype(BF16), preferred_element_type=F32) / total
+        score_ref[j % 2] = lax.dot_general(key, q, nt, preferred_element_type=F32)
+        gp_ref[j % 3] = lax.dot_general(value, go, nt, preferred_element_type=F32)
+
+    def soften(j):
+        cols = slice(j * HEAD, (j + 1) * HEAD)
+        top = None
+        for at in blocks:
+            score = score_ref[j % 2, at] * scale + bias_ref[at]
+            score_ref[j % 2, at] = score
+            part = fold(score, jnp.max)
+            top = part if top is None else jnp.maximum(top, part)
+        top = jnp.max(top, axis=0, keepdims=True)
+        total = jnp.zeros((8, tokens), F32)
+        for at in blocks:
+            expo = jnp.exp(score_ref[j % 2, at] - top)
+            expo_ref[j % 2, at] = expo
+            half_ref[j % 2, at] = expo.astype(BF16)
+            total = total + fold(expo, jnp.sum)
+        total = jnp.sum(total, axis=0, keepdims=True)
+        summed = jnp.dot(value_t, half_ref[j % 2], preferred_element_type=F32) / total
         att = summed.astype(BF16).astype(F32)
-        go_t = go.astype(F32).T
-        delta = jnp.sum(att * go_t, axis=0, keepdims=True)
+        delta = jnp.sum(att * go_ref[:, cols].astype(F32).T, axis=0, keepdims=True)
         att_ref[:, cols] = att.T.astype(BF16)
-        probs = expo * (1.0 / total)
-        grad_probs = lax.dot_general(value, go, nt, preferred_element_type=F32)
-        grad_scores = (probs * (grad_probs - delta)).astype(BF16)
-        probs_ref[:, cols] = probs.astype(BF16)
-        grads_ref[:, cols] = grad_scores
-        dq = jnp.dot(key_t, grad_scores, preferred_element_type=F32) * scale
+        return 1.0 / total, delta
+
+    def gradients(j, inverse, delta):
+        cols = slice(j * HEAD, (j + 1) * HEAD)
+        for at in blocks:
+            probs = expo_ref[j % 2, at] * inverse
+            probs_ref[at, cols] = probs.astype(BF16)
+            grads_ref[at, cols] = (probs * (gp_ref[j % 3, at] - delta)).astype(BF16)
+        dq = jnp.dot(key_t, grads_ref[:, cols], preferred_element_type=F32) * scale
         dq_ref[:, cols] = dq.T.astype(BF16)
+
+    products(0)
+    products(1)
+    rows_of = soften(0)
+    for j in range(group):
+        if j + 2 < group:
+            products(j + 2)
+        following = soften(j + 1) if j + 1 < group else None
+        gradients(j, *rows_of)
+        rows_of = following
     grad_key = jnp.dot(grads_ref[...], q_rows[...], preferred_element_type=F32) * scale
     grad_value = jnp.dot(probs_ref[...], go_rows[...], preferred_element_type=F32)
     kv_width = own_ref.shape[1] // 2
@@ -345,6 +379,10 @@
             pltpu.VMEM((tokens * group_cols // HEAD, HEAD), BF16),
             pltpu.VMEM((tokens * group_cols // HEAD, HEAD), BF16),
             pltpu.VMEM((span, tokens), F32),
+            pltpu.VMEM((2, span, tokens), F32),
+            pltpu.VMEM((2, span, tokens), F32),
+            pltpu.VMEM((2, span, tokens), BF16),
+            pltpu.VMEM((3, span, tokens), F32),
         ],
         compiler_params=pltpu.CompilerParams(vmem_limit_bytes=VMEM_LIMIT),
         name="attention",
@@ -355,7 +393,7 @@
     pieces, (own_ref, send_ref, acc_ref) = refs[:-3], refs[-3:]
     tokens = mine_ref.shape[0]
     nt = (((1,), (1,)), ((), ()))
-    order = sorted(zip(NEAR + FAR, pieces), key=lambda entry: entry[0])
+    order = sorted(zip(NEAR + MORE + FAR, pieces), key=lambda entry: entry[0])
     for (side, first), piece in order:
         width = piece.shape[1]
         cols = slice(side * width, (side + 1) * width)
@@ -433,8 +471,8 @@
 
 def grad_weight_kernel(place_ref, *refs):
     columns, grads, left, right = refs[:4], refs[4:12], refs[12:14], refs[14:18]
-    out_ref, gain_ref = refs[18:]
-    rows_each = UNIT // 2
+    first_ref, second_ref, gain_ref = refs[18:]
+    rows_each, cut = UNIT // 2, UNIT // 4
     grad = jnp.concatenate([g[...] for g in grads], axis=0)
     half = grad.shape[1] // 2
     for i in range(4):
@@ -462,15 +500,17 @@
             gain_ref[pl.ds(at[z], 1), :] = jnp.sum(turned, axis=0, keepdims=True)
             for h in (0, 1):
                 top = z * UNIT + h * rows_each
-                out_ref[2 * at[z] + h, :rows_each, :] = part[top : top + rows_each].astype(BF16)
+                block = part[top : top + rows_each].astype(BF16)
+                first_ref[2 * at[z] + h, :cut, :] = block[:cut]
+                second_ref[2 * at[z] + h] = block[cut:]
     rest = jnp.concatenate([gain_ref[u : u + 1, :] for u in range(8)], axis=1)
     terms = []
     for _ in range(3):
         terms.append(rest.astype(BF16).astype(F32))
         rest = rest - terms[-1]
     terms = jnp.concatenate(terms + [jnp.zeros((5, rest.shape[1]), F32)], axis=0).astype(BF16)
-    for block in range(out_ref.shape[0]):
-        out_ref[block, rows_each:, :] = terms
+    for i in range(first_ref.shape[0]):
+        first_ref[i, cut:, :] = terms
 
 
 def grad_weight_part(place, columns, grads, left, right):
@@ -479,8 +519,11 @@
     return pl.pallas_call(
         grad_weight_kernel,
         in_specs=[pl.BlockSpec(memory_space=pltpu.SMEM)] + [whole] * 18,
-        out_specs=whole,
-        out_shape=jax.ShapeDtypeStruct((2 * units, UNIT // 2 + 8, width), BF16),
+        out_specs=[whole] * 2,
+        out_shape=[
+            jax.ShapeDtypeStruct((2 * units, UNIT // 4 + 8, width), BF16),
+            jax.ShapeDtypeStruct((2 * units, UNIT // 4, width), BF16),
+        ],
         scratch_shapes=[pltpu.VMEM((units, UNIT), F32)],
         compiler_params=pltpu.CompilerParams(vmem_limit_bytes=VMEM_LIMIT),
         name="grad_weight",
@@ -519,12 +562,13 @@
     doc = (segment_ids + 1).astype(F32)
     doc_rows = jnp.broadcast_to(doc, (8, tokens))
 
-    near, far = gather_weight(kv_weight)
+    near, more, far = gather_weight(kv_weight)
     own, send, inv = normalize(core, source, gain)
     other = shift(send, "core", 1)
     blocks = spread(x, own, other)
 
-    kv_near = project_near(table, own, other, near)
+    kv_near = project_lot(table, own, other, NEAR, near)
+    kv_near = project_lot(table, own, other, MORE, more, kv_near)
     kv_mine, kv_theirs = project_far(table, own, other, kv_near, far)
     kv_own = finish(kv_mine, shift(kv_theirs, "core", 1), doc_rows)
 
@@ -543,14 +587,18 @@
     for block in fars:
         grads += [block, shift(block, "core", 1)]
 
-    mine, theirs = grad_normed(table, grad_own, grad_other, near + far)
-    left_own, right_own = near[:2], [near[6], near[8], near[10], far[2]]
-    partial = grad_weight_part(unit_place, columns, grads, left_own, right_own)
-    arrived = lax.all_to_all(partial, ("zlo", "y", "zhi"), 0, 0, tiled=True)
+    mine, theirs = grad_normed(table, grad_own, grad_other, near + more + far)
+    left_own, right_own = near[:2], [near[4], near[6], near[7], far[2]]
+    halves = grad_weight_part(unit_place, columns, grads, left_own, right_own)
+    group = ("zlo", "y", "zhi")
+    arrived = lax.all_to_all(halves[0], group, 0, 0, tiled=True)
+    arrived, later = lax.optimization_barrier((arrived, halves[1]))
     arrived = jnp.sum(arrived.astype(F32), axis=0)
-    grad_weight = arrived[: kv_weight.shape[0]]
-    sums = arrived[kv_weight.shape[0] :]
+    cut = kv_weight.shape[0] // 2
+    sums = arrived[cut:]
     grad_gain = gather_gain(sums[0] + sums[1] + sums[2]) / norm_gain
+    rest = lax.all_to_all(later, group, 0, 0, tiled=True)
+    grad_weight = rows([arrived[:cut], jnp.sum(rest.astype(F32), axis=0)])
     theirs = shift(theirs, "core", 1)
     grad_input = norm_back(core, mine, theirs, source, inv, gain)
     return attended[None], grad_queries[None], grad_input[None], grad_weight, grad_gain

time: 288 us -> 263 us (0.913); the launches traced: 287 us -> 258 us
  waiting for transfers between devices: 111 us -> 69.1 us
  starting transfers between devices: 98.4 us -> 108 us
  Pallas kernels: 65.5 us -> 69.2 us
    ppermute x39, waiting for transfers between devices: 69.1 us -> 44.1 us  [shift(): return lax.ppermute(value, axis, [(i, (i + by) % n) for i in range(n)])]
    all_to_all x1 -> x2, waiting for transfers between devices: 29.2 us -> 13.1 us  [the longest x1 13.1 us: step(): arrived = lax.all_to_all(halves[0], group, 0, 0, tiled=True)]
    pallas_call x3 -> x6, Pallas kernels: 10.6 us -> 16.7 us  [the longest x2 9.18 us: project_lot(): pl.pallas_call(functools.partial(project_lot_kernel, lot=lot), in_specs=[...]
    all_to_all x1 -> x2, starting transfers between devices: 4.26 us -> 9.23 us  [the longest x1 5.3 us: step(): rest = lax.all_to_all(later, group, 0, 0, tiled=True)]
    ppermute x8, starting transfers between devices: 14.8 us -> 19.3 us  [shift_seq(): return lax.ppermute(value, SEQ, pairs)]
    ppermute x8, waiting for transfers between devices: 13 us -> 9.74 us  [shift_seq(): return lax.ppermute(value, SEQ, pairs)]
  transfers between devices with their start and end apart: 49 -> 50, of which waited for: 20 -> 20; matrix products, arithmetic and copies ran while one was open for 2% -> 2% of each run, Pallas kernels for 11% -> 14%
where the time goes in v4:
time: 263 us; the launch traced here: 258 us
  starting transfers between devices  108 us (41%)
  Pallas kernels  69.2 us (26%)
  waiting for transfers between devices  69.1 us (26%)
  local copies, waits for them, and re-layouts  6.24 us (2%)
  other arithmetic  4.42 us (2%)
    ppermute x39, starting transfers between devices, shift(): return lax.ppermute(value, axis, [(i, (i + by) % n) for i in range(n)])  75 us
    ppermute x39, waiting for transfers between devices, shift(): return lax.ppermute(value, axis, [(i, (i + by) % n) for i in range(n)])  44.1 us
    ppermute x8, starting transfers between devices, shift_seq(): return lax.ppermute(value, SEQ, pairs)  19.3 us
    pallas_call x1, Pallas kernels, attention(): pl.pallas_call(attention_kernel, grid=(kv_heads,), in_specs=[pl.BlockSpec...  19.2 us
    all_to_all x1, waiting for transfers between devices, step(): arrived = lax.all_to_all(halves[0], group, 0, 0, tiled=True)  13.1 us
    ppermute x8, waiting for transfers between devices, shift_seq(): return lax.ppermute(value, SEQ, pairs)  9.74 us
    pallas_call x2, Pallas kernels, project_lot(): pl.pallas_call(functools.partial(project_lot_kernel, lot=lot), in_specs=[...  9.18 us
    pallas_call x4, Pallas kernels, join(): pl.pallas_call(join_kernel, in_specs=[whole] * len(pieces), out_specs=who...  7.54 us
  transfers between devices with their start and end apart: 50, of which 20 were waited for; matrix products, arithmetic and copies ran while one was open for 2% of the time, Pallas kernels for 14%

profile of v4, /device:TPU:1, one launch (start us, length us, event | category | flops | bytes accessed | tf_op | source)
XLA Modules:
  0.0 258.3 jit_solution(15167385550339460219)
XLA Ops:
  0.6 4.7 %collective-permute-start.3 = (bf16[64,1024]{1,0:T(8,128)(2,1)}, bf16[64,1024]{1,0:T(8,128)(2,1)S(1)}, u32[]{:S(2)}, u32[]{:S(2)}) collective-permute-start(bf16[64,1024]{1,0:T(8,128)(2,1)} %param.12), channel_id=1, source_target_pairs={{0,65},{1,64},{64,1},{65,0},{2,67},{3,66},{66,3},{67,2},{4,69},{5,... | collective-permute-start | bytes 393224 | tf_op jit(solution)/shard_map/ppermute | solution.py:81
  6.6 2.1 collective-permute-done.3
  9.6 3.0 %collective-permute-done.1 = bf16[64,1024]{1,0:T(8,128)(2,1)S(1)} collective-permute-done((bf16[64,1024]{1,0:T(8,128)(2,1)}, bf16[64,1024]{1,0:T(8,128)(2,1)S(1)}, u32[]{:S(2)}, u32[]{:S(2)}) %collective-permute-start.1) | collective-permute-done | bytes 131104 | tf_op jit(solution)/shard_map/ppermute | solution.py:27
  13.7 1.4 collective-permute-start.5
  16.3 1.5 collective-permute-start.4
  17.8 1.5 collective-permute-start.10
  19.3 2.2 collective-permute-done.5.refs_1_
  21.6 4.4 %norm.1 = (bf16[32,128,128]{2,1,0:T(8,128)(2,1)}, bf16[32,128,128]{2,1,0:T(8,128)(2,1)}, f32[128,128]{1,0:T(8,128)}) custom-call(s32[1]{0:T(128)} %bitcast.2.core_ref, bf16[128,8192]{1,0:T(8,128)(2,1)} %bitcast.20, f32[1,8192]{1,0:T(1,128)} %bitcast.25), custom_call_target="tpu_custom_call" | custom-call | tf_op jit(solution)/shard_map/norm/pallas_call | solution.py:129
  26.0 2.6 collective-permute-start
  28.5 1.9 join.6.refs_0_.refs_12_
  30.4 1.3 collective-permute-start.16
  31.7 1.9 join.7.refs_4_.refs_14_
  33.6 1.9 collective-permute-start.17
  35.5 1.3 collective-permute-start.18
  36.8 1.4 collective-permute-start.7
  39.2 2.3 collective-permute-done.7.refs_2_
  41.5 5.8 %collective-permute-done.12.refs_1_ = bf16[128,512]{1,0:T(8,128)(2,1)S(1)} collective-permute-done((bf16[128,512]{1,0:T(8,128)(2,1)S(1)}, bf16[128,512]{1,0:T(8,128)(2,1)S(1)}, u32[]{:S(2)}, u32[]{:S(2)}) %collective-permute-start.12) | collective-permute-done | bytes 131104 | tf_op jit(solution)/shard_map/ppermute | solution.py:27
  47.3 2.1 collective-permute-start.13
  49.5 1.9 collective-permute-done.13.refs_2_
  51.4 2.7 %collective-permute-start.19 = (bf16[512,512]{1,0:T(8,128)(2,1)}, bf16[512,512]{1,0:T(8,128)(2,1)S(1)}, u32[]{:S(2)}, u32[]{:S(2)}) collective-permute-start(bf16[512,512]{1,0:T(8,128)(2,1)} %join.7.refs_4_.refs_14_), channel_id=1, source_target_pairs={{0,48},{16,0},{32,16},{48,32},{1,49},{17,1},{33,17},{49,33},{2,50}... | collective-permute-start | bytes 1572872 | tf_op jit(solution)/shard_map/ppermute | solution.py:27
  54.1 1.9 join.4.refs_1_.refs_13_
  56.0 1.9 join.5.refs_5_
  59.0 2.6 collective-permute-start.9
  64.1 1.8 collective-permute-start.20
  65.9 5.7 %collective-permute-done.8.refs_0_.refs_8_ = bf16[512,512]{1,0:T(8,128)(2,1)S(1)} collective-permute-done((bf16[512,512]{1,0:T(8,128)(2,1)}, bf16[512,512]{1,0:T(8,128)(2,1)S(1)}, u32[]{:S(2)}, u32[]{:S(2)}) %collective-permute-start.8) | collective-permute-done | bytes 524320 | tf_op jit(solution)/shard_map/ppermute | solution.py:27
  71.5 2.7 %collective-permute-start.21 = (bf16[512,512]{1,0:T(8,128)(2,1)}, bf16[512,512]{1,0:T(8,128)(2,1)}, u32[]{:S(2)}, u32[]{:S(2)}) collective-permute-start(bf16[512,512]{1,0:T(8,128)(2,1)} %collective-permute-done.9.refs_1_.refs_9_), channel_id=1, source_target_pairs={{0,6},{2,0},{4,2},{6,4},{1,7},{3,1},{5,3},{7,5},{8,14},{10,8},{12,... | collective-permute-start | bytes 1572872 | tf_op jit(solution)/shard_map/ppermute | solution.py:27
  75.0 2.6 %collective-permute-start.23 = (bf16[512,512]{1,0:T(8,128)(2,1)}, bf16[512,512]{1,0:T(8,128)(2,1)}, u32[]{:S(2)}, u32[]{:S(2)}) collective-permute-start(bf16[512,512]{1,0:T(8,128)(2,1)} %collective-permute-done.15.refs_3_.refs_11_), channel_id=1, source_target_pairs={{0,48},{16,0},{32,16},{48,32},{1,49},{17,1},{33,17},{49,33},{2,50}... | collective-permute-start | bytes 1572872 | tf_op jit(solution)/shard_map/ppermute | solution.py:27
  78.4 5.0 %project_lot.2.refs_4_ = f32[256,1024]{1,0:T(8,128)} custom-call(s32[64]{0:T(128)} %reshape.117.table_ref, bf16[32,128,128]{2,1,0:T(8,128)(2,1)} %get-tuple-element.27.own_ref, bf16[32,128,128]{2,1,0:T(8,128)(2,1)} %copy-done, bf16[512,512]{1,0:T(8,128)(2,1)} %join.6.refs_0_.refs_12_, bf16[512,512]{1,0:T(8,128)(2,1)} %join.4.refs_1_.refs_13_, ...), custom_call_target="tpu_custom_call" | custom-call | tf_op jit(solution)/shard_map/project_lot/pallas_call | solution.py:200
  83.4 4.2 %project_lot.3.near_ref = f32[256,1024]{1,0:T(8,128)} custom-call(s32[64]{0:T(128)} %reshape.117.table_ref, bf16[32,128,128]{2,1,0:T(8,128)(2,1)} %get-tuple-element.27.own_ref, bf16[32,128,128]{2,1,0:T(8,128)(2,1)} %copy-done, bf16[512,512]{1,0:T(8,128)(2,1)} %copy-done.9, bf16[512,512]{1,0:T(8,128)(2,1)} %collective-permute-done.9.refs_1_.refs_9_, ...), custom_call_target="tpu_custom_call" | custom-call | tf_op jit(solution)/shard_map/project_lot/pallas_call | solution.py:200
  88.4 4.2 %project_far.1 = (f32[128,1024]{1,0:T(8,128)}, f32[128,1024]{1,0:T(8,128)}) custom-call(s32[64]{0:T(128)} %reshape.117.table_ref, bf16[32,128,128]{2,1,0:T(8,128)(2,1)} %get-tuple-element.27.own_ref, bf16[32,128,128]{2,1,0:T(8,128)(2,1)} %copy-done, f32[256,1024]{1,0:T(8,128)} %project_lot.3.near_ref, ...), custom_call_target="tpu_custom_call" | custom-call | tf_op jit(solution)/shard_map/project_far/pallas_call | solution.py:226
  92.6 4.4 %collective-permute-start.24 = (f32[128,1024]{1,0:T(8,128)}, f32[128,1024]{1,0:T(8,128)S(1)}, u32[]{:S(2)}, u32[]{:S(2)}) collective-permute-start(f32[128,1024]{1,0:T(8,128)} %get-tuple-element.30), channel_id=1, source_target_pairs={{0,8},{8,0},{1,9},{9,1},{2,10},{10,2},{3,11},{11,3},{4,12},{12,4},... | collective-permute-start | bytes 1572872 | tf_op jit(solution)/shard_map/ppermute | solution.py:27
  99.5 2.0 finish.1.refs_0_.refs_5_.refs_10_
  101.5 3.6 %collective-permute-start.25 = (bf16[136,1024]{1,0:T(8,128)(2,1)}, bf16[136,1024]{1,0:T(8,128)(2,1)S(1)}, u32[]{:S(2)}, u32[]{:S(2)}) collective-permute-start(bf16[136,1024]{1,0:T(8,128)(2,1)} %finish.1.refs_0_.refs_5_.refs_10_), channel_id=1, source_target_pairs={{0,1},{1,2},{2,3},{3,4},{4,5},{5,6},{6,7},{8,9},{9,10},{10,11},{11... | collective-permute-start | bytes 835592 | tf_op jit(solution)/shard_map/ppermute | solution.py:33
  105.1 2.8 %collective-permute-start.26 = (bf16[136,1024]{1,0:T(8,128)(2,1)}, bf16[136,1024]{1,0:T(8,128)(2,1)S(1)}, u32[]{:S(2)}, u32[]{:S(2)}) collective-permute-start(bf16[136,1024]{1,0:T(8,128)(2,1)} %finish.1.refs_0_.refs_5_.refs_10_), channel_id=1, source_target_pairs={{0,2},{1,3},{2,4},{3,5},{4,6},{5,7},{8,10},{9,11},{10,12},{11,13},... | collective-permute-start | bytes 835592 | tf_op jit(solution)/shard_map/ppermute | solution.py:33
  107.8 6.0 %collective-permute-start.27 = (bf16[136,1024]{1,0:T(8,128)(2,1)}, bf16[136,1024]{1,0:T(8,128)(2,1)S(1)}, u32[]{:S(2)}, u32[]{:S(2)}) collective-permute-start(bf16[136,1024]{1,0:T(8,128)(2,1)} %finish.1.refs_0_.refs_5_.refs_10_), channel_id=1, source_target_pairs={{0,3},{1,4},{2,5},{3,6},{4,7},{8,11},{9,12},{10,13},{11,14},{12,15... | collective-permute-start | bytes 835592 | tf_op jit(solution)/shard_map/ppermute | solution.py:33
  113.9 1.5 collective-permute-start.28
  115.5 3.8 %collective-permute-done.27.refs_3_.refs_8_.refs_13_ = bf16[136,1024]{1,0:T(8,128)(2,1)S(1)} collective-permute-done((bf16[136,1024]{1,0:T(8,128)(2,1)}, bf16[136,1024]{1,0:T(8,128)(2,1)S(1)}, u32[]{:S(2)}, u32[]{:S(2)}) %collective-permute-start.27) | collective-permute-done | bytes 278560 | tf_op jit(solution)/shard_map/ppermute | solution.py:33
  119.3 6.0 %collective-permute-done.28.refs_4_.refs_9_.refs_14_ = bf16[136,1024]{1,0:T(8,128)(2,1)S(1)} collective-permute-done((bf16[136,1024]{1,0:T(8,128)(2,1)}, bf16[136,1024]{1,0:T(8,128)(2,1)S(1)}, u32[]{:S(2)}, u32[]{:S(2)}) %collective-permute-start.28) | collective-permute-done | bytes 278560 | tf_op jit(solution)/shard_map/ppermute | solution.py:33
  126.0 19.2 %attention.1 = (bf16[128,4096]{1,0:T(8,128)(2,1)}, bf16[128,4096]{1,0:T(8,128)(2,1)}, f32[128,1024]{1,0:T(8,128)}, bf16[128,1024]{1,0:T(8,128)(2,1)}, bf16[128,1...) custom-call(f32[1,128]{1,0:T(1,128)} %get-tuple-element.61.doc_ref, ...), custom_call_target="tpu_custom_call" | custom-call | tf_op jit(solution)/shard_map/attention/pallas_call | solution.py:362
  145.1 1.4 collective-permute-start.32
  146.6 1.3 collective-permute-start.31
  147.9 1.3 collective-permute-start.30
  149.2 1.3 collective-permute-start.29
  150.5 3.0 %spread.1 = (bf16[2,8,128,128]{3,2,1,0:T(8,128)(2,1)}, bf16[2,8,128,128]{3,2,1,0:T(8,128)(2,1)}, bf16[2,8,128,128]{3,2,1,0:T(8,128)(2,1)}, bf16[2,8,128,128]{3,2,1,0:T(8,128)(2,1)}) custom-call(s32[1]{0:T(128)} %bitcast.9.x_ref, bf16[32,128,128]{2,1,0:T(8,128)(2,1)} %get-tuple-element.27.own_ref, bf16[32,128,128]{2,1,0:T(8,128)(2,1)} %copy-done), custom_call_target="tpu_custom_call" | custom-call | tf_op jit(solution)/shard_map/spread/pallas_call | solution.py:161
  153.5 7.1 %collective-permute-start.35 = (bf16[2,8,128,128]{3,2,1,0:T(8,128)(2,1)}, bf16[2,8,128,128]{3,2,1,0:T(8,128)(2,1)S(1)}, u32[]{:S(2)}, u32[]{:S(2)}) collective-permute-start(bf16[2,8,128,128]{3,2,1,0:T(8,128)(2,1)} %get-tuple-element.42), channel_id=1, source_target_pairs={{0,2},{2,4},{4,6},{6,0},{1,3},{3,5},{5,7},{7,1},{8,10},{10,12},{12... | collective-permute-start | bytes 1572872 | tf_op jit(solution)/shard_map/ppermute | solution.py:27
  160.6 4.3 %collective-permute-start.36 = (bf16[2,8,128,128]{3,2,1,0:T(8,128)(2,1)}, bf16[2,8,128,128]{3,2,1,0:T(8,128)(2,1)S(1)}, u32[]{:S(2)}, u32[]{:S(2)}) collective-permute-start(bf16[2,8,128,128]{3,2,1,0:T(8,128)(2,1)} %get-tuple-element.43), channel_id=1, source_target_pairs={{0,4},{2,6},{4,0},{6,2},{1,5},{3,7},{5,1},{7,3},{8,12},{10,14},{12... | collective-permute-start | bytes 1572872 | tf_op jit(solution)/shard_map/ppermute | solution.py:27
  165.1 5.1 %collective-permute-start.38 = (bf16[128,1024]{1,0:T(8,128)(2,1)S(1)}, bf16[128,1024]{1,0:T(8,128)(2,1)S(1)}, u32[]{:S(2)}, u32[]{:S(2)}) collective-permute-start(bf16[128,1024]{1,0:T(8,128)(2,1)S(1)} %add_convert_fusion.mine_ref.refs_4_), channel_id=1, source_target_pairs={{0,2},{2,4},{4,6},{6,0},{1,3},{3,5},{5,7},{7,1},{8,10},{10,12},{12... | collective-permute-start | bytes 786440 | tf_op jit(solution)/shard_map/ppermute | solution.py:27
  170.1 1.9 collective-permute-start.40
  172.0 2.5 collective-permute-done.35.refs_1_
  175.6 11.0 %collective-permute-done.36.refs_2_ = bf16[2,8,128,128]{3,2,1,0:T(8,128)(2,1)S(1)} collective-permute-done((bf16[2,8,128,128]{3,2,1,0:T(8,128)(2,1)}, bf16[2,8,128,128]{3,2,1,0:T(8,128)(2,1)S(1)}, u32[]{:S(2)}, u32[]{:S(2)}) %collective-permute-start.36) | collective-permute-done | bytes 524320 | tf_op jit(solution)/shard_map/ppermute | solution.py:27
  186.6 4.9 %collective-permute-start.33 = (bf16[128,1024]{1,0:T(8,128)(2,1)S(1)}, bf16[128,1024]{1,0:T(8,128)(2,1)S(1)}, u32[]{:S(2)}, u32[]{:S(2)}) collective-permute-start(bf16[128,1024]{1,0:T(8,128)(2,1)S(1)} %add_convert_fusion.mine_ref.refs_4_), channel_id=1, source_target_pairs={{0,8},{8,0},{1,9},{9,1},{2,10},{10,2},{3,11},{11,3},{4,12},{12,4},... | collective-permute-start | bytes 786440 | tf_op jit(solution)/shard_map/ppermute | solution.py:27
  191.4 3.3 %collective-permute-start.39 = (bf16[128,1024]{1,0:T(8,128)(2,1)S(1)}, bf16[128,1024]{1,0:T(8,128)(2,1)S(1)}, u32[]{:S(2)}, u32[]{:S(2)}) collective-permute-start(bf16[128,1024]{1,0:T(8,128)(2,1)S(1)} %collective-permute-done.38.refs_6_), channel_id=1, source_target_pairs={{0,8},{8,0},{1,9},{9,1},{2,10},{10,2},{3,11},{11,3},{4,12},{12,4},... | collective-permute-start | bytes 786440 | tf_op jit(solution)/shard_map/ppermute | solution.py:27
  194.7 3.1 %collective-permute-done.40.refs_8_ = bf16[128,1024]{1,0:T(8,128)(2,1)S(1)} collective-permute-done((bf16[128,1024]{1,0:T(8,128)(2,1)S(1)}, bf16[128,1024]{1,0:T(8,128)(2,1)S(1)}, u32[]{:S(2)}, u32[]{:S(2)}) %collective-permute-start.40) | collective-permute-done | bytes 262176 | tf_op jit(solution)/shard_map/ppermute | solution.py:27
  197.8 2.6 %collective-permute-start.41 = (bf16[128,1024]{1,0:T(8,128)(2,1)S(1)}, bf16[128,1024]{1,0:T(8,128)(2,1)S(1)}, u32[]{:S(2)}, u32[]{:S(2)}) collective-permute-start(bf16[128,1024]{1,0:T(8,128)(2,1)S(1)} %collective-permute-done.40.refs_8_), channel_id=1, source_target_pairs={{0,8},{8,0},{1,9},{9,1},{2,10},{10,2},{3,11},{11,3},{4,12},{12,4},... | collective-permute-start | bytes 786440 | tf_op jit(solution)/shard_map/ppermute | solution.py:27
  201.7 1.6 collective-permute-start.43
  205.0 6.9 %grad_weight.1 = (bf16[16,40,1024]{2,1,0:T(8,128)(2,1)}, bf16[16,32,1024]{2,1,0:T(8,128)(2,1)}) custom-call(s32[8]{0:T(128)} %fusion.place_ref, bf16[2,8,128,128]{3,2,1,0:T(8,128)(2,1)} %get-tuple-element.41.refs_0_, bf16[2,8,128,128]{3,2,1,0:T(8,128)(2,1)} %copy-done.22, bf16[2,8,128,128]{3,2,1,0:T(8,128)(2,1)} %copy-done.23, ...), custom_call_target="tpu_custom_call" | custom-call | tf_op jit(solution)/shard_map/grad_weight/pallas_call | solution.py:519
  212.0 3.9 %all-to-all-start = ((bf16[16,40,1024]{2,1,0:T(8,128)(2,1)}), bf16[16,40,1024]{2,1,0:T(8,128)(2,1)S(1)}, u32[]{:S(2)}, u32[]{:S(2)}) async-start(bf16[16,40,1024]{2,1,0:T(8,128)(2,1)} %get-tuple-element.45), calls=%async_computation | async-start | bytes 2621440 | tf_op jit(solution)/shard_map/all_to_all | solution.py:594
  215.9 7.4 %grad_normed.1 = (bf16[32,128,128]{2,1,0:T(8,128)(2,1)}, bf16[32,128,128]{2,1,0:T(8,128)(2,1)}) custom-call(s32[64]{0:T(128)} %reshape.117.table_ref, bf16[128,1024]{1,0:T(8,128)(2,1)} %copy-done.8, bf16[128,1024]{1,0:T(8,128)(2,1)} %copy-done.14, bf16[512,512]{1,0:T(8,128)(2,1)} %join.6.refs_0_.refs_12_, bf16[512,512]{1,0:T(8,128)(2,1)} %join.4.refs_1_.refs_13_, ...), custom_call_target="tpu_custom_call" | custom-call | tf_op jit(solution)/shard_map/grad_normed/pallas_call | solution.py:416
  223.4 13.1 %all-to-all-done = bf16[16,40,1024]{2,1,0:T(8,128)(2,1)S(1)} async-done(((bf16[16,40,1024]{2,1,0:T(8,128)(2,1)}), bf16[16,40,1024]{2,1,0:T(8,128)(2,1)S(1)}, u32[]{:S(2)}, u32[]{:S(2)}) %all-to-all-start) | async-done | bytes 1310752 | tf_op jit(solution)/shard_map/all_to_all | solution.py:594
  236.6 5.3 %all-to-all-start.1 = ((bf16[16,32,1024]{2,1,0:T(8,128)(2,1)}), bf16[16,32,1024]{2,1,0:T(8,128)(2,1)S(1)}, u32[]{:S(2)}, u32[]{:S(2)}) async-start(bf16[16,32,1024]{2,1,0:T(8,128)(2,1)} %get-tuple-element.48), calls=%async_computation.1 | async-start | bytes 2097152 | tf_op jit(solution)/shard_map/all_to_all | solution.py:600
  242.8 1.8 collective-permute-start.44
  245.5 2.6 %collective-permute-start.45 = (f32[2,1024]{1,0:T(2,128)S(1)}, f32[2,1024]{1,0:T(2,128)S(1)}, u32[]{:S(2)}, u32[]{:S(2)}) collective-permute-start(f32[2,1024]{1,0:T(2,128)S(1)} %maximum_select_fusion.1), channel_id=1, source_target_pairs={{0,6},{2,0},{4,2},{6,4},{1,7},{3,1},{5,3},{7,5},{8,14},{10,8},{12,... | collective-permute-start | bytes 24584 | tf_op jit(solution)/shard_map/ppermute | solution.py:27
  248.1 1.9 collective-permute-start.46
  251.1 5.5 %norm_back.1 = bf16[128,8192]{1,0:T(8,128)(2,1)} custom-call(s32[1]{0:T(128)} %bitcast.2.core_ref, bf16[32,128,128]{2,1,0:T(8,128)(2,1)} %get-tuple-element.38.own_ref, bf16[32,128,128]{2,1,0:T(8,128)(2,1)} %copy-done.11, bf16[128,8192]{1,0:T(8,128)(2,1)} %bitcast.21, f32[128,128]{1,0:T(8,128)} %get-tuple-element.40.inv_ref, f32[1,8192]{1,0:T(1,128)} %bitcast.26), custom_call_target="tpu_custom_call" | custom-call | tf_op jit(solution)/shard_map/norm_back/pallas_call | solution.py:455
  (150 shorter events, 23.7 us)
Async XLA Ops:
  0.6 8.1 %collective-permute-start.3 = (bf16[64,1024]{1,0:T(8,128)(2,1)}, bf16[64,1024]{1,0:T(8,128)(2,1)S(1)}, u32[]{:S(2)}, u32[]{:S(2)}) collective-permute-start(bf16[64,1024]{1,0:T(8,128)(2,1)} %param.12), channel_id=1, source_target_pairs={{0,65},{1,64},{64,1},{65,0},{2,67},{3,66},{66,3},{67,2},{4,69},{5,... | collective-permute-start | bytes 393224 | tf_op jit(solution)/shard_map/ppermute | solution.py:81
  5.3 4.3 %collective-permute-start.2 = (bf16[64,1024]{1,0:T(8,128)(2,1)}, bf16[64,1024]{1,0:T(8,128)(2,1)S(1)}, u32[]{:S(2)}, u32[]{:S(2)}) collective-permute-start(bf16[64,1024]{1,0:T(8,128)(2,1)} %param.12), channel_id=1, source_target_pairs={{0,64},{64,0},{1,65},{65,1},{2,66},{66,2},{3,67},{67,3},{4,68},{68... | collective-permute-start | bytes 393224 | tf_op jit(solution)/shard_map/ppermute | solution.py:27
  5.3 7.2 %collective-permute-start.1 = (bf16[64,1024]{1,0:T(8,128)(2,1)}, bf16[64,1024]{1,0:T(8,128)(2,1)S(1)}, u32[]{:S(2)}, u32[]{:S(2)}) collective-permute-start(bf16[64,1024]{1,0:T(8,128)(2,1)} %param.12), channel_id=1, source_target_pairs={{0,1},{1,0},{2,3},{3,2},{4,5},{5,4},{6,7},{7,6},{8,9},{9,8},{10,11... | collective-permute-start | bytes 393224 | tf_op jit(solution)/shard_map/ppermute | solution.py:27
  13.7 14.9 %copy-start.13 = (bf16[256,512]{1,0:T(8,128)(2,1)}, bf16[256,512]{1,0:T(8,128)(2,1)S(1)}, u32[]{:S(2)}) copy-start(bf16[256,512]{1,0:T(8,128)(2,1)S(1)} %get-tuple-element.50.refs_0_) | copy-start | bytes 786436
  13.7 18.0 %copy-start.12 = (bf16[256,512]{1,0:T(8,128)(2,1)}, bf16[256,512]{1,0:T(8,128)(2,1)S(1)}, u32[]{:S(2)}) copy-start(bf16[256,512]{1,0:T(8,128)(2,1)S(1)} %get-tuple-element.49.refs_0_) | copy-start | bytes 786436
  13.7 7.8 %collective-permute-start.5 = (bf16[256,512]{1,0:T(8,128)(2,1)S(1)}, bf16[256,512]{1,0:T(8,128)(2,1)S(1)}, u32[]{:S(2)}, u32[]{:S(2)}) collective-permute-start(bf16[256,512]{1,0:T(8,128)(2,1)S(1)} %get-tuple-element.50.refs_0_), channel_id=1, source_target_pairs={{0,16},{16,32},{32,48},{48,0},{1,17},{17,33},{33,49},{49,1},{2,18}... | collective-permute-start | bytes 786440 | tf_op jit(solution)/shard_map/ppermute | solution.py:27
  15.1 15.4 %collective-permute-start.11 = (bf16[256,512]{1,0:T(8,128)(2,1)S(1)}, bf16[256,512]{1,0:T(8,128)(2,1)S(1)}, u32[]{:S(2)}, u32[]{:S(2)}) collective-permute-start(bf16[256,512]{1,0:T(8,128)(2,1)S(1)} %get-tuple-element.49.refs_0_), channel_id=1, source_target_pairs={{0,2},{2,4},{4,6},{6,0},{1,3},{3,5},{5,7},{7,1},{8,10},{10,12},{12... | collective-permute-start | bytes 786440 | tf_op jit(solution)/shard_map/ppermute | solution.py:27
  16.3 17.3 %collective-permute-start.4 = (bf16[256,512]{1,0:T(8,128)(2,1)S(1)}, bf16[256,512]{1,0:T(8,128)(2,1)S(1)}, u32[]{:S(2)}, u32[]{:S(2)}) collective-permute-start(bf16[256,512]{1,0:T(8,128)(2,1)S(1)} %get-tuple-element.50.refs_0_), channel_id=1, source_target_pairs={{0,48},{16,0},{32,16},{48,32},{1,49},{17,1},{33,17},{49,33},{2,50}... | collective-permute-start | bytes 786440 | tf_op jit(solution)/shard_map/ppermute | solution.py:27
  17.8 17.7 %collective-permute-start.10 = (bf16[256,512]{1,0:T(8,128)(2,1)S(1)}, bf16[256,512]{1,0:T(8,128)(2,1)S(1)}, u32[]{:S(2)}, u32[]{:S(2)}) collective-permute-start(bf16[256,512]{1,0:T(8,128)(2,1)S(1)} %get-tuple-element.49.refs_0_), channel_id=1, source_target_pairs={{0,6},{2,0},{4,2},{6,4},{1,7},{3,1},{5,3},{7,5},{8,14},{10,8},{12,... | collective-permute-start | bytes 786440 | tf_op jit(solution)/shard_map/ppermute | solution.py:27
  21.5 15.3 %collective-permute-start.6 = (bf16[128,512]{1,0:T(8,128)(2,1)S(1)}, bf16[128,512]{1,0:T(8,128)(2,1)S(1)}, u32[]{:S(2)}, u32[]{:S(2)}) collective-permute-start(bf16[128,512]{1,0:T(8,128)(2,1)S(1)} %slice.45), channel_id=1, source_target_pairs={{0,16},{16,32},{32,48},{48,0},{1,17},{17,33},{33,49},{49,1},{2,18}... | collective-permute-start | bytes 393224 | tf_op jit(solution)/shard_map/ppermute | solution.py:27
  26.0 38.1 %collective-permute-start = (bf16[32,128,128]{2,1,0:T(8,128)(2,1)}, bf16[32,128,128]{2,1,0:T(8,128)(2,1)S(1)}, u32[]{:S(2)}, u32[]{:S(2)}) collective-permute-start(bf16[32,128,128]{2,1,0:T(8,128)(2,1)} %get-tuple-element.28), channel_id=1, source_target_pairs={{0,8},{8,0},{1,9},{9,1},{2,10},{10,2},{3,11},{11,3},{4,12},{12,4},... | collective-permute-start | bytes 3145736 | tf_op jit(solution)/shard_map/ppermute | solution.py:27
  30.4 31.4 %copy-start.34 = (s32[4]{0:T(128)S(1)}, s32[4]{0:T(128)}, u32[]{:S(2)}) copy-start(s32[4]{0:T(128)} %constant.117.clone) | copy-start | bytes 52
  30.4 27.4 %collective-permute-start.16 = (bf16[512,512]{1,0:T(8,128)(2,1)}, bf16[512,512]{1,0:T(8,128)(2,1)}, u32[]{:S(2)}, u32[]{:S(2)}) collective-permute-start(bf16[512,512]{1,0:T(8,128)(2,1)} %join.6.refs_0_.refs_12_), channel_id=1, source_target_pairs={{0,2},{2,4},{4,6},{6,0},{1,3},{3,5},{5,7},{7,1},{8,10},{10,12},{12... | collective-permute-start | bytes 1572872 | tf_op jit(solution)/shard_map/ppermute | solution.py:27
  33.6 20.5 %copy-start.15 = (bf16[256,512]{1,0:T(8,128)(2,1)}, bf16[256,512]{1,0:T(8,128)(2,1)S(1)}, u32[]{:S(2)}) copy-start(bf16[256,512]{1,0:T(8,128)(2,1)S(1)} %collective-permute-done.4.refs_0_) | copy-start | bytes 786436
  33.6 25.4 %collective-permute-start.17 = (bf16[512,512]{1,0:T(8,128)(2,1)}, bf16[512,512]{1,0:T(8,128)(2,1)S(1)}, u32[]{:S(2)}, u32[]{:S(2)}) collective-permute-start(bf16[512,512]{1,0:T(8,128)(2,1)} %join.6.refs_0_.refs_12_), channel_id=1, source_target_pairs={{0,6},{2,0},{4,2},{6,4},{1,7},{3,1},{5,3},{7,5},{8,14},{10,8},{12,... | collective-permute-start | bytes 1572872 | tf_op jit(solution)/shard_map/ppermute | solution.py:27
  35.5 20.5 %copy-start.16 = (bf16[256,512]{1,0:T(8,128)(2,1)}, bf16[256,512]{1,0:T(8,128)(2,1)S(1)}, u32[]{:S(2)}) copy-start(bf16[256,512]{1,0:T(8,128)(2,1)S(1)} %collective-permute-done.10.refs_0_) | copy-start | bytes 786436
  35.5 26.0 %collective-permute-start.18 = (bf16[512,512]{1,0:T(8,128)(2,1)}, bf16[512,512]{1,0:T(8,128)(2,1)S(1)}, u32[]{:S(2)}, u32[]{:S(2)}) collective-permute-start(bf16[512,512]{1,0:T(8,128)(2,1)} %join.7.refs_4_.refs_14_), channel_id=1, source_target_pairs={{0,16},{16,32},{32,48},{48,0},{1,17},{17,33},{33,49},{49,1},{2,18}... | collective-permute-start | bytes 1572872 | tf_op jit(solution)/shard_map/ppermute | solution.py:27
  36.8 17.3 %copy-start.31 = (bf16[128,512]{1,0:T(8,128)(2,1)}, bf16[128,512]{1,0:T(8,128)(2,1)S(1)}, u32[]{:S(2)}) copy-start(bf16[128,512]{1,0:T(8,128)(2,1)S(1)} %collective-permute-done.6.refs_1_) | copy-start | bytes 393220
  36.8 4.7 %collective-permute-start.7 = (bf16[128,512]{1,0:T(8,128)(2,1)S(1)}, bf16[128,512]{1,0:T(8,128)(2,1)S(1)}, u32[]{:S(2)}, u32[]{:S(2)}) collective-permute-start(bf16[128,512]{1,0:T(8,128)(2,1)S(1)} %slice.46), channel_id=1, source_target_pairs={{0,48},{16,0},{32,16},{48,32},{1,49},{17,1},{33,17},{49,33},{2,50}... | collective-permute-start | bytes 393224 | tf_op jit(solution)/shard_map/ppermute | solution.py:27
  41.5 5.9 %collective-permute-start.12 = (bf16[128,512]{1,0:T(8,128)(2,1)S(1)}, bf16[128,512]{1,0:T(8,128)(2,1)S(1)}, u32[]{:S(2)}, u32[]{:S(2)}) collective-permute-start(bf16[128,512]{1,0:T(8,128)(2,1)S(1)} %slice.48), channel_id=1, source_target_pairs={{0,2},{2,4},{4,6},{6,0},{1,3},{3,5},{5,7},{7,1},{8,10},{10,12},{12... | collective-permute-start | bytes 393224 | tf_op jit(solution)/shard_map/ppermute | solution.py:27
  47.3 4.1 %collective-permute-start.13 = (bf16[128,512]{1,0:T(8,128)(2,1)S(1)}, bf16[128,512]{1,0:T(8,128)(2,1)}, u32[]{:S(2)}, u32[]{:S(2)}) collective-permute-start(bf16[128,512]{1,0:T(8,128)(2,1)S(1)} %slice.49), channel_id=1, source_target_pairs={{0,6},{2,0},{4,2},{6,4},{1,7},{3,1},{5,3},{7,5},{8,14},{10,8},{12,... | collective-permute-start | bytes 393224 | tf_op jit(solution)/shard_map/ppermute | solution.py:27
  51.4 11.5 %collective-permute-start.19 = (bf16[512,512]{1,0:T(8,128)(2,1)}, bf16[512,512]{1,0:T(8,128)(2,1)S(1)}, u32[]{:S(2)}, u32[]{:S(2)}) collective-permute-start(bf16[512,512]{1,0:T(8,128)(2,1)} %join.7.refs_4_.refs_14_), channel_id=1, source_target_pairs={{0,48},{16,0},{32,16},{48,32},{1,49},{17,1},{33,17},{49,33},{2,50}... | collective-permute-start | bytes 1572872 | tf_op jit(solution)/shard_map/ppermute | solution.py:27
  57.9 13.6 %collective-permute-start.8 = (bf16[512,512]{1,0:T(8,128)(2,1)}, bf16[512,512]{1,0:T(8,128)(2,1)S(1)}, u32[]{:S(2)}, u32[]{:S(2)}) collective-permute-start(bf16[512,512]{1,0:T(8,128)(2,1)} %join.4.refs_1_.refs_13_), channel_id=1, source_target_pairs={{0,2},{2,4},{4,6},{6,0},{1,3},{3,5},{5,7},{7,1},{8,10},{10,12},{12... | collective-permute-start | bytes 1572872 | tf_op jit(solution)/shard_map/ppermute | solution.py:27
  59.0 12.6 %collective-permute-start.9 = (bf16[512,512]{1,0:T(8,128)(2,1)}, bf16[512,512]{1,0:T(8,128)(2,1)}, u32[]{:S(2)}, u32[]{:S(2)}) collective-permute-start(bf16[512,512]{1,0:T(8,128)(2,1)} %join.4.refs_1_.refs_13_), channel_id=1, source_target_pairs={{0,6},{2,0},{4,2},{6,4},{1,7},{3,1},{5,3},{7,5},{8,14},{10,8},{12,... | collective-permute-start | bytes 1572872 | tf_op jit(solution)/shard_map/ppermute | solution.py:27
  61.5 16.9 %copy-start.1 = (bf16[512,512]{1,0:T(8,128)(2,1)}, bf16[512,512]{1,0:T(8,128)(2,1)S(1)}, u32[]{:S(2)}) copy-start(bf16[512,512]{1,0:T(8,128)(2,1)S(1)} %collective-permute-done.18.refs_6_.refs_15_) | copy-start | bytes 1572868
  61.5 13.4 %collective-permute-start.15 = (bf16[512,512]{1,0:T(8,128)(2,1)}, bf16[512,512]{1,0:T(8,128)(2,1)}, u32[]{:S(2)}, u32[]{:S(2)}) collective-permute-start(bf16[512,512]{1,0:T(8,128)(2,1)} %join.5.refs_5_), channel_id=1, source_target_pairs={{0,48},{16,0},{32,16},{48,32},{1,49},{17,1},{33,17},{49,33},{2,50}... | collective-permute-start | bytes 1572872 | tf_op jit(solution)/shard_map/ppermute | solution.py:27
  62.9 15.5 %copy-start.2 = (bf16[512,512]{1,0:T(8,128)(2,1)}, bf16[512,512]{1,0:T(8,128)(2,1)S(1)}, u32[]{:S(2)}) copy-start(bf16[512,512]{1,0:T(8,128)(2,1)S(1)} %collective-permute-done.19.refs_7_.refs_16_) | copy-start | bytes 1572868
  62.9 20.5 %collective-permute-start.14 = (bf16[512,512]{1,0:T(8,128)(2,1)}, bf16[512,512]{1,0:T(8,128)(2,1)}, u32[]{:S(2)}, u32[]{:S(2)}) collective-permute-start(bf16[512,512]{1,0:T(8,128)(2,1)} %join.5.refs_5_), channel_id=1, source_target_pairs={{0,16},{16,32},{32,48},{48,0},{1,17},{17,33},{33,49},{49,1},{2,18}... | collective-permute-start | bytes 1572872 | tf_op jit(solution)/shard_map/ppermute | solution.py:27
  64.1 14.3 %copy-start = (bf16[32,128,128]{2,1,0:T(8,128)(2,1)}, bf16[32,128,128]{2,1,0:T(8,128)(2,1)S(1)}, u32[]{:S(2)}) copy-start(bf16[32,128,128]{2,1,0:T(8,128)(2,1)S(1)} %collective-permute-done.other_ref) | copy-start | bytes 3145732
  64.1 23.5 %collective-permute-start.20 = (bf16[512,512]{1,0:T(8,128)(2,1)}, bf16[512,512]{1,0:T(8,128)(2,1)}, u32[]{:S(2)}, u32[]{:S(2)}) collective-permute-start(bf16[512,512]{1,0:T(8,128)(2,1)} %collective-permute-done.16.refs_2_), channel_id=1, source_target_pairs={{0,2},{2,4},{4,6},{6,0},{1,3},{3,5},{5,7},{7,1},{8,10},{10,12},{12... | collective-permute-start | bytes 1572872 | tf_op jit(solution)/shard_map/ppermute | solution.py:27
  71.5 16.1 %collective-permute-start.22 = (bf16[512,512]{1,0:T(8,128)(2,1)S(1)}, bf16[512,512]{1,0:T(8,128)(2,1)S(1)}, u32[]{:S(2)}, u32[]{:S(2)}) collective-permute-start(bf16[512,512]{1,0:T(8,128)(2,1)S(1)} %collective-permute-done.18.refs_6_.refs_15_), channel_id=1, source_target_pairs={{0,16},{16,32},{32,48},{48,0},{1,17},{17,33},{33,49},{49,1},{2,18}... | collective-permute-start | bytes 1572872 | tf_op jit(solution)/shard_map/ppermute | solution.py:27
  71.5 16.1 %collective-permute-start.21 = (bf16[512,512]{1,0:T(8,128)(2,1)}, bf16[512,512]{1,0:T(8,128)(2,1)}, u32[]{:S(2)}, u32[]{:S(2)}) collective-permute-start(bf16[512,512]{1,0:T(8,128)(2,1)} %collective-permute-done.9.refs_1_.refs_9_), channel_id=1, source_target_pairs={{0,6},{2,0},{4,2},{6,4},{1,7},{3,1},{5,3},{7,5},{8,14},{10,8},{12,... | collective-permute-start | bytes 1572872 | tf_op jit(solution)/shard_map/ppermute | solution.py:27
  75.0 12.7 %collective-permute-start.23 = (bf16[512,512]{1,0:T(8,128)(2,1)}, bf16[512,512]{1,0:T(8,128)(2,1)}, u32[]{:S(2)}, u32[]{:S(2)}) collective-permute-start(bf16[512,512]{1,0:T(8,128)(2,1)} %collective-permute-done.15.refs_3_.refs_11_), channel_id=1, source_target_pairs={{0,48},{16,0},{32,16},{48,32},{1,49},{17,1},{33,17},{49,33},{2,50}... | collective-permute-start | bytes 1572872 | tf_op jit(solution)/shard_map/ppermute | solution.py:27
  92.6 6.1 %collective-permute-start.24 = (f32[128,1024]{1,0:T(8,128)}, f32[128,1024]{1,0:T(8,128)S(1)}, u32[]{:S(2)}, u32[]{:S(2)}) collective-permute-start(f32[128,1024]{1,0:T(8,128)} %get-tuple-element.30), channel_id=1, source_target_pairs={{0,8},{8,0},{1,9},{9,1},{2,10},{10,2},{3,11},{11,3},{4,12},{12,4},... | collective-permute-start | bytes 1572872 | tf_op jit(solution)/shard_map/ppermute | solution.py:27
  101.5 14.0 %collective-permute-start.25 = (bf16[136,1024]{1,0:T(8,128)(2,1)}, bf16[136,1024]{1,0:T(8,128)(2,1)S(1)}, u32[]{:S(2)}, u32[]{:S(2)}) collective-permute-start(bf16[136,1024]{1,0:T(8,128)(2,1)} %finish.1.refs_0_.refs_5_.refs_10_), channel_id=1, source_target_pairs={{0,1},{1,2},{2,3},{3,4},{4,5},{5,6},{6,7},{8,9},{9,10},{10,11},{11... | collective-permute-start | bytes 835592 | tf_op jit(solution)/shard_map/ppermute | solution.py:33
  105.1 10.4 %collective-permute-start.26 = (bf16[136,1024]{1,0:T(8,128)(2,1)}, bf16[136,1024]{1,0:T(8,128)(2,1)S(1)}, u32[]{:S(2)}, u32[]{:S(2)}) collective-permute-start(bf16[136,1024]{1,0:T(8,128)(2,1)} %finish.1.refs_0_.refs_5_.refs_10_), channel_id=1, source_target_pairs={{0,2},{1,3},{2,4},{3,5},{4,6},{5,7},{8,10},{9,11},{10,12},{11,13},... | collective-permute-start | bytes 835592 | tf_op jit(solution)/shard_map/ppermute | solution.py:33
  107.8 11.4 %collective-permute-start.27 = (bf16[136,1024]{1,0:T(8,128)(2,1)}, bf16[136,1024]{1,0:T(8,128)(2,1)S(1)}, u32[]{:S(2)}, u32[]{:S(2)}) collective-permute-start(bf16[136,1024]{1,0:T(8,128)(2,1)} %finish.1.refs_0_.refs_5_.refs_10_), channel_id=1, source_target_pairs={{0,3},{1,4},{2,5},{3,6},{4,7},{8,11},{9,12},{10,13},{11,14},{12,15... | collective-permute-start | bytes 835592 | tf_op jit(solution)/shard_map/ppermute | solution.py:33
  113.9 11.3 %collective-permute-start.28 = (bf16[136,1024]{1,0:T(8,128)(2,1)}, bf16[136,1024]{1,0:T(8,128)(2,1)S(1)}, u32[]{:S(2)}, u32[]{:S(2)}) collective-permute-start(bf16[136,1024]{1,0:T(8,128)(2,1)} %finish.1.refs_0_.refs_5_.refs_10_), channel_id=1, source_target_pairs={{0,4},{1,5},{2,6},{3,7},{8,12},{9,13},{10,14},{11,15},{16,20},{17,... | collective-permute-start | bytes 835592 | tf_op jit(solution)/shard_map/ppermute | solution.py:33
  145.1 19.7 %copy-start.20 = (f32[128,1024]{1,0:T(8,128)S(1)}, f32[128,1024]{1,0:T(8,128)}, u32[]{:S(2)}) copy-start(f32[128,1024]{1,0:T(8,128)} %get-tuple-element.33) | copy-start | bytes 1572868
  145.1 15.5 %collective-permute-start.32 = (bf16[128,1024]{1,0:T(8,128)(2,1)}, bf16[128,1024]{1,0:T(8,128)(2,1)S(1)}, u32[]{:S(2)}, u32[]{:S(2)}) collective-permute-start(bf16[128,1024]{1,0:T(8,128)(2,1)} %get-tuple-element.37), channel_id=1, source_target_pairs={{4,0},{5,1},{6,2},{7,3},{12,8},{13,9},{14,10},{15,11},{20,16},{21,... | collective-permute-start | bytes 786440 | tf_op jit(solution)/shard_map/ppermute | solution.py:33
  146.6 18.3 %collective-permute-start.31 = (bf16[128,1024]{1,0:T(8,128)(2,1)}, bf16[128,1024]{1,0:T(8,128)(2,1)S(1)}, u32[]{:S(2)}, u32[]{:S(2)}) collective-permute-start(bf16[128,1024]{1,0:T(8,128)(2,1)} %get-tuple-element.36), channel_id=1, source_target_pairs={{3,0},{4,1},{5,2},{6,3},{7,4},{11,8},{12,9},{13,10},{14,11},{15,12... | collective-permute-start | bytes 786440 | tf_op jit(solution)/shard_map/ppermute | solution.py:33
  147.9 17.0 %collective-permute-start.30 = (bf16[128,1024]{1,0:T(8,128)(2,1)}, bf16[128,1024]{1,0:T(8,128)(2,1)S(1)}, u32[]{:S(2)}, u32[]{:S(2)}) collective-permute-start(bf16[128,1024]{1,0:T(8,128)(2,1)} %get-tuple-element.35), channel_id=1, source_target_pairs={{2,0},{3,1},{4,2},{5,3},{6,4},{7,5},{10,8},{11,9},{12,10},{13,11},... | collective-permute-start | bytes 786440 | tf_op jit(solution)/shard_map/ppermute | solution.py:33
  149.2 15.7 %collective-permute-start.29 = (bf16[128,1024]{1,0:T(8,128)(2,1)}, bf16[128,1024]{1,0:T(8,128)(2,1)S(1)}, u32[]{:S(2)}, u32[]{:S(2)}) collective-permute-start(bf16[128,1024]{1,0:T(8,128)(2,1)} %get-tuple-element.34), channel_id=1, source_target_pairs={{1,0},{2,1},{3,2},{4,3},{5,4},{6,5},{7,6},{9,8},{10,9},{11,10},{12... | collective-permute-start | bytes 786440 | tf_op jit(solution)/shard_map/ppermute | solution.py:33
  153.5 21.0 %collective-permute-start.35 = (bf16[2,8,128,128]{3,2,1,0:T(8,128)(2,1)}, bf16[2,8,128,128]{3,2,1,0:T(8,128)(2,1)S(1)}, u32[]{:S(2)}, u32[]{:S(2)}) collective-permute-start(bf16[2,8,128,128]{3,2,1,0:T(8,128)(2,1)} %get-tuple-element.42), channel_id=1, source_target_pairs={{0,2},{2,4},{4,6},{6,0},{1,3},{3,5},{5,7},{7,1},{8,10},{10,12},{12... | collective-permute-start | bytes 1572872 | tf_op jit(solution)/shard_map/ppermute | solution.py:27
  160.6 26.0 %collective-permute-start.36 = (bf16[2,8,128,128]{3,2,1,0:T(8,128)(2,1)}, bf16[2,8,128,128]{3,2,1,0:T(8,128)(2,1)S(1)}, u32[]{:S(2)}, u32[]{:S(2)}) collective-permute-start(bf16[2,8,128,128]{3,2,1,0:T(8,128)(2,1)} %get-tuple-element.43), channel_id=1, source_target_pairs={{0,4},{2,6},{4,0},{6,2},{1,5},{3,7},{5,1},{7,3},{8,12},{10,14},{12... | collective-permute-start | bytes 1572872 | tf_op jit(solution)/shard_map/ppermute | solution.py:27
  165.1 39.5 %copy-start.8 = (bf16[128,1024]{1,0:T(8,128)(2,1)}, bf16[128,1024]{1,0:T(8,128)(2,1)S(1)}, u32[]{:S(2)}) copy-start(bf16[128,1024]{1,0:T(8,128)(2,1)S(1)} %add_convert_fusion.mine_ref.refs_4_) | copy-start | bytes 786436
  165.1 26.4 %collective-permute-start.38 = (bf16[128,1024]{1,0:T(8,128)(2,1)S(1)}, bf16[128,1024]{1,0:T(8,128)(2,1)S(1)}, u32[]{:S(2)}, u32[]{:S(2)}) collective-permute-start(bf16[128,1024]{1,0:T(8,128)(2,1)S(1)} %add_convert_fusion.mine_ref.refs_4_), channel_id=1, source_target_pairs={{0,2},{2,4},{4,6},{6,0},{1,3},{3,5},{5,7},{7,1},{8,10},{10,12},{12... | collective-permute-start | bytes 786440 | tf_op jit(solution)/shard_map/ppermute | solution.py:27
  170.1 33.8 %collective-permute-start.37 = (bf16[2,8,128,128]{3,2,1,0:T(8,128)(2,1)}, bf16[2,8,128,128]{3,2,1,0:T(8,128)(2,1)S(1)}, u32[]{:S(2)}, u32[]{:S(2)}) collective-permute-start(bf16[2,8,128,128]{3,2,1,0:T(8,128)(2,1)} %get-tuple-element.44), channel_id=1, source_target_pairs={{0,6},{2,0},{4,2},{6,4},{1,7},{3,1},{5,3},{7,5},{8,14},{10,8},{12,... | collective-permute-start | bytes 1572872 | tf_op jit(solution)/shard_map/ppermute | solution.py:27
  170.1 27.7 %collective-permute-start.40 = (bf16[128,1024]{1,0:T(8,128)(2,1)S(1)}, bf16[128,1024]{1,0:T(8,128)(2,1)S(1)}, u32[]{:S(2)}, u32[]{:S(2)}) collective-permute-start(bf16[128,1024]{1,0:T(8,128)(2,1)S(1)} %add_convert_fusion.mine_ref.refs_4_), channel_id=1, source_target_pairs={{0,4},{2,6},{4,0},{6,2},{1,5},{3,7},{5,1},{7,3},{8,12},{10,14},{12... | collective-permute-start | bytes 786440 | tf_op jit(solution)/shard_map/ppermute | solution.py:27
  174.5 30.1 %copy-start.22 = (bf16[2,8,128,128]{3,2,1,0:T(8,128)(2,1)}, bf16[2,8,128,128]{3,2,1,0:T(8,128)(2,1)S(1)}, u32[]{:S(2)}) copy-start(bf16[2,8,128,128]{3,2,1,0:T(8,128)(2,1)S(1)} %collective-permute-done.35.refs_1_) | copy-start | bytes 1572868
  174.5 27.2 %collective-permute-start.42 = (bf16[128,1024]{1,0:T(8,128)(2,1)S(1)}, bf16[128,1024]{1,0:T(8,128)(2,1)S(1)}, u32[]{:S(2)}, u32[]{:S(2)}) collective-permute-start(bf16[128,1024]{1,0:T(8,128)(2,1)S(1)} %add_convert_fusion.mine_ref.refs_4_), channel_id=1, source_target_pairs={{0,6},{2,0},{4,2},{6,4},{1,7},{3,1},{5,3},{7,5},{8,14},{10,8},{12,... | collective-permute-start | bytes 786440 | tf_op jit(solution)/shard_map/ppermute | solution.py:27
  186.6 18.0 %copy-start.23 = (bf16[2,8,128,128]{3,2,1,0:T(8,128)(2,1)}, bf16[2,8,128,128]{3,2,1,0:T(8,128)(2,1)S(1)}, u32[]{:S(2)}) copy-start(bf16[2,8,128,128]{3,2,1,0:T(8,128)(2,1)S(1)} %collective-permute-done.36.refs_2_) | copy-start | bytes 1572868
  186.6 17.4 %collective-permute-start.33 = (bf16[128,1024]{1,0:T(8,128)(2,1)S(1)}, bf16[128,1024]{1,0:T(8,128)(2,1)S(1)}, u32[]{:S(2)}, u32[]{:S(2)}) collective-permute-start(bf16[128,1024]{1,0:T(8,128)(2,1)S(1)} %add_convert_fusion.mine_ref.refs_4_), channel_id=1, source_target_pairs={{0,8},{8,0},{1,9},{9,1},{2,10},{10,2},{3,11},{11,3},{4,12},{12,4},... | collective-permute-start | bytes 786440 | tf_op jit(solution)/shard_map/ppermute | solution.py:27
  191.4 13.2 %copy-start.26 = (bf16[128,1024]{1,0:T(8,128)(2,1)}, bf16[128,1024]{1,0:T(8,128)(2,1)S(1)}, u32[]{:S(2)}) copy-start(bf16[128,1024]{1,0:T(8,128)(2,1)S(1)} %collective-permute-done.38.refs_6_) | copy-start | bytes 786436
  191.4 12.6 %collective-permute-start.39 = (bf16[128,1024]{1,0:T(8,128)(2,1)S(1)}, bf16[128,1024]{1,0:T(8,128)(2,1)S(1)}, u32[]{:S(2)}, u32[]{:S(2)}) collective-permute-start(bf16[128,1024]{1,0:T(8,128)(2,1)S(1)} %collective-permute-done.38.refs_6_), channel_id=1, source_target_pairs={{0,8},{8,0},{1,9},{9,1},{2,10},{10,2},{3,11},{11,3},{4,12},{12,4},... | collective-permute-start | bytes 786440 | tf_op jit(solution)/shard_map/ppermute | solution.py:27
  197.8 6.2 %collective-permute-start.41 = (bf16[128,1024]{1,0:T(8,128)(2,1)S(1)}, bf16[128,1024]{1,0:T(8,128)(2,1)S(1)}, u32[]{:S(2)}, u32[]{:S(2)}) collective-permute-start(bf16[128,1024]{1,0:T(8,128)(2,1)S(1)} %collective-permute-done.40.refs_8_), channel_id=1, source_target_pairs={{0,8},{8,0},{1,9},{9,1},{2,10},{10,2},{3,11},{11,3},{4,12},{12,4},... | collective-permute-start | bytes 786440 | tf_op jit(solution)/shard_map/ppermute | solution.py:27
  201.7 2.9 %collective-permute-start.43 = (bf16[128,1024]{1,0:T(8,128)(2,1)S(1)}, bf16[128,1024]{1,0:T(8,128)(2,1)}, u32[]{:S(2)}, u32[]{:S(2)}) collective-permute-start(bf16[128,1024]{1,0:T(8,128)(2,1)S(1)} %collective-permute-done.42.refs_10_), channel_id=1, source_target_pairs={{0,8},{8,0},{1,9},{9,1},{2,10},{10,2},{3,11},{11,3},{4,12},{12,4},... | collective-permute-start | bytes 786440 | tf_op jit(solution)/shard_map/ppermute | solution.py:27
  212.0 24.6 %all-to-all-start = ((bf16[16,40,1024]{2,1,0:T(8,128)(2,1)}), bf16[16,40,1024]{2,1,0:T(8,128)(2,1)S(1)}, u32[]{:S(2)}, u32[]{:S(2)}) async-start(bf16[16,40,1024]{2,1,0:T(8,128)(2,1)} %get-tuple-element.45), calls=%async_computation | async-start | bytes 2621440 | tf_op jit(solution)/shard_map/all_to_all | solution.py:594
  223.3 26.8 %collective-permute-start.34 = (bf16[32,128,128]{2,1,0:T(8,128)(2,1)}, bf16[32,128,128]{2,1,0:T(8,128)(2,1)S(1)}, u32[]{:S(2)}, u32[]{:S(2)}) collective-permute-start(bf16[32,128,128]{2,1,0:T(8,128)(2,1)} %get-tuple-element.39), channel_id=1, source_target_pairs={{0,8},{8,0},{1,9},{9,1},{2,10},{10,2},{3,11},{11,3},{4,12},{12,4},... | collective-permute-start | bytes 3145736 | tf_op jit(solution)/shard_map/ppermute | solution.py:27
  236.6 20.8 %all-to-all-start.1 = ((bf16[16,32,1024]{2,1,0:T(8,128)(2,1)}), bf16[16,32,1024]{2,1,0:T(8,128)(2,1)S(1)}, u32[]{:S(2)}, u32[]{:S(2)}) async-start(bf16[16,32,1024]{2,1,0:T(8,128)(2,1)} %get-tuple-element.48), calls=%async_computation.1 | async-start | bytes 2097152 | tf_op jit(solution)/shard_map/all_to_all | solution.py:600
  242.8 2.6 %collective-permute-start.44 = (f32[1024]{0:T(1024)S(1)}, f32[1024]{0:T(1024)S(1)}, u32[]{:S(2)}, u32[]{:S(2)}) collective-permute-start(f32[1024]{0:T(1024)S(1)} %bitcast.28), channel_id=1, source_target_pairs={{0,8},{8,0},{1,9},{9,1},{2,10},{10,2},{3,11},{11,3},{4,12},{12,4},... | collective-permute-start | bytes 12296 | tf_op jit(solution)/shard_map/ppermute | solution.py:27
  245.5 11.1 %collective-permute-start.45 = (f32[2,1024]{1,0:T(2,128)S(1)}, f32[2,1024]{1,0:T(2,128)S(1)}, u32[]{:S(2)}, u32[]{:S(2)}) collective-permute-start(f32[2,1024]{1,0:T(2,128)S(1)} %maximum_select_fusion.1), channel_id=1, source_target_pairs={{0,6},{2,0},{4,2},{6,4},{1,7},{3,1},{5,3},{7,5},{8,14},{10,8},{12,... | collective-permute-start | bytes 24584 | tf_op jit(solution)/shard_map/ppermute | solution.py:27
  248.1 8.5 %collective-permute-start.46 = (f32[2,1024]{1,0:T(2,128)S(1)}, f32[2,1024]{1,0:T(2,128)S(1)}, u32[]{:S(2)}, u32[]{:S(2)}) collective-permute-start(f32[2,1024]{1,0:T(2,128)S(1)} %maximum_select_fusion.1), channel_id=1, source_target_pairs={{0,4},{2,6},{4,0},{6,2},{1,5},{3,7},{5,1},{7,3},{8,12},{10,14},{12... | collective-permute-start | bytes 24584 | tf_op jit(solution)/shard_map/ppermute | solution.py:27
  250.0 6.6 %collective-permute-start.47 = (f32[2,1024]{1,0:T(2,128)S(1)}, f32[2,1024]{1,0:T(2,128)S(1)}, u32[]{:S(2)}, u32[]{:S(2)}) collective-permute-start(f32[2,1024]{1,0:T(2,128)S(1)} %maximum_select_fusion.1), channel_id=1, source_target_pairs={{0,2},{2,4},{4,6},{6,0},{1,3},{3,5},{5,7},{7,1},{8,10},{10,12},{12... | collective-permute-start | bytes 24584 | tf_op jit(solution)/shard_map/ppermute | solution.py:27
  (23 other events, 112.7 us)

commit v5 on v4

--- a/solution.py
+++ b/solution.py
@@ -33,17 +33,20 @@
     return lax.ppermute(value, SEQ, pairs)
 
 
+def in_vmem(arrays):
+    return [pltpu.with_memory_space_constraint(a, pltpu.VMEM) for a in arrays]
+
+
 def rows(pieces):
     return jnp.concatenate(pieces, axis=0)
 
 
 def ring4(value, axis):
-    half = value.shape[0] // 2
     before = shift(value, axis, 1)
     after = shift(value, axis, -1)
-    far = [shift(before[:half], axis, 1), shift(after[half:], axis, -1)]
+    far = shift(value, axis, 2)
     first = join([value, before])
-    second = join([after] + far)
+    second = join([after, far])
     return first, second
 
 
@@ -72,7 +75,7 @@
         out_specs=whole,
         out_shape=jax.ShapeDtypeStruct((size, pieces[0].shape[1]), BF16),
         name="join",
-    )(*pieces)
+    )(*in_vmem(pieces))
 
 
 def gather_weight(weight):
@@ -205,7 +208,7 @@
         out_shape=jax.ShapeDtypeStruct((2 * tokens, width), F32),
         compiler_params=pltpu.CompilerParams(vmem_limit_bytes=VMEM_LIMIT),
         name="project_lot",
-    )(table, own, other, *pieces, *before)
+    )(table, *in_vmem((own, other, *pieces, *before)))
 
 
 def project_far_kernel(table_ref, own_ref, other_ref, near_ref, *refs):
@@ -230,17 +233,17 @@
         out_shape=[jax.ShapeDtypeStruct((tokens, near.shape[1]), F32)] * 2,
         compiler_params=pltpu.CompilerParams(vmem_limit_bytes=VMEM_LIMIT),
         name="project_far",
-    )(table, own, other, near, *pieces)
+    )(table, *in_vmem((own, other, near, *pieces)))
 
 
 def finish_kernel(mine_ref, other_ref, doc_ref, out_ref):
     tokens = mine_ref.shape[0]
     out_ref[:tokens, :] = (mine_ref[...] + other_ref[...]).astype(BF16)
     out_ref[tokens:, :] = jnp.zeros((8, out_ref.shape[1]), BF16)
-    out_ref[tokens:, :tokens] = doc_ref[...].astype(BF16)
-
-
-def finish(mine, other, doc_rows):
+    out_ref[tokens:, :tokens] = jnp.broadcast_to(doc_ref[...], (8, tokens)).astype(BF16)
+
+
+def finish(mine, other, doc):
     tokens, width = mine.shape
     whole = pl.BlockSpec(memory_space=pltpu.VMEM)
     return pl.pallas_call(
@@ -249,7 +252,7 @@
         out_specs=whole,
         out_shape=jax.ShapeDtypeStruct((tokens + 8, width), BF16),
         name="finish",
-    )(mine, other, doc_rows)
+    )(*in_vmem([mine, other]), doc)
 
 
 def attention_kernel(doc_ref, q_ref, go_ref, *refs):
@@ -527,7 +530,7 @@
         scratch_shapes=[pltpu.VMEM((units, UNIT), F32)],
         compiler_params=pltpu.CompilerParams(vmem_limit_bytes=VMEM_LIMIT),
         name="grad_weight",
-    )(place, *columns, *grads, *left, *right)
+    )(place, *columns, *in_vmem(grads), *left, *right)
 
 
 def gather_gain(total):
@@ -549,7 +552,6 @@
 
 def step(layer_input, queries, grad_out, segment_ids, kv_weight, norm_gain):
     source = layer_input[0]
-    tokens = source.shape[0]
     core = lax.axis_index("core").astype(jnp.int32)[None]
     x = lax.axis_index("x").astype(jnp.int32)[None]
     gain = norm_gain[None]
@@ -560,8 +562,6 @@
     unit_place = ((zs + turn) % 2 * 4 + (ys + rel) % 4).astype(jnp.int32)
 
     doc = (segment_ids + 1).astype(F32)
-    doc_rows = jnp.broadcast_to(doc, (8, tokens))
-
     near, more, far = gather_weight(kv_weight)
     own, send, inv = normalize(core, source, gain)
     other = shift(send, "core", 1)
@@ -570,7 +570,7 @@
     kv_near = project_lot(table, own, other, NEAR, near)
     kv_near = project_lot(table, own, other, MORE, more, kv_near)
     kv_mine, kv_theirs = project_far(table, own, other, kv_near, far)
-    kv_own = finish(kv_mine, shift(kv_theirs, "core", 1), doc_rows)
+    kv_own = finish(kv_mine, shift(kv_theirs, "core", 1), doc)
 
     kv_blocks = [kv_own] + [shift_seq(kv_own, k) for k in range(1, BACK + 1)]
     columns = [shift(block, "x", by) if by else block for by, block in enumerate(blocks)]

time: 263 us -> 262 us (level)
  waiting for transfers between devices: 69.1 us -> 84.6 us
  starting transfers between devices: 108 us -> 96.2 us
  Pallas kernels: 69.2 us -> 62.3 us
  local copies, waits for them, and re-layouts: 6.24 us -> 9.71 us
    ppermute x39 -> x37, waiting for transfers between devices: 44.1 us -> 56.8 us  [shift(): return lax.ppermute(value, axis, [(i, (i + by) % n) for i in range(n)])]
    ppermute x39 -> x37, starting transfers between devices: 75 us -> 65.8 us  [shift(): return lax.ppermute(value, axis, [(i, (i + by) % n) for i in range(n)])]
    unnamed x72 -> x52, local copies, waits for them, and re-layouts: 3.85 us -> 8.82 us
    ppermute x8, starting transfers between devices: 19.3 us -> 16 us  [shift_seq(): return lax.ppermute(value, SEQ, pairs)]
    pallas_call x4, Pallas kernels: 7.54 us -> 4.33 us  [join(): pl.pallas_call(join_kernel, in_specs=[whole] * len(pieces), out_specs=who...]
  transfers between devices with their start and end apart: 50 -> 48, of which waited for: 20 -> 25; matrix products, arithmetic and copies ran while one was open for 2% -> 1% of each run, Pallas kernels for 14% -> 12%
where the time goes in v5:
time: 262 us; the launch traced here: 258 us
  starting transfers between devices  96.2 us (37%)
  waiting for transfers between devices  84.6 us (32%)
  Pallas kernels  62.3 us (24%)
  local copies, waits for them, and re-layouts  9.71 us (4%)
  other arithmetic  4.41 us (2%)
    ppermute x37, starting transfers between devices, shift(): return lax.ppermute(value, axis, [(i, (i + by) % n) for i in range(n)])  65.8 us
    ppermute x37, waiting for transfers between devices, shift(): return lax.ppermute(value, axis, [(i, (i + by) % n) for i in range(n)])  56.8 us
    pallas_call x1, Pallas kernels, attention(): pl.pallas_call(attention_kernel, grid=(kv_heads,), in_specs=[pl.BlockSpec...  19.2 us
    ppermute x8, starting transfers between devices, shift_seq(): return lax.ppermute(value, SEQ, pairs)  16 us
    all_to_all x1, waiting for transfers between devices, step(): arrived = lax.all_to_all(halves[0], group, 0, 0, tiled=True)  13 us
    ppermute x8, waiting for transfers between devices, shift_seq(): return lax.ppermute(value, SEQ, pairs)  12.2 us
    unnamed x52, local copies, waits for them, and re-layouts  8.82 us
    pallas_call x1, Pallas kernels, grad_normed(): pl.pallas_call(grad_normed_kernel, in_specs=[pl.BlockSpec(memory_space=pl...  7.37 us
  transfers between devices with their start and end apart: 48, of which 25 were waited for; matrix products, arithmetic and copies ran while one was open for 1% of the time, Pallas kernels for 12%

profile of v5, /device:TPU:1, one launch (start us, length us, event | category | flops | bytes accessed | tf_op | source)
XLA Modules:
  0.0 258.2 jit_solution(3616849494281757444)
XLA Ops:
  0.6 4.7 %collective-permute-start.3 = (bf16[64,1024]{1,0:T(8,128)(2,1)}, bf16[64,1024]{1,0:T(8,128)(2,1)S(1)}, u32[]{:S(2)}, u32[]{:S(2)}) collective-permute-start(bf16[64,1024]{1,0:T(8,128)(2,1)} %param.12), channel_id=1, source_target_pairs={{0,65},{1,64},{64,1},{65,0},{2,67},{3,66},{66,3},{67,2},{4,69},{5,... | collective-permute-start | bytes 393224 | tf_op jit(solution)/shard_map/ppermute | solution.py:84
  5.3 1.3 collective-permute-start.1
  6.6 2.1 collective-permute-done.3
  9.6 3.0 %collective-permute-done.1 = bf16[64,1024]{1,0:T(8,128)(2,1)S(1)} collective-permute-done((bf16[64,1024]{1,0:T(8,128)(2,1)}, bf16[64,1024]{1,0:T(8,128)(2,1)S(1)}, u32[]{:S(2)}, u32[]{:S(2)}) %collective-permute-start.1) | collective-permute-done | bytes 131104 | tf_op jit(solution)/shard_map/ppermute | solution.py:27
  13.7 2.8 %collective-permute-start.4 = (bf16[256,512]{1,0:T(8,128)(2,1)S(1)}, bf16[256,512]{1,0:T(8,128)(2,1)S(1)}, u32[]{:S(2)}, u32[]{:S(2)}) collective-permute-start(bf16[256,512]{1,0:T(8,128)(2,1)S(1)} %get-tuple-element.50.refs_0_), channel_id=1, source_target_pairs={{0,48},{16,0},{32,16},{48,32},{1,49},{17,1},{33,17},{49,33},{2,50}... | collective-permute-start | bytes 786440 | tf_op jit(solution)/shard_map/ppermute | solution.py:27
  16.8 2.5 collective-permute-start.8
  20.5 1.2 collective-permute-done.4.refs_0_
  21.7 2.4 collective-permute-done.5.refs_1_
  24.9 1.2 collective-permute-start.6
  26.1 1.5 collective-permute-start.7
  28.4 4.1 %collective-permute-start.11 = (bf16[512,512]{1,0:T(8,128)(2,1)}, bf16[512,512]{1,0:T(8,128)(2,1)}, u32[]{:S(2)}, u32[]{:S(2)}) collective-permute-start(bf16[512,512]{1,0:T(8,128)(2,1)} %join.5.refs_5_), channel_id=1, source_target_pairs={{0,48},{16,0},{32,16},{48,32},{1,49},{17,1},{33,17},{49,33},{2,50}... | collective-permute-start | bytes 1572872 | tf_op jit(solution)/shard_map/ppermute | solution.py:27
  32.6 4.5 %norm.1 = (bf16[32,128,128]{2,1,0:T(8,128)(2,1)}, bf16[32,128,128]{2,1,0:T(8,128)(2,1)}, f32[128,128]{1,0:T(8,128)}) custom-call(s32[1]{0:T(128)} %bitcast.2.core_ref, bf16[128,8192]{1,0:T(8,128)(2,1)} %bitcast.18, f32[1,8192]{1,0:T(1,128)} %bitcast.23), custom_call_target="tpu_custom_call" | custom-call | tf_op jit(solution)/shard_map/norm/pallas_call | solution.py:132
  37.0 4.7 %collective-permute-start = (bf16[32,128,128]{2,1,0:T(8,128)(2,1)}, bf16[32,128,128]{2,1,0:T(8,128)(2,1)}, u32[]{:S(2)}, u32[]{:S(2)}) collective-permute-start(bf16[32,128,128]{2,1,0:T(8,128)(2,1)} %get-tuple-element.28), channel_id=1, source_target_pairs={{0,8},{8,0},{1,9},{9,1},{2,10},{10,2},{3,11},{11,3},{4,12},{12,4},... | collective-permute-start | bytes 3145736 | tf_op jit(solution)/shard_map/ppermute | solution.py:27
  42.6 8.3 %collective-permute-done.15.refs_1_ = bf16[256,512]{1,0:T(8,128)(2,1)} collective-permute-done((bf16[256,512]{1,0:T(8,128)(2,1)S(1)}, bf16[256,512]{1,0:T(8,128)(2,1)}, u32[]{:S(2)}, u32[]{:S(2)}) %collective-permute-start.15) | collective-permute-done | bytes 262176 | tf_op jit(solution)/shard_map/ppermute | solution.py:27
  50.8 1.8 join.7.refs_4_.refs_14_
  53.5 2.7 %collective-permute-start.14 = (bf16[512,512]{1,0:T(8,128)(2,1)}, bf16[512,512]{1,0:T(8,128)(2,1)}, u32[]{:S(2)}, u32[]{:S(2)}) collective-permute-start(bf16[512,512]{1,0:T(8,128)(2,1)} %join.6.refs_0_.refs_12_), channel_id=1, source_target_pairs={{0,6},{2,0},{4,2},{6,4},{1,7},{3,1},{5,3},{7,5},{8,14},{10,8},{12,... | collective-permute-start | bytes 1572872 | tf_op jit(solution)/shard_map/ppermute | solution.py:27
  56.2 2.7 %collective-permute-start.17 = (bf16[512,512]{1,0:T(8,128)(2,1)}, bf16[512,512]{1,0:T(8,128)(2,1)S(1)}, u32[]{:S(2)}, u32[]{:S(2)}) collective-permute-start(bf16[512,512]{1,0:T(8,128)(2,1)} %join.7.refs_4_.refs_14_), channel_id=1, source_target_pairs={{0,48},{16,0},{32,16},{48,32},{1,49},{17,1},{33,17},{49,33},{2,50}... | collective-permute-start | bytes 1572872 | tf_op jit(solution)/shard_map/ppermute | solution.py:27
  58.9 6.0 %collective-permute-done.13.refs_2_ = bf16[512,512]{1,0:T(8,128)(2,1)} collective-permute-done((bf16[512,512]{1,0:T(8,128)(2,1)}, bf16[512,512]{1,0:T(8,128)(2,1)}, u32[]{:S(2)}, u32[]{:S(2)}) %collective-permute-start.13) | collective-permute-done | bytes 524320 | tf_op jit(solution)/shard_map/ppermute | solution.py:27
  64.9 1.6 collective-permute-done.14.refs_3_
  66.5 3.0 %collective-permute-done.16.refs_6_.refs_15_ = bf16[512,512]{1,0:T(8,128)(2,1)S(1)} collective-permute-done((bf16[512,512]{1,0:T(8,128)(2,1)}, bf16[512,512]{1,0:T(8,128)(2,1)S(1)}, u32[]{:S(2)}, u32[]{:S(2)}) %collective-permute-start.16) | collective-permute-done | bytes 524320 | tf_op jit(solution)/shard_map/ppermute | solution.py:27
  70.0 2.7 %collective-permute-start.21 = (bf16[512,512]{1,0:T(8,128)(2,1)}, bf16[512,512]{1,0:T(8,128)(2,1)}, u32[]{:S(2)}, u32[]{:S(2)}) collective-permute-start(bf16[512,512]{1,0:T(8,128)(2,1)} %collective-permute-done.11.refs_3_.refs_11_), channel_id=1, source_target_pairs={{0,48},{16,0},{32,16},{48,32},{1,49},{17,1},{33,17},{49,33},{2,50}... | collective-permute-start | bytes 1572872 | tf_op jit(solution)/shard_map/ppermute | solution.py:27
  75.6 3.8 %project_lot.2.refs_4_ = f32[256,1024]{1,0:T(8,128)} custom-call(s32[64]{0:T(128)} %reshape.117.table_ref, bf16[32,128,128]{2,1,0:T(8,128)(2,1)S(1)} %copy-done, bf16[32,128,128]{2,1,0:T(8,128)(2,1)} %collective-permute-done.other_ref, bf16[512,512]{1,0:T(8,128)(2,1)S(1)} %copy-done.2, bf16[512,512]{1,0:T(8,128)(2,1)S(1)} %copy-done.1, ...), custom_call_target="tpu_custom_call" | custom-call | tf_op jit(solution)/shard_map/project_lot/pallas_call | solution.py:203
  79.5 1.5 collective-permute-done.10.refs_2_.refs_10_
  80.9 1.2 copy-done.8
  82.1 3.4 %project_lot.3.near_ref = f32[256,1024]{1,0:T(8,128)} custom-call(s32[64]{0:T(128)} %reshape.117.table_ref, bf16[32,128,128]{2,1,0:T(8,128)(2,1)S(1)} %copy-done, bf16[32,128,128]{2,1,0:T(8,128)(2,1)} %collective-permute-done.other_ref, bf16[512,512]{1,0:T(8,128)(2,1)S(1)} %copy-done.11, bf16[512,512]{1,0:T(8,128)(2,1)} %collective-permute-done.7.refs_1_.refs_9_, ...), custom_call_target="tpu_custom_call" | custom-call | tf_op jit(solution)/shard_map/project_lot/pallas_call | solution.py:203
  85.5 6.6 %collective-permute-done.20.refs_2_.refs_14_.refs_17_ = bf16[512,512]{1,0:T(8,128)(2,1)} collective-permute-done((bf16[512,512]{1,0:T(8,128)(2,1)S(1)}, bf16[512,512]{1,0:T(8,128)(2,1)}, u32[]{:S(2)}, u32[]{:S(2)}) %collective-permute-start.20) | collective-permute-done | bytes 524320 | tf_op jit(solution)/shard_map/ppermute | solution.py:27
  92.1 1.2 copy-done.7
  93.4 3.5 %project_far.1 = (f32[128,1024]{1,0:T(8,128)}, f32[128,1024]{1,0:T(8,128)}) custom-call(s32[64]{0:T(128)} %reshape.117.table_ref, bf16[32,128,128]{2,1,0:T(8,128)(2,1)S(1)} %copy-done, bf16[32,128,128]{2,1,0:T(8,128)(2,1)} %collective-permute-done.other_ref, f32[256,1024]{1,0:T(8,128)S(1)} %copy-done.7, ...), custom_call_target="tpu_custom_call" | custom-call | tf_op jit(solution)/shard_map/project_far/pallas_call | solution.py:229
  96.8 2.4 collective-permute-start.22
  99.7 1.2 collective-permute-done.22.other_ref
  102.0 1.4 finish.1.refs_0_.refs_5_.refs_10_
  103.4 3.6 %collective-permute-start.23 = (bf16[136,1024]{1,0:T(8,128)(2,1)}, bf16[136,1024]{1,0:T(8,128)(2,1)S(1)}, u32[]{:S(2)}, u32[]{:S(2)}) collective-permute-start(bf16[136,1024]{1,0:T(8,128)(2,1)} %finish.1.refs_0_.refs_5_.refs_10_), channel_id=1, source_target_pairs={{0,1},{1,2},{2,3},{3,4},{4,5},{5,6},{6,7},{8,9},{9,10},{10,11},{11... | collective-permute-start | bytes 835592 | tf_op jit(solution)/shard_map/ppermute | solution.py:33
  107.1 1.3 collective-permute-start.24
  108.4 4.1 %collective-permute-start.25 = (bf16[136,1024]{1,0:T(8,128)(2,1)}, bf16[136,1024]{1,0:T(8,128)(2,1)S(1)}, u32[]{:S(2)}, u32[]{:S(2)}) collective-permute-start(bf16[136,1024]{1,0:T(8,128)(2,1)} %finish.1.refs_0_.refs_5_.refs_10_), channel_id=1, source_target_pairs={{0,3},{1,4},{2,5},{3,6},{4,7},{8,11},{9,12},{10,13},{11,14},{12,15... | collective-permute-start | bytes 835592 | tf_op jit(solution)/shard_map/ppermute | solution.py:33
  112.5 1.7 collective-permute-start.26
  114.3 6.0 %collective-permute-done.25.refs_3_.refs_8_.refs_13_ = bf16[136,1024]{1,0:T(8,128)(2,1)S(1)} collective-permute-done((bf16[136,1024]{1,0:T(8,128)(2,1)}, bf16[136,1024]{1,0:T(8,128)(2,1)S(1)}, u32[]{:S(2)}, u32[]{:S(2)}) %collective-permute-start.25) | collective-permute-done | bytes 278560 | tf_op jit(solution)/shard_map/ppermute | solution.py:33
  120.3 6.0 %collective-permute-done.26.refs_4_.refs_9_.refs_14_ = bf16[136,1024]{1,0:T(8,128)(2,1)S(1)} collective-permute-done((bf16[136,1024]{1,0:T(8,128)(2,1)}, bf16[136,1024]{1,0:T(8,128)(2,1)S(1)}, u32[]{:S(2)}, u32[]{:S(2)}) %collective-permute-start.26) | collective-permute-done | bytes 278560 | tf_op jit(solution)/shard_map/ppermute | solution.py:33
  126.9 19.2 %attention.1 = (bf16[128,4096]{1,0:T(8,128)(2,1)}, bf16[128,4096]{1,0:T(8,128)(2,1)}, f32[128,1024]{1,0:T(8,128)}, bf16[128,1024]{1,0:T(8,128)(2,1)}, bf16[128,1...) custom-call(f32[1,128]{1,0:T(1,128)} %add_convert_fusion.1.doc_ref, ...), custom_call_target="tpu_custom_call" | custom-call | tf_op jit(solution)/shard_map/attention/pallas_call | solution.py:365
  146.1 1.4 collective-permute-start.30
  147.5 1.3 collective-permute-start.29
  148.8 1.3 collective-permute-start.28
  150.1 1.3 collective-permute-start.27
  151.4 3.0 %spread.1 = (bf16[2,8,128,128]{3,2,1,0:T(8,128)(2,1)}, bf16[2,8,128,128]{3,2,1,0:T(8,128)(2,1)}, bf16[2,8,128,128]{3,2,1,0:T(8,128)(2,1)}, bf16[2,8,128,128]{3,2,1,0:T(8,128)(2,1)}) custom-call(s32[1]{0:T(128)} %bitcast.8.x_ref, bf16[32,128,128]{2,1,0:T(8,128)(2,1)} %get-tuple-element.27.own_ref, bf16[32,128,128]{2,1,0:T(8,128)(2,1)} %collective-permute-done.other_ref), custom_call_target="tpu_custom_call" | custom-call | tf_op jit(solution)/shard_map/spread/pallas_call | solution.py:164
  154.4 6.7 %collective-permute-start.33 = (bf16[2,8,128,128]{3,2,1,0:T(8,128)(2,1)}, bf16[2,8,128,128]{3,2,1,0:T(8,128)(2,1)S(1)}, u32[]{:S(2)}, u32[]{:S(2)}) collective-permute-start(bf16[2,8,128,128]{3,2,1,0:T(8,128)(2,1)} %get-tuple-element.42), channel_id=1, source_target_pairs={{0,2},{2,4},{4,6},{6,0},{1,3},{3,5},{5,7},{7,1},{8,10},{10,12},{12... | collective-permute-start | bytes 1572872 | tf_op jit(solution)/shard_map/ppermute | solution.py:27
  161.1 4.3 %collective-permute-start.34 = (bf16[2,8,128,128]{3,2,1,0:T(8,128)(2,1)}, bf16[2,8,128,128]{3,2,1,0:T(8,128)(2,1)S(1)}, u32[]{:S(2)}, u32[]{:S(2)}) collective-permute-start(bf16[2,8,128,128]{3,2,1,0:T(8,128)(2,1)} %get-tuple-element.43), channel_id=1, source_target_pairs={{0,4},{2,6},{4,0},{6,2},{1,5},{3,7},{5,1},{7,3},{8,12},{10,14},{12... | collective-permute-start | bytes 1572872 | tf_op jit(solution)/shard_map/ppermute | solution.py:27
  165.7 3.8 %collective-permute-start.36 = (bf16[128,1024]{1,0:T(8,128)(2,1)S(1)}, bf16[128,1024]{1,0:T(8,128)(2,1)S(1)}, u32[]{:S(2)}, u32[]{:S(2)}) collective-permute-start(bf16[128,1024]{1,0:T(8,128)(2,1)S(1)} %add_convert_fusion.mine_ref.refs_4_), channel_id=1, source_target_pairs={{0,2},{2,4},{4,6},{6,0},{1,3},{3,5},{5,7},{7,1},{8,10},{10,12},{12... | collective-permute-start | bytes 786440 | tf_op jit(solution)/shard_map/ppermute | solution.py:27
  169.9 1.7 collective-permute-start.38
  171.6 3.7 %collective-permute-done.33.refs_1_ = bf16[2,8,128,128]{3,2,1,0:T(8,128)(2,1)S(1)} collective-permute-done((bf16[2,8,128,128]{3,2,1,0:T(8,128)(2,1)}, bf16[2,8,128,128]{3,2,1,0:T(8,128)(2,1)S(1)}, u32[]{:S(2)}, u32[]{:S(2)}) %collective-permute-start.33) | collective-permute-done | bytes 524320 | tf_op jit(solution)/shard_map/ppermute | solution.py:27
  176.4 11.0 %collective-permute-done.34.refs_2_ = bf16[2,8,128,128]{3,2,1,0:T(8,128)(2,1)S(1)} collective-permute-done((bf16[2,8,128,128]{3,2,1,0:T(8,128)(2,1)}, bf16[2,8,128,128]{3,2,1,0:T(8,128)(2,1)S(1)}, u32[]{:S(2)}, u32[]{:S(2)}) %collective-permute-start.34) | collective-permute-done | bytes 524320 | tf_op jit(solution)/shard_map/ppermute | solution.py:27
  187.4 4.4 %collective-permute-start.31 = (bf16[128,1024]{1,0:T(8,128)(2,1)S(1)}, bf16[128,1024]{1,0:T(8,128)(2,1)S(1)}, u32[]{:S(2)}, u32[]{:S(2)}) collective-permute-start(bf16[128,1024]{1,0:T(8,128)(2,1)S(1)} %add_convert_fusion.mine_ref.refs_4_), channel_id=1, source_target_pairs={{0,8},{8,0},{1,9},{9,1},{2,10},{10,2},{3,11},{11,3},{4,12},{12,4},... | collective-permute-start | bytes 786440 | tf_op jit(solution)/shard_map/ppermute | solution.py:27
  192.1 2.9 %collective-permute-start.37 = (bf16[128,1024]{1,0:T(8,128)(2,1)S(1)}, bf16[128,1024]{1,0:T(8,128)(2,1)S(1)}, u32[]{:S(2)}, u32[]{:S(2)}) collective-permute-start(bf16[128,1024]{1,0:T(8,128)(2,1)S(1)} %collective-permute-done.36.refs_6_), channel_id=1, source_target_pairs={{0,8},{8,0},{1,9},{9,1},{2,10},{10,2},{3,11},{11,3},{4,12},{12,4},... | collective-permute-start | bytes 786440 | tf_op jit(solution)/shard_map/ppermute | solution.py:27
  195.0 3.6 %collective-permute-done.38.refs_8_ = bf16[128,1024]{1,0:T(8,128)(2,1)S(1)} collective-permute-done((bf16[128,1024]{1,0:T(8,128)(2,1)S(1)}, bf16[128,1024]{1,0:T(8,128)(2,1)S(1)}, u32[]{:S(2)}, u32[]{:S(2)}) %collective-permute-start.38) | collective-permute-done | bytes 262176 | tf_op jit(solution)/shard_map/ppermute | solution.py:27
  198.6 2.4 collective-permute-start.39
  201.0 1.2 collective-permute-done.40.refs_10_
  202.2 1.6 collective-permute-start.41
  205.0 6.3 %grad_weight.1 = (bf16[16,40,1024]{2,1,0:T(8,128)(2,1)}, bf16[16,32,1024]{2,1,0:T(8,128)(2,1)}) custom-call(s32[8]{0:T(128)} %fusion.place_ref, bf16[2,8,128,128]{3,2,1,0:T(8,128)(2,1)} %get-tuple-element.41.refs_0_, bf16[2,8,128,128]{3,2,1,0:T(8,128)(2,1)} %copy-done.21, bf16[2,8,128,128]{3,2,1,0:T(8,128)(2,1)} %copy-done.22, ...), custom_call_target="tpu_custom_call" | custom-call | tf_op jit(solution)/shard_map/grad_weight/pallas_call | solution.py:522
  211.3 3.9 %all-to-all-start = ((bf16[16,40,1024]{2,1,0:T(8,128)(2,1)}), bf16[16,40,1024]{2,1,0:T(8,128)(2,1)S(1)}, u32[]{:S(2)}, u32[]{:S(2)}) async-start(bf16[16,40,1024]{2,1,0:T(8,128)(2,1)} %get-tuple-element.45), calls=%async_computation | async-start | bytes 2621440 | tf_op jit(solution)/shard_map/all_to_all | solution.py:594
  215.3 7.4 %grad_normed.1 = (bf16[32,128,128]{2,1,0:T(8,128)(2,1)}, bf16[32,128,128]{2,1,0:T(8,128)(2,1)}) custom-call(s32[64]{0:T(128)} %reshape.117.table_ref, bf16[128,1024]{1,0:T(8,128)(2,1)} %copy-done.9, bf16[128,1024]{1,0:T(8,128)(2,1)} %copy-done.12, bf16[512,512]{1,0:T(8,128)(2,1)} %join.6.refs_0_.refs_12_, bf16[512,512]{1,0:T(8,128)(2,1)} %join.4.refs_1_.refs_13_, ...), custom_call_target="tpu_custom_call" | custom-call | tf_op jit(solution)/shard_map/grad_normed/pallas_call | solution.py:419
  223.0 13.0 %all-to-all-done = bf16[16,40,1024]{2,1,0:T(8,128)(2,1)S(1)} async-done(((bf16[16,40,1024]{2,1,0:T(8,128)(2,1)}), bf16[16,40,1024]{2,1,0:T(8,128)(2,1)S(1)}, u32[]{:S(2)}, u32[]{:S(2)}) %all-to-all-start) | async-done | bytes 1310752 | tf_op jit(solution)/shard_map/all_to_all | solution.py:594
  235.9 5.8 %all-to-all-start.1 = ((bf16[16,32,1024]{2,1,0:T(8,128)(2,1)}), bf16[16,32,1024]{2,1,0:T(8,128)(2,1)S(1)}, u32[]{:S(2)}, u32[]{:S(2)}) async-start(bf16[16,32,1024]{2,1,0:T(8,128)(2,1)} %get-tuple-element.48), calls=%async_computation.1 | async-start | bytes 2097152 | tf_op jit(solution)/shard_map/all_to_all | solution.py:600
  242.7 1.6 collective-permute-start.42
  245.1 2.4 collective-permute-start.43
  247.4 1.5 collective-permute-start.44
  250.4 5.6 %norm_back.1 = bf16[128,8192]{1,0:T(8,128)(2,1)} custom-call(s32[1]{0:T(128)} %bitcast.2.core_ref, bf16[32,128,128]{2,1,0:T(8,128)(2,1)} %get-tuple-element.38.own_ref, bf16[32,128,128]{2,1,0:T(8,128)(2,1)} %copy-done.18, bf16[128,8192]{1,0:T(8,128)(2,1)} %bitcast.19, f32[128,128]{1,0:T(8,128)} %get-tuple-element.40.inv_ref, f32[1,8192]{1,0:T(1,128)} %bitcast.24), custom_call_target="tpu_custom_call" | custom-call | tf_op jit(solution)/shard_map/norm_back/pallas_call | solution.py:458
  (121 shorter events, 21.8 us)
Async XLA Ops:
  0.6 8.1 %collective-permute-start.3 = (bf16[64,1024]{1,0:T(8,128)(2,1)}, bf16[64,1024]{1,0:T(8,128)(2,1)S(1)}, u32[]{:S(2)}, u32[]{:S(2)}) collective-permute-start(bf16[64,1024]{1,0:T(8,128)(2,1)} %param.12), channel_id=1, source_target_pairs={{0,65},{1,64},{64,1},{65,0},{2,67},{3,66},{66,3},{67,2},{4,69},{5,... | collective-permute-start | bytes 393224 | tf_op jit(solution)/shard_map/ppermute | solution.py:84
  5.3 4.3 %collective-permute-start.2 = (bf16[64,1024]{1,0:T(8,128)(2,1)}, bf16[64,1024]{1,0:T(8,128)(2,1)S(1)}, u32[]{:S(2)}, u32[]{:S(2)}) collective-permute-start(bf16[64,1024]{1,0:T(8,128)(2,1)} %param.12), channel_id=1, source_target_pairs={{0,64},{64,0},{1,65},{65,1},{2,66},{66,2},{3,67},{67,3},{4,68},{68... | collective-permute-start | bytes 393224 | tf_op jit(solution)/shard_map/ppermute | solution.py:27
  5.3 7.2 %collective-permute-start.1 = (bf16[64,1024]{1,0:T(8,128)(2,1)}, bf16[64,1024]{1,0:T(8,128)(2,1)S(1)}, u32[]{:S(2)}, u32[]{:S(2)}) collective-permute-start(bf16[64,1024]{1,0:T(8,128)(2,1)} %param.12), channel_id=1, source_target_pairs={{0,1},{1,0},{2,3},{3,2},{4,5},{5,4},{6,7},{7,6},{8,9},{9,8},{10,11... | collective-permute-start | bytes 393224 | tf_op jit(solution)/shard_map/ppermute | solution.py:27
  13.7 8.0 %collective-permute-start.4 = (bf16[256,512]{1,0:T(8,128)(2,1)S(1)}, bf16[256,512]{1,0:T(8,128)(2,1)S(1)}, u32[]{:S(2)}, u32[]{:S(2)}) collective-permute-start(bf16[256,512]{1,0:T(8,128)(2,1)S(1)} %get-tuple-element.50.refs_0_), channel_id=1, source_target_pairs={{0,48},{16,0},{32,16},{48,32},{1,49},{17,1},{33,17},{49,33},{2,50}... | collective-permute-start | bytes 786440 | tf_op jit(solution)/shard_map/ppermute | solution.py:27
  16.5 7.6 %collective-permute-start.5 = (bf16[256,512]{1,0:T(8,128)(2,1)S(1)}, bf16[256,512]{1,0:T(8,128)(2,1)S(1)}, u32[]{:S(2)}, u32[]{:S(2)}) collective-permute-start(bf16[256,512]{1,0:T(8,128)(2,1)S(1)} %get-tuple-element.50.refs_0_), channel_id=1, source_target_pairs={{0,32},{16,48},{32,0},{48,16},{1,33},{17,49},{33,1},{49,17},{2,34}... | collective-permute-start | bytes 786440 | tf_op jit(solution)/shard_map/ppermute | solution.py:27
  16.8 10.7 %collective-permute-start.8 = (bf16[256,512]{1,0:T(8,128)(2,1)S(1)}, bf16[256,512]{1,0:T(8,128)(2,1)S(1)}, u32[]{:S(2)}, u32[]{:S(2)}) collective-permute-start(bf16[256,512]{1,0:T(8,128)(2,1)S(1)} %get-tuple-element.49.refs_0_), channel_id=1, source_target_pairs={{0,6},{2,0},{4,2},{6,4},{1,7},{3,1},{5,3},{7,5},{8,14},{10,8},{12,... | collective-permute-start | bytes 786440 | tf_op jit(solution)/shard_map/ppermute | solution.py:27
  19.3 8.3 %collective-permute-start.9 = (bf16[256,512]{1,0:T(8,128)(2,1)S(1)}, bf16[256,512]{1,0:T(8,128)(2,1)S(1)}, u32[]{:S(2)}, u32[]{:S(2)}) collective-permute-start(bf16[256,512]{1,0:T(8,128)(2,1)S(1)} %get-tuple-element.49.refs_0_), channel_id=1, source_target_pairs={{0,4},{2,6},{4,0},{6,2},{1,5},{3,7},{5,1},{7,3},{8,12},{10,14},{12... | collective-permute-start | bytes 786440 | tf_op jit(solution)/shard_map/ppermute | solution.py:27
  19.8 21.9 %collective-permute-start.12 = (bf16[256,512]{1,0:T(8,128)(2,1)S(1)}, bf16[256,512]{1,0:T(8,128)(2,1)S(1)}, u32[]{:S(2)}, u32[]{:S(2)}) collective-permute-start(bf16[256,512]{1,0:T(8,128)(2,1)S(1)} %get-tuple-element.50.refs_0_), channel_id=1, source_target_pairs={{0,16},{16,32},{32,48},{48,0},{1,17},{17,33},{33,49},{49,1},{2,18}... | collective-permute-start | bytes 786440 | tf_op jit(solution)/shard_map/ppermute | solution.py:27
  24.9 27.7 %collective-permute-start.6 = (bf16[512,512]{1,0:T(8,128)(2,1)}, bf16[512,512]{1,0:T(8,128)(2,1)S(1)}, u32[]{:S(2)}, u32[]{:S(2)}) collective-permute-start(bf16[512,512]{1,0:T(8,128)(2,1)} %join.4.refs_1_.refs_13_), channel_id=1, source_target_pairs={{0,2},{2,4},{4,6},{6,0},{1,3},{3,5},{5,7},{7,1},{8,10},{10,12},{12... | collective-permute-start | bytes 1572872 | tf_op jit(solution)/shard_map/ppermute | solution.py:27
  26.1 30.0 %collective-permute-start.7 = (bf16[512,512]{1,0:T(8,128)(2,1)}, bf16[512,512]{1,0:T(8,128)(2,1)}, u32[]{:S(2)}, u32[]{:S(2)}) collective-permute-start(bf16[512,512]{1,0:T(8,128)(2,1)} %join.4.refs_1_.refs_13_), channel_id=1, source_target_pairs={{0,6},{2,0},{4,2},{6,4},{1,7},{3,1},{5,3},{7,5},{8,14},{10,8},{12,... | collective-permute-start | bytes 1572872 | tf_op jit(solution)/shard_map/ppermute | solution.py:27
  28.4 27.7 %collective-permute-start.11 = (bf16[512,512]{1,0:T(8,128)(2,1)}, bf16[512,512]{1,0:T(8,128)(2,1)}, u32[]{:S(2)}, u32[]{:S(2)}) collective-permute-start(bf16[512,512]{1,0:T(8,128)(2,1)} %join.5.refs_5_), channel_id=1, source_target_pairs={{0,48},{16,0},{32,16},{48,32},{1,49},{17,1},{33,17},{49,33},{2,50}... | collective-permute-start | bytes 1572872 | tf_op jit(solution)/shard_map/ppermute | solution.py:27
  32.5 26.3 %copy-start.24 = (s32[4]{0:T(128)S(1)}, s32[4]{0:T(128)}, u32[]{:S(2)}) copy-start(s32[4]{0:T(128)} %constant.117.clone) | copy-start | bytes 52
  32.6 32.4 %copy-start.4 = (bf16[512,512]{1,0:T(8,128)(2,1)S(1)}, bf16[512,512]{1,0:T(8,128)(2,1)}, u32[]{:S(2)}) copy-start(bf16[512,512]{1,0:T(8,128)(2,1)} %join.5.refs_5_) | copy-start | bytes 1572868
  32.6 41.0 %copy-start.1 = (bf16[512,512]{1,0:T(8,128)(2,1)S(1)}, bf16[512,512]{1,0:T(8,128)(2,1)}, u32[]{:S(2)}) copy-start(bf16[512,512]{1,0:T(8,128)(2,1)} %join.4.refs_1_.refs_13_) | copy-start | bytes 1572868
  37.0 36.5 %copy-start = (bf16[32,128,128]{2,1,0:T(8,128)(2,1)S(1)}, bf16[32,128,128]{2,1,0:T(8,128)(2,1)}, u32[]{:S(2)}) copy-start(bf16[32,128,128]{2,1,0:T(8,128)(2,1)} %get-tuple-element.27.own_ref) | copy-start | bytes 3145732
  37.0 33.0 %collective-permute-start = (bf16[32,128,128]{2,1,0:T(8,128)(2,1)}, bf16[32,128,128]{2,1,0:T(8,128)(2,1)}, u32[]{:S(2)}, u32[]{:S(2)}) collective-permute-start(bf16[32,128,128]{2,1,0:T(8,128)(2,1)} %get-tuple-element.28), channel_id=1, source_target_pairs={{0,8},{8,0},{1,9},{9,1},{2,10},{10,2},{3,11},{11,3},{4,12},{12,4},... | collective-permute-start | bytes 3145736 | tf_op jit(solution)/shard_map/ppermute | solution.py:27
  41.7 9.1 %collective-permute-start.15 = (bf16[256,512]{1,0:T(8,128)(2,1)S(1)}, bf16[256,512]{1,0:T(8,128)(2,1)}, u32[]{:S(2)}, u32[]{:S(2)}) collective-permute-start(bf16[256,512]{1,0:T(8,128)(2,1)S(1)} %get-tuple-element.49.refs_0_), channel_id=1, source_target_pairs={{0,2},{2,4},{4,6},{6,0},{1,3},{3,5},{5,7},{7,1},{8,10},{10,12},{12... | collective-permute-start | bytes 786440 | tf_op jit(solution)/shard_map/ppermute | solution.py:27
  50.8 14.1 %collective-permute-start.13 = (bf16[512,512]{1,0:T(8,128)(2,1)}, bf16[512,512]{1,0:T(8,128)(2,1)}, u32[]{:S(2)}, u32[]{:S(2)}) collective-permute-start(bf16[512,512]{1,0:T(8,128)(2,1)} %join.6.refs_0_.refs_12_), channel_id=1, source_target_pairs={{0,2},{2,4},{4,6},{6,0},{1,3},{3,5},{5,7},{7,1},{8,10},{10,12},{12... | collective-permute-start | bytes 1572872 | tf_op jit(solution)/shard_map/ppermute | solution.py:27
  53.5 13.0 %collective-permute-start.14 = (bf16[512,512]{1,0:T(8,128)(2,1)}, bf16[512,512]{1,0:T(8,128)(2,1)}, u32[]{:S(2)}, u32[]{:S(2)}) collective-permute-start(bf16[512,512]{1,0:T(8,128)(2,1)} %join.6.refs_0_.refs_12_), channel_id=1, source_target_pairs={{0,6},{2,0},{4,2},{6,4},{1,7},{3,1},{5,3},{7,5},{8,14},{10,8},{12,... | collective-permute-start | bytes 1572872 | tf_op jit(solution)/shard_map/ppermute | solution.py:27
  56.2 13.4 %collective-permute-start.16 = (bf16[512,512]{1,0:T(8,128)(2,1)}, bf16[512,512]{1,0:T(8,128)(2,1)S(1)}, u32[]{:S(2)}, u32[]{:S(2)}) collective-permute-start(bf16[512,512]{1,0:T(8,128)(2,1)} %join.7.refs_4_.refs_14_), channel_id=1, source_target_pairs={{0,16},{16,32},{32,48},{48,0},{1,17},{17,33},{33,49},{49,1},{2,18}... | collective-permute-start | bytes 1572872 | tf_op jit(solution)/shard_map/ppermute | solution.py:27
  56.2 13.9 %collective-permute-start.17 = (bf16[512,512]{1,0:T(8,128)(2,1)}, bf16[512,512]{1,0:T(8,128)(2,1)S(1)}, u32[]{:S(2)}, u32[]{:S(2)}) collective-permute-start(bf16[512,512]{1,0:T(8,128)(2,1)} %join.7.refs_4_.refs_14_), channel_id=1, source_target_pairs={{0,48},{16,0},{32,16},{48,32},{1,49},{17,1},{33,17},{49,33},{2,50}... | collective-permute-start | bytes 1572872 | tf_op jit(solution)/shard_map/ppermute | solution.py:27
  64.9 16.0 %collective-permute-start.10 = (bf16[512,512]{1,0:T(8,128)(2,1)S(1)}, bf16[512,512]{1,0:T(8,128)(2,1)}, u32[]{:S(2)}, u32[]{:S(2)}) collective-permute-start(bf16[512,512]{1,0:T(8,128)(2,1)S(1)} %copy-done.4), channel_id=1, source_target_pairs={{0,16},{16,32},{32,48},{48,0},{1,17},{17,33},{33,49},{49,1},{2,18}... | collective-permute-start | bytes 1572872 | tf_op jit(solution)/shard_map/ppermute | solution.py:27
  66.5 19.0 %collective-permute-start.18 = (bf16[512,512]{1,0:T(8,128)(2,1)}, bf16[512,512]{1,0:T(8,128)(2,1)}, u32[]{:S(2)}, u32[]{:S(2)}) collective-permute-start(bf16[512,512]{1,0:T(8,128)(2,1)} %collective-permute-done.13.refs_2_), channel_id=1, source_target_pairs={{0,2},{2,4},{4,6},{6,0},{1,3},{3,5},{5,7},{7,1},{8,10},{10,12},{12... | collective-permute-start | bytes 1572872 | tf_op jit(solution)/shard_map/ppermute | solution.py:27
  69.6 9.9 %copy-start.5 = (bf16[512,512]{1,0:T(8,128)(2,1)}, bf16[512,512]{1,0:T(8,128)(2,1)S(1)}, u32[]{:S(2)}) copy-start(bf16[512,512]{1,0:T(8,128)(2,1)S(1)} %collective-permute-done.16.refs_6_.refs_15_) | copy-start | bytes 1572868
  69.6 15.9 %collective-permute-start.19 = (bf16[512,512]{1,0:T(8,128)(2,1)}, bf16[512,512]{1,0:T(8,128)(2,1)}, u32[]{:S(2)}, u32[]{:S(2)}) collective-permute-start(bf16[512,512]{1,0:T(8,128)(2,1)} %collective-permute-done.7.refs_1_.refs_9_), channel_id=1, source_target_pairs={{0,6},{2,0},{4,2},{6,4},{1,7},{3,1},{5,3},{7,5},{8,14},{10,8},{12,... | collective-permute-start | bytes 1572872 | tf_op jit(solution)/shard_map/ppermute | solution.py:27
  70.0 9.4 %copy-start.6 = (bf16[512,512]{1,0:T(8,128)(2,1)}, bf16[512,512]{1,0:T(8,128)(2,1)S(1)}, u32[]{:S(2)}) copy-start(bf16[512,512]{1,0:T(8,128)(2,1)S(1)} %collective-permute-done.17.refs_7_.refs_16_) | copy-start | bytes 1572868
  70.0 22.1 %collective-permute-start.20 = (bf16[512,512]{1,0:T(8,128)(2,1)S(1)}, bf16[512,512]{1,0:T(8,128)(2,1)}, u32[]{:S(2)}, u32[]{:S(2)}) collective-permute-start(bf16[512,512]{1,0:T(8,128)(2,1)S(1)} %collective-permute-done.16.refs_6_.refs_15_), channel_id=1, source_target_pairs={{0,16},{16,32},{32,48},{48,0},{1,17},{17,33},{33,49},{49,1},{2,18}... | collective-permute-start | bytes 1572872 | tf_op jit(solution)/shard_map/ppermute | solution.py:27
  70.0 22.1 %collective-permute-start.21 = (bf16[512,512]{1,0:T(8,128)(2,1)}, bf16[512,512]{1,0:T(8,128)(2,1)}, u32[]{:S(2)}, u32[]{:S(2)}) collective-permute-start(bf16[512,512]{1,0:T(8,128)(2,1)} %collective-permute-done.11.refs_3_.refs_11_), channel_id=1, source_target_pairs={{0,48},{16,0},{32,16},{48,32},{1,49},{17,1},{33,17},{49,33},{2,50}... | collective-permute-start | bytes 1572872 | tf_op jit(solution)/shard_map/ppermute | solution.py:27
  82.1 17.1 %copy-start.25 = (s32[1,128]{1,0:T(1,128)S(1)}, s32[1,128]{1,0:T(1,128)}, u32[]{:S(2)}) copy-start(s32[1,128]{1,0:T(1,128)} %param.11) | copy-start | bytes 1540
  96.8 4.1 %collective-permute-start.22 = (f32[128,1024]{1,0:T(8,128)}, f32[128,1024]{1,0:T(8,128)S(1)}, u32[]{:S(2)}, u32[]{:S(2)}) collective-permute-start(f32[128,1024]{1,0:T(8,128)} %get-tuple-element.30), channel_id=1, source_target_pairs={{0,8},{8,0},{1,9},{9,1},{2,10},{10,2},{3,11},{11,3},{4,12},{12,4},... | collective-permute-start | bytes 1572872 | tf_op jit(solution)/shard_map/ppermute | solution.py:27
  103.4 10.8 %collective-permute-start.23 = (bf16[136,1024]{1,0:T(8,128)(2,1)}, bf16[136,1024]{1,0:T(8,128)(2,1)S(1)}, u32[]{:S(2)}, u32[]{:S(2)}) collective-permute-start(bf16[136,1024]{1,0:T(8,128)(2,1)} %finish.1.refs_0_.refs_5_.refs_10_), channel_id=1, source_target_pairs={{0,1},{1,2},{2,3},{3,4},{4,5},{5,6},{6,7},{8,9},{9,10},{10,11},{11... | collective-permute-start | bytes 835592 | tf_op jit(solution)/shard_map/ppermute | solution.py:33
  107.1 7.2 %collective-permute-start.24 = (bf16[136,1024]{1,0:T(8,128)(2,1)}, bf16[136,1024]{1,0:T(8,128)(2,1)S(1)}, u32[]{:S(2)}, u32[]{:S(2)}) collective-permute-start(bf16[136,1024]{1,0:T(8,128)(2,1)} %finish.1.refs_0_.refs_5_.refs_10_), channel_id=1, source_target_pairs={{0,2},{1,3},{2,4},{3,5},{4,6},{5,7},{8,10},{9,11},{10,12},{11,13},... | collective-permute-start | bytes 835592 | tf_op jit(solution)/shard_map/ppermute | solution.py:33
  108.4 11.9 %collective-permute-start.25 = (bf16[136,1024]{1,0:T(8,128)(2,1)}, bf16[136,1024]{1,0:T(8,128)(2,1)S(1)}, u32[]{:S(2)}, u32[]{:S(2)}) collective-permute-start(bf16[136,1024]{1,0:T(8,128)(2,1)} %finish.1.refs_0_.refs_5_.refs_10_), channel_id=1, source_target_pairs={{0,3},{1,4},{2,5},{3,6},{4,7},{8,11},{9,12},{10,13},{11,14},{12,15... | collective-permute-start | bytes 835592 | tf_op jit(solution)/shard_map/ppermute | solution.py:33
  112.5 13.8 %collective-permute-start.26 = (bf16[136,1024]{1,0:T(8,128)(2,1)}, bf16[136,1024]{1,0:T(8,128)(2,1)S(1)}, u32[]{:S(2)}, u32[]{:S(2)}) collective-permute-start(bf16[136,1024]{1,0:T(8,128)(2,1)} %finish.1.refs_0_.refs_5_.refs_10_), channel_id=1, source_target_pairs={{0,4},{1,5},{2,6},{3,7},{8,12},{9,13},{10,14},{11,15},{16,20},{17,... | collective-permute-start | bytes 835592 | tf_op jit(solution)/shard_map/ppermute | solution.py:33
  114.2 12.0 %copy-start.14 = (bf16[136,1024]{1,0:T(8,128)(2,1)}, bf16[136,1024]{1,0:T(8,128)(2,1)S(1)}, u32[]{:S(2)}) copy-start(bf16[136,1024]{1,0:T(8,128)(2,1)S(1)} %collective-permute-done.23.refs_1_.refs_6_.refs_11_) | copy-start | bytes 835588
  114.3 11.9 %copy-start.15 = (bf16[136,1024]{1,0:T(8,128)(2,1)}, bf16[136,1024]{1,0:T(8,128)(2,1)S(1)}, u32[]{:S(2)}) copy-start(bf16[136,1024]{1,0:T(8,128)(2,1)S(1)} %collective-permute-done.24.refs_2_.refs_7_.refs_12_) | copy-start | bytes 835588
  120.3 6.0 %copy-start.16 = (bf16[136,1024]{1,0:T(8,128)(2,1)}, bf16[136,1024]{1,0:T(8,128)(2,1)S(1)}, u32[]{:S(2)}) copy-start(bf16[136,1024]{1,0:T(8,128)(2,1)S(1)} %collective-permute-done.25.refs_3_.refs_8_.refs_13_) | copy-start | bytes 835588
  146.1 19.5 %copy-start.20 = (f32[128,1024]{1,0:T(8,128)S(1)}, f32[128,1024]{1,0:T(8,128)}, u32[]{:S(2)}) copy-start(f32[128,1024]{1,0:T(8,128)} %get-tuple-element.33) | copy-start | bytes 1572868
  146.1 15.0 %collective-permute-start.30 = (bf16[128,1024]{1,0:T(8,128)(2,1)}, bf16[128,1024]{1,0:T(8,128)(2,1)S(1)}, u32[]{:S(2)}, u32[]{:S(2)}) collective-permute-start(bf16[128,1024]{1,0:T(8,128)(2,1)} %get-tuple-element.37), channel_id=1, source_target_pairs={{4,0},{5,1},{6,2},{7,3},{12,8},{13,9},{14,10},{15,11},{20,16},{21,... | collective-permute-start | bytes 786440 | tf_op jit(solution)/shard_map/ppermute | solution.py:33
  147.5 17.9 %collective-permute-start.29 = (bf16[128,1024]{1,0:T(8,128)(2,1)}, bf16[128,1024]{1,0:T(8,128)(2,1)S(1)}, u32[]{:S(2)}, u32[]{:S(2)}) collective-permute-start(bf16[128,1024]{1,0:T(8,128)(2,1)} %get-tuple-element.36), channel_id=1, source_target_pairs={{3,0},{4,1},{5,2},{6,3},{7,4},{11,8},{12,9},{13,10},{14,11},{15,12... | collective-permute-start | bytes 786440 | tf_op jit(solution)/shard_map/ppermute | solution.py:33
  148.8 16.6 %collective-permute-start.28 = (bf16[128,1024]{1,0:T(8,128)(2,1)}, bf16[128,1024]{1,0:T(8,128)(2,1)S(1)}, u32[]{:S(2)}, u32[]{:S(2)}) collective-permute-start(bf16[128,1024]{1,0:T(8,128)(2,1)} %get-tuple-element.35), channel_id=1, source_target_pairs={{2,0},{3,1},{4,2},{5,3},{6,4},{7,5},{10,8},{11,9},{12,10},{13,11},... | collective-permute-start | bytes 786440 | tf_op jit(solution)/shard_map/ppermute | solution.py:33
  150.1 15.4 %collective-permute-start.27 = (bf16[128,1024]{1,0:T(8,128)(2,1)}, bf16[128,1024]{1,0:T(8,128)(2,1)S(1)}, u32[]{:S(2)}, u32[]{:S(2)}) collective-permute-start(bf16[128,1024]{1,0:T(8,128)(2,1)} %get-tuple-element.34), channel_id=1, source_target_pairs={{1,0},{2,1},{3,2},{4,3},{5,4},{6,5},{7,6},{9,8},{10,9},{11,10},{12... | collective-permute-start | bytes 786440 | tf_op jit(solution)/shard_map/ppermute | solution.py:33
  154.4 20.8 %collective-permute-start.33 = (bf16[2,8,128,128]{3,2,1,0:T(8,128)(2,1)}, bf16[2,8,128,128]{3,2,1,0:T(8,128)(2,1)S(1)}, u32[]{:S(2)}, u32[]{:S(2)}) collective-permute-start(bf16[2,8,128,128]{3,2,1,0:T(8,128)(2,1)} %get-tuple-element.42), channel_id=1, source_target_pairs={{0,2},{2,4},{4,6},{6,0},{1,3},{3,5},{5,7},{7,1},{8,10},{10,12},{12... | collective-permute-start | bytes 1572872 | tf_op jit(solution)/shard_map/ppermute | solution.py:27
  161.1 26.2 %collective-permute-start.34 = (bf16[2,8,128,128]{3,2,1,0:T(8,128)(2,1)}, bf16[2,8,128,128]{3,2,1,0:T(8,128)(2,1)S(1)}, u32[]{:S(2)}, u32[]{:S(2)}) collective-permute-start(bf16[2,8,128,128]{3,2,1,0:T(8,128)(2,1)} %get-tuple-element.43), channel_id=1, source_target_pairs={{0,4},{2,6},{4,0},{6,2},{1,5},{3,7},{5,1},{7,3},{8,12},{10,14},{12... | collective-permute-start | bytes 1572872 | tf_op jit(solution)/shard_map/ppermute | solution.py:27
  165.7 45.6 %copy-start.9 = (bf16[128,1024]{1,0:T(8,128)(2,1)}, bf16[128,1024]{1,0:T(8,128)(2,1)S(1)}, u32[]{:S(2)}) copy-start(bf16[128,1024]{1,0:T(8,128)(2,1)S(1)} %add_convert_fusion.mine_ref.refs_4_) | copy-start | bytes 786436
  165.7 26.4 %collective-permute-start.36 = (bf16[128,1024]{1,0:T(8,128)(2,1)S(1)}, bf16[128,1024]{1,0:T(8,128)(2,1)S(1)}, u32[]{:S(2)}, u32[]{:S(2)}) collective-permute-start(bf16[128,1024]{1,0:T(8,128)(2,1)S(1)} %add_convert_fusion.mine_ref.refs_4_), channel_id=1, source_target_pairs={{0,2},{2,4},{4,6},{6,0},{1,3},{3,5},{5,7},{7,1},{8,10},{10,12},{12... | collective-permute-start | bytes 786440 | tf_op jit(solution)/shard_map/ppermute | solution.py:27
  169.6 34.9 %collective-permute-start.35 = (bf16[2,8,128,128]{3,2,1,0:T(8,128)(2,1)}, bf16[2,8,128,128]{3,2,1,0:T(8,128)(2,1)}, u32[]{:S(2)}, u32[]{:S(2)}) collective-permute-start(bf16[2,8,128,128]{3,2,1,0:T(8,128)(2,1)} %get-tuple-element.44), channel_id=1, source_target_pairs={{0,6},{2,0},{4,2},{6,4},{1,7},{3,1},{5,3},{7,5},{8,14},{10,8},{12,... | collective-permute-start | bytes 1572872 | tf_op jit(solution)/shard_map/ppermute | solution.py:27
  169.9 28.7 %collective-permute-start.38 = (bf16[128,1024]{1,0:T(8,128)(2,1)S(1)}, bf16[128,1024]{1,0:T(8,128)(2,1)S(1)}, u32[]{:S(2)}, u32[]{:S(2)}) collective-permute-start(bf16[128,1024]{1,0:T(8,128)(2,1)S(1)} %add_convert_fusion.mine_ref.refs_4_), channel_id=1, source_target_pairs={{0,4},{2,6},{4,0},{6,2},{1,5},{3,7},{5,1},{7,3},{8,12},{10,14},{12... | collective-permute-start | bytes 786440 | tf_op jit(solution)/shard_map/ppermute | solution.py:27
  175.3 29.7 %copy-start.21 = (bf16[2,8,128,128]{3,2,1,0:T(8,128)(2,1)}, bf16[2,8,128,128]{3,2,1,0:T(8,128)(2,1)S(1)}, u32[]{:S(2)}) copy-start(bf16[2,8,128,128]{3,2,1,0:T(8,128)(2,1)S(1)} %collective-permute-done.33.refs_1_) | copy-start | bytes 1572868
  175.3 27.0 %collective-permute-start.40 = (bf16[128,1024]{1,0:T(8,128)(2,1)S(1)}, bf16[128,1024]{1,0:T(8,128)(2,1)S(1)}, u32[]{:S(2)}, u32[]{:S(2)}) collective-permute-start(bf16[128,1024]{1,0:T(8,128)(2,1)S(1)} %add_convert_fusion.mine_ref.refs_4_), channel_id=1, source_target_pairs={{0,6},{2,0},{4,2},{6,4},{1,7},{3,1},{5,3},{7,5},{8,14},{10,8},{12,... | collective-permute-start | bytes 786440 | tf_op jit(solution)/shard_map/ppermute | solution.py:27
  187.4 17.6 %copy-start.22 = (bf16[2,8,128,128]{3,2,1,0:T(8,128)(2,1)}, bf16[2,8,128,128]{3,2,1,0:T(8,128)(2,1)S(1)}, u32[]{:S(2)}) copy-start(bf16[2,8,128,128]{3,2,1,0:T(8,128)(2,1)S(1)} %collective-permute-done.34.refs_2_) | copy-start | bytes 1572868
  187.4 17.2 %collective-permute-start.31 = (bf16[128,1024]{1,0:T(8,128)(2,1)S(1)}, bf16[128,1024]{1,0:T(8,128)(2,1)S(1)}, u32[]{:S(2)}, u32[]{:S(2)}) collective-permute-start(bf16[128,1024]{1,0:T(8,128)(2,1)S(1)} %add_convert_fusion.mine_ref.refs_4_), channel_id=1, source_target_pairs={{0,8},{8,0},{1,9},{9,1},{2,10},{10,2},{3,11},{11,3},{4,12},{12,4},... | collective-permute-start | bytes 786440 | tf_op jit(solution)/shard_map/ppermute | solution.py:27
  192.1 12.4 %collective-permute-start.37 = (bf16[128,1024]{1,0:T(8,128)(2,1)S(1)}, bf16[128,1024]{1,0:T(8,128)(2,1)S(1)}, u32[]{:S(2)}, u32[]{:S(2)}) collective-permute-start(bf16[128,1024]{1,0:T(8,128)(2,1)S(1)} %collective-permute-done.36.refs_6_), channel_id=1, source_target_pairs={{0,8},{8,0},{1,9},{9,1},{2,10},{10,2},{3,11},{11,3},{4,12},{12,4},... | collective-permute-start | bytes 786440 | tf_op jit(solution)/shard_map/ppermute | solution.py:27
  198.6 6.0 %collective-permute-start.39 = (bf16[128,1024]{1,0:T(8,128)(2,1)S(1)}, bf16[128,1024]{1,0:T(8,128)(2,1)S(1)}, u32[]{:S(2)}, u32[]{:S(2)}) collective-permute-start(bf16[128,1024]{1,0:T(8,128)(2,1)S(1)} %collective-permute-done.38.refs_8_), channel_id=1, source_target_pairs={{0,8},{8,0},{1,9},{9,1},{2,10},{10,2},{3,11},{11,3},{4,12},{12,4},... | collective-permute-start | bytes 786440 | tf_op jit(solution)/shard_map/ppermute | solution.py:27
  202.2 2.8 %collective-permute-start.41 = (bf16[128,1024]{1,0:T(8,128)(2,1)S(1)}, bf16[128,1024]{1,0:T(8,128)(2,1)S(1)}, u32[]{:S(2)}, u32[]{:S(2)}) collective-permute-start(bf16[128,1024]{1,0:T(8,128)(2,1)S(1)} %collective-permute-done.40.refs_10_), channel_id=1, source_target_pairs={{0,8},{8,0},{1,9},{9,1},{2,10},{10,2},{3,11},{11,3},{4,12},{12,4},... | collective-permute-start | bytes 786440 | tf_op jit(solution)/shard_map/ppermute | solution.py:27
  204.5 6.8 %copy-start.12 = (bf16[128,1024]{1,0:T(8,128)(2,1)}, bf16[128,1024]{1,0:T(8,128)(2,1)S(1)}, u32[]{:S(2)}) copy-start(bf16[128,1024]{1,0:T(8,128)(2,1)S(1)} %collective-permute-done.31.theirs_ref.refs_5_) | copy-start | bytes 786436
  211.3 24.6 %all-to-all-start = ((bf16[16,40,1024]{2,1,0:T(8,128)(2,1)}), bf16[16,40,1024]{2,1,0:T(8,128)(2,1)S(1)}, u32[]{:S(2)}, u32[]{:S(2)}) async-start(bf16[16,40,1024]{2,1,0:T(8,128)(2,1)} %get-tuple-element.45), calls=%async_computation | async-start | bytes 2621440 | tf_op jit(solution)/shard_map/all_to_all | solution.py:594
  222.6 26.8 %collective-permute-start.32 = (bf16[32,128,128]{2,1,0:T(8,128)(2,1)}, bf16[32,128,128]{2,1,0:T(8,128)(2,1)S(1)}, u32[]{:S(2)}, u32[]{:S(2)}) collective-permute-start(bf16[32,128,128]{2,1,0:T(8,128)(2,1)} %get-tuple-element.39), channel_id=1, source_target_pairs={{0,8},{8,0},{1,9},{9,1},{2,10},{10,2},{3,11},{11,3},{4,12},{12,4},... | collective-permute-start | bytes 3145736 | tf_op jit(solution)/shard_map/ppermute | solution.py:27
  235.9 21.3 %all-to-all-start.1 = ((bf16[16,32,1024]{2,1,0:T(8,128)(2,1)}), bf16[16,32,1024]{2,1,0:T(8,128)(2,1)S(1)}, u32[]{:S(2)}, u32[]{:S(2)}) async-start(bf16[16,32,1024]{2,1,0:T(8,128)(2,1)} %get-tuple-element.48), calls=%async_computation.1 | async-start | bytes 2097152 | tf_op jit(solution)/shard_map/all_to_all | solution.py:600
  242.7 2.4 collective-permute-start.42
  245.1 10.9 %collective-permute-start.43 = (f32[2,1024]{1,0:T(2,128)S(1)}, f32[2,1024]{1,0:T(2,128)S(1)}, u32[]{:S(2)}, u32[]{:S(2)}) collective-permute-start(f32[2,1024]{1,0:T(2,128)S(1)} %maximum_select_fusion.1), channel_id=1, source_target_pairs={{0,6},{2,0},{4,2},{6,4},{1,7},{3,1},{5,3},{7,5},{8,14},{10,8},{12,... | collective-permute-start | bytes 24584 | tf_op jit(solution)/shard_map/ppermute | solution.py:27
  247.4 8.6 %collective-permute-start.44 = (f32[2,1024]{1,0:T(2,128)S(1)}, f32[2,1024]{1,0:T(2,128)S(1)}, u32[]{:S(2)}, u32[]{:S(2)}) collective-permute-start(f32[2,1024]{1,0:T(2,128)S(1)} %maximum_select_fusion.1), channel_id=1, source_target_pairs={{0,4},{2,6},{4,0},{6,2},{1,5},{3,7},{5,1},{7,3},{8,12},{10,14},{12... | collective-permute-start | bytes 24584 | tf_op jit(solution)/shard_map/ppermute | solution.py:27
  248.9 7.1 %collective-permute-start.45 = (f32[2,1024]{1,0:T(2,128)S(1)}, f32[2,1024]{1,0:T(2,128)S(1)}, u32[]{:S(2)}, u32[]{:S(2)}) collective-permute-start(f32[2,1024]{1,0:T(2,128)S(1)} %maximum_select_fusion.1), channel_id=1, source_target_pairs={{0,2},{2,4},{4,6},{6,0},{1,3},{3,5},{5,7},{7,1},{8,10},{10,12},{12... | collective-permute-start | bytes 24584 | tf_op jit(solution)/shard_map/ppermute | solution.py:27
  250.4 7.0 %slice-start = ((f32[40,1024]{1,0:T(8,128)}), f32[32,1024]{1,0:T(8,128)S(1)}, s32[]{:S(2)}) async-start(f32[40,1024]{1,0:T(8,128)} %copy-done.19), calls=%async_computation.2 | async-start | bytes 262144 | tf_op jit(solution)/shard_map/slice | solution.py:601
  (11 other events, 19.7 us)

commit v6 on v5

--- a/solution.py
+++ b/solution.py
@@ -572,7 +572,8 @@
     kv_mine, kv_theirs = project_far(table, own, other, kv_near, far)
     kv_own = finish(kv_mine, shift(kv_theirs, "core", 1), doc)
 
-    kv_blocks = [kv_own] + [shift_seq(kv_own, k) for k in range(1, BACK + 1)]
+    distant = [shift_seq(kv_own, k) for k in (3, 4)]
+    kv_blocks = [kv_own] + [shift_seq(kv_own, k) for k in (1, 2)] + distant
     columns = [shift(block, "x", by) if by else block for by, block in enumerate(blocks)]
     attended, grad_queries, grad_here, *grad_back = attention(
         doc, queries[0], grad_out[0], kv_blocks
@@ -583,7 +584,8 @@
     grad_own = total.astype(BF16)
     grad_other = shift(grad_own, "core", 1)
     grads = [grad_own, grad_other]
-    fars = [shift(grad_own, "x", by) for by in range(1, 4)]
+    opposite = shift(grad_own, "x", 2)
+    fars = [shift(grad_own, "x", 1), opposite, shift(grad_own, "x", 3)]
     for block in fars:
         grads += [block, shift(block, "core", 1)]
 

time: 262 us -> 262 us (level)
  no operation moved by 1% of the time
where the time goes in v6:
time: 262 us; the launch traced here: 258 us
  starting transfers between devices  96.2 us (37%)
  waiting for transfers between devices  84.6 us (32%)
  Pallas kernels  62.3 us (24%)
  local copies, waits for them, and re-layouts  9.71 us (4%)
  other arithmetic  4.41 us (2%)
    ppermute x37, starting transfers between devices, shift(): return lax.ppermute(value, axis, [(i, (i + by) % n) for i in range(n)])  65.8 us
    ppermute x37, waiting for transfers between devices, shift(): return lax.ppermute(value, axis, [(i, (i + by) % n) for i in range(n)])  56.8 us
    pallas_call x1, Pallas kernels, attention(): pl.pallas_call(attention_kernel, grid=(kv_heads,), in_specs=[pl.BlockSpec...  19.2 us
    ppermute x8, starting transfers between devices, shift_seq(): return lax.ppermute(value, SEQ, pairs)  16 us
    all_to_all x1, waiting for transfers between devices, step(): arrived = lax.all_to_all(halves[0], group, 0, 0, tiled=True)  13 us
    ppermute x8, waiting for transfers between devices, shift_seq(): return lax.ppermute(value, SEQ, pairs)  12.2 us
    unnamed x52, local copies, waits for them, and re-layouts  8.82 us
    pallas_call x1, Pallas kernels, grad_normed(): pl.pallas_call(grad_normed_kernel, in_specs=[pl.BlockSpec(memory_space=pl...  7.37 us
  transfers between devices with their start and end apart: 48, of which 25 were waited for; matrix products, arithmetic and copies ran while one was open for 1% of the time, Pallas kernels for 12%

profile of v6, /device:TPU:1, one launch (start us, length us, event | category | flops | bytes accessed | tf_op | source)
XLA Modules:
  0.0 258.2 jit_solution(3616849494281757444)
XLA Ops:
  0.6 4.7 %collective-permute-start.3 = (bf16[64,1024]{1,0:T(8,128)(2,1)}, bf16[64,1024]{1,0:T(8,128)(2,1)S(1)}, u32[]{:S(2)}, u32[]{:S(2)}) collective-permute-start(bf16[64,1024]{1,0:T(8,128)(2,1)} %param.12), channel_id=1, source_target_pairs={{0,65},{1,64},{64,1},{65,0},{2,67},{3,66},{66,3},{67,2},{4,69},{5,... | collective-permute-start | bytes 393224 | tf_op jit(solution)/shard_map/ppermute | solution.py:84
  5.3 1.3 collective-permute-start.1
  6.6 2.1 collective-permute-done.3
  9.6 3.0 %collective-permute-done.1 = bf16[64,1024]{1,0:T(8,128)(2,1)S(1)} collective-permute-done((bf16[64,1024]{1,0:T(8,128)(2,1)}, bf16[64,1024]{1,0:T(8,128)(2,1)S(1)}, u32[]{:S(2)}, u32[]{:S(2)}) %collective-permute-start.1) | collective-permute-done | bytes 131104 | tf_op jit(solution)/shard_map/ppermute | solution.py:27
  13.7 2.8 %collective-permute-start.4 = (bf16[256,512]{1,0:T(8,128)(2,1)S(1)}, bf16[256,512]{1,0:T(8,128)(2,1)S(1)}, u32[]{:S(2)}, u32[]{:S(2)}) collective-permute-start(bf16[256,512]{1,0:T(8,128)(2,1)S(1)} %get-tuple-element.50.refs_0_), channel_id=1, source_target_pairs={{0,48},{16,0},{32,16},{48,32},{1,49},{17,1},{33,17},{49,33},{2,50}... | collective-permute-start | bytes 786440 | tf_op jit(solution)/shard_map/ppermute | solution.py:27
  16.8 2.5 collective-permute-start.8
  20.5 1.2 collective-permute-done.4.refs_0_
  21.7 2.4 collective-permute-done.5.refs_1_
  24.9 1.2 collective-permute-start.6
  26.1 1.5 collective-permute-start.7
  28.4 4.1 %collective-permute-start.11 = (bf16[512,512]{1,0:T(8,128)(2,1)}, bf16[512,512]{1,0:T(8,128)(2,1)}, u32[]{:S(2)}, u32[]{:S(2)}) collective-permute-start(bf16[512,512]{1,0:T(8,128)(2,1)} %join.5.refs_5_), channel_id=1, source_target_pairs={{0,48},{16,0},{32,16},{48,32},{1,49},{17,1},{33,17},{49,33},{2,50}... | collective-permute-start | bytes 1572872 | tf_op jit(solution)/shard_map/ppermute | solution.py:27
  32.6 4.5 %norm.1 = (bf16[32,128,128]{2,1,0:T(8,128)(2,1)}, bf16[32,128,128]{2,1,0:T(8,128)(2,1)}, f32[128,128]{1,0:T(8,128)}) custom-call(s32[1]{0:T(128)} %bitcast.2.core_ref, bf16[128,8192]{1,0:T(8,128)(2,1)} %bitcast.18, f32[1,8192]{1,0:T(1,128)} %bitcast.23), custom_call_target="tpu_custom_call" | custom-call | tf_op jit(solution)/shard_map/norm/pallas_call | solution.py:132
  37.0 4.7 %collective-permute-start = (bf16[32,128,128]{2,1,0:T(8,128)(2,1)}, bf16[32,128,128]{2,1,0:T(8,128)(2,1)}, u32[]{:S(2)}, u32[]{:S(2)}) collective-permute-start(bf16[32,128,128]{2,1,0:T(8,128)(2,1)} %get-tuple-element.28), channel_id=1, source_target_pairs={{0,8},{8,0},{1,9},{9,1},{2,10},{10,2},{3,11},{11,3},{4,12},{12,4},... | collective-permute-start | bytes 3145736 | tf_op jit(solution)/shard_map/ppermute | solution.py:27
  42.6 8.3 %collective-permute-done.15.refs_1_ = bf16[256,512]{1,0:T(8,128)(2,1)} collective-permute-done((bf16[256,512]{1,0:T(8,128)(2,1)S(1)}, bf16[256,512]{1,0:T(8,128)(2,1)}, u32[]{:S(2)}, u32[]{:S(2)}) %collective-permute-start.15) | collective-permute-done | bytes 262176 | tf_op jit(solution)/shard_map/ppermute | solution.py:27
  50.8 1.8 join.7.refs_4_.refs_14_
  53.5 2.7 %collective-permute-start.14 = (bf16[512,512]{1,0:T(8,128)(2,1)}, bf16[512,512]{1,0:T(8,128)(2,1)}, u32[]{:S(2)}, u32[]{:S(2)}) collective-permute-start(bf16[512,512]{1,0:T(8,128)(2,1)} %join.6.refs_0_.refs_12_), channel_id=1, source_target_pairs={{0,6},{2,0},{4,2},{6,4},{1,7},{3,1},{5,3},{7,5},{8,14},{10,8},{12,... | collective-permute-start | bytes 1572872 | tf_op jit(solution)/shard_map/ppermute | solution.py:27
  56.2 2.7 %collective-permute-start.17 = (bf16[512,512]{1,0:T(8,128)(2,1)}, bf16[512,512]{1,0:T(8,128)(2,1)S(1)}, u32[]{:S(2)}, u32[]{:S(2)}) collective-permute-start(bf16[512,512]{1,0:T(8,128)(2,1)} %join.7.refs_4_.refs_14_), channel_id=1, source_target_pairs={{0,48},{16,0},{32,16},{48,32},{1,49},{17,1},{33,17},{49,33},{2,50}... | collective-permute-start | bytes 1572872 | tf_op jit(solution)/shard_map/ppermute | solution.py:27
  58.9 6.0 %collective-permute-done.13.refs_2_ = bf16[512,512]{1,0:T(8,128)(2,1)} collective-permute-done((bf16[512,512]{1,0:T(8,128)(2,1)}, bf16[512,512]{1,0:T(8,128)(2,1)}, u32[]{:S(2)}, u32[]{:S(2)}) %collective-permute-start.13) | collective-permute-done | bytes 524320 | tf_op jit(solution)/shard_map/ppermute | solution.py:27
  64.9 1.6 collective-permute-done.14.refs_3_
  66.5 3.0 %collective-permute-done.16.refs_6_.refs_15_ = bf16[512,512]{1,0:T(8,128)(2,1)S(1)} collective-permute-done((bf16[512,512]{1,0:T(8,128)(2,1)}, bf16[512,512]{1,0:T(8,128)(2,1)S(1)}, u32[]{:S(2)}, u32[]{:S(2)}) %collective-permute-start.16) | collective-permute-done | bytes 524320 | tf_op jit(solution)/shard_map/ppermute | solution.py:27
  70.0 2.7 %collective-permute-start.21 = (bf16[512,512]{1,0:T(8,128)(2,1)}, bf16[512,512]{1,0:T(8,128)(2,1)}, u32[]{:S(2)}, u32[]{:S(2)}) collective-permute-start(bf16[512,512]{1,0:T(8,128)(2,1)} %collective-permute-done.11.refs_3_.refs_11_), channel_id=1, source_target_pairs={{0,48},{16,0},{32,16},{48,32},{1,49},{17,1},{33,17},{49,33},{2,50}... | collective-permute-start | bytes 1572872 | tf_op jit(solution)/shard_map/ppermute | solution.py:27
  75.6 3.8 %project_lot.2.refs_4_ = f32[256,1024]{1,0:T(8,128)} custom-call(s32[64]{0:T(128)} %reshape.117.table_ref, bf16[32,128,128]{2,1,0:T(8,128)(2,1)S(1)} %copy-done, bf16[32,128,128]{2,1,0:T(8,128)(2,1)} %collective-permute-done.other_ref, bf16[512,512]{1,0:T(8,128)(2,1)S(1)} %copy-done.2, bf16[512,512]{1,0:T(8,128)(2,1)S(1)} %copy-done.1, ...), custom_call_target="tpu_custom_call" | custom-call | tf_op jit(solution)/shard_map/project_lot/pallas_call | solution.py:203
  79.5 1.5 collective-permute-done.10.refs_2_.refs_10_
  80.9 1.2 copy-done.8
  82.1 3.4 %project_lot.3.near_ref = f32[256,1024]{1,0:T(8,128)} custom-call(s32[64]{0:T(128)} %reshape.117.table_ref, bf16[32,128,128]{2,1,0:T(8,128)(2,1)S(1)} %copy-done, bf16[32,128,128]{2,1,0:T(8,128)(2,1)} %collective-permute-done.other_ref, bf16[512,512]{1,0:T(8,128)(2,1)S(1)} %copy-done.11, bf16[512,512]{1,0:T(8,128)(2,1)} %collective-permute-done.7.refs_1_.refs_9_, ...), custom_call_target="tpu_custom_call" | custom-call | tf_op jit(solution)/shard_map/project_lot/pallas_call | solution.py:203
  85.5 6.6 %collective-permute-done.20.refs_2_.refs_14_.refs_17_ = bf16[512,512]{1,0:T(8,128)(2,1)} collective-permute-done((bf16[512,512]{1,0:T(8,128)(2,1)S(1)}, bf16[512,512]{1,0:T(8,128)(2,1)}, u32[]{:S(2)}, u32[]{:S(2)}) %collective-permute-start.20) | collective-permute-done | bytes 524320 | tf_op jit(solution)/shard_map/ppermute | solution.py:27
  92.1 1.2 copy-done.7
  93.4 3.5 %project_far.1 = (f32[128,1024]{1,0:T(8,128)}, f32[128,1024]{1,0:T(8,128)}) custom-call(s32[64]{0:T(128)} %reshape.117.table_ref, bf16[32,128,128]{2,1,0:T(8,128)(2,1)S(1)} %copy-done, bf16[32,128,128]{2,1,0:T(8,128)(2,1)} %collective-permute-done.other_ref, f32[256,1024]{1,0:T(8,128)S(1)} %copy-done.7, ...), custom_call_target="tpu_custom_call" | custom-call | tf_op jit(solution)/shard_map/project_far/pallas_call | solution.py:229
  96.8 2.4 collective-permute-start.22
  99.7 1.2 collective-permute-done.22.other_ref
  102.0 1.4 finish.1.refs_0_.refs_5_.refs_10_
  103.4 3.6 %collective-permute-start.23 = (bf16[136,1024]{1,0:T(8,128)(2,1)}, bf16[136,1024]{1,0:T(8,128)(2,1)S(1)}, u32[]{:S(2)}, u32[]{:S(2)}) collective-permute-start(bf16[136,1024]{1,0:T(8,128)(2,1)} %finish.1.refs_0_.refs_5_.refs_10_), channel_id=1, source_target_pairs={{0,1},{1,2},{2,3},{3,4},{4,5},{5,6},{6,7},{8,9},{9,10},{10,11},{11... | collective-permute-start | bytes 835592 | tf_op jit(solution)/shard_map/ppermute | solution.py:33
  107.1 1.3 collective-permute-start.24
  108.4 4.1 %collective-permute-start.25 = (bf16[136,1024]{1,0:T(8,128)(2,1)}, bf16[136,1024]{1,0:T(8,128)(2,1)S(1)}, u32[]{:S(2)}, u32[]{:S(2)}) collective-permute-start(bf16[136,1024]{1,0:T(8,128)(2,1)} %finish.1.refs_0_.refs_5_.refs_10_), channel_id=1, source_target_pairs={{0,3},{1,4},{2,5},{3,6},{4,7},{8,11},{9,12},{10,13},{11,14},{12,15... | collective-permute-start | bytes 835592 | tf_op jit(solution)/shard_map/ppermute | solution.py:33
  112.5 1.7 collective-permute-start.26
  114.3 6.0 %collective-permute-done.25.refs_3_.refs_8_.refs_13_ = bf16[136,1024]{1,0:T(8,128)(2,1)S(1)} collective-permute-done((bf16[136,1024]{1,0:T(8,128)(2,1)}, bf16[136,1024]{1,0:T(8,128)(2,1)S(1)}, u32[]{:S(2)}, u32[]{:S(2)}) %collective-permute-start.25) | collective-permute-done | bytes 278560 | tf_op jit(solution)/shard_map/ppermute | solution.py:33
  120.3 6.0 %collective-permute-done.26.refs_4_.refs_9_.refs_14_ = bf16[136,1024]{1,0:T(8,128)(2,1)S(1)} collective-permute-done((bf16[136,1024]{1,0:T(8,128)(2,1)}, bf16[136,1024]{1,0:T(8,128)(2,1)S(1)}, u32[]{:S(2)}, u32[]{:S(2)}) %collective-permute-start.26) | collective-permute-done | bytes 278560 | tf_op jit(solution)/shard_map/ppermute | solution.py:33
  126.9 19.2 %attention.1 = (bf16[128,4096]{1,0:T(8,128)(2,1)}, bf16[128,4096]{1,0:T(8,128)(2,1)}, f32[128,1024]{1,0:T(8,128)}, bf16[128,1024]{1,0:T(8,128)(2,1)}, bf16[128,1...) custom-call(f32[1,128]{1,0:T(1,128)} %add_convert_fusion.1.doc_ref, ...), custom_call_target="tpu_custom_call" | custom-call | tf_op jit(solution)/shard_map/attention/pallas_call | solution.py:365
  146.1 1.4 collective-permute-start.30
  147.5 1.3 collective-permute-start.29
  148.8 1.3 collective-permute-start.28
  150.1 1.3 collective-permute-start.27
  151.4 3.0 %spread.1 = (bf16[2,8,128,128]{3,2,1,0:T(8,128)(2,1)}, bf16[2,8,128,128]{3,2,1,0:T(8,128)(2,1)}, bf16[2,8,128,128]{3,2,1,0:T(8,128)(2,1)}, bf16[2,8,128,128]{3,2,1,0:T(8,128)(2,1)}) custom-call(s32[1]{0:T(128)} %bitcast.8.x_ref, bf16[32,128,128]{2,1,0:T(8,128)(2,1)} %get-tuple-element.27.own_ref, bf16[32,128,128]{2,1,0:T(8,128)(2,1)} %collective-permute-done.other_ref), custom_call_target="tpu_custom_call" | custom-call | tf_op jit(solution)/shard_map/spread/pallas_call | solution.py:164
  154.4 6.7 %collective-permute-start.33 = (bf16[2,8,128,128]{3,2,1,0:T(8,128)(2,1)}, bf16[2,8,128,128]{3,2,1,0:T(8,128)(2,1)S(1)}, u32[]{:S(2)}, u32[]{:S(2)}) collective-permute-start(bf16[2,8,128,128]{3,2,1,0:T(8,128)(2,1)} %get-tuple-element.42), channel_id=1, source_target_pairs={{0,2},{2,4},{4,6},{6,0},{1,3},{3,5},{5,7},{7,1},{8,10},{10,12},{12... | collective-permute-start | bytes 1572872 | tf_op jit(solution)/shard_map/ppermute | solution.py:27
  161.1 4.3 %collective-permute-start.34 = (bf16[2,8,128,128]{3,2,1,0:T(8,128)(2,1)}, bf16[2,8,128,128]{3,2,1,0:T(8,128)(2,1)S(1)}, u32[]{:S(2)}, u32[]{:S(2)}) collective-permute-start(bf16[2,8,128,128]{3,2,1,0:T(8,128)(2,1)} %get-tuple-element.43), channel_id=1, source_target_pairs={{0,4},{2,6},{4,0},{6,2},{1,5},{3,7},{5,1},{7,3},{8,12},{10,14},{12... | collective-permute-start | bytes 1572872 | tf_op jit(solution)/shard_map/ppermute | solution.py:27
  165.7 3.8 %collective-permute-start.36 = (bf16[128,1024]{1,0:T(8,128)(2,1)S(1)}, bf16[128,1024]{1,0:T(8,128)(2,1)S(1)}, u32[]{:S(2)}, u32[]{:S(2)}) collective-permute-start(bf16[128,1024]{1,0:T(8,128)(2,1)S(1)} %add_convert_fusion.mine_ref.refs_4_), channel_id=1, source_target_pairs={{0,2},{2,4},{4,6},{6,0},{1,3},{3,5},{5,7},{7,1},{8,10},{10,12},{12... | collective-permute-start | bytes 786440 | tf_op jit(solution)/shard_map/ppermute | solution.py:27
  169.9 1.7 collective-permute-start.38
  171.6 3.7 %collective-permute-done.33.refs_1_ = bf16[2,8,128,128]{3,2,1,0:T(8,128)(2,1)S(1)} collective-permute-done((bf16[2,8,128,128]{3,2,1,0:T(8,128)(2,1)}, bf16[2,8,128,128]{3,2,1,0:T(8,128)(2,1)S(1)}, u32[]{:S(2)}, u32[]{:S(2)}) %collective-permute-start.33) | collective-permute-done | bytes 524320 | tf_op jit(solution)/shard_map/ppermute | solution.py:27
  176.4 11.0 %collective-permute-done.34.refs_2_ = bf16[2,8,128,128]{3,2,1,0:T(8,128)(2,1)S(1)} collective-permute-done((bf16[2,8,128,128]{3,2,1,0:T(8,128)(2,1)}, bf16[2,8,128,128]{3,2,1,0:T(8,128)(2,1)S(1)}, u32[]{:S(2)}, u32[]{:S(2)}) %collective-permute-start.34) | collective-permute-done | bytes 524320 | tf_op jit(solution)/shard_map/ppermute | solution.py:27
  187.4 4.4 %collective-permute-start.31 = (bf16[128,1024]{1,0:T(8,128)(2,1)S(1)}, bf16[128,1024]{1,0:T(8,128)(2,1)S(1)}, u32[]{:S(2)}, u32[]{:S(2)}) collective-permute-start(bf16[128,1024]{1,0:T(8,128)(2,1)S(1)} %add_convert_fusion.mine_ref.refs_4_), channel_id=1, source_target_pairs={{0,8},{8,0},{1,9},{9,1},{2,10},{10,2},{3,11},{11,3},{4,12},{12,4},... | collective-permute-start | bytes 786440 | tf_op jit(solution)/shard_map/ppermute | solution.py:27
  192.1 2.9 %collective-permute-start.37 = (bf16[128,1024]{1,0:T(8,128)(2,1)S(1)}, bf16[128,1024]{1,0:T(8,128)(2,1)S(1)}, u32[]{:S(2)}, u32[]{:S(2)}) collective-permute-start(bf16[128,1024]{1,0:T(8,128)(2,1)S(1)} %collective-permute-done.36.refs_6_), channel_id=1, source_target_pairs={{0,8},{8,0},{1,9},{9,1},{2,10},{10,2},{3,11},{11,3},{4,12},{12,4},... | collective-permute-start | bytes 786440 | tf_op jit(solution)/shard_map/ppermute | solution.py:27
  195.0 3.6 %collective-permute-done.38.refs_8_ = bf16[128,1024]{1,0:T(8,128)(2,1)S(1)} collective-permute-done((bf16[128,1024]{1,0:T(8,128)(2,1)S(1)}, bf16[128,1024]{1,0:T(8,128)(2,1)S(1)}, u32[]{:S(2)}, u32[]{:S(2)}) %collective-permute-start.38) | collective-permute-done | bytes 262176 | tf_op jit(solution)/shard_map/ppermute | solution.py:27
  198.6 2.4 collective-permute-start.39
  201.0 1.2 collective-permute-done.40.refs_10_
  202.2 1.6 collective-permute-start.41
  205.0 6.3 %grad_weight.1 = (bf16[16,40,1024]{2,1,0:T(8,128)(2,1)}, bf16[16,32,1024]{2,1,0:T(8,128)(2,1)}) custom-call(s32[8]{0:T(128)} %fusion.place_ref, bf16[2,8,128,128]{3,2,1,0:T(8,128)(2,1)} %get-tuple-element.41.refs_0_, bf16[2,8,128,128]{3,2,1,0:T(8,128)(2,1)} %copy-done.21, bf16[2,8,128,128]{3,2,1,0:T(8,128)(2,1)} %copy-done.22, ...), custom_call_target="tpu_custom_call" | custom-call | tf_op jit(solution)/shard_map/grad_weight/pallas_call | solution.py:522
  211.3 3.9 %all-to-all-start = ((bf16[16,40,1024]{2,1,0:T(8,128)(2,1)}), bf16[16,40,1024]{2,1,0:T(8,128)(2,1)S(1)}, u32[]{:S(2)}, u32[]{:S(2)}) async-start(bf16[16,40,1024]{2,1,0:T(8,128)(2,1)} %get-tuple-element.45), calls=%async_computation | async-start | bytes 2621440 | tf_op jit(solution)/shard_map/all_to_all | solution.py:596
  215.3 7.4 %grad_normed.1 = (bf16[32,128,128]{2,1,0:T(8,128)(2,1)}, bf16[32,128,128]{2,1,0:T(8,128)(2,1)}) custom-call(s32[64]{0:T(128)} %reshape.117.table_ref, bf16[128,1024]{1,0:T(8,128)(2,1)} %copy-done.9, bf16[128,1024]{1,0:T(8,128)(2,1)} %copy-done.12, bf16[512,512]{1,0:T(8,128)(2,1)} %join.6.refs_0_.refs_12_, bf16[512,512]{1,0:T(8,128)(2,1)} %join.4.refs_1_.refs_13_, ...), custom_call_target="tpu_custom_call" | custom-call | tf_op jit(solution)/shard_map/grad_normed/pallas_call | solution.py:419
  223.0 13.0 %all-to-all-done = bf16[16,40,1024]{2,1,0:T(8,128)(2,1)S(1)} async-done(((bf16[16,40,1024]{2,1,0:T(8,128)(2,1)}), bf16[16,40,1024]{2,1,0:T(8,128)(2,1)S(1)}, u32[]{:S(2)}, u32[]{:S(2)}) %all-to-all-start) | async-done | bytes 1310752 | tf_op jit(solution)/shard_map/all_to_all | solution.py:596
  235.9 5.8 %all-to-all-start.1 = ((bf16[16,32,1024]{2,1,0:T(8,128)(2,1)}), bf16[16,32,1024]{2,1,0:T(8,128)(2,1)S(1)}, u32[]{:S(2)}, u32[]{:S(2)}) async-start(bf16[16,32,1024]{2,1,0:T(8,128)(2,1)} %get-tuple-element.48), calls=%async_computation.1 | async-start | bytes 2097152 | tf_op jit(solution)/shard_map/all_to_all | solution.py:602
  242.7 1.6 collective-permute-start.42
  245.1 2.4 collective-permute-start.43
  247.4 1.5 collective-permute-start.44
  250.4 5.6 %norm_back.1 = bf16[128,8192]{1,0:T(8,128)(2,1)} custom-call(s32[1]{0:T(128)} %bitcast.2.core_ref, bf16[32,128,128]{2,1,0:T(8,128)(2,1)} %get-tuple-element.38.own_ref, bf16[32,128,128]{2,1,0:T(8,128)(2,1)} %copy-done.18, bf16[128,8192]{1,0:T(8,128)(2,1)} %bitcast.19, f32[128,128]{1,0:T(8,128)} %get-tuple-element.40.inv_ref, f32[1,8192]{1,0:T(1,128)} %bitcast.24), custom_call_target="tpu_custom_call" | custom-call | tf_op jit(solution)/shard_map/norm_back/pallas_call | solution.py:458
  (121 shorter events, 21.8 us)
Async XLA Ops:
  0.6 8.1 %collective-permute-start.3 = (bf16[64,1024]{1,0:T(8,128)(2,1)}, bf16[64,1024]{1,0:T(8,128)(2,1)S(1)}, u32[]{:S(2)}, u32[]{:S(2)}) collective-permute-start(bf16[64,1024]{1,0:T(8,128)(2,1)} %param.12), channel_id=1, source_target_pairs={{0,65},{1,64},{64,1},{65,0},{2,67},{3,66},{66,3},{67,2},{4,69},{5,... | collective-permute-start | bytes 393224 | tf_op jit(solution)/shard_map/ppermute | solution.py:84
  5.3 4.3 %collective-permute-start.2 = (bf16[64,1024]{1,0:T(8,128)(2,1)}, bf16[64,1024]{1,0:T(8,128)(2,1)S(1)}, u32[]{:S(2)}, u32[]{:S(2)}) collective-permute-start(bf16[64,1024]{1,0:T(8,128)(2,1)} %param.12), channel_id=1, source_target_pairs={{0,64},{64,0},{1,65},{65,1},{2,66},{66,2},{3,67},{67,3},{4,68},{68... | collective-permute-start | bytes 393224 | tf_op jit(solution)/shard_map/ppermute | solution.py:27
  5.3 7.2 %collective-permute-start.1 = (bf16[64,1024]{1,0:T(8,128)(2,1)}, bf16[64,1024]{1,0:T(8,128)(2,1)S(1)}, u32[]{:S(2)}, u32[]{:S(2)}) collective-permute-start(bf16[64,1024]{1,0:T(8,128)(2,1)} %param.12), channel_id=1, source_target_pairs={{0,1},{1,0},{2,3},{3,2},{4,5},{5,4},{6,7},{7,6},{8,9},{9,8},{10,11... | collective-permute-start | bytes 393224 | tf_op jit(solution)/shard_map/ppermute | solution.py:27
  13.7 8.0 %collective-permute-start.4 = (bf16[256,512]{1,0:T(8,128)(2,1)S(1)}, bf16[256,512]{1,0:T(8,128)(2,1)S(1)}, u32[]{:S(2)}, u32[]{:S(2)}) collective-permute-start(bf16[256,512]{1,0:T(8,128)(2,1)S(1)} %get-tuple-element.50.refs_0_), channel_id=1, source_target_pairs={{0,48},{16,0},{32,16},{48,32},{1,49},{17,1},{33,17},{49,33},{2,50}... | collective-permute-start | bytes 786440 | tf_op jit(solution)/shard_map/ppermute | solution.py:27
  16.5 7.6 %collective-permute-start.5 = (bf16[256,512]{1,0:T(8,128)(2,1)S(1)}, bf16[256,512]{1,0:T(8,128)(2,1)S(1)}, u32[]{:S(2)}, u32[]{:S(2)}) collective-permute-start(bf16[256,512]{1,0:T(8,128)(2,1)S(1)} %get-tuple-element.50.refs_0_), channel_id=1, source_target_pairs={{0,32},{16,48},{32,0},{48,16},{1,33},{17,49},{33,1},{49,17},{2,34}... | collective-permute-start | bytes 786440 | tf_op jit(solution)/shard_map/ppermute | solution.py:27
  16.8 10.7 %collective-permute-start.8 = (bf16[256,512]{1,0:T(8,128)(2,1)S(1)}, bf16[256,512]{1,0:T(8,128)(2,1)S(1)}, u32[]{:S(2)}, u32[]{:S(2)}) collective-permute-start(bf16[256,512]{1,0:T(8,128)(2,1)S(1)} %get-tuple-element.49.refs_0_), channel_id=1, source_target_pairs={{0,6},{2,0},{4,2},{6,4},{1,7},{3,1},{5,3},{7,5},{8,14},{10,8},{12,... | collective-permute-start | bytes 786440 | tf_op jit(solution)/shard_map/ppermute | solution.py:27
  19.3 8.3 %collective-permute-start.9 = (bf16[256,512]{1,0:T(8,128)(2,1)S(1)}, bf16[256,512]{1,0:T(8,128)(2,1)S(1)}, u32[]{:S(2)}, u32[]{:S(2)}) collective-permute-start(bf16[256,512]{1,0:T(8,128)(2,1)S(1)} %get-tuple-element.49.refs_0_), channel_id=1, source_target_pairs={{0,4},{2,6},{4,0},{6,2},{1,5},{3,7},{5,1},{7,3},{8,12},{10,14},{12... | collective-permute-start | bytes 786440 | tf_op jit(solution)/shard_map/ppermute | solution.py:27
  19.8 21.9 %collective-permute-start.12 = (bf16[256,512]{1,0:T(8,128)(2,1)S(1)}, bf16[256,512]{1,0:T(8,128)(2,1)S(1)}, u32[]{:S(2)}, u32[]{:S(2)}) collective-permute-start(bf16[256,512]{1,0:T(8,128)(2,1)S(1)} %get-tuple-element.50.refs_0_), channel_id=1, source_target_pairs={{0,16},{16,32},{32,48},{48,0},{1,17},{17,33},{33,49},{49,1},{2,18}... | collective-permute-start | bytes 786440 | tf_op jit(solution)/shard_map/ppermute | solution.py:27
  24.9 27.7 %collective-permute-start.6 = (bf16[512,512]{1,0:T(8,128)(2,1)}, bf16[512,512]{1,0:T(8,128)(2,1)S(1)}, u32[]{:S(2)}, u32[]{:S(2)}) collective-permute-start(bf16[512,512]{1,0:T(8,128)(2,1)} %join.4.refs_1_.refs_13_), channel_id=1, source_target_pairs={{0,2},{2,4},{4,6},{6,0},{1,3},{3,5},{5,7},{7,1},{8,10},{10,12},{12... | collective-permute-start | bytes 1572872 | tf_op jit(solution)/shard_map/ppermute | solution.py:27
  26.1 30.0 %collective-permute-start.7 = (bf16[512,512]{1,0:T(8,128)(2,1)}, bf16[512,512]{1,0:T(8,128)(2,1)}, u32[]{:S(2)}, u32[]{:S(2)}) collective-permute-start(bf16[512,512]{1,0:T(8,128)(2,1)} %join.4.refs_1_.refs_13_), channel_id=1, source_target_pairs={{0,6},{2,0},{4,2},{6,4},{1,7},{3,1},{5,3},{7,5},{8,14},{10,8},{12,... | collective-permute-start | bytes 1572872 | tf_op jit(solution)/shard_map/ppermute | solution.py:27
  28.4 27.7 %collective-permute-start.11 = (bf16[512,512]{1,0:T(8,128)(2,1)}, bf16[512,512]{1,0:T(8,128)(2,1)}, u32[]{:S(2)}, u32[]{:S(2)}) collective-permute-start(bf16[512,512]{1,0:T(8,128)(2,1)} %join.5.refs_5_), channel_id=1, source_target_pairs={{0,48},{16,0},{32,16},{48,32},{1,49},{17,1},{33,17},{49,33},{2,50}... | collective-permute-start | bytes 1572872 | tf_op jit(solution)/shard_map/ppermute | solution.py:27
  32.5 26.3 %copy-start.24 = (s32[4]{0:T(128)S(1)}, s32[4]{0:T(128)}, u32[]{:S(2)}) copy-start(s32[4]{0:T(128)} %constant.117.clone) | copy-start | bytes 52
  32.6 32.4 %copy-start.4 = (bf16[512,512]{1,0:T(8,128)(2,1)S(1)}, bf16[512,512]{1,0:T(8,128)(2,1)}, u32[]{:S(2)}) copy-start(bf16[512,512]{1,0:T(8,128)(2,1)} %join.5.refs_5_) | copy-start | bytes 1572868
  32.6 41.0 %copy-start.1 = (bf16[512,512]{1,0:T(8,128)(2,1)S(1)}, bf16[512,512]{1,0:T(8,128)(2,1)}, u32[]{:S(2)}) copy-start(bf16[512,512]{1,0:T(8,128)(2,1)} %join.4.refs_1_.refs_13_) | copy-start | bytes 1572868
  37.0 36.5 %copy-start = (bf16[32,128,128]{2,1,0:T(8,128)(2,1)S(1)}, bf16[32,128,128]{2,1,0:T(8,128)(2,1)}, u32[]{:S(2)}) copy-start(bf16[32,128,128]{2,1,0:T(8,128)(2,1)} %get-tuple-element.27.own_ref) | copy-start | bytes 3145732
  37.0 33.0 %collective-permute-start = (bf16[32,128,128]{2,1,0:T(8,128)(2,1)}, bf16[32,128,128]{2,1,0:T(8,128)(2,1)}, u32[]{:S(2)}, u32[]{:S(2)}) collective-permute-start(bf16[32,128,128]{2,1,0:T(8,128)(2,1)} %get-tuple-element.28), channel_id=1, source_target_pairs={{0,8},{8,0},{1,9},{9,1},{2,10},{10,2},{3,11},{11,3},{4,12},{12,4},... | collective-permute-start | bytes 3145736 | tf_op jit(solution)/shard_map/ppermute | solution.py:27
  41.7 9.1 %collective-permute-start.15 = (bf16[256,512]{1,0:T(8,128)(2,1)S(1)}, bf16[256,512]{1,0:T(8,128)(2,1)}, u32[]{:S(2)}, u32[]{:S(2)}) collective-permute-start(bf16[256,512]{1,0:T(8,128)(2,1)S(1)} %get-tuple-element.49.refs_0_), channel_id=1, source_target_pairs={{0,2},{2,4},{4,6},{6,0},{1,3},{3,5},{5,7},{7,1},{8,10},{10,12},{12... | collective-permute-start | bytes 786440 | tf_op jit(solution)/shard_map/ppermute | solution.py:27
  50.8 14.1 %collective-permute-start.13 = (bf16[512,512]{1,0:T(8,128)(2,1)}, bf16[512,512]{1,0:T(8,128)(2,1)}, u32[]{:S(2)}, u32[]{:S(2)}) collective-permute-start(bf16[512,512]{1,0:T(8,128)(2,1)} %join.6.refs_0_.refs_12_), channel_id=1, source_target_pairs={{0,2},{2,4},{4,6},{6,0},{1,3},{3,5},{5,7},{7,1},{8,10},{10,12},{12... | collective-permute-start | bytes 1572872 | tf_op jit(solution)/shard_map/ppermute | solution.py:27
  53.5 13.0 %collective-permute-start.14 = (bf16[512,512]{1,0:T(8,128)(2,1)}, bf16[512,512]{1,0:T(8,128)(2,1)}, u32[]{:S(2)}, u32[]{:S(2)}) collective-permute-start(bf16[512,512]{1,0:T(8,128)(2,1)} %join.6.refs_0_.refs_12_), channel_id=1, source_target_pairs={{0,6},{2,0},{4,2},{6,4},{1,7},{3,1},{5,3},{7,5},{8,14},{10,8},{12,... | collective-permute-start | bytes 1572872 | tf_op jit(solution)/shard_map/ppermute | solution.py:27
  56.2 13.4 %collective-permute-start.16 = (bf16[512,512]{1,0:T(8,128)(2,1)}, bf16[512,512]{1,0:T(8,128)(2,1)S(1)}, u32[]{:S(2)}, u32[]{:S(2)}) collective-permute-start(bf16[512,512]{1,0:T(8,128)(2,1)} %join.7.refs_4_.refs_14_), channel_id=1, source_target_pairs={{0,16},{16,32},{32,48},{48,0},{1,17},{17,33},{33,49},{49,1},{2,18}... | collective-permute-start | bytes 1572872 | tf_op jit(solution)/shard_map/ppermute | solution.py:27
  56.2 13.9 %collective-permute-start.17 = (bf16[512,512]{1,0:T(8,128)(2,1)}, bf16[512,512]{1,0:T(8,128)(2,1)S(1)}, u32[]{:S(2)}, u32[]{:S(2)}) collective-permute-start(bf16[512,512]{1,0:T(8,128)(2,1)} %join.7.refs_4_.refs_14_), channel_id=1, source_target_pairs={{0,48},{16,0},{32,16},{48,32},{1,49},{17,1},{33,17},{49,33},{2,50}... | collective-permute-start | bytes 1572872 | tf_op jit(solution)/shard_map/ppermute | solution.py:27
  64.9 16.0 %collective-permute-start.10 = (bf16[512,512]{1,0:T(8,128)(2,1)S(1)}, bf16[512,512]{1,0:T(8,128)(2,1)}, u32[]{:S(2)}, u32[]{:S(2)}) collective-permute-start(bf16[512,512]{1,0:T(8,128)(2,1)S(1)} %copy-done.4), channel_id=1, source_target_pairs={{0,16},{16,32},{32,48},{48,0},{1,17},{17,33},{33,49},{49,1},{2,18}... | collective-permute-start | bytes 1572872 | tf_op jit(solution)/shard_map/ppermute | solution.py:27
  66.5 19.0 %collective-permute-start.18 = (bf16[512,512]{1,0:T(8,128)(2,1)}, bf16[512,512]{1,0:T(8,128)(2,1)}, u32[]{:S(2)}, u32[]{:S(2)}) collective-permute-start(bf16[512,512]{1,0:T(8,128)(2,1)} %collective-permute-done.13.refs_2_), channel_id=1, source_target_pairs={{0,2},{2,4},{4,6},{6,0},{1,3},{3,5},{5,7},{7,1},{8,10},{10,12},{12... | collective-permute-start | bytes 1572872 | tf_op jit(solution)/shard_map/ppermute | solution.py:27
  69.6 9.9 %copy-start.5 = (bf16[512,512]{1,0:T(8,128)(2,1)}, bf16[512,512]{1,0:T(8,128)(2,1)S(1)}, u32[]{:S(2)}) copy-start(bf16[512,512]{1,0:T(8,128)(2,1)S(1)} %collective-permute-done.16.refs_6_.refs_15_) | copy-start | bytes 1572868
  69.6 15.9 %collective-permute-start.19 = (bf16[512,512]{1,0:T(8,128)(2,1)}, bf16[512,512]{1,0:T(8,128)(2,1)}, u32[]{:S(2)}, u32[]{:S(2)}) collective-permute-start(bf16[512,512]{1,0:T(8,128)(2,1)} %collective-permute-done.7.refs_1_.refs_9_), channel_id=1, source_target_pairs={{0,6},{2,0},{4,2},{6,4},{1,7},{3,1},{5,3},{7,5},{8,14},{10,8},{12,... | collective-permute-start | bytes 1572872 | tf_op jit(solution)/shard_map/ppermute | solution.py:27
  70.0 9.4 %copy-start.6 = (bf16[512,512]{1,0:T(8,128)(2,1)}, bf16[512,512]{1,0:T(8,128)(2,1)S(1)}, u32[]{:S(2)}) copy-start(bf16[512,512]{1,0:T(8,128)(2,1)S(1)} %collective-permute-done.17.refs_7_.refs_16_) | copy-start | bytes 1572868
  70.0 22.1 %collective-permute-start.20 = (bf16[512,512]{1,0:T(8,128)(2,1)S(1)}, bf16[512,512]{1,0:T(8,128)(2,1)}, u32[]{:S(2)}, u32[]{:S(2)}) collective-permute-start(bf16[512,512]{1,0:T(8,128)(2,1)S(1)} %collective-permute-done.16.refs_6_.refs_15_), channel_id=1, source_target_pairs={{0,16},{16,32},{32,48},{48,0},{1,17},{17,33},{33,49},{49,1},{2,18}... | collective-permute-start | bytes 1572872 | tf_op jit(solution)/shard_map/ppermute | solution.py:27
  70.0 22.1 %collective-permute-start.21 = (bf16[512,512]{1,0:T(8,128)(2,1)}, bf16[512,512]{1,0:T(8,128)(2,1)}, u32[]{:S(2)}, u32[]{:S(2)}) collective-permute-start(bf16[512,512]{1,0:T(8,128)(2,1)} %collective-permute-done.11.refs_3_.refs_11_), channel_id=1, source_target_pairs={{0,48},{16,0},{32,16},{48,32},{1,49},{17,1},{33,17},{49,33},{2,50}... | collective-permute-start | bytes 1572872 | tf_op jit(solution)/shard_map/ppermute | solution.py:27
  82.1 17.1 %copy-start.25 = (s32[1,128]{1,0:T(1,128)S(1)}, s32[1,128]{1,0:T(1,128)}, u32[]{:S(2)}) copy-start(s32[1,128]{1,0:T(1,128)} %param.11) | copy-start | bytes 1540
  96.8 4.1 %collective-permute-start.22 = (f32[128,1024]{1,0:T(8,128)}, f32[128,1024]{1,0:T(8,128)S(1)}, u32[]{:S(2)}, u32[]{:S(2)}) collective-permute-start(f32[128,1024]{1,0:T(8,128)} %get-tuple-element.30), channel_id=1, source_target_pairs={{0,8},{8,0},{1,9},{9,1},{2,10},{10,2},{3,11},{11,3},{4,12},{12,4},... | collective-permute-start | bytes 1572872 | tf_op jit(solution)/shard_map/ppermute | solution.py:27
  103.4 10.8 %collective-permute-start.23 = (bf16[136,1024]{1,0:T(8,128)(2,1)}, bf16[136,1024]{1,0:T(8,128)(2,1)S(1)}, u32[]{:S(2)}, u32[]{:S(2)}) collective-permute-start(bf16[136,1024]{1,0:T(8,128)(2,1)} %finish.1.refs_0_.refs_5_.refs_10_), channel_id=1, source_target_pairs={{0,1},{1,2},{2,3},{3,4},{4,5},{5,6},{6,7},{8,9},{9,10},{10,11},{11... | collective-permute-start | bytes 835592 | tf_op jit(solution)/shard_map/ppermute | solution.py:33
  107.1 7.2 %collective-permute-start.24 = (bf16[136,1024]{1,0:T(8,128)(2,1)}, bf16[136,1024]{1,0:T(8,128)(2,1)S(1)}, u32[]{:S(2)}, u32[]{:S(2)}) collective-permute-start(bf16[136,1024]{1,0:T(8,128)(2,1)} %finish.1.refs_0_.refs_5_.refs_10_), channel_id=1, source_target_pairs={{0,2},{1,3},{2,4},{3,5},{4,6},{5,7},{8,10},{9,11},{10,12},{11,13},... | collective-permute-start | bytes 835592 | tf_op jit(solution)/shard_map/ppermute | solution.py:33
  108.4 11.9 %collective-permute-start.25 = (bf16[136,1024]{1,0:T(8,128)(2,1)}, bf16[136,1024]{1,0:T(8,128)(2,1)S(1)}, u32[]{:S(2)}, u32[]{:S(2)}) collective-permute-start(bf16[136,1024]{1,0:T(8,128)(2,1)} %finish.1.refs_0_.refs_5_.refs_10_), channel_id=1, source_target_pairs={{0,3},{1,4},{2,5},{3,6},{4,7},{8,11},{9,12},{10,13},{11,14},{12,15... | collective-permute-start | bytes 835592 | tf_op jit(solution)/shard_map/ppermute | solution.py:33
  112.5 13.8 %collective-permute-start.26 = (bf16[136,1024]{1,0:T(8,128)(2,1)}, bf16[136,1024]{1,0:T(8,128)(2,1)S(1)}, u32[]{:S(2)}, u32[]{:S(2)}) collective-permute-start(bf16[136,1024]{1,0:T(8,128)(2,1)} %finish.1.refs_0_.refs_5_.refs_10_), channel_id=1, source_target_pairs={{0,4},{1,5},{2,6},{3,7},{8,12},{9,13},{10,14},{11,15},{16,20},{17,... | collective-permute-start | bytes 835592 | tf_op jit(solution)/shard_map/ppermute | solution.py:33
  114.2 12.0 %copy-start.14 = (bf16[136,1024]{1,0:T(8,128)(2,1)}, bf16[136,1024]{1,0:T(8,128)(2,1)S(1)}, u32[]{:S(2)}) copy-start(bf16[136,1024]{1,0:T(8,128)(2,1)S(1)} %collective-permute-done.23.refs_1_.refs_6_.refs_11_) | copy-start | bytes 835588
  114.3 11.9 %copy-start.15 = (bf16[136,1024]{1,0:T(8,128)(2,1)}, bf16[136,1024]{1,0:T(8,128)(2,1)S(1)}, u32[]{:S(2)}) copy-start(bf16[136,1024]{1,0:T(8,128)(2,1)S(1)} %collective-permute-done.24.refs_2_.refs_7_.refs_12_) | copy-start | bytes 835588
  120.3 6.0 %copy-start.16 = (bf16[136,1024]{1,0:T(8,128)(2,1)}, bf16[136,1024]{1,0:T(8,128)(2,1)S(1)}, u32[]{:S(2)}) copy-start(bf16[136,1024]{1,0:T(8,128)(2,1)S(1)} %collective-permute-done.25.refs_3_.refs_8_.refs_13_) | copy-start | bytes 835588
  146.1 19.5 %copy-start.20 = (f32[128,1024]{1,0:T(8,128)S(1)}, f32[128,1024]{1,0:T(8,128)}, u32[]{:S(2)}) copy-start(f32[128,1024]{1,0:T(8,128)} %get-tuple-element.33) | copy-start | bytes 1572868
  146.1 15.0 %collective-permute-start.30 = (bf16[128,1024]{1,0:T(8,128)(2,1)}, bf16[128,1024]{1,0:T(8,128)(2,1)S(1)}, u32[]{:S(2)}, u32[]{:S(2)}) collective-permute-start(bf16[128,1024]{1,0:T(8,128)(2,1)} %get-tuple-element.37), channel_id=1, source_target_pairs={{4,0},{5,1},{6,2},{7,3},{12,8},{13,9},{14,10},{15,11},{20,16},{21,... | collective-permute-start | bytes 786440 | tf_op jit(solution)/shard_map/ppermute | solution.py:33
  147.5 17.9 %collective-permute-start.29 = (bf16[128,1024]{1,0:T(8,128)(2,1)}, bf16[128,1024]{1,0:T(8,128)(2,1)S(1)}, u32[]{:S(2)}, u32[]{:S(2)}) collective-permute-start(bf16[128,1024]{1,0:T(8,128)(2,1)} %get-tuple-element.36), channel_id=1, source_target_pairs={{3,0},{4,1},{5,2},{6,3},{7,4},{11,8},{12,9},{13,10},{14,11},{15,12... | collective-permute-start | bytes 786440 | tf_op jit(solution)/shard_map/ppermute | solution.py:33
  148.8 16.6 %collective-permute-start.28 = (bf16[128,1024]{1,0:T(8,128)(2,1)}, bf16[128,1024]{1,0:T(8,128)(2,1)S(1)}, u32[]{:S(2)}, u32[]{:S(2)}) collective-permute-start(bf16[128,1024]{1,0:T(8,128)(2,1)} %get-tuple-element.35), channel_id=1, source_target_pairs={{2,0},{3,1},{4,2},{5,3},{6,4},{7,5},{10,8},{11,9},{12,10},{13,11},... | collective-permute-start | bytes 786440 | tf_op jit(solution)/shard_map/ppermute | solution.py:33
  150.1 15.4 %collective-permute-start.27 = (bf16[128,1024]{1,0:T(8,128)(2,1)}, bf16[128,1024]{1,0:T(8,128)(2,1)S(1)}, u32[]{:S(2)}, u32[]{:S(2)}) collective-permute-start(bf16[128,1024]{1,0:T(8,128)(2,1)} %get-tuple-element.34), channel_id=1, source_target_pairs={{1,0},{2,1},{3,2},{4,3},{5,4},{6,5},{7,6},{9,8},{10,9},{11,10},{12... | collective-permute-start | bytes 786440 | tf_op jit(solution)/shard_map/ppermute | solution.py:33
  154.4 20.8 %collective-permute-start.33 = (bf16[2,8,128,128]{3,2,1,0:T(8,128)(2,1)}, bf16[2,8,128,128]{3,2,1,0:T(8,128)(2,1)S(1)}, u32[]{:S(2)}, u32[]{:S(2)}) collective-permute-start(bf16[2,8,128,128]{3,2,1,0:T(8,128)(2,1)} %get-tuple-element.42), channel_id=1, source_target_pairs={{0,2},{2,4},{4,6},{6,0},{1,3},{3,5},{5,7},{7,1},{8,10},{10,12},{12... | collective-permute-start | bytes 1572872 | tf_op jit(solution)/shard_map/ppermute | solution.py:27
  161.1 26.2 %collective-permute-start.34 = (bf16[2,8,128,128]{3,2,1,0:T(8,128)(2,1)}, bf16[2,8,128,128]{3,2,1,0:T(8,128)(2,1)S(1)}, u32[]{:S(2)}, u32[]{:S(2)}) collective-permute-start(bf16[2,8,128,128]{3,2,1,0:T(8,128)(2,1)} %get-tuple-element.43), channel_id=1, source_target_pairs={{0,4},{2,6},{4,0},{6,2},{1,5},{3,7},{5,1},{7,3},{8,12},{10,14},{12... | collective-permute-start | bytes 1572872 | tf_op jit(solution)/shard_map/ppermute | solution.py:27
  165.7 45.6 %copy-start.9 = (bf16[128,1024]{1,0:T(8,128)(2,1)}, bf16[128,1024]{1,0:T(8,128)(2,1)S(1)}, u32[]{:S(2)}) copy-start(bf16[128,1024]{1,0:T(8,128)(2,1)S(1)} %add_convert_fusion.mine_ref.refs_4_) | copy-start | bytes 786436
  165.7 26.4 %collective-permute-start.36 = (bf16[128,1024]{1,0:T(8,128)(2,1)S(1)}, bf16[128,1024]{1,0:T(8,128)(2,1)S(1)}, u32[]{:S(2)}, u32[]{:S(2)}) collective-permute-start(bf16[128,1024]{1,0:T(8,128)(2,1)S(1)} %add_convert_fusion.mine_ref.refs_4_), channel_id=1, source_target_pairs={{0,2},{2,4},{4,6},{6,0},{1,3},{3,5},{5,7},{7,1},{8,10},{10,12},{12... | collective-permute-start | bytes 786440 | tf_op jit(solution)/shard_map/ppermute | solution.py:27
  169.6 34.9 %collective-permute-start.35 = (bf16[2,8,128,128]{3,2,1,0:T(8,128)(2,1)}, bf16[2,8,128,128]{3,2,1,0:T(8,128)(2,1)}, u32[]{:S(2)}, u32[]{:S(2)}) collective-permute-start(bf16[2,8,128,128]{3,2,1,0:T(8,128)(2,1)} %get-tuple-element.44), channel_id=1, source_target_pairs={{0,6},{2,0},{4,2},{6,4},{1,7},{3,1},{5,3},{7,5},{8,14},{10,8},{12,... | collective-permute-start | bytes 1572872 | tf_op jit(solution)/shard_map/ppermute | solution.py:27
  169.9 28.7 %collective-permute-start.38 = (bf16[128,1024]{1,0:T(8,128)(2,1)S(1)}, bf16[128,1024]{1,0:T(8,128)(2,1)S(1)}, u32[]{:S(2)}, u32[]{:S(2)}) collective-permute-start(bf16[128,1024]{1,0:T(8,128)(2,1)S(1)} %add_convert_fusion.mine_ref.refs_4_), channel_id=1, source_target_pairs={{0,4},{2,6},{4,0},{6,2},{1,5},{3,7},{5,1},{7,3},{8,12},{10,14},{12... | collective-permute-start | bytes 786440 | tf_op jit(solution)/shard_map/ppermute | solution.py:27
  175.3 29.7 %copy-start.21 = (bf16[2,8,128,128]{3,2,1,0:T(8,128)(2,1)}, bf16[2,8,128,128]{3,2,1,0:T(8,128)(2,1)S(1)}, u32[]{:S(2)}) copy-start(bf16[2,8,128,128]{3,2,1,0:T(8,128)(2,1)S(1)} %collective-permute-done.33.refs_1_) | copy-start | bytes 1572868
  175.3 27.0 %collective-permute-start.40 = (bf16[128,1024]{1,0:T(8,128)(2,1)S(1)}, bf16[128,1024]{1,0:T(8,128)(2,1)S(1)}, u32[]{:S(2)}, u32[]{:S(2)}) collective-permute-start(bf16[128,1024]{1,0:T(8,128)(2,1)S(1)} %add_convert_fusion.mine_ref.refs_4_), channel_id=1, source_target_pairs={{0,6},{2,0},{4,2},{6,4},{1,7},{3,1},{5,3},{7,5},{8,14},{10,8},{12,... | collective-permute-start | bytes 786440 | tf_op jit(solution)/shard_map/ppermute | solution.py:27
  187.4 17.6 %copy-start.22 = (bf16[2,8,128,128]{3,2,1,0:T(8,128)(2,1)}, bf16[2,8,128,128]{3,2,1,0:T(8,128)(2,1)S(1)}, u32[]{:S(2)}) copy-start(bf16[2,8,128,128]{3,2,1,0:T(8,128)(2,1)S(1)} %collective-permute-done.34.refs_2_) | copy-start | bytes 1572868
  187.4 17.2 %collective-permute-start.31 = (bf16[128,1024]{1,0:T(8,128)(2,1)S(1)}, bf16[128,1024]{1,0:T(8,128)(2,1)S(1)}, u32[]{:S(2)}, u32[]{:S(2)}) collective-permute-start(bf16[128,1024]{1,0:T(8,128)(2,1)S(1)} %add_convert_fusion.mine_ref.refs_4_), channel_id=1, source_target_pairs={{0,8},{8,0},{1,9},{9,1},{2,10},{10,2},{3,11},{11,3},{4,12},{12,4},... | collective-permute-start | bytes 786440 | tf_op jit(solution)/shard_map/ppermute | solution.py:27
  192.1 12.4 %collective-permute-start.37 = (bf16[128,1024]{1,0:T(8,128)(2,1)S(1)}, bf16[128,1024]{1,0:T(8,128)(2,1)S(1)}, u32[]{:S(2)}, u32[]{:S(2)}) collective-permute-start(bf16[128,1024]{1,0:T(8,128)(2,1)S(1)} %collective-permute-done.36.refs_6_), channel_id=1, source_target_pairs={{0,8},{8,0},{1,9},{9,1},{2,10},{10,2},{3,11},{11,3},{4,12},{12,4},... | collective-permute-start | bytes 786440 | tf_op jit(solution)/shard_map/ppermute | solution.py:27
  198.6 6.0 %collective-permute-start.39 = (bf16[128,1024]{1,0:T(8,128)(2,1)S(1)}, bf16[128,1024]{1,0:T(8,128)(2,1)S(1)}, u32[]{:S(2)}, u32[]{:S(2)}) collective-permute-start(bf16[128,1024]{1,0:T(8,128)(2,1)S(1)} %collective-permute-done.38.refs_8_), channel_id=1, source_target_pairs={{0,8},{8,0},{1,9},{9,1},{2,10},{10,2},{3,11},{11,3},{4,12},{12,4},... | collective-permute-start | bytes 786440 | tf_op jit(solution)/shard_map/ppermute | solution.py:27
  202.2 2.8 %collective-permute-start.41 = (bf16[128,1024]{1,0:T(8,128)(2,1)S(1)}, bf16[128,1024]{1,0:T(8,128)(2,1)S(1)}, u32[]{:S(2)}, u32[]{:S(2)}) collective-permute-start(bf16[128,1024]{1,0:T(8,128)(2,1)S(1)} %collective-permute-done.40.refs_10_), channel_id=1, source_target_pairs={{0,8},{8,0},{1,9},{9,1},{2,10},{10,2},{3,11},{11,3},{4,12},{12,4},... | collective-permute-start | bytes 786440 | tf_op jit(solution)/shard_map/ppermute | solution.py:27
  204.5 6.8 %copy-start.12 = (bf16[128,1024]{1,0:T(8,128)(2,1)}, bf16[128,1024]{1,0:T(8,128)(2,1)S(1)}, u32[]{:S(2)}) copy-start(bf16[128,1024]{1,0:T(8,128)(2,1)S(1)} %collective-permute-done.31.theirs_ref.refs_5_) | copy-start | bytes 786436
  211.3 24.6 %all-to-all-start = ((bf16[16,40,1024]{2,1,0:T(8,128)(2,1)}), bf16[16,40,1024]{2,1,0:T(8,128)(2,1)S(1)}, u32[]{:S(2)}, u32[]{:S(2)}) async-start(bf16[16,40,1024]{2,1,0:T(8,128)(2,1)} %get-tuple-element.45), calls=%async_computation | async-start | bytes 2621440 | tf_op jit(solution)/shard_map/all_to_all | solution.py:596
  222.6 26.8 %collective-permute-start.32 = (bf16[32,128,128]{2,1,0:T(8,128)(2,1)}, bf16[32,128,128]{2,1,0:T(8,128)(2,1)S(1)}, u32[]{:S(2)}, u32[]{:S(2)}) collective-permute-start(bf16[32,128,128]{2,1,0:T(8,128)(2,1)} %get-tuple-element.39), channel_id=1, source_target_pairs={{0,8},{8,0},{1,9},{9,1},{2,10},{10,2},{3,11},{11,3},{4,12},{12,4},... | collective-permute-start | bytes 3145736 | tf_op jit(solution)/shard_map/ppermute | solution.py:27
  235.9 21.3 %all-to-all-start.1 = ((bf16[16,32,1024]{2,1,0:T(8,128)(2,1)}), bf16[16,32,1024]{2,1,0:T(8,128)(2,1)S(1)}, u32[]{:S(2)}, u32[]{:S(2)}) async-start(bf16[16,32,1024]{2,1,0:T(8,128)(2,1)} %get-tuple-element.48), calls=%async_computation.1 | async-start | bytes 2097152 | tf_op jit(solution)/shard_map/all_to_all | solution.py:602
  242.7 2.4 collective-permute-start.42
  245.1 10.9 %collective-permute-start.43 = (f32[2,1024]{1,0:T(2,128)S(1)}, f32[2,1024]{1,0:T(2,128)S(1)}, u32[]{:S(2)}, u32[]{:S(2)}) collective-permute-start(f32[2,1024]{1,0:T(2,128)S(1)} %maximum_select_fusion.1), channel_id=1, source_target_pairs={{0,6},{2,0},{4,2},{6,4},{1,7},{3,1},{5,3},{7,5},{8,14},{10,8},{12,... | collective-permute-start | bytes 24584 | tf_op jit(solution)/shard_map/ppermute | solution.py:27
  247.4 8.6 %collective-permute-start.44 = (f32[2,1024]{1,0:T(2,128)S(1)}, f32[2,1024]{1,0:T(2,128)S(1)}, u32[]{:S(2)}, u32[]{:S(2)}) collective-permute-start(f32[2,1024]{1,0:T(2,128)S(1)} %maximum_select_fusion.1), channel_id=1, source_target_pairs={{0,4},{2,6},{4,0},{6,2},{1,5},{3,7},{5,1},{7,3},{8,12},{10,14},{12... | collective-permute-start | bytes 24584 | tf_op jit(solution)/shard_map/ppermute | solution.py:27
  248.9 7.1 %collective-permute-start.45 = (f32[2,1024]{1,0:T(2,128)S(1)}, f32[2,1024]{1,0:T(2,128)S(1)}, u32[]{:S(2)}, u32[]{:S(2)}) collective-permute-start(f32[2,1024]{1,0:T(2,128)S(1)} %maximum_select_fusion.1), channel_id=1, source_target_pairs={{0,2},{2,4},{4,6},{6,0},{1,3},{3,5},{5,7},{7,1},{8,10},{10,12},{12... | collective-permute-start | bytes 24584 | tf_op jit(solution)/shard_map/ppermute | solution.py:27
  250.4 7.0 %slice-start = ((f32[40,1024]{1,0:T(8,128)}), f32[32,1024]{1,0:T(8,128)S(1)}, s32[]{:S(2)}) async-start(f32[40,1024]{1,0:T(8,128)} %copy-done.19), calls=%async_computation.2 | async-start | bytes 262144 | tf_op jit(solution)/shard_map/slice | solution.py:603
  (11 other events, 19.7 us)
